TPU v7x, 8 devices: a whole 2x2x1 slice. The times are simulated.
8 devices in a mesh: tp: 8 (over z, y, x, core).
Axes of the slice: x: 2, y: 2, z: 1, core: 2. Of those that a mesh axis runs over, the one named last changes fastest.
Arguments:
- x_input: bfloat16 [2, 2048, 2048], P(None, 'tp')
- w_query: bfloat16 [2048, 2048], P(None, 'tp')
- w_key: bfloat16 [2048, 2048], P(None, 'tp')
- w_value: bfloat16 [2048, 2048], P(None, 'tp')
- w_out: bfloat16 [2048, 2048], P('tp')
- g_query: bfloat16 [2048], P('tp')
- g_key: bfloat16 [2048], P('tp')
- g_attn: bfloat16 [2048], replicated
- grad_y: bfloat16 [2, 2048, 2048], P(None, 'tp')
Outputs:
- output 1: bfloat16 [2, 2048, 2048], P(None, 'tp')
- output 2: bfloat16 [2, 2048, 2048], P(None, 'tp')
- output 3: bfloat16 [2048, 2048], P(None, 'tp')
- output 4: bfloat16 [2048, 2048], P(None, 'tp')
- output 5: bfloat16 [2048, 2048], P(None, 'tp')
- output 6: bfloat16 [2048, 2048], P('tp')
- output 7: bfloat16 [2048], P('tp')
- output 8: bfloat16 [2048], P('tp')
- output 9: bfloat16 [2048], replicated
All inputs are finite; a program needn't handle non-finite values.
Results may differ from a plain program's by a relative error of at most 0.0158848.
Values are sent between devices in bfloat16 or wider.
A program may use at most 1 GiB of HBM per device.

v0:
```python
import jax
import jax.numpy as jnp
from jax import lax
from jax.sharding import PartitionSpec as P

HEAD_SIZE = 128
ROPE_THETA = 500000.0
NORM_EPS = 1e-6


def rope_tables(seq_len):
    half_dim = HEAD_SIZE // 2
    inv_freq = 1.0 / (ROPE_THETA ** (jnp.arange(half_dim, dtype=jnp.float32) / half_dim))
    angles = jnp.arange(seq_len, dtype=jnp.float32)[:, None] * inv_freq[None, :]
    return jnp.cos(angles)[:, None, :], jnp.sin(angles)[:, None, :]


def rotate(values, cos_t, sin_t):
    lower_half, upper_half = jnp.split(values, 2, axis=-1)
    return jnp.concatenate([lower_half * cos_t - upper_half * sin_t, upper_half * cos_t + lower_half * sin_t], axis=-1)


def rotate_back(values, cos_t, sin_t):
    lower_half, upper_half = jnp.split(values, 2, axis=-1)
    return jnp.concatenate([lower_half * cos_t + upper_half * sin_t, upper_half * cos_t - lower_half * sin_t], axis=-1)


def local_block(x_loc, wq_loc, wk_loc, wv_loc, wo_loc, gq_loc, gk_loc, g_attn, dy_loc):
    batch_size, seq_loc, model_dim = x_loc.shape
    local_dim = wq_loc.shape[1]
    x_full = lax.all_gather(x_loc, 'tp', axis=1, tiled=True)
    seq_len = x_full.shape[1]
    head_shape = (batch_size, seq_len, local_dim // HEAD_SIZE, HEAD_SIZE)
    flat_shape = (batch_size, seq_len, local_dim)
    cos_t, sin_t = rope_tables(seq_len)
    causal = jnp.arange(seq_len)[:, None] >= jnp.arange(seq_len)[None, :]
    attn_scale = HEAD_SIZE ** -0.5
    q_raw = jnp.einsum('bsd,de->bse', x_full, wq_loc, preferred_element_type=jnp.float32)
    k_raw = jnp.einsum('bsd,de->bse', x_full, wk_loc, preferred_element_type=jnp.float32)
    v_heads = jnp.einsum('bsd,de->bse', x_full, wv_loc, preferred_element_type=jnp.float32).astype(jnp.bfloat16).reshape(head_shape)
    sq_sums = lax.psum(jnp.stack([jnp.sum(q_raw * q_raw, axis=-1), jnp.sum(k_raw * k_raw, axis=-1)]), 'tp')
    inv_rms = lax.rsqrt(sq_sums / model_dim + NORM_EPS)[..., None]
    q_unit = q_raw * inv_rms[0]
    k_unit = k_raw * inv_rms[1]
    gq_f = gq_loc.astype(jnp.float32)
    gk_f = gk_loc.astype(jnp.float32)
    q_rot = rotate((q_unit * gq_f).reshape(head_shape), cos_t, sin_t).astype(jnp.bfloat16)
    k_rot = rotate((k_unit * gk_f).reshape(head_shape), cos_t, sin_t).astype(jnp.bfloat16)
    scores = jnp.einsum('bqhd,bkhd->bhqk', q_rot, k_rot, preferred_element_type=jnp.float32) * attn_scale
    attn_probs = jax.nn.softmax(jnp.where(causal, scores, -1e30), axis=-1)
    probs_low = attn_probs.astype(jnp.bfloat16)
    attn_heads = jnp.einsum('bhqk,bkhd->bqhd', probs_low, v_heads, preferred_element_type=jnp.float32).astype(jnp.bfloat16).reshape(flat_shape)
    attn_part = jnp.einsum('bse,ed->bsd', attn_heads, wo_loc, preferred_element_type=jnp.float32)
    attn_loc = lax.psum_scatter(attn_part, 'tp', scatter_dimension=1, tiled=True)
    post_rms = lax.rsqrt(jnp.mean(attn_loc * attn_loc, axis=-1, keepdims=True) + NORM_EPS)
    normed = attn_loc * post_rms
    ga_f = g_attn.astype(jnp.float32)
    dy_f = dy_loc.astype(jnp.float32)
    y_loc = (x_loc.astype(jnp.float32) + normed * ga_f).astype(jnp.bfloat16)

    grad_ga = lax.psum(jnp.sum(dy_f * normed, axis=(0, 1)), 'tp')
    g_normed = dy_f * ga_f
    d_attn = post_rms * (g_normed - normed * jnp.mean(g_normed * normed, axis=-1, keepdims=True))
    d_attn_full = lax.all_gather(d_attn.astype(jnp.bfloat16), 'tp', axis=1, tiled=True)
    grad_wo = jnp.einsum('bse,bsd->ed', attn_heads, d_attn_full, preferred_element_type=jnp.float32)
    d_heads = jnp.einsum('bsd,ed->bse', d_attn_full, wo_loc, preferred_element_type=jnp.float32).astype(jnp.bfloat16).reshape(head_shape)
    d_probs = jnp.einsum('bqhd,bkhd->bhqk', d_heads, v_heads, preferred_element_type=jnp.float32)
    d_value = jnp.einsum('bhqk,bqhd->bkhd', probs_low, d_heads, preferred_element_type=jnp.float32).astype(jnp.bfloat16).reshape(flat_shape)
    d_scores = (attn_probs * (d_probs - jnp.sum(attn_probs * d_probs, axis=-1, keepdims=True)) * attn_scale).astype(jnp.bfloat16)
    dq_rot = jnp.einsum('bhqk,bkhd->bqhd', d_scores, k_rot, preferred_element_type=jnp.float32)
    dk_rot = jnp.einsum('bhqk,bqhd->bkhd', d_scores, q_rot, preferred_element_type=jnp.float32)
    dq_hat = rotate_back(dq_rot, cos_t, sin_t).reshape(flat_shape)
    dk_hat = rotate_back(dk_rot, cos_t, sin_t).reshape(flat_shape)
    grad_gq = jnp.sum(dq_hat * q_unit, axis=(0, 1))
    grad_gk = jnp.sum(dk_hat * k_unit, axis=(0, 1))
    dq_unit = dq_hat * gq_f
    dk_unit = dk_hat * gk_f
    unit_dots = lax.psum(jnp.stack([jnp.sum(dq_unit * q_unit, axis=-1), jnp.sum(dk_unit * k_unit, axis=-1)]), 'tp')[..., None] / model_dim
    dq_raw = (inv_rms[0] * (dq_unit - q_unit * unit_dots[0])).astype(jnp.bfloat16)
    dk_raw = (inv_rms[1] * (dk_unit - k_unit * unit_dots[1])).astype(jnp.bfloat16)
    grad_wq = jnp.einsum('bsd,bse->de', x_full, dq_raw, preferred_element_type=jnp.float32)
    grad_wk = jnp.einsum('bsd,bse->de', x_full, dk_raw, preferred_element_type=jnp.float32)
    grad_wv = jnp.einsum('bsd,bse->de', x_full, d_value, preferred_element_type=jnp.float32)
    dx_part = (jnp.einsum('bse,de->bsd', dq_raw, wq_loc, preferred_element_type=jnp.float32)
               + jnp.einsum('bse,de->bsd', dk_raw, wk_loc, preferred_element_type=jnp.float32)
               + jnp.einsum('bse,de->bsd', d_value, wv_loc, preferred_element_type=jnp.float32))
    grad_x = lax.psum_scatter(dx_part, 'tp', scatter_dimension=1, tiled=True) + dy_f
    return (y_loc, grad_x.astype(jnp.bfloat16), grad_wq.astype(jnp.bfloat16), grad_wk.astype(jnp.bfloat16),
            grad_wv.astype(jnp.bfloat16), grad_wo.astype(jnp.bfloat16), grad_gq.astype(jnp.bfloat16),
            grad_gk.astype(jnp.bfloat16), grad_ga.astype(jnp.bfloat16))


def solution(mesh):
    act_spec = P(None, 'tp', None)
    col_spec = P(None, 'tp')
    row_spec = P('tp', None)
    vec_spec = P('tp')
    in_specs = (act_spec, col_spec, col_spec, col_spec, row_spec, vec_spec, vec_spec, P(), act_spec)
    out_specs = (act_spec, act_spec, col_spec, col_spec, col_spec, row_spec, vec_spec, vec_spec, P())
    return jax.shard_map(local_block, mesh=mesh, in_specs=in_specs, out_specs=out_specs, check_vma=False)
```

profile of v0, /device:TPU:0, one launch (start us, length us, event | category | flops | bytes accessed | tf_op | source)
XLA Modules:
  0.0 1133.4 jit_solution(7917015215781033526)
XLA Ops:
  17.3 79.5 %all-gather.3.cloned.1.call-done = bf16[2,2048,2048]{2,1,0:T(8,128)(2,1)} async-done(((bf16[2,256,2048]{2,1,0:T(8,128)(2,1)}), bf16[2,2048,2048]{2,1,0:T(8,128)(2,1)}) %all-gather.3.cloned.1.call-update) | async-done | bytes 16777232 | tf_op jit(solution)/shard_map/all_gather | solution.py:31
  96.8 12.7 %multiply_reduce_fusion.4 = (f32[2,2048]{1,0:T(2,128)S(1)}, f32[2,2048,256]{1,2,0:T(8,128)}) fusion(bf16[2,2048,2048]{2,1,0:T(8,128)(2,1)} %all-gather.3.cloned.1.call-done, bf16[2048,256]{1,0:T(8,128)(2,1)} %param.11), kind=kOutput, calls=%fused_computation.53 | convolution fusion | flops 4297060352 | bytes 22036480 | tf_op jit(solution)/shard_map/bsd,de->bse/dot_general | solution.py:39
  109.5 12.8 %multiply_reduce_fusion.5 = (f32[2,2048]{1,0:T(2,128)S(1)}, f32[2,2048,256]{1,2,0:T(8,128)}) fusion(bf16[2,2048,2048]{2,1,0:T(8,128)(2,1)} %all-gather.3.cloned.1.call-done, bf16[2048,256]{1,0:T(8,128)(2,1)S(1)} %copy-done), kind=kOutput, calls=%fused_computation.54 | convolution fusion | flops 4297060352 | bytes 22036480 | tf_op jit(solution)/shard_map/bsd,de->bse/dot_general | solution.py:38
  122.3 22.4 %psum.21 = f32[2,2,2048]{2,1,0:T(2,128)S(1)} all-reduce(f32[2,2,2048]{2,1,0:T(2,128)S(1)} %pad_maximum_fusion.4), channel_id=1, replica_groups=mesh['tp'=8] {'tp'}, use_global_device_ids=true, to_apply=%region_2.0 | all-reduce | flops 8192 | bytes 65536 | tf_op jit(solution)/shard_map/psum | solution.py:41
  170.1 9.6 subtract_convert_fusion.1
  179.6 39.7 %fusion.80 = (f32[2,2,2048]{2,1,0:T(2,128)S(1)}, f32[2,2,2048,2048]{2,3,1,0:T(8,128)}) fusion(pred[2048,2048]{0,1:T(8,128)(4,1)} %iota_compare_fusion, bf16[2,2048,2,64]{3,1,2,0:T(8,128)(2,1)} %get-tuple-element.42, bf16[2,2048,2,64]{3,1,2,0:T(8,128)(2,1)} %get-tuple-element.43, bf16[2,2048,2,64]{3,1,2,0:T(8,128)(2,1)} %get-tuple-element.27, ...), kind=kOutput, calls=%fused_computation.111 | convolution fusion | flops 4370466816 | bytes 75530240 | tf_op jit(solution)/shard_map/sub | solution.py:50
  219.3 10.0 convolution_convert_fusion.1
  229.3 38.7 %fusion.36 = bf16[2,2,128,2048]{3,2,1,0:T(8,128)(2,1)S(1)} fusion(bf16[2,2048,2,128]{1,3,2,0:T(8,128)(2,1)} %bitcast.132, f32[2,2,2048]{2,1,0:T(2,128)S(1)} %get-tuple-element.54, pred[2048,2048]{0,1:T(8,128)(4,1)} %iota_compare_fusion, bf16[2,2048,2,64]{3,1,2,0:T(8,128)(2,1)} %get-tuple-element.42, bf16[2,2048,2,64]{3,1,2,0:T(8,128)(2,1)} %get-tuple-element.43, ...), kind=kOutput, calls=%fused_computation.59 | convolution fusion | flops 8683268096 | bytes 12615680 | tf_op jit(solution)/shard_map/bhqk,bkhd->bqhd/dot_general | solution.py:52
  268.0 15.1 %fusion.50 = f32[2,2048,2048]{2,1,0:T(8,128)} fusion(bf16[2,2048,256]{1,2,0:T(8,128)(2,1)S(1)} %bitcast.130, bf16[256,2048]{1,0:T(8,128)(2,1)} %param.13), kind=kOutput, calls=%fused_computation.77 | convolution fusion | flops 4294967296 | bytes 36700160 | tf_op jit(solution)/shard_map/bse,ed->bsd/dot_general | solution.py:53
  283.8 197.4 %reduce-scatter.3.cloned.1.call-done = f32[2,256,2048]{2,1,0:T(8,128)} async-done(((f32[2,2048,2048]{2,1,0:T(8,128)}), f32[2,256,2048]{2,1,0:T(8,128)}) %reduce-scatter.3.cloned.1.call-update) | async-done | bytes 4194320 | tf_op jit(solution)/shard_map/reduce_scatter | solution.py:54
  489.6 39.7 %fusion.115 = bf16[2,2,2048,2048]{2,3,1,0:T(8,128)(2,1)} fusion(f32[2,2,2048]{2,1,0:T(2,128)S(1)} %get-tuple-element.54, pred[2048,2048]{0,1:T(8,128)(4,1)} %iota_compare_fusion, bf16[2,2048,2,64]{3,1,2,0:T(8,128)(2,1)} %get-tuple-element.42, bf16[2,2048,2,64]{3,1,2,0:T(8,128)(2,1)} %get-tuple-element.43, ...), kind=kOutput, calls=%fused_computation.16.clone.clone.clone.1 | convolution fusion | flops 4387252224 | bytes 41975808 | tf_op jit(solution)/shard_map/sub | solution.py:50
  529.3 44.4 %all-gather.5.cloned.1.call-done = bf16[2,2048,2048]{2,1,0:T(8,128)(2,1)} async-done(((bf16[2,256,2048]{2,1,0:T(8,128)(2,1)}), bf16[2,2048,2048]{2,1,0:T(8,128)(2,1)}) %all-gather.5.cloned.1.call-update) | async-done | bytes 16777232 | tf_op jit(solution)/shard_map/all_gather | solution.py:64
  573.8 10.5 convolution_convert_fusion
  584.3 23.1 %fusion.81 = f32[2,2,2048,2048]{2,3,1,0:T(8,128)} fusion(bf16[2,2048,2,128]{1,3,2,0:T(8,128)(2,1)S(1)} %bitcast.124, bf16[2,2048,2,128]{1,3,2,0:T(8,128)(2,1)S(1)} %bitcast.133), kind=kOutput, calls=%fused_computation.112 | convolution fusion | flops 4294967296 | bytes 71303168 | tf_op jit(solution)/shard_map/bqhd,bkhd->bhqk/dot_general | solution.py:67
  607.5 84.4 %fusion.30 = f32[2,2048,2,128]{3,1,2,0:T(8,128)} fusion(f32[2,2,2048,2048]{2,3,1,0:T(8,128)} %fusion.81, bf16[2,2048,2,64]{3,1,2,0:T(8,128)(2,1)} %get-tuple-element.42, bf16[2,2048,2,64]{3,1,2,0:T(8,128)(2,1)} %get-tuple-element.43, f32[2,2,2048,2048]{2,3,1,0:T(8,128)} %get-tuple-element.55, f32[2,2,2048]{2,1,0:T(2,128)S(1)} %get-tuple-element.54), kind=kOutput, calls=%fused_computation.57 | convolution fusion | flops 4416612352 | bytes 140541952 | tf_op jit(solution)/shard_map/bhqk,bkhd->bqhd/dot_general | solution.py:70
  691.8 85.0 %fusion.33 = f32[2,2048,2,128]{3,1,2,0:T(8,128)} fusion(f32[2,2,2048,2048]{2,3,1,0:T(8,128)} %fusion.81, bf16[2,2048,2,64]{3,1,2,0:T(8,128)(2,1)} %get-tuple-element.27, bf16[2,2048,2,64]{3,1,2,0:T(8,128)(2,1)} %get-tuple-element.26, f32[2,2,2048,2048]{2,3,1,0:T(8,128)} %get-tuple-element.55, f32[2,2,2048]{2,1,0:T(2,128)S(1)} %get-tuple-element.54), kind=kOutput, calls=%fused_computation.58 | convolution fusion | flops 4416612352 | bytes 140541952 | tf_op jit(solution)/shard_map/bhqk,bqhd->bkhd/dot_general | solution.py:71
  776.8 17.0 %fusion.39 = bf16[2,2,128,2048]{3,2,1,0:T(8,128)(2,1)} fusion(bf16[2,2048,2,128]{1,3,2,0:T(8,128)(2,1)S(1)} %bitcast.125, bf16[2,2,2048,2048]{2,3,1,0:T(8,128)(2,1)} %fusion.115), kind=kOutput, calls=%fused_computation.60 | convolution fusion | flops 4296015872 | bytes 37748736 | tf_op jit(solution)/shard_map/bhqk,bqhd->bkhd/dot_general | solution.py:68
  793.8 11.0 multiply_add_fusion
  807.8 5.4 copy.36
  813.2 6.6 pad_maximum_fusion
  819.8 5.4 copy.32
  825.2 7.8 fusion.28
  833.1 23.0 %all-reduce = (f32[2,2,2048]{2,1,0:T(2,128)S(1)}, bf16[2048]{0:T(1024)(128)(2,1)}) all-reduce(f32[2,2,2048]{2,1,0:T(2,128)S(1)} %pad_maximum_fusion.5, f32[2048]{0:T(1024)S(1)} %copy-done.23), channel_id=1, replica_groups=mesh['tp'=8] {'tp'}, use_global_device_ids=true, to_apply=%region_11.12 | all-reduce | flops 10240 | bytes 77824 | tf_op jit(solution)/shard_map/psum | solution.py:78
  856.2 4.8 multiply_convert_fusion.2
  863.6 13.1 %fusion.56 = f32[2,2048,2048]{2,1,0:T(8,128)} fusion(bf16[2,2048,256]{1,2,0:T(8,128)(2,1)S(1)} %multiply_convert_fusion.2, bf16[2048,256]{1,0:T(8,128)(2,1)S(1)} %copy-done), kind=kOutput, calls=%fused_computation.83 | convolution fusion | flops 4294967296 | bytes 36700160 | tf_op jit(solution)/shard_map/bse,de->bsd/dot_general | solution.py:84
  876.8 13.1 %fusion.52 = f32[2,2048,2048]{2,1,0:T(8,128)} fusion(bf16[2,2048,256]{1,2,0:T(8,128)(2,1)S(1)} %multiply_convert_fusion.1, bf16[2048,256]{1,0:T(8,128)(2,1)S(1)} %copy-done.17), kind=kOutput, calls=%fused_computation.79 | convolution fusion | flops 4294967296 | bytes 36700160 | tf_op jit(solution)/shard_map/bse,de->bsd/dot_general | solution.py:85
  889.9 34.3 %add_add_fusion = f32[2,2048,2048]{2,1,0:T(8,128)} fusion(f32[2,2048,2048]{2,1,0:T(8,128)} %fusion.56, f32[2,2048,2048]{2,1,0:T(8,128)} %fusion.52, bf16[2,2048,256]{1,2,0:T(8,128)(2,1)S(1)} %bitcast.126, bf16[2048,256]{1,0:T(8,128)(2,1)} %param.12), kind=kOutput, calls=%fused_computation.8 | convolution fusion | flops 4311744512 | bytes 103809024 | tf_op jit(solution)/shard_map/bse,de->bsd/dot_general | solution.py:86
  924.2 9.2 fusion.46
  936.0 12.0 %fusion.48 = bf16[2048,256]{0,1:T(8,128)(2,1)} fusion(bf16[2,2048,256]{1,2,0:T(8,128)(2,1)} %copy-done.9, bf16[2,2048,2048]{2,1,0:T(8,128)(2,1)} %all-gather.3.cloned.1.call-done), kind=kOutput, calls=%fused_computation.73 | convolution fusion | flops 4295491584 | bytes 19922944 | tf_op jit(solution)/shard_map/bsd,bse->de/dot_general | solution.py:81
  950.2 9.2 fusion.47
  961.7 12.0 %fusion.45 = bf16[256,2048]{1,0:T(8,128)(2,1)} fusion(bf16[2,2048,256]{1,2,0:T(8,128)(2,1)} %bitcast.131, bf16[2,2048,2048]{2,1,0:T(8,128)(2,1)} %all-gather.5.cloned.1.call-done), kind=kOutput, calls=%fused_computation.70 | convolution fusion | flops 4295491584 | bytes 19922944 | tf_op jit(solution)/shard_map/bse,bsd->ed/dot_general | solution.py:65
  973.7 148.6 %reduce-scatter.5.cloned.1.call-done = f32[2,256,2048]{2,1,0:T(8,128)} async-done(((f32[2,2048,2048]{2,1,0:T(8,128)}), f32[2,256,2048]{2,1,0:T(8,128)}) %reduce-scatter.5.cloned.1.call-update) | async-done | bytes 4194320 | tf_op jit(solution)/shard_map/reduce_scatter | solution.py:87
  (97 shorter events, 61.3 us)
Async XLA Ops:
  7.2 102.3 %copy-start = (bf16[2048,256]{1,0:T(8,128)(2,1)S(1)}, bf16[2048,256]{1,0:T(8,128)(2,1)}, u32[]{:S(2)}) copy-start(bf16[2048,256]{1,0:T(8,128)(2,1)} %param.10) | copy-start | bytes 3145732
  7.2 89.6 %all-gather.3.cloned.1.call-start = ((), (), s32[]{:S(2)}) async-start(), calls=%async_computation.2 | async-start | bytes 18874368 | tf_op jit(solution)/shard_map/all_gather | solution.py:31
  7.9 473.3 %reduce-scatter.3.cloned.1.call-start = ((), (), s32[]{:S(2)}) async-start(), calls=%async_computation.3 | async-start | bytes 37748736 | tf_op jit(solution)/shard_map/reduce_scatter | solution.py:54
  8.6 136.1 %copy-start.26 = (f32[256]{0:T(256)}, f32[256]{0:T(256)S(1)}, u32[]{:S(2)}) copy-start(f32[256]{0:T(256)S(1)} %convert_element_type.88) | copy-start | bytes 3076
  9.3 148.2 %copy-start.24 = (f32[256]{0:T(256)}, f32[256]{0:T(256)S(1)}, u32[]{:S(2)}) copy-start(f32[256]{0:T(256)S(1)} %convert_element_type.89) | copy-start | bytes 3076
  13.2 156.9 %copy-start.12 = (f32[2048,64]{1,0:T(8,128)}, f32[2048,64]{1,0:T(8,128)S(1)}, u32[]{:S(2)}) copy-start(f32[2048,64]{1,0:T(8,128)S(1)} %get-tuple-element.48) | copy-start | bytes 1572868
  13.2 156.9 %copy-start.13 = (f32[2048,64]{1,0:T(8,128)}, f32[2048,64]{1,0:T(8,128)S(1)}, u32[]{:S(2)}) copy-start(f32[2048,64]{1,0:T(8,128)S(1)} %get-tuple-element.49) | copy-start | bytes 1572868
  144.7 2.8 copy-start.21
  144.7 12.7 %copy-start.19 = (f32[2,2048]{1,0:T(2,128)}, f32[2,2048]{1,0:T(2,128)S(1)}, u32[]{:S(2)}) copy-start(f32[2,2048]{1,0:T(2,128)S(1)} %get-tuple-element.47) | copy-start | bytes 49156
  179.6 39.7 %copy-start.18 = (bf16[2048,256]{1,0:T(8,128)(2,1)S(1)}, bf16[2048,256]{1,0:T(8,128)(2,1)}, u32[]{:S(2)}) copy-start(bf16[2048,256]{1,0:T(8,128)(2,1)} %param.12) | copy-start | bytes 3145732
  268.0 15.2 %copy-start.15 = (bf16[2,2,128,2048]{3,2,1,0:T(8,128)(2,1)}, bf16[2,2,128,2048]{3,2,1,0:T(8,128)(2,1)S(1)}, u32[]{:S(2)}) copy-start(bf16[2,2,128,2048]{3,2,1,0:T(8,128)(2,1)S(1)} %fusion.36) | copy-start | bytes 6291460
  283.2 200.8 %copy-start.7 = (bf16[2,256,2048]{2,1,0:T(8,128)(2,1)S(1)}, bf16[2,256,2048]{2,1,0:T(8,128)(2,1)}, u32[]{:S(2)}) copy-start(bf16[2,256,2048]{2,1,0:T(8,128)(2,1)} %param.17) | copy-start | bytes 6291460
  283.2 290.6 %all-gather.5.cloned.1.call-start = ((), (), s32[]{:S(2)}) async-start(), calls=%async_computation.4 | async-start | bytes 18874368 | tf_op jit(solution)/shard_map/all_gather | solution.py:64
  481.3 3.4 copy-start.6
  484.0 2.7 copy-start.14
  489.5 632.7 %reduce-scatter.5.cloned.1.call-start = ((), (), s32[]{:S(2)}) async-start(), calls=%async_computation.5 | async-start | bytes 37748736 | tf_op jit(solution)/shard_map/reduce_scatter | solution.py:87
  529.3 55.0 %copy-start.16 = (bf16[2,2048,256]{1,2,0:T(8,128)(2,1)S(1)}, bf16[2,2048,256]{1,2,0:T(8,128)(2,1)}, u32[]{:S(2)}) copy-start(bf16[2,2048,256]{1,2,0:T(8,128)(2,1)} %convolution_convert_fusion.1) | copy-start | bytes 6291460
  584.3 23.2 %copy-start.1 = (bf16[2,2048,256]{1,2,0:T(8,128)(2,1)}, bf16[2,2048,256]{1,2,0:T(8,128)(2,1)S(1)}, u32[]{:S(2)}) copy-start(bf16[2,2048,256]{1,2,0:T(8,128)(2,1)S(1)} %convolution_convert_fusion) | copy-start | bytes 6291460
  691.8 85.0 %copy-start.2 = (bf16[2,2048,256]{1,2,0:T(8,128)(2,1)S(1)}, bf16[2,2048,256]{1,2,0:T(8,128)(2,1)}, u32[]{:S(2)}) copy-start(bf16[2,2048,256]{1,2,0:T(8,128)(2,1)} %copy-done.1) | copy-start | bytes 6291460
  819.8 5.5 copy-start.20
  819.8 5.5 copy-start.22
  819.8 5.5 copy-start.25
  819.8 5.5 copy-start.27
  825.2 7.9 copy-start.23
  856.2 4.8 copy-start.4
  856.2 6.1 copy-start.5
  861.0 2.6 copy-start.9
  863.6 13.2 %copy-start.10 = (bf16[2,2048,256]{1,2,0:T(8,128)(2,1)}, bf16[2,2048,256]{1,2,0:T(8,128)(2,1)S(1)}, u32[]{:S(2)}) copy-start(bf16[2,2048,256]{1,2,0:T(8,128)(2,1)S(1)} %multiply_convert_fusion.1) | copy-start | bytes 6291460
  863.6 13.2 %copy-start.17 = (bf16[2048,256]{1,0:T(8,128)(2,1)S(1)}, bf16[2048,256]{1,0:T(8,128)(2,1)}, u32[]{:S(2)}) copy-start(bf16[2048,256]{1,0:T(8,128)(2,1)} %param.11) | copy-start | bytes 3145732
  876.8 13.1 %copy-start.3 = (bf16[2,2,128,2048]{3,2,1,0:T(8,128)(2,1)S(1)}, bf16[2,2,128,2048]{3,2,1,0:T(8,128)(2,1)}, u32[]{:S(2)}) copy-start(bf16[2,2,128,2048]{3,2,1,0:T(8,128)(2,1)} %fusion.39) | copy-start | bytes 6291460
  935.9 14.3 %copy-start.11 = (bf16[2,2048,256]{1,2,0:T(8,128)(2,1)S(1)}, bf16[2,2048,256]{1,2,0:T(8,128)(2,1)}, u32[]{:S(2)}) copy-start(bf16[2,2048,256]{1,2,0:T(8,128)(2,1)} %copy-done.10) | copy-start | bytes 6291460
  961.7 160.6 %copy-start.8 = (bf16[2,256,2048]{2,1,0:T(8,128)(2,1)S(1)}, bf16[2,256,2048]{2,1,0:T(8,128)(2,1)}, u32[]{:S(2)}) copy-start(bf16[2,256,2048]{2,1,0:T(8,128)(2,1)} %param.17) | copy-start | bytes 6291460
  (1 other events, 0.7 us)
Sparse Core Ops, SparseCore 0:
  9.8 86.8 all-gather.2
  283.3 197.9 reduce-scatter.2
  489.7 84.0 all-gather.4
  924.3 197.8 reduce-scatter.4
where the time goes:
time: 1140 us; the launch traced here: 1130 us
  matrix products  492 us (43%)
  waiting for transfers between devices  471 us (41%)
  other arithmetic  70.6 us (6%)
  blocking collectives  45.4 us (4%)
  local copies, waits for them, and re-layouts  40.3 us (4%)
  between operations  14.6 us (1%)
    reduce_scatter x1, waiting for transfers between devices, local_block(): lax.psum_scatter(attn_part, 'tp', scatter_dimension=1, tiled=True)  197 us
    reduce_scatter x1, waiting for transfers between devices, local_block(): lax.psum_scatter(dx_part, 'tp', scatter_dimension=1, tiled=True) + dy_f  149 us
    dot_general x1, matrix products, local_block(): jnp.einsum('bhqk,bqhd->bkhd', d_scores, q_rot, preferred_element_type=jnp...  85 us
    dot_general x1, matrix products, local_block(): jnp.einsum('bhqk,bkhd->bqhd', d_scores, k_rot, preferred_element_type=jnp...  84.4 us
    all_gather x1, waiting for transfers between devices, local_block(): x_full = lax.all_gather(x_loc, 'tp', axis=1, tiled=True)  79.5 us
    sub x2, matrix products, local_block(): attn_probs = jax.nn.softmax(jnp.where(causal, scores, -1e+30), axis=-1)  79.4 us
    all_gather x1, waiting for transfers between devices, local_block(): lax.all_gather(d_attn.astype(jnp.bfloat16), 'tp', axis=1, tiled=True)  44.4 us
    dot_general x1, matrix products, local_block(): jnp.einsum('bhqk,bkhd->bqhd', probs_low, v_heads, preferred_element_type=...  38.7 us
  transfers between devices with their start and end apart: 4, of which 4 were waited for; matrix products, arithmetic and copies ran while one was open for 9% of the time, Pallas kernels for 0%

commit v1 on v0

v1 whole, which is shorter than its diff:
```python
import functools
import math

import jax
import jax.numpy as jnp
from jax import lax
from jax.experimental import pallas as pl
from jax.experimental.pallas import tpu as pltpu
from jax.sharding import PartitionSpec as P

HD = 128
ROPE_THETA = 500000.0
EPS = 1e-6
DIM = 2048
SEQ = 2048
LOC = 256
TOK = 256
BLK = 512
NB = SEQ // BLK
NDEV = 8
SCALE = HD ** -0.5
C2 = SCALE * math.log2(math.e)
MESH = pl.DeviceIdType.MESH
BF = jnp.bfloat16
F32 = jnp.float32
VMEM_MAX = 60 * 1024 * 1024

NT = (((1,), (1,)), ((), ()))
NN = (((1,), (0,)), ((), ()))


def dot(a, b, dims=NN):
    return lax.dot_general(a, b, dims, preferred_element_type=F32)


def sds(shape, dtype):
    return jax.ShapeDtypeStruct(shape, dtype)


def cost(flops, nbytes, trans=0):
    return pl.CostEstimate(flops=int(flops), bytes_accessed=int(nbytes), transcendentals=int(trans))


def params(**kw):
    return pltpu.CompilerParams(vmem_limit_bytes=VMEM_MAX, **kw)


def peer_of(me, mask):
    core, ax, ay = me % 2, (me // 2) % 2, me // 4
    core = 1 - core if mask & 1 else core
    ax = 1 - ax if mask & 2 else ax
    ay = 1 - ay if mask & 4 else ay
    return ay * 4 + ax * 2 + core


ORDER = (6, 7, 2, 4, 3, 5, 1)


def entry_barrier(me):
    barrier = pltpu.get_barrier_semaphore()
    for mask in ORDER:
        pl.semaphore_signal(barrier, inc=1, device_id=(peer_of(me, mask),), device_id_type=MESH)
    pl.semaphore_wait(barrier, NDEV - 1)


def rope_tables():
    half = HD // 2
    inv_freq = 1.0 / (ROPE_THETA ** (jnp.arange(half, dtype=F32) / half))
    angles = jnp.arange(SEQ, dtype=F32)[:, None] * inv_freq[None, :]
    cos, sin = jnp.cos(angles), jnp.sin(angles)
    return jnp.concatenate([cos, cos], axis=1), jnp.concatenate([-sin, sin], axis=1)


def row_sums(vals):
    folded = vals[:, :HD]
    for start in range(HD, vals.shape[1], HD):
        folded = folded + vals[:, start:start + HD]
    return jnp.sum(folded.T, axis=0, keepdims=True)


def as_column(row):
    return jnp.broadcast_to(row, (HD, row.shape[1])).T


def proj_kernel(x_ref, w_ref, q_ref, k_ref, v_ref, s_ref):
    i = pl.program_id(0)
    x = x_ref[...]
    q = dot(x, w_ref[:, :LOC])
    q_ref[...] = q
    s_ref[pl.ds(i, 1), :] = row_sums(q * q)
    k = dot(x, w_ref[:, LOC:2 * LOC])
    k_ref[...] = k
    s_ref[pl.ds(i + NB, 1), :] = row_sums(k * k)
    v_ref[...] = dot(x, w_ref[:, 2 * LOC:]).astype(BF)


def project(x, w):
    row = pl.BlockSpec((BLK, LOC), lambda i: (i, 0))
    return pl.pallas_call(
        proj_kernel,
        grid=(NB,),
        in_specs=[pl.BlockSpec((BLK, DIM), lambda i: (i, 0)), pl.BlockSpec((DIM, 3 * LOC), lambda i: (0, 0))],
        out_specs=[row, row, row, pl.BlockSpec((2 * NB, BLK), lambda i: (0, 0))],
        out_shape=[sds((SEQ, LOC), F32), sds((SEQ, LOC), F32), sds((SEQ, LOC), BF), sds((2 * NB, BLK), F32)],
        compiler_params=params(dimension_semantics=("arbitrary",)),
        cost_estimate=cost(2 * SEQ * DIM * 3 * LOC, 16e6),
        name="proj",
    )(x, w)


def exchange(me, srcs, slots, send_sems, recv_sems):
    entry_barrier(me)
    copies = []
    for n, (src, slot) in enumerate(zip(srcs, slots)):
        for p, mask in enumerate(ORDER):
            copies.append(pltpu.make_async_remote_copy(
                src_ref=src, dst_ref=slot.at[p], send_sem=send_sems.at[n, p], recv_sem=recv_sems.at[n, p],
                device_id=(peer_of(me, mask),), device_id_type=MESH))
    for c in copies:
        c.start()
    for c in copies:
        c.wait()


def ordered_total(me, src, slot):
    own = src[...]
    total = jnp.zeros_like(own)
    for dev in range(NDEV):
        term = jnp.where(me == dev, own, 0.0)
        for p, mask in enumerate(ORDER):
            term = term + jnp.where(peer_of(me, mask) == dev, slot[p], 0.0)
        total = total + term
    return total


def rotated(v, cos, sin):
    out = []
    for h in range(v.shape[1] // HD):
        part = v[:, h * HD:(h + 1) * HD]
        out.append(part * cos + pltpu.roll(part, HD // 2, 1) * sin)
    return out


def norm_kernel(q_ref, k_ref, s_ref, gq_ref, gk_ref, cos_ref, sin_ref, qo_ref, ko_ref, iq_ref, ik_ref,
                slot, total, send_sems, recv_sems):
    i = pl.program_id(0)
    me = lax.axis_index('tp')

    @pl.when(i == 0)
    def _():
        exchange(me, [s_ref], [slot], send_sems, recv_sems)
        total[...] = lax.rsqrt(ordered_total(me, s_ref, slot) / DIM + EPS)

    cos, sin = cos_ref[...], sin_ref[...]
    for src, dst, inv_ref, g_ref, row in ((q_ref, qo_ref, iq_ref, gq_ref, i), (k_ref, ko_ref, ik_ref, gk_ref, i + NB)):
        inv = as_column(total[pl.ds(row, 1), :])
        inv_ref[...] = inv
        g = g_ref[...].astype(F32)
        for h in range(LOC // HD):
            sl = slice(h * HD, (h + 1) * HD)
            hat = src[:, sl] * inv * g[:, sl]
            dst[:, sl] = (hat * cos + pltpu.roll(hat, HD // 2, 1) * sin).astype(BF)


def norm_rope(q, k, s, gq, gk, cos, sin, cid):
    row = pl.BlockSpec((BLK, LOC), lambda i: (i, 0))
    half = pl.BlockSpec((BLK, HD), lambda i: (i, 0))
    gain = pl.BlockSpec((1, LOC), lambda i: (0, 0))
    return pl.pallas_call(
        norm_kernel,
        grid=(NB,),
        in_specs=[row, row, pl.BlockSpec((2 * NB, BLK), lambda i: (0, 0)), gain, gain, half, half],
        out_specs=[row, row, half, half],
        out_shape=[sds((SEQ, LOC), BF), sds((SEQ, LOC), BF), sds((SEQ, HD), F32), sds((SEQ, HD), F32)],
        scratch_shapes=[pltpu.VMEM((NDEV - 1, 2 * NB, BLK), F32), pltpu.VMEM((2 * NB, BLK), F32),
                        pltpu.SemaphoreType.DMA((1, NDEV - 1)), pltpu.SemaphoreType.DMA((1, NDEV - 1))],
        compiler_params=params(dimension_semantics=("arbitrary",), collective_id=cid, has_side_effects=True),
        cost_estimate=cost(2e9, 10e6),
        name="norm_rope",
    )(q, k, s, gq, gk, cos, sin)


def causal_mask():
    keys = lax.broadcasted_iota(jnp.int32, (BLK, BLK), 0)
    queries = lax.broadcasted_iota(jnp.int32, (BLK, BLK), 1)
    return keys <= queries


def attn_kernel(q_ref, k_ref, v_ref, o_ref, lse_ref, p_scr, vt_scr, acc_scr):
    h, qi = pl.program_id(0), pl.program_id(1)

    @pl.when(qi == 0)
    def _():
        vt_scr[...] = v_ref[...].T

    qb = q_ref[...]

    def scores(j):
        return dot(k_ref[pl.ds(pl.multiple_of(j * BLK, BLK), BLK), :], qb, NT)

    def first(j, m):
        s = scores(j)
        p_scr[j] = s
        return jnp.maximum(m, jnp.max(s.reshape(BLK // 8, 8, BLK), axis=0))

    s = jnp.where(causal_mask(), scores(qi), -1e30)
    p_scr[qi] = s
    m = lax.fori_loop(0, qi, first, jnp.max(s.reshape(BLK // 8, 8, BLK), axis=0))
    m = jnp.max(m, axis=0, keepdims=True)

    def second(j, l):
        p = jnp.exp2((p_scr[j] - m) * C2)
        p_scr[j] = p
        return l + jnp.sum(p.reshape(BLK // 8, 8, BLK), axis=0)

    l = lax.fori_loop(0, qi + 1, second, jnp.zeros((8, BLK), F32))
    l = jnp.sum(l, axis=0, keepdims=True)
    rl = 1.0 / l
    lse_ref[pl.ds(h * NB + qi, 1), :] = m * C2 + jnp.log2(l)

    acc_scr[...] = jnp.zeros_like(acc_scr)

    def third(j, carry):
        p = (p_scr[j] * rl).astype(BF)
        acc_scr[...] += dot(vt_scr[:, pl.ds(pl.multiple_of(j * BLK, BLK), BLK)], p)
        return carry

    lax.fori_loop(0, qi + 1, third, 0)
    o_ref[...] = acc_scr[...].T.astype(BF)


def attention(q, k, v):
    blk = pl.BlockSpec((BLK, HD), lambda h, i: (i, h))
    full = pl.BlockSpec((SEQ, HD), lambda h, i: (0, h))
    return pl.pallas_call(
        attn_kernel,
        grid=(2, NB),
        in_specs=[blk, full, full],
        out_specs=[blk, pl.BlockSpec((2 * NB, BLK), lambda h, i: (0, 0))],
        out_shape=[sds((SEQ, LOC), BF), sds((2 * NB, BLK), F32)],
        scratch_shapes=[pltpu.VMEM((NB, BLK, BLK), F32), pltpu.VMEM((HD, SEQ), BF), pltpu.VMEM((HD, BLK), F32)],
        compiler_params=params(dimension_semantics=("arbitrary", "arbitrary")),
        cost_estimate=cost(9e9, 6e6),
        name="attn_fwd",
    )(q, k, v)


def heads_to_tokens_kernel(src, dst, send_sems, recv_sems, own_sem):
    me = lax.axis_index('tp')
    width = src.shape[1]
    entry_barrier(me)
    here = dst.at[:, pl.ds(pl.multiple_of(me * width, width), width)]
    copies = []
    for p, mask in enumerate(ORDER):
        peer = peer_of(me, mask)
        copies.append(pltpu.make_async_remote_copy(
            src_ref=src.at[pl.ds(pl.multiple_of(peer * TOK, TOK), TOK), :], dst_ref=here,
            send_sem=send_sems.at[p], recv_sem=recv_sems.at[p], device_id=(peer,), device_id_type=MESH))
    for c in copies:
        c.start()
    own = pltpu.make_async_copy(src.at[pl.ds(pl.multiple_of(me * TOK, TOK), TOK), :], here, own_sem)
    own.start()
    own.wait()
    for c in copies:
        c.wait()


def tokens_to_heads_kernel(src, dst, send_sems, recv_sems, own_sem):
    me = lax.axis_index('tp')
    width = dst.shape[1]
    entry_barrier(me)
    here = dst.at[pl.ds(pl.multiple_of(me * TOK, TOK), TOK), :]
    copies = []
    for p, mask in enumerate(ORDER):
        peer = peer_of(me, mask)
        copies.append(pltpu.make_async_remote_copy(
            src_ref=src.at[:, pl.ds(pl.multiple_of(peer * width, width), width)], dst_ref=here,
            send_sem=send_sems.at[p], recv_sem=recv_sems.at[p], device_id=(peer,), device_id_type=MESH))
    for c in copies:
        c.start()
    own = pltpu.make_async_copy(src.at[:, pl.ds(pl.multiple_of(me * width, width), width)], here, own_sem)
    own.start()
    own.wait()
    for c in copies:
        c.wait()


def all_to_all(kernel, src, out_shape, cid):
    return pl.pallas_call(
        kernel,
        in_specs=[pl.BlockSpec(memory_space=pl.ANY)],
        out_specs=pl.BlockSpec(memory_space=pl.ANY),
        out_shape=sds(out_shape, BF),
        scratch_shapes=[pltpu.SemaphoreType.DMA((NDEV - 1,)), pltpu.SemaphoreType.DMA((NDEV - 1,)),
                        pltpu.SemaphoreType.DMA],
        compiler_params=pltpu.CompilerParams(collective_id=cid, has_side_effects=True),
        cost_estimate=cost(5e9, 2 * src.size),
        name="a2a",
    )(src)


def out_kernel(o_ref, wo_ref, x_ref, dy_ref, ga_ref, y_ref, da_ref, dh_ref, gga_ref, a_scr):
    step = DIM // NB
    o = o_ref[...]

    def fwd(j, carry):
        cols = pl.ds(pl.multiple_of(j * step, step), step)
        a_scr[:, cols] = dot(o, wo_ref[:, cols])
        return carry

    lax.fori_loop(0, NB, fwd, 0)
    a = a_scr[...]
    r = lax.rsqrt(jnp.mean(a * a, axis=-1, keepdims=True) + EPS)
    n = a * r
    ga = ga_ref[...].astype(F32)
    dy = dy_ref[...].astype(F32)
    y_ref[...] = (x_ref[...].astype(F32) + n * ga).astype(BF)
    col = jnp.sum(dy * n, axis=0, keepdims=True)
    for i in range(8):
        gga_ref[i:i + 1, :] = col[:, i * (DIM // 8):(i + 1) * (DIM // 8)]
    gn = dy * ga
    da_ref[...] = (r * (gn - n * jnp.mean(gn * n, axis=-1, keepdims=True))).astype(BF)
    da = da_ref[...]

    def bwd(j, carry):
        rows = pl.ds(pl.multiple_of(j * step, step), step)
        dh_ref[:, rows] = dot(da, wo_ref[rows, :], NT).astype(BF)
        return carry

    lax.fori_loop(0, NB, bwd, 0)


def out_block(o, wo, x, dy, ga):
    spec = pl.BlockSpec(memory_space=pltpu.VMEM)
    return pl.pallas_call(
        out_kernel,
        in_specs=[spec] * 5,
        out_specs=[spec] * 4,
        out_shape=[sds((TOK, DIM), BF), sds((TOK, DIM), BF), sds((TOK, DIM), BF), sds((8, DIM // 8), F32)],
        scratch_shapes=[pltpu.VMEM((TOK, DIM), F32)],
        compiler_params=params(),
        cost_estimate=cost(4 * TOK * DIM * DIM, 14e6),
        name="out_block",
    )(o, wo, x, dy, ga)


def attn_bwd_kernel(q_ref, k_ref, v_ref, do_ref, lse_ref, qr_ref, kr_ref, iq_ref, ik_ref, gq_ref, gk_ref, cos_ref, sin_ref,
                    dqu_ref, dku_ref, dv_ref, dots_ref, gg_ref,
                    p_scr, dp_scr, kt_scr, dqt_scr, dq_scr, dk_scr, dv_scr):
    h, qi = pl.program_id(0), pl.program_id(1)

    @pl.when(qi == 0)
    def _():
        kt_scr[...] = k_ref[...].T
        dk_scr[...] = jnp.zeros_like(dk_scr)
        dv_scr[...] = jnp.zeros_like(dv_scr)

    qb = q_ref[...]
    dob = do_ref[...]
    lse = lse_ref[pl.ds(h * NB + qi, 1), :]

    def first(j, acc, diag=False):
        rows = pl.ds(pl.multiple_of(j * BLK, BLK), BLK)
        p = jnp.exp2(dot(k_ref[rows, :], qb, NT) * C2 - lse)
        if diag:
            p = jnp.where(causal_mask(), p, 0.0)
        dp = dot(v_ref[rows, :], dob, NT)
        p_scr[j] = p
        dp_scr[j] = dp
        dv_scr[rows, :] += dot(p.astype(BF), dob)
        return acc + jnp.sum((p * dp).reshape(BLK // 8, 8, BLK), axis=0)

    acc = first(qi, jnp.zeros((8, BLK), F32), True)
    acc = lax.fori_loop(0, qi, first, acc)
    delta = jnp.sum(acc, axis=0, keepdims=True)
    dqt_scr[...] = jnp.zeros_like(dqt_scr)

    def second(j, carry):
        rows = pl.ds(pl.multiple_of(j * BLK, BLK), BLK)
        ds = (p_scr[j] * (dp_scr[j] - delta) * SCALE).astype(BF)
        dk_scr[rows, :] += dot(ds, qb)
        dqt_scr[...] += dot(kt_scr[:, rows], ds)
        return carry

    lax.fori_loop(0, qi + 1, second, 0)
    dq_scr[pl.ds(pl.multiple_of(qi * BLK, BLK), BLK), :] = dqt_scr[...].T

    @pl.when(qi == NB - 1)
    def _():
        dv_ref[...] = dv_scr[...].astype(BF)

        @pl.when(h == 0)
        def _():
            dots_ref[...] = jnp.zeros_like(dots_ref)

        gg_ref[...] = jnp.zeros_like(gg_ref)

        def tail(i, carry):
            rows = pl.ds(pl.multiple_of(i * BLK, BLK), BLK)
            cos, sin = cos_ref[rows, :], sin_ref[rows, :]
            for n, (d_scr, raw_ref, inv_ref, g_ref, out_ref) in enumerate((
                    (dq_scr, qr_ref, iq_ref, gq_ref, dqu_ref), (dk_scr, kr_ref, ik_ref, gk_ref, dku_ref))):
                d = d_scr[rows, :]
                hat = d * cos - pltpu.roll(d, HD // 2, 1) * sin
                unit = raw_ref[rows, :] * inv_ref[rows, :]
                gg_ref[n:n + 1, :] += jnp.sum(hat * unit, axis=0, keepdims=True)
                du = hat * g_ref[...].astype(F32)
                out_ref[rows, :] = du
                dots_ref[pl.ds(i + n * NB, 1), :] += row_sums(du * unit)
            return carry

        lax.fori_loop(0, NB, tail, 0)


def attention_bwd(q, k, v, do, lse, qr, kr, iq, ik, gq, gk, cos, sin):
    blk = pl.BlockSpec((BLK, HD), lambda h, i: (i, h))
    full = pl.BlockSpec((SEQ, HD), lambda h, i: (0, h))
    shared = pl.BlockSpec((SEQ, HD), lambda h, i: (0, 0))
    gain = pl.BlockSpec((1, HD), lambda h, i: (0, h))
    rows = pl.BlockSpec((2 * NB, BLK), lambda h, i: (0, 0))
    return pl.pallas_call(
        attn_bwd_kernel,
        grid=(2, NB),
        in_specs=[blk, full, full, blk, rows, full, full, shared, shared, gain, gain, shared, shared],
        out_specs=[full, full, full, rows, pl.BlockSpec((8, HD), lambda h, i: (0, h))],
        out_shape=[sds((SEQ, LOC), F32), sds((SEQ, LOC), F32), sds((SEQ, LOC), BF), sds((2 * NB, BLK), F32),
                   sds((8, LOC), F32)],
        scratch_shapes=[pltpu.VMEM((NB, BLK, BLK), F32), pltpu.VMEM((NB, BLK, BLK), F32), pltpu.VMEM((HD, SEQ), BF),
                        pltpu.VMEM((HD, BLK), F32), pltpu.VMEM((SEQ, HD), F32), pltpu.VMEM((SEQ, HD), F32),
                        pltpu.VMEM((SEQ, HD), F32)],
        compiler_params=params(dimension_semantics=("arbitrary", "arbitrary")),
        cost_estimate=cost(16e9, 16e6),
        name="attn_bwd",
    )(q, k, v, do, lse, qr, kr, iq, ik, gq, gk, cos, sin)


def norm_bwd_kernel(dqu_ref, dku_ref, dv_ref, qr_ref, kr_ref, iq_ref, ik_ref, dots_ref, ga_ref, out_ref, gga_ref,
                    slot, ga_slot, total, send_sems, recv_sems):
    i = pl.program_id(0)
    me = lax.axis_index('tp')

    @pl.when(i == 0)
    def _():
        exchange(me, [dots_ref, ga_ref], [slot, ga_slot], send_sems, recv_sems)
        total[...] = ordered_total(me, dots_ref, slot) / DIM
        gga_ref[...] = ordered_total(me, ga_ref, ga_slot)

    for n, (du_ref, raw_ref, inv_ref) in enumerate(((dqu_ref, qr_ref, iq_ref), (dku_ref, kr_ref, ik_ref))):
        dots = as_column(total[pl.ds(i + n * NB, 1), :])
        inv = inv_ref[...]
        for h in range(LOC // HD):
            sl = slice(h * HD, (h + 1) * HD)
            unit = raw_ref[:, sl] * inv
            out_ref[:, n * LOC + h * HD:n * LOC + (h + 1) * HD] = (inv * (du_ref[:, sl] - unit * dots)).astype(BF)
    out_ref[:, 2 * LOC:] = dv_ref[...]


def norm_bwd(dqu, dku, dv, qr, kr, iq, ik, dots, gga, cid):
    row = pl.BlockSpec((BLK, LOC), lambda i: (i, 0))
    half = pl.BlockSpec((BLK, HD), lambda i: (i, 0))
    rows = pl.BlockSpec((2 * NB, BLK), lambda i: (0, 0))
    gsp = pl.BlockSpec((8, DIM // 8), lambda i: (0, 0))
    return pl.pallas_call(
        norm_bwd_kernel,
        grid=(NB,),
        in_specs=[row, row, row, row, row, half, half, rows, gsp],
        out_specs=[pl.BlockSpec((BLK, 3 * LOC), lambda i: (i, 0)), gsp],
        out_shape=[sds((SEQ, 3 * LOC), BF), sds((8, DIM // 8), F32)],
        scratch_shapes=[pltpu.VMEM((NDEV - 1, 2 * NB, BLK), F32), pltpu.VMEM((NDEV - 1, 8, DIM // 8), F32),
                        pltpu.VMEM((2 * NB, BLK), F32),
                        pltpu.SemaphoreType.DMA((2, NDEV - 1)), pltpu.SemaphoreType.DMA((2, NDEV - 1))],
        compiler_params=params(dimension_semantics=("arbitrary",), collective_id=cid, has_side_effects=True),
        cost_estimate=cost(2e9, 14e6),
        name="norm_bwd",
    )(dqu, dku, dv, qr, kr, iq, ik, dots, gga)


def dx_kernel(d0_ref, d1_ref, w_ref, dy0_ref, dy1_ref, dx0_ref, dx1_ref, acc0, acc1):
    i = pl.program_id(0)

    @pl.when(i == 0)
    def _():
        acc0[...] = dy0_ref[...].astype(F32)
        acc1[...] = dy1_ref[...].astype(F32)

    w = w_ref[0]
    acc0[...] += dot(d0_ref[...], w, NT)
    acc1[...] += dot(d1_ref[...], w, NT)

    @pl.when(i == NDEV - 1)
    def _():
        dx0_ref[...] = acc0[...].astype(BF)
        dx1_ref[...] = acc1[...].astype(BF)


def dx_block(d0, d1, w, dy0, dy1):
    part = pl.BlockSpec((TOK, 3 * LOC), lambda i: (0, i))
    full = pl.BlockSpec((TOK, DIM), lambda i: (0, 0))
    return pl.pallas_call(
        dx_kernel,
        grid=(NDEV,),
        in_specs=[part, part, pl.BlockSpec((1, DIM, 3 * LOC), lambda i: (i, 0, 0)), full, full],
        out_specs=[full, full],
        out_shape=[sds((TOK, DIM), BF)] * 2,
        scratch_shapes=[pltpu.VMEM((TOK, DIM), F32)] * 2,
        compiler_params=params(dimension_semantics=("arbitrary",)),
        cost_estimate=cost(2 * 2 * TOK * DIM * 3 * DIM, 40e6),
        name="dx",
    )(d0, d1, w, dy0, dy1)


def wgrad_kernel(transposed, l0_ref, l1_ref, r0_ref, r1_ref, *rest):
    *outs, acc = rest
    i = pl.program_id(0)

    @pl.when(i == 0)
    def _():
        acc[...] = jnp.zeros_like(acc)

    @pl.when(i < NB)
    def _():
        acc[...] += dot(l0_ref[...].T, r0_ref[...])

    @pl.when(i >= NB)
    def _():
        acc[...] += dot(l1_ref[...].T, r1_ref[...])

    @pl.when(i == 2 * NB - 1)
    def _():
        for n, out in enumerate(outs):
            part = acc[n * LOC:(n + 1) * LOC, :]
            out[...] = (part.T if transposed else part).astype(BF)


def wgrad(left, right, transposed):
    width = left[0].shape[1]
    count = width // LOC
    first = lambda i: (jnp.minimum(i, NB - 1), 0)
    second = lambda i: (jnp.maximum(i - NB, 0), 0)
    shape = (DIM, LOC) if transposed else (LOC, DIM)
    return pl.pallas_call(
        functools.partial(wgrad_kernel, transposed),
        grid=(2 * NB,),
        in_specs=[pl.BlockSpec((BLK, width), first), pl.BlockSpec((BLK, width), second),
                  pl.BlockSpec((BLK, DIM), first), pl.BlockSpec((BLK, DIM), second)],
        out_specs=[pl.BlockSpec(shape, lambda i: (0, 0))] * count,
        out_shape=[sds(shape, BF)] * count,
        scratch_shapes=[pltpu.VMEM((width, DIM), F32)],
        compiler_params=params(dimension_semantics=("arbitrary",)),
        cost_estimate=cost(2 * 2 * SEQ * width * DIM, 20e6),
        name="wgrad",
    )(*left, *right)


def local_block(x_loc, wq, wk, wv, wo, gq, gk, ga, dy_loc):
    gather = functools.partial(lax.all_gather, axis_name='tp')
    w_loc = jnp.concatenate([wq, wk, wv], axis=1)
    gq, gk, ga = gq[None, :], gk[None, :], ga[None, :]
    cos, sin = rope_tables()
    xs, dys = [x_loc[0], x_loc[1]], [dy_loc[0], dy_loc[1]]
    x_full = []
    for b in range(2):
        src = xs[b] if b == 0 else lax.optimization_barrier((xs[b], x_full[0][:8, :HD]))[0]
        x_full.append(gather(xs[b], axis=0, tiled=True))
    wo_src = lax.optimization_barrier((wo, x_full[1][:8, :HD]))[0]
    wo_full = gather(wo_src, axis=0, tiled=True)
    w_src = lax.optimization_barrier((w_loc, wo_full[:8, :HD]))[0]
    w_full = gather(w_src, axis=0, tiled=False)

    fwd, o_recv = [], []
    for b in range(2):
        q_raw, k_raw, v, s = project(x_full[b], w_loc)
        q_rot, k_rot, iq, ik = norm_rope(q_raw, k_raw, s, gq, gk, cos, sin, 1 + b)
        o, lse = attention(q_rot, k_rot, v)
        o_recv.append(all_to_all(heads_to_tokens_kernel, o, (TOK, DIM), 3 + b))
        fwd.append((q_raw, k_raw, v, q_rot, k_rot, iq, ik, o, lse))
    ys, das, dhs, ggas = [], [], [], []
    for b in range(2):
        y, da, dh, gga = out_block(o_recv[b], wo_full, xs[b], dys[b], ga)
        ys.append(y)
        das.append(da)
        dhs.append(all_to_all(tokens_to_heads_kernel, dh, (SEQ, LOC), 5 + b))
        ggas.append(gga)
    da_full = [gather(das[b], axis=0, tiled=True) for b in range(2)]
    ds, d_recv, gga_sum, ggs = [], [], [], []
    for b in range(2):
        q_raw, k_raw, v, q_rot, k_rot, iq, ik, o, lse = fwd[b]
        dqu, dku, dv, dots, gg = attention_bwd(q_rot, k_rot, v, dhs[b], lse, q_raw, k_raw, iq, ik, gq, gk, cos, sin)
        d, gsum = norm_bwd(dqu, dku, dv, q_raw, k_raw, iq, ik, dots, ggas[b], 7 + b)
        ds.append(d)
        gga_sum.append(gsum)
        ggs.append(gg)
        d_recv.append(all_to_all(heads_to_tokens_kernel, d, (TOK, 3 * DIM), 9 + b))
    gwq, gwk, gwv = wgrad(ds, x_full, True)
    gwo, = wgrad([fwd[0][7], fwd[1][7]], da_full, False)
    dx0, dx1 = dx_block(d_recv[0], d_recv[1], w_full, dys[0], dys[1])
    gg = ggs[0] + ggs[1]
    grad_ga = (gga_sum[0] + gga_sum[1]).reshape(DIM).astype(BF)
    return (jnp.stack(ys), jnp.stack([dx0, dx1]), gwq, gwk, gwv, gwo, gg[0].astype(BF), gg[1].astype(BF), grad_ga)


def solution(mesh):
    act, col, row, vec = P(None, 'tp', None), P(None, 'tp'), P('tp', None), P('tp')
    in_specs = (act, col, col, col, row, vec, vec, P(), act)
    out_specs = (act, act, col, col, col, row, vec, vec, P())
    return jax.shard_map(local_block, mesh=mesh, in_specs=in_specs, out_specs=out_specs, check_vma=False)
```

time: 1140 us -> 570 us (0.50)
  matrix products: 492 us -> 0 us
  Pallas kernels: 0 us -> 453 us
  waiting for transfers between devices: 471 us -> 79.2 us
  other arithmetic: 70.6 us -> 11.1 us
  blocking collectives: 45.4 us -> 0 us
  local copies, waits for them, and re-layouts: 40.3 us -> 11 us
    pallas_call x0 -> x21, Pallas kernels: none -> 453 us  [the longest x6 201 us: all_to_all(): pl.pallas_call(kernel, in_specs=[pl.BlockSpec(memory_space=pl.ANY)], out_...]
    dot_general x17 -> x0, matrix products: 412 us -> none  [the longest x1 85 us: local_block(): jnp.einsum('bhqk,bqhd->bkhd', d_scores, q_rot, preferred_element_type=jnp...]
    reduce_scatter x2 -> x0, waiting for transfers between devices: 346 us -> none  [the longest x1 197 us: local_block(): lax.psum_scatter(attn_part, 'tp', scatter_dimension=1, tiled=True)]
    sub x2 -> x0, matrix products: 79.4 us -> none  [local_block(): attn_probs = jax.nn.softmax(jnp.where(causal, scores, -1e+30), axis=-1)]
    all_gather x2 -> x6, waiting for transfers between devices: 124 us -> 77.3 us  [the longest x2 75.4 us: local_block(): x_full.append(gather(xs[b], axis=0, tiled=True))]
    psum x2 -> x0, blocking collectives: 45.4 us -> none  [the longest x1 23 us: local_block(): lax.psum(jnp.stack([jnp.sum(dq_unit * q_unit, axis=-1), jnp.sum(dk_unit *...]
    unnamed x65 -> x25, local copies, waits for them, and re-layouts: 24.9 us -> 3.33 us
    convert_element_type x7 -> x0, other arithmetic: 14.4 us -> none  [the longest x1 4.78 us: local_block(): (inv_rms[0] * (dq_unit - q_unit * unit_dots[0])).astype(jnp.bfloat16)]
  transfers between devices with their start and end apart: 4 -> 6, of which waited for: 4 -> 3; matrix products, arithmetic and copies ran while one was open for 9% -> 3% of each run, Pallas kernels for 0% -> 76%
where the time goes in v1:
time: 570 us; the launch traced here: 569 us
  Pallas kernels  453 us (79%)
  waiting for transfers between devices  79.2 us (14%)
  between operations  14.3 us (3%)
  other arithmetic  11.1 us (2%)
  local copies, waits for them, and re-layouts  11 us (2%)
    pallas_call x6, Pallas kernels, all_to_all(): pl.pallas_call(kernel, in_specs=[pl.BlockSpec(memory_space=pl.ANY)], out_...  201 us
    all_gather x2, waiting for transfers between devices, local_block(): x_full.append(gather(xs[b], axis=0, tiled=True))  75.4 us
    pallas_call x2, Pallas kernels, attention_bwd(): pl.pallas_call(attn_bwd_kernel, grid=(2, NB), in_specs=[blk, full, full,...  59.7 us
    pallas_call x2, Pallas kernels, attention(): pl.pallas_call(attn_kernel, grid=(2, NB), in_specs=[blk, full, full], out...  34.9 us
    pallas_call x2, Pallas kernels, wgrad(): pl.pallas_call(functools.partial(wgrad_kernel, transposed), grid=(2 * NB,...  33.5 us
    pallas_call x2, Pallas kernels, norm_bwd(): pl.pallas_call(norm_bwd_kernel, grid=(NB,), in_specs=[row, row, row, row,...  30.4 us
    pallas_call x2, Pallas kernels, out_block(): pl.pallas_call(out_kernel, in_specs=[spec] * 5, out_specs=[spec] * 4, out...  25.9 us
    pallas_call x2, Pallas kernels, norm_rope(): pl.pallas_call(norm_kernel, grid=(NB,), in_specs=[row, row, pl.BlockSpec(...  24.7 us
  transfers between devices with their start and end apart: 6, of which 3 were waited for; matrix products, arithmetic and copies ran while one was open for 3% of the time, Pallas kernels for 76%

profile of v1, /device:TPU:0, one launch (start us, length us, event | category | flops | bytes accessed | tf_op | source)
XLA Modules:
  0.0 568.8 jit_solution(2536428878548022688)
XLA Ops:
  7.2 3.8 slice_bitcast_fusion.3
  14.4 1.4 constant_dynamic-update-slice_fusion.2
  15.8 1.3 constant_dynamic-update-slice_fusion.1
  17.2 3.9 fusion.2
  21.1 2.0 pad_maximum_fusion.2
  23.1 1.5 slice_bitcast_fusion.1
  24.6 37.8 %all-gather.16.cloned.1.call-done = bf16[1,2048,2048]{2,1,0:T(8,128)(2,1)} async-done(((bf16[1,256,2048]{2,1,0:T(8,128)(2,1)}), bf16[1,2048,2048]{2,1,0:T(8,128)(2,1)}) %all-gather.16.cloned.1.call-update) | async-done | bytes 8388624 | tf_op jit(solution)/shard_map/all_gather | solution.py:564
  62.4 11.0 %proj.2 = (f32[2048,256]{1,0:T(8,128)}, f32[2048,256]{1,0:T(8,128)}, bf16[2048,256]{1,0:T(8,128)(2,1)}, f32[8,512]{1,0:T(8,128)}) custom-call(bf16[2048,2048]{1,0:T(8,128)(2,1)} %bitcast.24, bf16[2048,768]{1,0:T(8,128)(2,1)} %copy-done), custom_call_target="tpu_custom_call" | custom-call | flops 6442450944 | bytes 16000000 | tf_op jit(solution)/shard_map/proj/pallas_call | solution.py:99
  73.4 12.3 %norm_rope.2 = (bf16[2048,256]{1,0:T(8,128)(2,1)}, bf16[2048,256]{1,0:T(8,128)(2,1)}, f32[2048,128]{1,0:T(8,128)}, f32[2048,128]{1,0:T(8,128)}) custom-call(f32[2048,256]{1,0:T(8,128)} %get-tuple-element.56.q_ref.qr_ref, f32[2048,256]{1,0:T(8,128)} %get-tuple-element.57.k_ref.kr_ref, f32[8,512]{1,0:T(8,128)} %get-tuple-element.58.s_ref, ...), custom_call_target="tpu_custom_call" | custom-call | flops 2000000000 | bytes 10000000 | tf_op jit(solution)/shard_map/norm_rope/pallas_call | solution.py:169
  85.7 17.4 %attn_fwd.2 = (bf16[2048,256]{1,0:T(8,128)(2,1)}, f32[8,512]{1,0:T(8,128)}) custom-call(bf16[2048,256]{1,0:T(8,128)(2,1)} %get-tuple-element.59.q_ref, bf16[2048,256]{1,0:T(8,128)(2,1)} %get-tuple-element.60.k_ref, bf16[2048,256]{1,0:T(8,128)(2,1)} %get-tuple-element.61.v_ref), custom_call_target="tpu_custom_call" | custom-call | flops 8999999488 | bytes 6000000 | tf_op jit(solution)/shard_map/attn_fwd/pallas_call | solution.py:235
  103.1 20.2 %a2a.6.o_ref = bf16[256,2048]{1,0:T(8,128)(2,1)} custom-call(bf16[2048,256]{1,0:T(8,128)(2,1)} %get-tuple-element.62.src.l0_ref), custom_call_target="tpu_custom_call" | custom-call | flops 5000000000 | bytes 1048576 | tf_op jit(solution)/shard_map/a2a/pallas_call | solution.py:289
  123.3 1.8 all-gather.10.cloned.1.call-done.wo_ref
  125.2 13.0 %out_block.2 = (bf16[256,2048]{1,0:T(8,128)(2,1)}, bf16[256,2048]{1,0:T(8,128)(2,1)}, bf16[256,2048]{1,0:T(8,128)(2,1)}, f32[8,256]{1,0:T(8,128)}) custom-call(bf16[256,2048]{1,0:T(8,128)(2,1)} %a2a.6.o_ref, bf16[2048,2048]{1,0:T(8,128)(2,1)} %all-gather.10.cloned.1.call-done.wo_ref, bf16[256,2048]{1,0:T(8,128)(2,1)} %get-tuple-element.107.x_ref, ...), custom_call_target="tpu_custom_call" | custom-call | flops 4294967296 | bytes 14000000 | tf_op jit(solution)/shard_map/out_block/pallas_call | solution.py:335
  138.4 37.6 %all-gather.18.cloned.1.call-done = bf16[1,2048,2048]{2,1,0:T(8,128)(2,1)} async-done(((bf16[1,256,2048]{2,1,0:T(8,128)(2,1)}), bf16[1,2048,2048]{2,1,0:T(8,128)(2,1)}) %all-gather.18.cloned.1.call-update) | async-done | bytes 8388624 | tf_op jit(solution)/shard_map/all_gather | solution.py:564
  176.0 10.9 %proj.3 = (f32[2048,256]{1,0:T(8,128)}, f32[2048,256]{1,0:T(8,128)}, bf16[2048,256]{1,0:T(8,128)(2,1)}, f32[8,512]{1,0:T(8,128)}) custom-call(bf16[2048,2048]{1,0:T(8,128)(2,1)} %bitcast.26, bf16[2048,768]{1,0:T(8,128)(2,1)} %copy-done), custom_call_target="tpu_custom_call" | custom-call | flops 6442450944 | bytes 16000000 | tf_op jit(solution)/shard_map/proj/pallas_call | solution.py:99
  186.9 12.3 %norm_rope.3 = (bf16[2048,256]{1,0:T(8,128)(2,1)}, bf16[2048,256]{1,0:T(8,128)(2,1)}, f32[2048,128]{1,0:T(8,128)}, f32[2048,128]{1,0:T(8,128)}) custom-call(f32[2048,256]{1,0:T(8,128)} %get-tuple-element.64.q_ref.qr_ref, f32[2048,256]{1,0:T(8,128)} %get-tuple-element.65.k_ref.kr_ref, f32[8,512]{1,0:T(8,128)} %get-tuple-element.66.s_ref, ...), custom_call_target="tpu_custom_call" | custom-call | flops 2000000000 | bytes 10000000 | tf_op jit(solution)/shard_map/norm_rope/pallas_call | solution.py:169
  199.3 17.5 %attn_fwd.3 = (bf16[2048,256]{1,0:T(8,128)(2,1)}, f32[8,512]{1,0:T(8,128)}) custom-call(bf16[2048,256]{1,0:T(8,128)(2,1)} %get-tuple-element.67.q_ref, bf16[2048,256]{1,0:T(8,128)(2,1)} %get-tuple-element.68.k_ref, bf16[2048,256]{1,0:T(8,128)(2,1)} %get-tuple-element.69.v_ref), custom_call_target="tpu_custom_call" | custom-call | flops 8999999488 | bytes 6000000 | tf_op jit(solution)/shard_map/attn_fwd/pallas_call | solution.py:235
  216.8 20.0 %a2a.7.o_ref = bf16[256,2048]{1,0:T(8,128)(2,1)} custom-call(bf16[2048,256]{1,0:T(8,128)(2,1)} %get-tuple-element.70.src.l1_ref), custom_call_target="tpu_custom_call" | custom-call | flops 5000000000 | bytes 1048576 | tf_op jit(solution)/shard_map/a2a/pallas_call | solution.py:289
  236.7 13.0 %out_block.3 = (bf16[256,2048]{1,0:T(8,128)(2,1)}, bf16[256,2048]{1,0:T(8,128)(2,1)}, bf16[256,2048]{1,0:T(8,128)(2,1)}, f32[8,256]{1,0:T(8,128)}) custom-call(bf16[256,2048]{1,0:T(8,128)(2,1)} %a2a.7.o_ref, bf16[2048,2048]{1,0:T(8,128)(2,1)} %all-gather.10.cloned.1.call-done.wo_ref, bf16[256,2048]{1,0:T(8,128)(2,1)} %get-tuple-element.108.x_ref, ...), custom_call_target="tpu_custom_call" | custom-call | flops 4294967296 | bytes 14000000 | tf_op jit(solution)/shard_map/out_block/pallas_call | solution.py:335
  250.3 22.2 %a2a.10.do_ref = bf16[2048,256]{1,0:T(8,128)(2,1)} custom-call(bf16[256,2048]{1,0:T(8,128)(2,1)} %get-tuple-element.82.src), custom_call_target="tpu_custom_call" | custom-call | flops 5000000000 | bytes 1048576 | tf_op jit(solution)/shard_map/a2a/pallas_call | solution.py:289
  272.5 29.9 %attn_bwd.3 = (f32[2048,256]{1,0:T(8,128)}, f32[2048,256]{1,0:T(8,128)}, bf16[2048,256]{1,0:T(8,128)(2,1)}, f32[8,512]{1,0:T(8,128)}, f32[8,256]{1,0:T(8,128)}) custom-call(bf16[2048,256]{1,0:T(8,128)(2,1)} %get-tuple-element.67.q_ref, bf16[2048,256]{1,0:T(8,128)(2,1)} %get-tuple-element.68.k_ref, bf16[2048,256]{1,0:T(8,128)(2,1)} %get-tuple-element.69.v_ref, ...), custom_call_target="tpu_custom_call" | custom-call | flops 16000000000 | bytes 16000000 | tf_op jit(solution)/shard_map/attn_bwd/pallas_call | solution.py:421
  302.3 14.5 %norm_bwd.3 = (bf16[2048,768]{1,0:T(8,128)(2,1)}, f32[8,256]{1,0:T(8,128)}) custom-call(f32[2048,256]{1,0:T(8,128)} %get-tuple-element.86.dqu_ref, f32[2048,256]{1,0:T(8,128)} %get-tuple-element.87.dku_ref, bf16[2048,256]{1,0:T(8,128)(2,1)} %get-tuple-element.88.dv_ref, f32[2048,256]{1,0:T(8,128)} %get-tuple-element.64.q_ref.qr_ref, ...), custom_call_target="tpu_custom_call" | custom-call | flops 2000000000 | bytes 14000000 | tf_op jit(solution)/shard_map/norm_bwd/pallas_call | solution.py:463
  316.9 25.6 %a2a.8.do_ref = bf16[2048,256]{1,0:T(8,128)(2,1)} custom-call(bf16[256,2048]{1,0:T(8,128)(2,1)} %get-tuple-element.72.src), custom_call_target="tpu_custom_call" | custom-call | flops 5000000000 | bytes 1048576 | tf_op jit(solution)/shard_map/a2a/pallas_call | solution.py:289
  342.5 29.9 %attn_bwd.2 = (f32[2048,256]{1,0:T(8,128)}, f32[2048,256]{1,0:T(8,128)}, bf16[2048,256]{1,0:T(8,128)(2,1)}, f32[8,512]{1,0:T(8,128)}, f32[8,256]{1,0:T(8,128)}) custom-call(bf16[2048,256]{1,0:T(8,128)(2,1)} %get-tuple-element.59.q_ref, bf16[2048,256]{1,0:T(8,128)(2,1)} %get-tuple-element.60.k_ref, bf16[2048,256]{1,0:T(8,128)(2,1)} %get-tuple-element.61.v_ref, ...), custom_call_target="tpu_custom_call" | custom-call | flops 16000000000 | bytes 16000000 | tf_op jit(solution)/shard_map/attn_bwd/pallas_call | solution.py:421
  372.4 15.9 %norm_bwd.2 = (bf16[2048,768]{1,0:T(8,128)(2,1)}, f32[8,256]{1,0:T(8,128)}) custom-call(f32[2048,256]{1,0:T(8,128)} %get-tuple-element.76.dqu_ref, f32[2048,256]{1,0:T(8,128)} %get-tuple-element.77.dku_ref, bf16[2048,256]{1,0:T(8,128)(2,1)} %get-tuple-element.78.dv_ref, f32[2048,256]{1,0:T(8,128)} %get-tuple-element.56.q_ref.qr_ref, ...), custom_call_target="tpu_custom_call" | custom-call | flops 2000000000 | bytes 14000000 | tf_op jit(solution)/shard_map/norm_bwd/pallas_call | solution.py:463
  390.1 1.5 pad_maximum_fusion
  391.6 70.7 %a2a.11.d1_ref = bf16[256,6144]{1,0:T(8,128)(2,1)} custom-call(bf16[2048,768]{1,0:T(8,128)(2,1)} %get-tuple-element.91.src.l1_ref), custom_call_target="tpu_custom_call" | custom-call | flops 5000000000 | bytes 3145728 | tf_op jit(solution)/shard_map/a2a/pallas_call | solution.py:289
  462.3 42.6 %a2a.9.d0_ref = bf16[256,6144]{1,0:T(8,128)(2,1)} custom-call(bf16[2048,768]{1,0:T(8,128)(2,1)} %get-tuple-element.81.src.l0_ref), custom_call_target="tpu_custom_call" | custom-call | flops 5000000000 | bytes 3145728 | tf_op jit(solution)/shard_map/a2a/pallas_call | solution.py:289
  504.9 20.8 %wgrad.2 = (bf16[2048,256]{1,0:T(8,128)(2,1)}, bf16[2048,256]{1,0:T(8,128)(2,1)}, bf16[2048,256]{1,0:T(8,128)(2,1)}) custom-call(bf16[2048,768]{1,0:T(8,128)(2,1)} %get-tuple-element.81.src.l0_ref, bf16[2048,768]{1,0:T(8,128)(2,1)} %get-tuple-element.91.src.l1_ref, bf16[2048,2048]{1,0:T(8,128)(2,1)} %bitcast.25, bf16[2048,2048]{1,0:T(8,128)(2,1)} %bitcast.27), custom_call_target="tpu_custom_call" | custom-call | flops 12884901888 | bytes 20000000 | tf_op jit(solution)/shard_map/wgrad/pallas_call | solution.py:541
  525.7 12.7 %wgrad.3 = bf16[256,2048]{1,0:T(8,128)(2,1)} custom-call(bf16[2048,256]{1,0:T(8,128)(2,1)} %get-tuple-element.62.src.l0_ref, bf16[2048,256]{1,0:T(8,128)(2,1)} %get-tuple-element.70.src.l1_ref, bf16[2048,2048]{1,0:T(8,128)(2,1)} %all-gather.12.cloned.1.call-done.r0_ref, bf16[2048,2048]{1,0:T(8,128)(2,1)} %all-gather.14.cloned.1.call-done.r1_ref), custom_call_target="tpu_custom_call" | custom-call | flops 4294967296 | bytes 20000000 | tf_op jit(solution)/shard_map/wgrad/pallas_call | solution.py:541
  538.4 20.5 %dx.1 = (bf16[256,2048]{1,0:T(8,128)(2,1)}, bf16[256,2048]{1,0:T(8,128)(2,1)}) custom-call(bf16[256,6144]{1,0:T(8,128)(2,1)} %a2a.9.d0_ref, bf16[256,6144]{1,0:T(8,128)(2,1)} %a2a.11.d1_ref, bf16[8,2048,768]{2,1,0:T(8,128)(2,1)} %bitcast.23, bf16[256,2048]{1,0:T(8,128)(2,1)} %get-tuple-element.105.dy_ref.dy0_ref, ...), custom_call_target="tpu_custom_call" | custom-call | flops 12884901888 | bytes 40000000 | tf_op jit(solution)/shard_map/dx/pallas_call | solution.py:499
  558.9 3.1 pad_maximum_fusion.1
  (46 shorter events, 6.1 us)
Async XLA Ops:
  7.2 55.2 %all-gather.16.cloned.1.call-start = ((), (), s32[]{:S(2)}) async-start(), calls=%async_computation.3 | async-start | bytes 9437184 | tf_op jit(solution)/shard_map/all_gather | solution.py:564
  11.0 1.6 copy-start.9
  11.0 2.1 copy-start.10
  11.0 2.7 copy-start.8
  11.1 114.1 %all-gather.10.cloned.1.call-start = ((), (), s32[]{:S(2)}) async-start(), calls=%async_computation | async-start | bytes 9437184 | tf_op jit(solution)/shard_map/all_gather | solution.py:566
  11.8 164.2 %all-gather.18.cloned.1.call-start = ((), (), s32[]{:S(2)}) async-start(), calls=%async_computation.4 | async-start | bytes 9437184 | tf_op jit(solution)/shard_map/all_gather | solution.py:564
  12.6 513.1 %all-gather.12.cloned.1.call-start = ((), (), s32[]{:S(2)}) async-start(), calls=%async_computation.1 | async-start | bytes 9437184 | tf_op jit(solution)/shard_map/all_gather | solution.py:584
  14.4 2.7 copy-start.2
  17.2 5.9 %copy-start = (bf16[2048,768]{1,0:T(8,128)(2,1)}, bf16[2048,768]{1,0:T(8,128)(2,1)S(1)}, u32[]{:S(2)}) copy-start(bf16[2048,768]{1,0:T(8,128)(2,1)S(1)} %constant_dynamic-update-slice_fusion.w_ref) | copy-start | bytes 9437188
  21.1 2.0 copy-start.1
  138.2 387.5 %all-gather.14.cloned.1.call-start = ((), (), s32[]{:S(2)}) async-start(), calls=%async_computation.2 | async-start | bytes 9437184 | tf_op jit(solution)/shard_map/all_gather | solution.py:584
  249.7 288.6 %all-gather.20.cloned.1.call-start = ((), (), s32[]{:S(2)}) async-start(), calls=%async_computation.5 | async-start | bytes 28311552 | tf_op jit(solution)/shard_map/all_gather | solution.py:568
  372.4 15.9 %copy-start.6 = (f32[8,256]{1,0:T(8,128)S(1)}, f32[8,256]{1,0:T(8,128)}, u32[]{:S(2)}) copy-start(f32[8,256]{1,0:T(8,128)} %get-tuple-element.102) | copy-start | bytes 24580
  372.4 17.2 %copy-start.5 = (f32[8,256]{1,0:T(8,128)S(1)}, f32[8,256]{1,0:T(8,128)}, u32[]{:S(2)}) copy-start(f32[8,256]{1,0:T(8,128)} %get-tuple-element.100) | copy-start | bytes 24580
  372.4 17.2 %copy-start.7 = (f32[8,256]{1,0:T(8,128)S(1)}, f32[8,256]{1,0:T(8,128)}, u32[]{:S(2)}) copy-start(f32[8,256]{1,0:T(8,128)} %get-tuple-element.99) | copy-start | bytes 24580
  372.4 17.8 %copy-start.3 = (bf16[256,2048]{1,0:T(8,128)(2,1)S(1)}, bf16[256,2048]{1,0:T(8,128)(2,1)}, u32[]{:S(2)}) copy-start(bf16[256,2048]{1,0:T(8,128)(2,1)} %get-tuple-element.63) | copy-start | bytes 3145732
  372.4 17.7 %copy-start.4 = (bf16[256,2048]{1,0:T(8,128)(2,1)S(1)}, bf16[256,2048]{1,0:T(8,128)(2,1)}, u32[]{:S(2)}) copy-start(bf16[256,2048]{1,0:T(8,128)(2,1)} %get-tuple-element.71) | copy-start | bytes 3145732
Sparse Core Ops, SparseCore 0:
  11.2 51.1 all-gather.15
  64.2 60.8 all-gather.9
  127.5 48.3 all-gather.17
  177.7 60.7 all-gather.11
  249.8 55.8 all-gather.13
  307.4 188.6 all-gather.19

commit v2 on v1

--- a/solution.py
+++ b/solution.py
@@ -82,7 +82,8 @@
     return jnp.broadcast_to(row, (HD, row.shape[1])).T
 
 
-def proj_kernel(x_ref, w_ref, q_ref, k_ref, v_ref, s_ref):
+def proj_kernel(x_ref, w_ref, *rest):
+    q_ref, k_ref, v_ref, s_ref = rest[-5:-1] if len(rest) == 6 else rest
     i = pl.program_id(0)
     x = x_ref[...]
     q = dot(x, w_ref[:, :LOC])
@@ -94,18 +95,21 @@
     v_ref[...] = dot(x, w_ref[:, 2 * LOC:]).astype(BF)
 
 
-def project(x, w):
+def project(x, w, through=()):
     row = pl.BlockSpec((BLK, LOC), lambda i: (i, 0))
+    whole = [pl.BlockSpec(memory_space=pl.ANY)] * len(through)
     return pl.pallas_call(
         proj_kernel,
         grid=(NB,),
-        in_specs=[pl.BlockSpec((BLK, DIM), lambda i: (i, 0)), pl.BlockSpec((DIM, 3 * LOC), lambda i: (0, 0))],
-        out_specs=[row, row, row, pl.BlockSpec((2 * NB, BLK), lambda i: (0, 0))],
-        out_shape=[sds((SEQ, LOC), F32), sds((SEQ, LOC), F32), sds((SEQ, LOC), BF), sds((2 * NB, BLK), F32)],
+        in_specs=[pl.BlockSpec((BLK, DIM), lambda i: (i, 0)), pl.BlockSpec((DIM, 3 * LOC), lambda i: (0, 0))] + whole,
+        out_specs=[row, row, row, pl.BlockSpec((2 * NB, BLK), lambda i: (0, 0))] + whole,
+        out_shape=[sds((SEQ, LOC), F32), sds((SEQ, LOC), F32), sds((SEQ, LOC), BF), sds((2 * NB, BLK), F32)]
+        + [sds(t.shape, t.dtype) for t in through],
+        input_output_aliases={2 + n: 4 + n for n in range(len(through))},
         compiler_params=params(dimension_semantics=("arbitrary",)),
         cost_estimate=cost(2 * SEQ * DIM * 3 * LOC, 16e6),
         name="proj",
-    )(x, w)
+    )(x, w, *through)
 
 
 def exchange(me, srcs, slots, send_sems, recv_sems):
@@ -186,14 +190,21 @@
     return keys <= queries
 
 
-def attn_kernel(q_ref, k_ref, v_ref, o_ref, lse_ref, p_scr, vt_scr, acc_scr):
-    h, qi = pl.program_id(0), pl.program_id(1)
-
-    @pl.when(qi == 0)
+def attn_kernel(q_ref, k_ref, v_ref, o_ref, lse_ref, recv_ref, p_scr, vt_scr, acc_scr, o_scr, send_sems, recv_sems, own_sems):
+    h, step = pl.program_id(0), pl.program_id(1)
+    me = lax.axis_index('tp')
+    qi = (me // 2 + 1 + step) % NB
+    rows = pl.ds(pl.multiple_of(qi * BLK, BLK), BLK)
+
+    @pl.when(jnp.logical_and(h == 0, step == 0))
+    def _():
+        entry_barrier(me)
+
+    @pl.when(step == 0)
     def _():
         vt_scr[...] = v_ref[...].T
 
-    qb = q_ref[...]
+    qb = q_ref[rows, :]
 
     def scores(j):
         return dot(k_ref[pl.ds(pl.multiple_of(j * BLK, BLK), BLK), :], qb, NT)
@@ -226,80 +237,67 @@
         return carry
 
     lax.fori_loop(0, qi + 1, third, 0)
-    o_ref[...] = acc_scr[...].T.astype(BF)
-
-
-def attention(q, k, v):
-    blk = pl.BlockSpec((BLK, HD), lambda h, i: (i, h))
+    out = acc_scr[...].T.astype(BF)
+    o_scr[h, step] = out
+    o_ref[rows, :] = out
+
+    def block_copy(hh, st, half, remote):
+        dest = 2 * ((me // 2 + 1 + st) % NB) + half
+        src = o_scr.at[hh, st, pl.ds(half * TOK, TOK), :]
+        dst = recv_ref.at[:, pl.ds(pl.multiple_of(me * LOC + hh * HD, HD), HD)]
+        if remote:
+            return dest, pltpu.make_async_remote_copy(
+                src_ref=src, dst_ref=dst, send_sem=send_sems.at[hh, st, half], recv_sem=recv_sems.at[hh, me],
+                device_id=(dest,), device_id_type=MESH)
+        return dest, pltpu.make_async_copy(src, dst, own_sems.at[hh])
+
+    for half in range(2):
+        dest, away = block_copy(h, step, half, True)
+        _, here = block_copy(h, step, half, False)
+        pl.when(dest != me)(away.start)
+        pl.when(dest == me)(here.start)
+
+    @pl.when(jnp.logical_and(h == 1, step == NB - 1))
+    def _():
+        for hh in range(2):
+            for st in range(NB):
+                for half in range(2):
+                    dest, away = block_copy(hh, st, half, True)
+                    _, here = block_copy(hh, st, half, False)
+                    if st < NB - 1:
+                        away.wait_send()
+                    else:
+                        pl.when(dest != me)(away.wait_send)
+                        pl.when(dest == me)(here.wait)
+            for mask in ORDER:
+                peer = peer_of(me, mask)
+                pltpu.make_async_remote_copy(
+                    src_ref=o_scr.at[0, 0, pl.ds(0, TOK), :],
+                    dst_ref=recv_ref.at[:, pl.ds(pl.multiple_of(peer * LOC + hh * HD, HD), HD)],
+                    send_sem=send_sems.at[0, 0, 0], recv_sem=recv_sems.at[hh, peer],
+                    device_id=(peer,), device_id_type=MESH).wait_recv()
+
+
+def attention(q, k, v, cid):
     full = pl.BlockSpec((SEQ, HD), lambda h, i: (0, h))
     return pl.pallas_call(
         attn_kernel,
         grid=(2, NB),
-        in_specs=[blk, full, full],
-        out_specs=[blk, pl.BlockSpec((2 * NB, BLK), lambda h, i: (0, 0))],
-        out_shape=[sds((SEQ, LOC), BF), sds((2 * NB, BLK), F32)],
-        scratch_shapes=[pltpu.VMEM((NB, BLK, BLK), F32), pltpu.VMEM((HD, SEQ), BF), pltpu.VMEM((HD, BLK), F32)],
-        compiler_params=params(dimension_semantics=("arbitrary", "arbitrary")),
+        in_specs=[full, full, full],
+        out_specs=[full, pl.BlockSpec((2 * NB, BLK), lambda h, i: (0, 0)), pl.BlockSpec(memory_space=pl.ANY)],
+        out_shape=[sds((SEQ, LOC), BF), sds((2 * NB, BLK), F32), sds((TOK, DIM), BF)],
+        scratch_shapes=[pltpu.VMEM((NB, BLK, BLK), F32), pltpu.VMEM((HD, SEQ), BF), pltpu.VMEM((HD, BLK), F32),
+                        pltpu.VMEM((2, NB, BLK, HD), BF), pltpu.SemaphoreType.DMA((2, NB, 2)),
+                        pltpu.SemaphoreType.DMA((2, NDEV)), pltpu.SemaphoreType.DMA((2,))],
+        compiler_params=params(dimension_semantics=("arbitrary", "arbitrary"), collective_id=cid, has_side_effects=True),
         cost_estimate=cost(9e9, 6e6),
         name="attn_fwd",
     )(q, k, v)
 
 
-def heads_to_tokens_kernel(src, dst, send_sems, recv_sems, own_sem):
+def out_kernel(o_ref, wo_ref, x_ref, dy_ref, ga_ref, y_ref, da_ref, gga_ref, recv_ref, a_scr, dh_scr, send_sems, recv_sems, own_sem):
     me = lax.axis_index('tp')
-    width = src.shape[1]
     entry_barrier(me)
-    here = dst.at[:, pl.ds(pl.multiple_of(me * width, width), width)]
-    copies = []
-    for p, mask in enumerate(ORDER):
-        peer = peer_of(me, mask)
-        copies.append(pltpu.make_async_remote_copy(
-            src_ref=src.at[pl.ds(pl.multiple_of(peer * TOK, TOK), TOK), :], dst_ref=here,
-            send_sem=send_sems.at[p], recv_sem=recv_sems.at[p], device_id=(peer,), device_id_type=MESH))
-    for c in copies:
-        c.start()
-    own = pltpu.make_async_copy(src.at[pl.ds(pl.multiple_of(me * TOK, TOK), TOK), :], here, own_sem)
-    own.start()
-    own.wait()
-    for c in copies:
-        c.wait()
-
-
-def tokens_to_heads_kernel(src, dst, send_sems, recv_sems, own_sem):
-    me = lax.axis_index('tp')
-    width = dst.shape[1]
-    entry_barrier(me)
-    here = dst.at[pl.ds(pl.multiple_of(me * TOK, TOK), TOK), :]
-    copies = []
-    for p, mask in enumerate(ORDER):
-        peer = peer_of(me, mask)
-        copies.append(pltpu.make_async_remote_copy(
-            src_ref=src.at[:, pl.ds(pl.multiple_of(peer * width, width), width)], dst_ref=here,
-            send_sem=send_sems.at[p], recv_sem=recv_sems.at[p], device_id=(peer,), device_id_type=MESH))
-    for c in copies:
-        c.start()
-    own = pltpu.make_async_copy(src.at[:, pl.ds(pl.multiple_of(me * width, width), width)], here, own_sem)
-    own.start()
-    own.wait()
-    for c in copies:
-        c.wait()
-
-
-def all_to_all(kernel, src, out_shape, cid):
-    return pl.pallas_call(
-        kernel,
-        in_specs=[pl.BlockSpec(memory_space=pl.ANY)],
-        out_specs=pl.BlockSpec(memory_space=pl.ANY),
-        out_shape=sds(out_shape, BF),
-        scratch_shapes=[pltpu.SemaphoreType.DMA((NDEV - 1,)), pltpu.SemaphoreType.DMA((NDEV - 1,)),
-                        pltpu.SemaphoreType.DMA],
-        compiler_params=pltpu.CompilerParams(collective_id=cid, has_side_effects=True),
-        cost_estimate=cost(5e9, 2 * src.size),
-        name="a2a",
-    )(src)
-
-
-def out_kernel(o_ref, wo_ref, x_ref, dy_ref, ga_ref, y_ref, da_ref, dh_ref, gga_ref, a_scr):
     step = DIM // NB
     o = o_ref[...]
 
@@ -321,25 +319,52 @@
     gn = dy * ga
     da_ref[...] = (r * (gn - n * jnp.mean(gn * n, axis=-1, keepdims=True))).astype(BF)
     da = da_ref[...]
-
-    def bwd(j, carry):
-        rows = pl.ds(pl.multiple_of(j * step, step), step)
-        dh_ref[:, rows] = dot(da, wo_ref[rows, :], NT).astype(BF)
+    mine = recv_ref.at[pl.ds(pl.multiple_of(me * TOK, TOK), TOK), :]
+
+    def block_copy(st, half):
+        dest = 2 * ((me // 2 + 1 + st) % NB) + half
+        src = dh_scr.at[st, :, pl.ds(half * LOC, LOC)]
+        away = pltpu.make_async_remote_copy(
+            src_ref=src, dst_ref=mine, send_sem=send_sems.at[st, half], recv_sem=recv_sems.at[me],
+            device_id=(dest,), device_id_type=MESH)
+        return dest, away, pltpu.make_async_copy(src, mine, own_sem)
+
+    def bwd(st, carry):
+        blk = (me // 2 + 1 + st) % NB
+        dh_scr[st] = dot(da, wo_ref[pl.ds(pl.multiple_of(blk * step, step), step), :], NT).astype(BF)
+        for half in range(2):
+            dest, away, here = block_copy(st, half)
+            pl.when(dest != me)(away.start)
+            pl.when(dest == me)(here.start)
         return carry
 
     lax.fori_loop(0, NB, bwd, 0)
-
-
-def out_block(o, wo, x, dy, ga):
+    for st in range(NB):
+        for half in range(2):
+            dest, away, here = block_copy(st, half)
+            if st < NB - 1:
+                away.wait_send()
+            else:
+                pl.when(dest != me)(away.wait_send)
+                pl.when(dest == me)(here.wait)
+    for mask in ORDER:
+        peer = peer_of(me, mask)
+        pltpu.make_async_remote_copy(
+            src_ref=dh_scr.at[0, :, pl.ds(0, LOC)], dst_ref=recv_ref.at[pl.ds(pl.multiple_of(peer * TOK, TOK), TOK), :],
+            send_sem=send_sems.at[0, 0], recv_sem=recv_sems.at[peer], device_id=(peer,), device_id_type=MESH).wait_recv()
+
+
+def out_block(o, wo, x, dy, ga, cid):
     spec = pl.BlockSpec(memory_space=pltpu.VMEM)
     return pl.pallas_call(
         out_kernel,
         in_specs=[spec] * 5,
-        out_specs=[spec] * 4,
-        out_shape=[sds((TOK, DIM), BF), sds((TOK, DIM), BF), sds((TOK, DIM), BF), sds((8, DIM // 8), F32)],
-        scratch_shapes=[pltpu.VMEM((TOK, DIM), F32)],
-        compiler_params=params(),
-        cost_estimate=cost(4 * TOK * DIM * DIM, 14e6),
+        out_specs=[spec] * 3 + [pl.BlockSpec(memory_space=pl.ANY)],
+        out_shape=[sds((TOK, DIM), BF), sds((TOK, DIM), BF), sds((8, DIM // 8), F32), sds((SEQ, LOC), BF)],
+        scratch_shapes=[pltpu.VMEM((TOK, DIM), F32), pltpu.VMEM((NB, TOK, DIM // NB), BF), pltpu.SemaphoreType.DMA((NB, 2)),
+                        pltpu.SemaphoreType.DMA((NDEV,)), pltpu.SemaphoreType.DMA],
+        compiler_params=params(collective_id=cid, has_side_effects=True),
+        cost_estimate=cost(4 * TOK * DIM * DIM + 5e9, 14e6),
         name="out_block",
     )(o, wo, x, dy, ga)
 
@@ -475,81 +500,194 @@
     )(dqu, dku, dv, qr, kr, iq, ik, dots, gga)
 
 
-def dx_kernel(d0_ref, d1_ref, w_ref, dy0_ref, dy1_ref, dx0_ref, dx1_ref, acc0, acc1):
-    i = pl.program_id(0)
-
-    @pl.when(i == 0)
-    def _():
-        acc0[...] = dy0_ref[...].astype(F32)
-        acc1[...] = dy1_ref[...].astype(F32)
-
-    w = w_ref[0]
-    acc0[...] += dot(d0_ref[...], w, NT)
-    acc1[...] += dot(d1_ref[...], w, NT)
-
-    @pl.when(i == NDEV - 1)
-    def _():
-        dx0_ref[...] = acc0[...].astype(BF)
-        dx1_ref[...] = acc1[...].astype(BF)
-
-
-def dx_block(d0, d1, w, dy0, dy1):
-    part = pl.BlockSpec((TOK, 3 * LOC), lambda i: (0, i))
-    full = pl.BlockSpec((TOK, DIM), lambda i: (0, 0))
+HALF = DIM // 2
+CH = 256
+
+
+def grads_kernel(d0, d1, w, x0, x1, o0, o1, da0, da1, dy_ref, dx_ref, gwq_ref, gwk_ref, gwv_ref, gwo_ref,
+                 d_all, w_all, sbuf, r1, r2, fin, acc, xbuf, obuf,
+                 dl_sems, dsnd_sems, drcv_sems, w_sems, s1_sems, r1_sems, s2_sems, r2_sems, fs_sems, fr_sems, x_sems, o_sems):
+    me = lax.axis_index('tp')
+    core, chip = me % 2, me // 2
+    partner = peer_of(me, 1)
+    first = peer_of(me, 2) * (1 - core) + peer_of(me, 4) * core
+    second = peer_of(me, 4) * (1 - core) + peer_of(me, 2) * core
+    diag_chip, first_chip, second_chip = peer_of(me, 6) // 2, first // 2, second // 2
+    d_src = (d0, d1)
+
+    barrier = pltpu.get_barrier_semaphore()
+    for dev in (partner, first, second):
+        pl.semaphore_signal(barrier, inc=1, device_id=(dev,), device_id_type=MESH)
+    pl.semaphore_wait(barrier, 3)
+
+    def rows_of(blk):
+        return pl.ds(pl.multiple_of(blk * BLK, BLK), BLK)
+
+    def half_rows(c):
+        return pl.ds(pl.multiple_of(c * HALF, HALF), HALF)
+
+    chips = (diag_chip, first_chip, second_chip, chip)
+    w_out = pltpu.make_async_remote_copy(
+        src_ref=w.at[half_rows(1 - core), :], dst_ref=w_all.at[1], send_sem=w_sems.at[0], recv_sem=w_sems.at[1],
+        device_id=(partner,), device_id_type=MESH)
+    w_own = pltpu.make_async_copy(w.at[half_rows(core), :], w_all.at[0], w_sems.at[2])
+    w_out.start()
+    w_own.start()
+    swaps, loads = [], []
+    for kind in range(4):
+        for b in range(2):
+            n = 2 * kind + b
+            rows = rows_of(chips[kind])
+            loads.append(pltpu.make_async_copy(d_src[b].at[rows, :], d_all.at[0, b, rows, :], dl_sems.at[n]))
+            kp = {0: 0, 1: 2, 2: 1, 3: 3}[kind]
+            prow = rows_of(chips[kp])
+            swaps.append(pltpu.make_async_remote_copy(
+                src_ref=d_src[b].at[prow, :], dst_ref=d_all.at[1, b, prow, :], send_sem=dsnd_sems.at[n],
+                recv_sem=drcv_sems.at[n], device_id=(partner,), device_id_type=MESH))
+    for load, swap in zip(loads, swaps):
+        swap.start()
+        load.start()
+    w_own.wait()
+    w_out.wait()
+
+    def arrived(n, b, blk):
+        rows = rows_of(blk)
+        pltpu.make_async_copy(d0.at[rows, :], d_all.at[0, b, rows, :], dl_sems.at[n]).wait()
+        pltpu.make_async_remote_copy(
+            src_ref=d0.at[rows, :], dst_ref=d_all.at[1, b, rows, :], send_sem=dsnd_sems.at[n],
+            recv_sem=drcv_sems.at[n], device_id=(partner,), device_id_type=MESH).wait()
+
+    def partial(b, blk):
+        rows = rows_of(blk)
+        return dot(d_all[0, b, rows, :], w_all[0], NT) + dot(d_all[1, b, rows, :], w_all[1], NT)
+
+    def to_first(n):
+        return pltpu.make_async_remote_copy(
+            src_ref=sbuf.at[n], dst_ref=r1.at[n], send_sem=s1_sems.at[n], recv_sem=r1_sems.at[n],
+            device_id=(first,), device_id_type=MESH)
+
+    def to_second(b):
+        return pltpu.make_async_remote_copy(
+            src_ref=r1.at[b], dst_ref=r2.at[b], send_sem=s2_sems.at[b], recv_sem=r2_sems.at[b],
+            device_id=(second,), device_id_type=MESH)
+
+    def to_partner(b):
+        return pltpu.make_async_remote_copy(
+            src_ref=r1.at[2 + b, pl.ds(pl.multiple_of((1 - core) * TOK, TOK), TOK), :], dst_ref=fin.at[b],
+            send_sem=fs_sems.at[b], recv_sem=fr_sems.at[b], device_id=(partner,), device_id_type=MESH)
+
+    def phase1(n, carry):
+        kind, b = n // 2, n % 2
+        blk = diag_chip * (1 - kind) + first_chip * kind
+        arrived(n, b, blk)
+        sbuf[n] = partial(b, blk)
+        to_first(n).start()
+        return carry
+
+    lax.fori_loop(0, 4, phase1, 0)
+    for n in range(4, 8):
+        arrived(n, n % 2, chips[n // 2])
+
+    steps = SEQ // CH
+
+    def chunk(i):
+        return pl.ds(pl.multiple_of(i * CH, CH), CH)
+
+    def stream(pairs, body):
+        def fetch(i):
+            return [pltpu.make_async_copy(src.at[chunk(i), :], buf.at[i % 2], sems.at[i % 2]) for src, buf, sems in pairs]
+
+        for c in fetch(0):
+            c.start()
+
+        def it(i, carry):
+            @pl.when(i + 1 < steps)
+            def _():
+                for c in fetch(i + 1):
+                    c.start()
+
+            for c in fetch(i):
+                c.wait()
+            body(i)
+            return carry
+
+        lax.fori_loop(0, steps, it, 0)
+
+    def wgrad(b, src):
+        def body(i):
+            left = d_all[0, b, chunk(i), :].T
+            for c in range(3):
+                part = slice(c * LOC, (c + 1) * LOC)
+                acc[part, :] += dot(left[part, :], xbuf[i % 2])
+
+        stream([(src, xbuf, x_sems)], body)
+
+    def forward_second(b, carry):
+        to_first(b).wait_recv()
+        r1[b] += partial(b, second_chip)
+        to_second(b).start()
+        return carry
+
+    acc[...] = jnp.zeros_like(acc)
+    wgrad(0, x0)
+    forward_second(0, 0)
+    wgrad(1, x1)
+    for n, ref in enumerate((gwq_ref, gwk_ref, gwv_ref)):
+        ref[...] = acc[n * LOC:(n + 1) * LOC, :].T.astype(BF)
+    forward_second(1, 0)
+    acc[:LOC, :] = jnp.zeros((LOC, DIM), F32)
+
+    def wo_body(i):
+        acc[:LOC, :] += dot(obuf[i % 2].T, xbuf[i % 2])
+
+    for o_src, da_src in ((o0, da0), (o1, da1)):
+        stream([(da_src, xbuf, x_sems), (o_src, obuf, o_sems)], wo_body)
+    gwo_ref[...] = acc[:LOC, :].astype(BF)
+
+    def own_part(b, carry):
+        r1_own = partial(b, chip)
+        to_first(2 + b).wait_recv()
+        to_second(b).wait_recv()
+        r1[2 + b] += r1_own + r2[b]
+        to_partner(b).start()
+        cols = half_rows(core)
+        rows = pl.ds(pl.multiple_of(core * TOK, TOK), TOK)
+        dx_ref[b, :, cols] = (r1[2 + b, rows, :] + dy_ref[b, :, cols].astype(F32)).astype(BF)
+        return carry
+
+    lax.fori_loop(0, 2, own_part, 0)
+
+    def finish(b, carry):
+        to_partner(b).wait()
+        cols = half_rows(1 - core)
+        dx_ref[b, :, cols] = (fin[b] + dy_ref[b, :, cols].astype(F32)).astype(BF)
+        to_second(b).wait_send()
+        to_first(b).wait_send()
+        to_first(2 + b).wait_send()
+        return carry
+
+    lax.fori_loop(0, 2, finish, 0)
+
+
+def grads(d0, d1, w, x0, x1, o0, o1, da0, da1, dy, cid):
+    vm = pl.BlockSpec(memory_space=pltpu.VMEM)
+    far = pl.BlockSpec(memory_space=pl.ANY)
+    dma = pltpu.SemaphoreType.DMA
     return pl.pallas_call(
-        dx_kernel,
-        grid=(NDEV,),
-        in_specs=[part, part, pl.BlockSpec((1, DIM, 3 * LOC), lambda i: (i, 0, 0)), full, full],
-        out_specs=[full, full],
-        out_shape=[sds((TOK, DIM), BF)] * 2,
-        scratch_shapes=[pltpu.VMEM((TOK, DIM), F32)] * 2,
-        compiler_params=params(dimension_semantics=("arbitrary",)),
-        cost_estimate=cost(2 * 2 * TOK * DIM * 3 * DIM, 40e6),
-        name="dx",
-    )(d0, d1, w, dy0, dy1)
-
-
-def wgrad_kernel(transposed, l0_ref, l1_ref, r0_ref, r1_ref, *rest):
-    *outs, acc = rest
-    i = pl.program_id(0)
-
-    @pl.when(i == 0)
-    def _():
-        acc[...] = jnp.zeros_like(acc)
-
-    @pl.when(i < NB)
-    def _():
-        acc[...] += dot(l0_ref[...].T, r0_ref[...])
-
-    @pl.when(i >= NB)
-    def _():
-        acc[...] += dot(l1_ref[...].T, r1_ref[...])
-
-    @pl.when(i == 2 * NB - 1)
-    def _():
-        for n, out in enumerate(outs):
-            part = acc[n * LOC:(n + 1) * LOC, :]
-            out[...] = (part.T if transposed else part).astype(BF)
-
-
-def wgrad(left, right, transposed):
-    width = left[0].shape[1]
-    count = width // LOC
-    first = lambda i: (jnp.minimum(i, NB - 1), 0)
-    second = lambda i: (jnp.maximum(i - NB, 0), 0)
-    shape = (DIM, LOC) if transposed else (LOC, DIM)
-    return pl.pallas_call(
-        functools.partial(wgrad_kernel, transposed),
-        grid=(2 * NB,),
-        in_specs=[pl.BlockSpec((BLK, width), first), pl.BlockSpec((BLK, width), second),
-                  pl.BlockSpec((BLK, DIM), first), pl.BlockSpec((BLK, DIM), second)],
-        out_specs=[pl.BlockSpec(shape, lambda i: (0, 0))] * count,
-        out_shape=[sds(shape, BF)] * count,
-        scratch_shapes=[pltpu.VMEM((width, DIM), F32)],
-        compiler_params=params(dimension_semantics=("arbitrary",)),
-        cost_estimate=cost(2 * 2 * SEQ * width * DIM, 20e6),
-        name="wgrad",
-    )(*left, *right)
+        grads_kernel,
+        in_specs=[far] * 9 + [vm],
+        out_specs=[vm] * 5,
+        out_shape=[sds((2, TOK, DIM), BF)] + [sds((DIM, LOC), BF)] * 3 + [sds((LOC, DIM), BF)],
+        scratch_shapes=[pltpu.VMEM((2, 2, SEQ, 3 * LOC), BF), pltpu.VMEM((2, HALF, 3 * LOC), BF),
+                        pltpu.VMEM((4, BLK, HALF), F32), pltpu.VMEM((4, BLK, HALF), F32), pltpu.VMEM((2, BLK, HALF), F32),
+                        pltpu.VMEM((2, TOK, HALF), F32), pltpu.VMEM((3 * LOC, DIM), F32),
+                        pltpu.VMEM((2, CH, DIM), BF), pltpu.VMEM((2, CH, LOC), BF),
+                        dma((8,)), dma((8,)), dma((8,)), dma((3,)), dma((4,)), dma((4,)), dma((2,)), dma((2,)),
+                        dma((2,)), dma((2,)), dma((2,)), dma((2,))],
+        compiler_params=pltpu.CompilerParams(vmem_limit_bytes=67043328, collective_id=cid, has_side_effects=True),
+        cost_estimate=cost(100e9, 40e6),
+        name="grads",
+    )(d0, d1, w, x0, x1, o0, o1, da0, da1, dy)
 
 
 def local_block(x_loc, wq, wk, wv, wo, gq, gk, ga, dy_loc):
@@ -558,31 +696,26 @@
     gq, gk, ga = gq[None, :], gk[None, :], ga[None, :]
     cos, sin = rope_tables()
     xs, dys = [x_loc[0], x_loc[1]], [dy_loc[0], dy_loc[1]]
-    x_full = []
-    for b in range(2):
-        src = xs[b] if b == 0 else lax.optimization_barrier((xs[b], x_full[0][:8, :HD]))[0]
-        x_full.append(gather(xs[b], axis=0, tiled=True))
-    wo_src = lax.optimization_barrier((wo, x_full[1][:8, :HD]))[0]
-    wo_full = gather(wo_src, axis=0, tiled=True)
-    w_src = lax.optimization_barrier((w_loc, wo_full[:8, :HD]))[0]
-    w_full = gather(w_src, axis=0, tiled=False)
+    x_full = [gather(xs[b], axis=0, tiled=True) for b in range(2)]
 
     fwd, o_recv = [], []
     for b in range(2):
-        q_raw, k_raw, v, s = project(x_full[b], w_loc)
+        q_raw, k_raw, v, s, *through = project(x_full[b], w_loc, (wo,) if b == 0 else ())
+        if b == 0:
+            wo_full = gather(through[0], axis=0, tiled=True)
         q_rot, k_rot, iq, ik = norm_rope(q_raw, k_raw, s, gq, gk, cos, sin, 1 + b)
-        o, lse = attention(q_rot, k_rot, v)
-        o_recv.append(all_to_all(heads_to_tokens_kernel, o, (TOK, DIM), 3 + b))
+        o, lse, recv = attention(q_rot, k_rot, v, 3 + b)
+        o_recv.append(recv)
         fwd.append((q_raw, k_raw, v, q_rot, k_rot, iq, ik, o, lse))
     ys, das, dhs, ggas = [], [], [], []
     for b in range(2):
-        y, da, dh, gga = out_block(o_recv[b], wo_full, xs[b], dys[b], ga)
+        y, da, gga, dh = out_block(o_recv[b], wo_full, xs[b], dys[b], ga, 5 + b)
         ys.append(y)
         das.append(da)
-        dhs.append(all_to_all(tokens_to_heads_kernel, dh, (SEQ, LOC), 5 + b))
+        dhs.append(dh)
         ggas.append(gga)
     da_full = [gather(das[b], axis=0, tiled=True) for b in range(2)]
-    ds, d_recv, gga_sum, ggs = [], [], [], []
+    ds, gga_sum, ggs = [], [], []
     for b in range(2):
         q_raw, k_raw, v, q_rot, k_rot, iq, ik, o, lse = fwd[b]
         dqu, dku, dv, dots, gg = attention_bwd(q_rot, k_rot, v, dhs[b], lse, q_raw, k_raw, iq, ik, gq, gk, cos, sin)
@@ -590,13 +723,10 @@
         ds.append(d)
         gga_sum.append(gsum)
         ggs.append(gg)
-        d_recv.append(all_to_all(heads_to_tokens_kernel, d, (TOK, 3 * DIM), 9 + b))
-    gwq, gwk, gwv = wgrad(ds, x_full, True)
-    gwo, = wgrad([fwd[0][7], fwd[1][7]], da_full, False)
-    dx0, dx1 = dx_block(d_recv[0], d_recv[1], w_full, dys[0], dys[1])
+    dx, gwq, gwk, gwv, gwo = grads(ds[0], ds[1], w_loc, x_full[0], x_full[1], fwd[0][7], fwd[1][7], da_full[0], da_full[1], dy_loc, 9)
     gg = ggs[0] + ggs[1]
     grad_ga = (gga_sum[0] + gga_sum[1]).reshape(DIM).astype(BF)
-    return (jnp.stack(ys), jnp.stack([dx0, dx1]), gwq, gwk, gwv, gwo, gg[0].astype(BF), gg[1].astype(BF), grad_ga)
+    return (jnp.stack(ys), dx, gwq, gwk, gwv, gwo, gg[0].astype(BF), gg[1].astype(BF), grad_ga)
 
 
 def solution(mesh):

time: 570 us -> 538 us (0.944)
  Pallas kernels: 453 us -> 406 us
  local copies, waits for them, and re-layouts: 11 us -> 20.6 us
  waiting for transfers between devices: 79.2 us -> 87.1 us
    pallas_call x13 -> x5, Pallas kernels: 316 us -> 270 us  [the longest x1 152 us: grads(): pl.pallas_call(grads_kernel, in_specs=[far] * 9 + [vm], out_specs=[vm] *...]
    unnamed x25 -> x43, local copies, waits for them, and re-layouts: 3.33 us -> 13.5 us
    all_gather x4 -> x3, waiting for transfers between devices: 77.2 us -> 86.3 us  [the longest x2 77.4 us: local_block(): x_full = [gather(xs[b], axis=0, tiled=True) for b in range(2)]]
  transfers between devices with their start and end apart: 6 -> 5, of which waited for: 3 -> 3; matrix products, arithmetic and copies ran while one was open for 3% -> 3% of each run, Pallas kernels for 76% -> 45%
where the time goes in v2:
time: 538 us; the launch traced here: 537 us
  Pallas kernels  406 us (75%)
  waiting for transfers between devices  87.1 us (16%)
  local copies, waits for them, and re-layouts  20.6 us (4%)
  between operations  14 us (3%)
  other arithmetic  8.08 us (2%)
    pallas_call x1, Pallas kernels, grads(): pl.pallas_call(grads_kernel, in_specs=[far] * 9 + [vm], out_specs=[vm] *...  152 us
    all_gather x2, waiting for transfers between devices, local_block(): x_full = [gather(xs[b], axis=0, tiled=True) for b in range(2)]  77.4 us
    pallas_call x2, Pallas kernels, attention_bwd(): pl.pallas_call(attn_bwd_kernel, grid=(2, NB), in_specs=[blk, full, full,...  59.7 us
    pallas_call x2, Pallas kernels, attention(): pl.pallas_call(attn_kernel, grid=(2, NB), in_specs=[full, full, full], ou...  59.5 us
    pallas_call x2, Pallas kernels, out_block(): pl.pallas_call(out_kernel, in_specs=[spec] * 5, out_specs=[spec] * 3 + [p...  58.5 us
    pallas_call x2, Pallas kernels, norm_bwd(): pl.pallas_call(norm_bwd_kernel, grid=(NB,), in_specs=[row, row, row, row,...  30.1 us
    pallas_call x2, Pallas kernels, norm_rope(): pl.pallas_call(norm_kernel, grid=(NB,), in_specs=[row, row, pl.BlockSpec(...  24.6 us
    pallas_call x2, Pallas kernels, project(): pl.pallas_call(proj_kernel, grid=(NB,), in_specs=[pl.BlockSpec((BLK, DIM)...  21.9 us
  transfers between devices with their start and end apart: 5, of which 3 were waited for; matrix products, arithmetic and copies ran while one was open for 3% of the time, Pallas kernels for 45%

profile of v2, /device:TPU:0, one launch (start us, length us, event | category | flops | bytes accessed | tf_op | source)
XLA Modules:
  0.0 536.7 jit_solution(6178489124858444724)
XLA Ops:
  7.2 2.4 copy.29.rest_0_
  9.7 2.3 slice_bitcast_fusion.3
  12.0 1.1 constant_dynamic-update-slice_fusion.2
  13.5 1.2 constant_dynamic-update-slice_fusion.1
  14.7 1.1 constant_dynamic-update-slice_fusion.w_ref.w
  15.8 47.5 %all-gather.14.cloned.1.call-done = bf16[1,2048,2048]{2,1,0:T(8,128)(2,1)} async-done(((bf16[1,256,2048]{2,1,0:T(8,128)(2,1)}), bf16[1,2048,2048]{2,1,0:T(8,128)(2,1)}) %all-gather.14.cloned.1.call-update) | async-done | bytes 8388624 | tf_op jit(solution)/shard_map/all_gather | solution.py:699
  63.3 11.0 %proj.2 = (f32[2048,256]{1,0:T(8,128)}, f32[2048,256]{1,0:T(8,128)}, bf16[2048,256]{1,0:T(8,128)(2,1)}, f32[8,512]{1,0:T(8,128)}, bf16[256,2048]{1,0:T(8,128)(2,1)}) custom-call(bf16[2048,2048]{1,0:T(8,128)(2,1)} %bitcast.18, bf16[2048,768]{1,0:T(8,128)(2,1)} %constant_dynamic-update-slice_fusion.w_ref.w, ...), custom_call_target="tpu_custom_call", output_to_operand_aliasing={{4}: (2, {})} | custom-call | flops 6442450944 | bytes 16000000 | tf_op jit(solution)/shard_map/proj/pallas_call | solution.py:101
  74.4 0.7 all-gather.16.cloned.1.call-update
  77.0 3.9 fusion.2
  81.0 2.0 pad_maximum_fusion.1
  82.9 1.4 slice_bitcast_fusion.1
  84.4 12.3 %norm_rope.2 = (bf16[2048,256]{1,0:T(8,128)(2,1)}, bf16[2048,256]{1,0:T(8,128)(2,1)}, f32[2048,128]{1,0:T(8,128)}, f32[2048,128]{1,0:T(8,128)}) custom-call(f32[2048,256]{1,0:T(8,128)} %get-tuple-element.59.q_ref.qr_ref, f32[2048,256]{1,0:T(8,128)} %get-tuple-element.60.k_ref.kr_ref, f32[8,512]{1,0:T(8,128)} %get-tuple-element.61.s_ref, ...), custom_call_target="tpu_custom_call" | custom-call | flops 2000000000 | bytes 10000000 | tf_op jit(solution)/shard_map/norm_rope/pallas_call | solution.py:173
  96.7 29.8 %attn_fwd.2 = (bf16[2048,256]{1,0:T(8,128)(2,1)}, f32[8,512]{1,0:T(8,128)}, bf16[256,2048]{1,0:T(8,128)(2,1)}) custom-call(bf16[2048,256]{1,0:T(8,128)(2,1)} %get-tuple-element.62.q_ref, bf16[2048,256]{1,0:T(8,128)(2,1)} %get-tuple-element.63.k_ref, bf16[2048,256]{1,0:T(8,128)(2,1)} %get-tuple-element.64.v_ref), custom_call_target="tpu_custom_call" | custom-call | flops 8999999488 | bytes 6000000 | tf_op jit(solution)/shard_map/attn_fwd/pallas_call | solution.py:283
  126.5 8.9 %all-gather.8.cloned.1.call-done.wo_ref = bf16[2048,2048]{1,0:T(8,128)(2,1)} async-done(((bf16[256,2048]{1,0:T(8,128)(2,1)}), bf16[2048,2048]{1,0:T(8,128)(2,1)}) %all-gather.8.cloned.1.call-update) | async-done | bytes 8388624 | tf_op jit(solution)/shard_map/all_gather | solution.py:705
  135.4 32.0 %out_block.2 = (bf16[256,2048]{1,0:T(8,128)(2,1)}, bf16[256,2048]{1,0:T(8,128)(2,1)}, f32[8,256]{1,0:T(8,128)}, bf16[2048,256]{1,0:T(8,128)(2,1)}) custom-call(bf16[256,2048]{1,0:T(8,128)(2,1)} %get-tuple-element.65.o_ref, bf16[2048,2048]{1,0:T(8,128)(2,1)} %all-gather.8.cloned.1.call-done.wo_ref, bf16[256,2048]{1,0:T(8,128)(2,1)} %get-tuple-element.113.x_ref, ...), custom_call_target="tpu_custom_call" | custom-call | flops 9294966784 | bytes 14000000 | tf_op jit(solution)/shard_map/out_block/pallas_call | solution.py:359
  167.7 30.0 %all-gather.16.cloned.1.call-done = bf16[1,2048,2048]{2,1,0:T(8,128)(2,1)} async-done(((bf16[1,256,2048]{2,1,0:T(8,128)(2,1)}), bf16[1,2048,2048]{2,1,0:T(8,128)(2,1)}) %all-gather.16.cloned.1.call-update) | async-done | bytes 8388624 | tf_op jit(solution)/shard_map/all_gather | solution.py:699
  197.6 10.9 %proj.3 = (f32[2048,256]{1,0:T(8,128)}, f32[2048,256]{1,0:T(8,128)}, bf16[2048,256]{1,0:T(8,128)(2,1)}, f32[8,512]{1,0:T(8,128)}) custom-call(bf16[2048,2048]{1,0:T(8,128)(2,1)} %bitcast.20, bf16[2048,768]{1,0:T(8,128)(2,1)} %constant_dynamic-update-slice_fusion.w_ref.w), custom_call_target="tpu_custom_call" | custom-call | flops 6442450944 | bytes 16000000 | tf_op jit(solution)/shard_map/proj/pallas_call | solution.py:101
  208.6 12.3 %norm_rope.3 = (bf16[2048,256]{1,0:T(8,128)(2,1)}, bf16[2048,256]{1,0:T(8,128)(2,1)}, f32[2048,128]{1,0:T(8,128)}, f32[2048,128]{1,0:T(8,128)}) custom-call(f32[2048,256]{1,0:T(8,128)} %get-tuple-element.68.q_ref.qr_ref, f32[2048,256]{1,0:T(8,128)} %get-tuple-element.69.k_ref.kr_ref, f32[8,512]{1,0:T(8,128)} %get-tuple-element.70.s_ref, ...), custom_call_target="tpu_custom_call" | custom-call | flops 2000000000 | bytes 10000000 | tf_op jit(solution)/shard_map/norm_rope/pallas_call | solution.py:173
  220.8 29.7 %attn_fwd.3 = (bf16[2048,256]{1,0:T(8,128)(2,1)}, f32[8,512]{1,0:T(8,128)}, bf16[256,2048]{1,0:T(8,128)(2,1)}) custom-call(bf16[2048,256]{1,0:T(8,128)(2,1)} %get-tuple-element.71.q_ref, bf16[2048,256]{1,0:T(8,128)(2,1)} %get-tuple-element.72.k_ref, bf16[2048,256]{1,0:T(8,128)(2,1)} %get-tuple-element.73.v_ref), custom_call_target="tpu_custom_call" | custom-call | flops 8999999488 | bytes 6000000 | tf_op jit(solution)/shard_map/attn_fwd/pallas_call | solution.py:283
  250.6 26.5 %out_block.3 = (bf16[256,2048]{1,0:T(8,128)(2,1)}, bf16[256,2048]{1,0:T(8,128)(2,1)}, f32[8,256]{1,0:T(8,128)}, bf16[2048,256]{1,0:T(8,128)(2,1)}) custom-call(bf16[256,2048]{1,0:T(8,128)(2,1)} %get-tuple-element.74.o_ref, bf16[2048,2048]{1,0:T(8,128)(2,1)} %all-gather.8.cloned.1.call-done.wo_ref, bf16[256,2048]{1,0:T(8,128)(2,1)} %get-tuple-element.114.x_ref, ...), custom_call_target="tpu_custom_call" | custom-call | flops 9294966784 | bytes 14000000 | tf_op jit(solution)/shard_map/out_block/pallas_call | solution.py:359
  277.1 29.9 %attn_bwd.3 = (f32[2048,256]{1,0:T(8,128)}, f32[2048,256]{1,0:T(8,128)}, bf16[2048,256]{1,0:T(8,128)(2,1)}, f32[8,512]{1,0:T(8,128)}, f32[8,256]{1,0:T(8,128)}) custom-call(bf16[2048,256]{1,0:T(8,128)(2,1)} %get-tuple-element.71.q_ref, bf16[2048,256]{1,0:T(8,128)(2,1)} %get-tuple-element.72.k_ref, bf16[2048,256]{1,0:T(8,128)(2,1)} %get-tuple-element.73.v_ref, ...), custom_call_target="tpu_custom_call" | custom-call | flops 16000000000 | bytes 16000000 | tf_op jit(solution)/shard_map/attn_bwd/pallas_call | solution.py:446
  306.9 16.4 %norm_bwd.3 = (bf16[2048,768]{1,0:T(8,128)(2,1)}, f32[8,256]{1,0:T(8,128)}) custom-call(f32[2048,256]{1,0:T(8,128)} %get-tuple-element.90.dqu_ref, f32[2048,256]{1,0:T(8,128)} %get-tuple-element.91.dku_ref, bf16[2048,256]{1,0:T(8,128)(2,1)} %get-tuple-element.92.dv_ref, f32[2048,256]{1,0:T(8,128)} %get-tuple-element.68.q_ref.qr_ref, ...), custom_call_target="tpu_custom_call" | custom-call | flops 2000000000 | bytes 14000000 | tf_op jit(solution)/shard_map/norm_bwd/pallas_call | solution.py:488
  323.3 29.9 %attn_bwd.2 = (f32[2048,256]{1,0:T(8,128)}, f32[2048,256]{1,0:T(8,128)}, bf16[2048,256]{1,0:T(8,128)(2,1)}, f32[8,512]{1,0:T(8,128)}, f32[8,256]{1,0:T(8,128)}) custom-call(bf16[2048,256]{1,0:T(8,128)(2,1)} %get-tuple-element.62.q_ref, bf16[2048,256]{1,0:T(8,128)(2,1)} %get-tuple-element.63.k_ref, bf16[2048,256]{1,0:T(8,128)(2,1)} %get-tuple-element.64.v_ref, ...), custom_call_target="tpu_custom_call" | custom-call | flops 16000000000 | bytes 16000000 | tf_op jit(solution)/shard_map/attn_bwd/pallas_call | solution.py:446
  353.2 13.7 %norm_bwd.2 = (bf16[2048,768]{1,0:T(8,128)(2,1)}, f32[8,256]{1,0:T(8,128)}) custom-call(f32[2048,256]{1,0:T(8,128)} %get-tuple-element.80.dqu_ref, f32[2048,256]{1,0:T(8,128)} %get-tuple-element.81.dku_ref, bf16[2048,256]{1,0:T(8,128)(2,1)} %get-tuple-element.82.dv_ref, f32[2048,256]{1,0:T(8,128)} %get-tuple-element.59.q_ref.qr_ref, ...), custom_call_target="tpu_custom_call" | custom-call | flops 2000000000 | bytes 14000000 | tf_op jit(solution)/shard_map/norm_bwd/pallas_call | solution.py:488
  366.9 0.7 fusion.3
  368.8 1.5 pad_maximum_fusion
  370.3 152.1 %grads.1 = (bf16[2,256,2048]{2,1,0:T(8,128)(2,1)}, bf16[2048,256]{1,0:T(8,128)(2,1)}, bf16[2048,256]{1,0:T(8,128)(2,1)}, bf16[2048,256]{1,0:T(8,128)(2,1)}, bf16[256,2048]{1,0:T(8,128)(2,1)}) custom-call(bf16[2048,768]{1,0:T(8,128)(2,1)} %get-tuple-element.85.d0, bf16[2048,768]{1,0:T(8,128)(2,1)} %get-tuple-element.95.d1, ...), custom_call_target="tpu_custom_call" | custom-call | flops 99999997952 | bytes 40000000 | tf_op jit(solution)/shard_map/grads/pallas_call | solution.py:676
  522.4 3.2 copy.30
  525.7 1.0 copy.31
  527.3 1.0 copy.32
  528.3 1.0 copy.33
  529.2 1.0 copy.34
  (52 shorter events, 4.6 us)
Async XLA Ops:
  7.2 2.5 copy-start
  7.2 56.1 %all-gather.14.cloned.1.call-start = ((), (), s32[]{:S(2)}) async-start(), calls=%async_computation.3 | async-start | bytes 9437184 | tf_op jit(solution)/shard_map/all_gather | solution.py:699
  9.7 2.4 copy-start.2
  11.9 1.6 copy-start.3
  12.0 2.7 copy-start.4
  12.0 123.4 %all-gather.8.cloned.1.call-start = ((), (), s32[]{:S(2)}) async-start(), calls=%async_computation | async-start | bytes 9437184 | tf_op jit(solution)/shard_map/all_gather | solution.py:705
  74.3 1.0 copy-start.15
  74.3 1.6 copy-start.16
  74.3 2.2 copy-start.14
  74.3 123.3 %all-gather.16.cloned.1.call-start = ((), (), s32[]{:S(2)}) async-start(), calls=%async_computation.4 | async-start | bytes 9437184 | tf_op jit(solution)/shard_map/all_gather | solution.py:699
  75.0 295.3 %all-gather.10.cloned.1.call-start = ((), (), s32[]{:S(2)}) async-start(), calls=%async_computation.1 | async-start | bytes 9437184 | tf_op jit(solution)/shard_map/all_gather | solution.py:717
  80.9 2.0 copy-start.1
  167.4 202.9 %all-gather.12.cloned.1.call-start = ((), (), s32[]{:S(2)}) async-start(), calls=%async_computation.2 | async-start | bytes 9437184 | tf_op jit(solution)/shard_map/all_gather | solution.py:717
  353.2 13.8 %copy-start.12 = (f32[8,256]{1,0:T(8,128)S(1)}, f32[8,256]{1,0:T(8,128)}, u32[]{:S(2)}) copy-start(f32[8,256]{1,0:T(8,128)} %get-tuple-element.108) | copy-start | bytes 24580
  353.2 15.1 %copy-start.11 = (f32[8,256]{1,0:T(8,128)S(1)}, f32[8,256]{1,0:T(8,128)}, u32[]{:S(2)}) copy-start(f32[8,256]{1,0:T(8,128)} %get-tuple-element.106) | copy-start | bytes 24580
  353.2 15.1 %copy-start.13 = (f32[8,256]{1,0:T(8,128)S(1)}, f32[8,256]{1,0:T(8,128)}, u32[]{:S(2)}) copy-start(f32[8,256]{1,0:T(8,128)} %get-tuple-element.105) | copy-start | bytes 24580
  353.2 15.6 %copy-start.9 = (bf16[256,2048]{1,0:T(8,128)(2,1)S(1)}, bf16[256,2048]{1,0:T(8,128)(2,1)}, u32[]{:S(2)}) copy-start(bf16[256,2048]{1,0:T(8,128)(2,1)} %get-tuple-element.67) | copy-start | bytes 3145732
  353.2 15.6 %copy-start.10 = (bf16[256,2048]{1,0:T(8,128)(2,1)S(1)}, bf16[256,2048]{1,0:T(8,128)(2,1)}, u32[]{:S(2)}) copy-start(bf16[256,2048]{1,0:T(8,128)(2,1)} %get-tuple-element.75) | copy-start | bytes 3145732
  522.4 3.3 copy-start.8
  525.7 1.6 copy-start.7
  525.7 2.6 copy-start.6
  527.3 1.9 copy-start.5
Sparse Core Ops, SparseCore 0:
  12.1 51.1 all-gather.13
  74.4 60.8 all-gather.7
  137.8 59.8 all-gather.15
  199.3 60.8 all-gather.9
  277.2 51.7 all-gather.11

commit v3 on v2

--- a/solution.py
+++ b/solution.py
@@ -63,12 +63,101 @@
     pl.semaphore_wait(barrier, NDEV - 1)
 
 
-def rope_tables():
+def nbr_barrier(me):
+    barrier = pltpu.get_barrier_semaphore()
+    for mask in (1, 2, 4):
+        pl.semaphore_signal(barrier, inc=1, device_id=(peer_of(me, mask),), device_id_type=MESH)
+    pl.semaphore_wait(barrier, 3)
+
+
+DMA = pltpu.SemaphoreType.DMA
+ANYWHERE = pl.BlockSpec(memory_space=pl.ANY)
+BG_SEMS = [DMA((8,)), DMA((8,)), DMA((2,))]
+
+
+def shard_rows(dev, lo=0, count=TOK):
+    return pl.ds(pl.multiple_of(dev * TOK + lo, HD), count)
+
+
+def stage1(me, src, full, sems, lo=0, count=TOK, at=0):
+    send, recv, own = sems
+    there = full.at[shard_rows(me, lo, count), :]
+    part = src.at[pl.ds(lo, count), :]
+    copies = [pltpu.make_async_remote_copy(
+        src_ref=part, dst_ref=there, send_sem=send.at[at + k], recv_sem=recv.at[at + k],
+        device_id=(peer_of(me, mask),), device_id_type=MESH) for k, mask in enumerate((2, 4, 1))]
+    return copies + [pltpu.make_async_copy(part, there, own.at[0])]
+
+
+def stage2(me, full, sems, at=0):
+    send, recv, _ = sems
+    xn, yn = peer_of(me, 2), peer_of(me, 4)
+    half = TOK // 2
+    plan = ((shard_rows(yn, half, half), 2), (shard_rows(xn, 0, half), 4), (shard_rows(xn), 1), (shard_rows(yn), 1))
+    return [pltpu.make_async_remote_copy(
+        src_ref=full.at[rows, :], dst_ref=full.at[rows, :], send_sem=send.at[at + k], recv_sem=recv.at[at + k],
+        device_id=(peer_of(me, mask),), device_id_type=MESH) for k, (rows, mask) in enumerate(plan)]
+
+
+def stage3(me, full, sems, at=0):
+    send, recv, _ = sems
+    rows = shard_rows(peer_of(me, 6))
+    return [pltpu.make_async_remote_copy(
+        src_ref=full.at[rows, :], dst_ref=full.at[rows, :], send_sem=send.at[at], recv_sem=recv.at[at],
+        device_id=(peer_of(me, 1),), device_id_type=MESH)]
+
+
+def start(copies):
+    for c in copies:
+        c.start()
+
+
+def wait(copies):
+    for c in copies:
+        c.wait()
+
+
+def gather_kernel(x_ref, freq_ref, full_ref, cos_ref, sin_ref, *sems):
+    me = lax.axis_index('tp')
+    nbr_barrier(me)
+    first = stage1(me, x_ref.at[0], full_ref, sems)
+    start(first)
+    freq = freq_ref[...]
+    sign = jnp.where(lax.broadcasted_iota(jnp.int32, (TOK, HD), 1) < HD // 2, -1.0, 1.0)
+
+    def table(i, carry):
+        rows = pl.ds(pl.multiple_of(i * TOK, TOK), TOK)
+        pos = (lax.broadcasted_iota(jnp.int32, (TOK, HD), 0) + i * TOK).astype(F32)
+        angle = pos * freq
+        cos_ref[rows, :] = jnp.cos(angle)
+        sin_ref[rows, :] = jnp.sin(angle) * sign
+        return carry
+
+    lax.fori_loop(0, SEQ // TOK, table, 0)
+    wait(first)
+    second = stage2(me, full_ref, sems, 3)
+    start(second)
+    wait(second)
+    third = stage3(me, full_ref, sems, 7)
+    start(third)
+    wait(third)
+
+
+def first_gather(x, cid):
     half = HD // 2
     inv_freq = 1.0 / (ROPE_THETA ** (jnp.arange(half, dtype=F32) / half))
-    angles = jnp.arange(SEQ, dtype=F32)[:, None] * inv_freq[None, :]
-    cos, sin = jnp.cos(angles), jnp.sin(angles)
-    return jnp.concatenate([cos, cos], axis=1), jnp.concatenate([-sin, sin], axis=1)
+    freq = jnp.concatenate([inv_freq, inv_freq])[None, :]
+    vm = pl.BlockSpec(memory_space=pltpu.VMEM)
+    return pl.pallas_call(
+        gather_kernel,
+        in_specs=[ANYWHERE, vm],
+        out_specs=[ANYWHERE, vm, vm],
+        out_shape=[sds((SEQ, DIM), BF), sds((SEQ, HD), F32), sds((SEQ, HD), F32)],
+        scratch_shapes=BG_SEMS,
+        compiler_params=params(collective_id=cid, has_side_effects=True),
+        cost_estimate=cost(20e9, 20e6),
+        name="gather",
+    )(x, freq)
 
 
 def row_sums(vals):
@@ -82,48 +171,55 @@
     return jnp.broadcast_to(row, (HD, row.shape[1])).T
 
 
-def proj_kernel(x_ref, w_ref, *rest):
-    q_ref, k_ref, v_ref, s_ref = rest[-5:-1] if len(rest) == 6 else rest
+def proj_kernel(pick, x_ref, wq_ref, wk_ref, wv_ref, shard_ref, q_ref, k_ref, v_ref, s_ref, full_ref, *sems):
     i = pl.program_id(0)
+    me = lax.axis_index('tp')
+    src = shard_ref if pick is None else shard_ref.at[pick]
+
+    @pl.when(i == 0)
+    def _():
+        nbr_barrier(me)
+        start(stage1(me, src, full_ref, sems, 0, TOK // 2))
+
     x = x_ref[...]
-    q = dot(x, w_ref[:, :LOC])
+    q = dot(x, wq_ref[...])
     q_ref[...] = q
     s_ref[pl.ds(i, 1), :] = row_sums(q * q)
-    k = dot(x, w_ref[:, LOC:2 * LOC])
+    k = dot(x, wk_ref[...])
     k_ref[...] = k
     s_ref[pl.ds(i + NB, 1), :] = row_sums(k * k)
-    v_ref[...] = dot(x, w_ref[:, 2 * LOC:]).astype(BF)
-
-
-def project(x, w, through=()):
+    v_ref[...] = dot(x, wv_ref[...]).astype(BF)
+
+    @pl.when(i == NB - 1)
+    def _():
+        wait(stage1(me, src, full_ref, sems, 0, TOK // 2))
+
+
+def project(x, wq, wk, wv, shard, pick, cid):
     row = pl.BlockSpec((BLK, LOC), lambda i: (i, 0))
-    whole = [pl.BlockSpec(memory_space=pl.ANY)] * len(through)
+    wspec = pl.BlockSpec((DIM, LOC), lambda i: (0, 0))
     return pl.pallas_call(
-        proj_kernel,
+        functools.partial(proj_kernel, pick),
         grid=(NB,),
-        in_specs=[pl.BlockSpec((BLK, DIM), lambda i: (i, 0)), pl.BlockSpec((DIM, 3 * LOC), lambda i: (0, 0))] + whole,
-        out_specs=[row, row, row, pl.BlockSpec((2 * NB, BLK), lambda i: (0, 0))] + whole,
-        out_shape=[sds((SEQ, LOC), F32), sds((SEQ, LOC), F32), sds((SEQ, LOC), BF), sds((2 * NB, BLK), F32)]
-        + [sds(t.shape, t.dtype) for t in through],
-        input_output_aliases={2 + n: 4 + n for n in range(len(through))},
-        compiler_params=params(dimension_semantics=("arbitrary",)),
+        in_specs=[pl.BlockSpec((BLK, DIM), lambda i: (i, 0)), wspec, wspec, wspec, ANYWHERE],
+        out_specs=[row, row, row, pl.BlockSpec((2 * NB, BLK), lambda i: (0, 0)), ANYWHERE],
+        out_shape=[sds((SEQ, LOC), F32), sds((SEQ, LOC), F32), sds((SEQ, LOC), BF), sds((2 * NB, BLK), F32),
+                   sds((SEQ, DIM), BF)],
+        scratch_shapes=BG_SEMS,
+        compiler_params=params(dimension_semantics=("arbitrary",), collective_id=cid, has_side_effects=True),
         cost_estimate=cost(2 * SEQ * DIM * 3 * LOC, 16e6),
         name="proj",
-    )(x, w, *through)
+    )(x, wq, wk, wv, shard)
 
 
 def exchange(me, srcs, slots, send_sems, recv_sems):
-    entry_barrier(me)
     copies = []
     for n, (src, slot) in enumerate(zip(srcs, slots)):
         for p, mask in enumerate(ORDER):
             copies.append(pltpu.make_async_remote_copy(
                 src_ref=src, dst_ref=slot.at[p], send_sem=send_sems.at[n, p], recv_sem=recv_sems.at[n, p],
                 device_id=(peer_of(me, mask),), device_id_type=MESH))
-    for c in copies:
-        c.start()
-    for c in copies:
-        c.wait()
+    return copies
 
 
 def ordered_total(me, src, slot):
@@ -137,51 +233,54 @@
     return total
 
 
-def rotated(v, cos, sin):
-    out = []
-    for h in range(v.shape[1] // HD):
-        part = v[:, h * HD:(h + 1) * HD]
-        out.append(part * cos + pltpu.roll(part, HD // 2, 1) * sin)
-    return out
-
-
-def norm_kernel(q_ref, k_ref, s_ref, gq_ref, gk_ref, cos_ref, sin_ref, qo_ref, ko_ref, iq_ref, ik_ref,
-                slot, total, send_sems, recv_sems):
+def norm_kernel(pick, q_ref, k_ref, s_ref, gq_ref, gk_ref, cos_ref, sin_ref, shard_ref, full_in, qo_ref, ko_ref, iq_ref,
+                ik_ref, full_ref, slot, total, send_sems, recv_sems, *sems):
+    del full_in
     i = pl.program_id(0)
     me = lax.axis_index('tp')
+    src = shard_ref if pick is None else shard_ref.at[pick]
 
     @pl.when(i == 0)
     def _():
-        exchange(me, [s_ref], [slot], send_sems, recv_sems)
+        entry_barrier(me)
+        sums = exchange(me, [s_ref], [slot], send_sems, recv_sems)
+        start(sums)
+        start(stage1(me, src, full_ref, sems, TOK // 2, TOK // 2))
+        wait(sums)
         total[...] = lax.rsqrt(ordered_total(me, s_ref, slot) / DIM + EPS)
 
     cos, sin = cos_ref[...], sin_ref[...]
-    for src, dst, inv_ref, g_ref, row in ((q_ref, qo_ref, iq_ref, gq_ref, i), (k_ref, ko_ref, ik_ref, gk_ref, i + NB)):
+    for raw, dst, inv_ref, g_ref, row in ((q_ref, qo_ref, iq_ref, gq_ref, i), (k_ref, ko_ref, ik_ref, gk_ref, i + NB)):
         inv = as_column(total[pl.ds(row, 1), :])
         inv_ref[...] = inv
         g = g_ref[...].astype(F32)
         for h in range(LOC // HD):
             sl = slice(h * HD, (h + 1) * HD)
-            hat = src[:, sl] * inv * g[:, sl]
+            hat = raw[:, sl] * inv * g[:, sl]
             dst[:, sl] = (hat * cos + pltpu.roll(hat, HD // 2, 1) * sin).astype(BF)
 
-
-def norm_rope(q, k, s, gq, gk, cos, sin, cid):
+    @pl.when(i == NB - 1)
+    def _():
+        wait(stage1(me, src, full_ref, sems, TOK // 2, TOK // 2))
+
+
+def norm_rope(q, k, s, gq, gk, cos, sin, shard, full, pick, cid):
     row = pl.BlockSpec((BLK, LOC), lambda i: (i, 0))
     half = pl.BlockSpec((BLK, HD), lambda i: (i, 0))
     gain = pl.BlockSpec((1, LOC), lambda i: (0, 0))
     return pl.pallas_call(
-        norm_kernel,
+        functools.partial(norm_kernel, pick),
         grid=(NB,),
-        in_specs=[row, row, pl.BlockSpec((2 * NB, BLK), lambda i: (0, 0)), gain, gain, half, half],
-        out_specs=[row, row, half, half],
-        out_shape=[sds((SEQ, LOC), BF), sds((SEQ, LOC), BF), sds((SEQ, HD), F32), sds((SEQ, HD), F32)],
+        in_specs=[row, row, pl.BlockSpec((2 * NB, BLK), lambda i: (0, 0)), gain, gain, half, half, ANYWHERE, ANYWHERE],
+        out_specs=[row, row, half, half, ANYWHERE],
+        out_shape=[sds((SEQ, LOC), BF), sds((SEQ, LOC), BF), sds((SEQ, HD), F32), sds((SEQ, HD), F32), sds((SEQ, DIM), BF)],
+        input_output_aliases={8: 4},
         scratch_shapes=[pltpu.VMEM((NDEV - 1, 2 * NB, BLK), F32), pltpu.VMEM((2 * NB, BLK), F32),
-                        pltpu.SemaphoreType.DMA((1, NDEV - 1)), pltpu.SemaphoreType.DMA((1, NDEV - 1))],
+                        DMA((1, NDEV - 1)), DMA((1, NDEV - 1))] + BG_SEMS,
         compiler_params=params(dimension_semantics=("arbitrary",), collective_id=cid, has_side_effects=True),
         cost_estimate=cost(2e9, 10e6),
         name="norm_rope",
-    )(q, k, s, gq, gk, cos, sin)
+    )(q, k, s, gq, gk, cos, sin, shard, full)
 
 
 def causal_mask():
@@ -190,7 +289,9 @@
     return keys <= queries
 
 
-def attn_kernel(q_ref, k_ref, v_ref, o_ref, lse_ref, recv_ref, p_scr, vt_scr, acc_scr, o_scr, send_sems, recv_sems, own_sems):
+def attn_kernel(q_ref, k_ref, v_ref, full_in, o_ref, lse_ref, recv_ref, full_ref, p_scr, vt_scr, acc_scr, o_scr, send_sems,
+                recv_sems, own_sems, *sems):
+    del full_in
     h, step = pl.program_id(0), pl.program_id(1)
     me = lax.axis_index('tp')
     qi = (me // 2 + 1 + step) % NB
@@ -199,6 +300,12 @@
     @pl.when(jnp.logical_and(h == 0, step == 0))
     def _():
         entry_barrier(me)
+        start(stage2(me, full_ref, sems))
+
+    @pl.when(jnp.logical_and(h == 1, step == NB - 2))
+    def _():
+        wait(stage2(me, full_ref, sems))
+        start(stage3(me, full_ref, sems, 4))
 
     @pl.when(step == 0)
     def _():
@@ -259,6 +366,7 @@
 
     @pl.when(jnp.logical_and(h == 1, step == NB - 1))
     def _():
+        wait(stage3(me, full_ref, sems, 4))
         for hh in range(2):
             for st in range(NB):
                 for half in range(2):
@@ -278,21 +386,22 @@
                     device_id=(peer,), device_id_type=MESH).wait_recv()
 
 
-def attention(q, k, v, cid):
+def attention(q, k, v, gathered, cid):
     full = pl.BlockSpec((SEQ, HD), lambda h, i: (0, h))
     return pl.pallas_call(
         attn_kernel,
         grid=(2, NB),
-        in_specs=[full, full, full],
-        out_specs=[full, pl.BlockSpec((2 * NB, BLK), lambda h, i: (0, 0)), pl.BlockSpec(memory_space=pl.ANY)],
-        out_shape=[sds((SEQ, LOC), BF), sds((2 * NB, BLK), F32), sds((TOK, DIM), BF)],
+        in_specs=[full, full, full, ANYWHERE],
+        out_specs=[full, pl.BlockSpec((2 * NB, BLK), lambda h, i: (0, 0)), ANYWHERE, ANYWHERE],
+        out_shape=[sds((SEQ, LOC), BF), sds((2 * NB, BLK), F32), sds((TOK, DIM), BF), sds((SEQ, DIM), BF)],
+        input_output_aliases={3: 3},
         scratch_shapes=[pltpu.VMEM((NB, BLK, BLK), F32), pltpu.VMEM((HD, SEQ), BF), pltpu.VMEM((HD, BLK), F32),
                         pltpu.VMEM((2, NB, BLK, HD), BF), pltpu.SemaphoreType.DMA((2, NB, 2)),
-                        pltpu.SemaphoreType.DMA((2, NDEV)), pltpu.SemaphoreType.DMA((2,))],
+                        DMA((2, NDEV)), DMA((2,))] + BG_SEMS,
         compiler_params=params(dimension_semantics=("arbitrary", "arbitrary"), collective_id=cid, has_side_effects=True),
         cost_estimate=cost(9e9, 6e6),
         name="attn_fwd",
-    )(q, k, v)
+    )(q, k, v, gathered)
 
 
 def out_kernel(o_ref, wo_ref, x_ref, dy_ref, ga_ref, y_ref, da_ref, gga_ref, recv_ref, a_scr, dh_scr, send_sems, recv_sems, own_sem):
@@ -311,8 +420,8 @@
     r = lax.rsqrt(jnp.mean(a * a, axis=-1, keepdims=True) + EPS)
     n = a * r
     ga = ga_ref[...].astype(F32)
-    dy = dy_ref[...].astype(F32)
-    y_ref[...] = (x_ref[...].astype(F32) + n * ga).astype(BF)
+    dy = dy_ref[0].astype(F32)
+    y_ref[...] = (x_ref[0].astype(F32) + n * ga).astype(BF)
     col = jnp.sum(dy * n, axis=0, keepdims=True)
     for i in range(8):
         gga_ref[i:i + 1, :] = col[:, i * (DIM // 8):(i + 1) * (DIM // 8)]
@@ -354,25 +463,46 @@
             send_sem=send_sems.at[0, 0], recv_sem=recv_sems.at[peer], device_id=(peer,), device_id_type=MESH).wait_recv()
 
 
-def out_block(o, wo, x, dy, ga, cid):
-    spec = pl.BlockSpec(memory_space=pltpu.VMEM)
+def out_block(o, wo, x, dy, ga, b, cid):
+    def whole(*shape):
+        return pl.BlockSpec(shape, lambda i: (0,) * len(shape))
+
+    batch = pl.BlockSpec((1, TOK, DIM), lambda i: (b, 0, 0))
     return pl.pallas_call(
         out_kernel,
-        in_specs=[spec] * 5,
-        out_specs=[spec] * 3 + [pl.BlockSpec(memory_space=pl.ANY)],
+        grid=(1,),
+        in_specs=[whole(TOK, DIM), whole(DIM, DIM), batch, batch, whole(1, DIM)],
+        out_specs=[whole(TOK, DIM), whole(TOK, DIM), whole(8, DIM // 8), ANYWHERE],
         out_shape=[sds((TOK, DIM), BF), sds((TOK, DIM), BF), sds((8, DIM // 8), F32), sds((SEQ, LOC), BF)],
         scratch_shapes=[pltpu.VMEM((TOK, DIM), F32), pltpu.VMEM((NB, TOK, DIM // NB), BF), pltpu.SemaphoreType.DMA((NB, 2)),
                         pltpu.SemaphoreType.DMA((NDEV,)), pltpu.SemaphoreType.DMA],
-        compiler_params=params(collective_id=cid, has_side_effects=True),
+        compiler_params=params(dimension_semantics=("arbitrary",), collective_id=cid, has_side_effects=True),
         cost_estimate=cost(4 * TOK * DIM * DIM + 5e9, 14e6),
         name="out_block",
     )(o, wo, x, dy, ga)
 
 
-def attn_bwd_kernel(q_ref, k_ref, v_ref, do_ref, lse_ref, qr_ref, kr_ref, iq_ref, ik_ref, gq_ref, gk_ref, cos_ref, sin_ref,
-                    dqu_ref, dku_ref, dv_ref, dots_ref, gg_ref,
-                    p_scr, dp_scr, kt_scr, dqt_scr, dq_scr, dk_scr, dv_scr):
+def attn_bwd_kernel(older, q_ref, k_ref, v_ref, do_ref, lse_ref, qr_ref, kr_ref, iq_ref, ik_ref, gq_ref, gk_ref, cos_ref, sin_ref,
+                    shard_ref, *rest):
+    if older:
+        _, dqu_ref, dku_ref, dv_ref, dots_ref, gg_ref, full_ref, old_ref, *rest = rest
+    else:
+        dqu_ref, dku_ref, dv_ref, dots_ref, gg_ref, full_ref, *rest = rest
+    p_scr, dp_scr, kt_scr, dqt_scr, dq_scr, dk_scr, dv_scr, *sems = rest
     h, qi = pl.program_id(0), pl.program_id(1)
+    me = lax.axis_index('tp')
+
+    def moving():
+        return (stage3(me, old_ref, sems, 4) if older else []) + stage1(me, shard_ref, full_ref, sems)
+
+    @pl.when(jnp.logical_and(h == 0, qi == 0))
+    def _():
+        nbr_barrier(me)
+        start(moving())
+
+    @pl.when(jnp.logical_and(h == 1, qi == NB - 1))
+    def _():
+        wait(moving())
 
     @pl.when(qi == 0)
     def _():
@@ -437,36 +567,42 @@
         lax.fori_loop(0, NB, tail, 0)
 
 
-def attention_bwd(q, k, v, do, lse, qr, kr, iq, ik, gq, gk, cos, sin):
+def attention_bwd(q, k, v, do, lse, qr, kr, iq, ik, gq, gk, cos, sin, shard, old, cid):
     blk = pl.BlockSpec((BLK, HD), lambda h, i: (i, h))
     full = pl.BlockSpec((SEQ, HD), lambda h, i: (0, h))
     shared = pl.BlockSpec((SEQ, HD), lambda h, i: (0, 0))
     gain = pl.BlockSpec((1, HD), lambda h, i: (0, h))
     rows = pl.BlockSpec((2 * NB, BLK), lambda h, i: (0, 0))
     return pl.pallas_call(
-        attn_bwd_kernel,
+        functools.partial(attn_bwd_kernel, bool(old)),
         grid=(2, NB),
-        in_specs=[blk, full, full, blk, rows, full, full, shared, shared, gain, gain, shared, shared],
-        out_specs=[full, full, full, rows, pl.BlockSpec((8, HD), lambda h, i: (0, h))],
+        in_specs=[blk, full, full, blk, rows, full, full, shared, shared, gain, gain, shared, shared, ANYWHERE] + [ANYWHERE] * len(old),
+        out_specs=[full, full, full, rows, pl.BlockSpec((8, HD), lambda h, i: (0, h)), ANYWHERE] + [ANYWHERE] * len(old),
         out_shape=[sds((SEQ, LOC), F32), sds((SEQ, LOC), F32), sds((SEQ, LOC), BF), sds((2 * NB, BLK), F32),
-                   sds((8, LOC), F32)],
+                   sds((8, LOC), F32), sds((SEQ, DIM), BF)] + [sds((SEQ, DIM), BF)] * len(old),
+        input_output_aliases={14: 6} if old else {},
         scratch_shapes=[pltpu.VMEM((NB, BLK, BLK), F32), pltpu.VMEM((NB, BLK, BLK), F32), pltpu.VMEM((HD, SEQ), BF),
                         pltpu.VMEM((HD, BLK), F32), pltpu.VMEM((SEQ, HD), F32), pltpu.VMEM((SEQ, HD), F32),
-                        pltpu.VMEM((SEQ, HD), F32)],
-        compiler_params=params(dimension_semantics=("arbitrary", "arbitrary")),
+                        pltpu.VMEM((SEQ, HD), F32)] + BG_SEMS,
+        compiler_params=params(dimension_semantics=("arbitrary", "arbitrary"), collective_id=cid, has_side_effects=True),
         cost_estimate=cost(16e9, 16e6),
         name="attn_bwd",
-    )(q, k, v, do, lse, qr, kr, iq, ik, gq, gk, cos, sin)
-
-
-def norm_bwd_kernel(dqu_ref, dku_ref, dv_ref, qr_ref, kr_ref, iq_ref, ik_ref, dots_ref, ga_ref, out_ref, gga_ref,
-                    slot, ga_slot, total, send_sems, recv_sems):
+    )(q, k, v, do, lse, qr, kr, iq, ik, gq, gk, cos, sin, shard, *old)
+
+
+def norm_bwd_kernel(dqu_ref, dku_ref, dv_ref, qr_ref, kr_ref, iq_ref, ik_ref, dots_ref, ga_ref, full_in, out_ref, gga_ref,
+                    full_ref, slot, ga_slot, total, send_sems, recv_sems, *sems):
+    del full_in
     i = pl.program_id(0)
     me = lax.axis_index('tp')
 
     @pl.when(i == 0)
     def _():
-        exchange(me, [dots_ref, ga_ref], [slot, ga_slot], send_sems, recv_sems)
+        entry_barrier(me)
+        sums = exchange(me, [dots_ref, ga_ref], [slot, ga_slot], send_sems, recv_sems)
+        start(sums)
+        start(stage2(me, full_ref, sems))
+        wait(sums)
         total[...] = ordered_total(me, dots_ref, slot) / DIM
         gga_ref[...] = ordered_total(me, ga_ref, ga_slot)
 
@@ -479,8 +615,12 @@
             out_ref[:, n * LOC + h * HD:n * LOC + (h + 1) * HD] = (inv * (du_ref[:, sl] - unit * dots)).astype(BF)
     out_ref[:, 2 * LOC:] = dv_ref[...]
 
-
-def norm_bwd(dqu, dku, dv, qr, kr, iq, ik, dots, gga, cid):
+    @pl.when(i == NB - 1)
+    def _():
+        wait(stage2(me, full_ref, sems))
+
+
+def norm_bwd(dqu, dku, dv, qr, kr, iq, ik, dots, gga, full, cid):
     row = pl.BlockSpec((BLK, LOC), lambda i: (i, 0))
     half = pl.BlockSpec((BLK, HD), lambda i: (i, 0))
     rows = pl.BlockSpec((2 * NB, BLK), lambda i: (0, 0))
@@ -488,25 +628,27 @@
     return pl.pallas_call(
         norm_bwd_kernel,
         grid=(NB,),
-        in_specs=[row, row, row, row, row, half, half, rows, gsp],
-        out_specs=[pl.BlockSpec((BLK, 3 * LOC), lambda i: (i, 0)), gsp],
-        out_shape=[sds((SEQ, 3 * LOC), BF), sds((8, DIM // 8), F32)],
+        in_specs=[row, row, row, row, row, half, half, rows, gsp, ANYWHERE],
+        out_specs=[pl.BlockSpec((BLK, 3 * LOC), lambda i: (i, 0)), gsp, ANYWHERE],
+        out_shape=[sds((SEQ, 3 * LOC), BF), sds((8, DIM // 8), F32), sds((SEQ, DIM), BF)],
+        input_output_aliases={9: 2},
         scratch_shapes=[pltpu.VMEM((NDEV - 1, 2 * NB, BLK), F32), pltpu.VMEM((NDEV - 1, 8, DIM // 8), F32),
                         pltpu.VMEM((2 * NB, BLK), F32),
-                        pltpu.SemaphoreType.DMA((2, NDEV - 1)), pltpu.SemaphoreType.DMA((2, NDEV - 1))],
+                        DMA((2, NDEV - 1)), DMA((2, NDEV - 1))] + BG_SEMS,
         compiler_params=params(dimension_semantics=("arbitrary",), collective_id=cid, has_side_effects=True),
         cost_estimate=cost(2e9, 14e6),
         name="norm_bwd",
-    )(dqu, dku, dv, qr, kr, iq, ik, dots, gga)
+    )(dqu, dku, dv, qr, kr, iq, ik, dots, gga, full)
 
 
 HALF = DIM // 2
 CH = 256
 
 
-def grads_kernel(d0, d1, w, x0, x1, o0, o1, da0, da1, dy_ref, dx_ref, gwq_ref, gwk_ref, gwv_ref, gwo_ref,
+def grads_kernel(d0, d1, wq, wk, wv, x0, x1, o0, o1, da0, da1_in, dy_ref, dx_ref, gwq_ref, gwk_ref, gwv_ref, gwo_ref, da1,
                  d_all, w_all, sbuf, r1, r2, fin, acc, xbuf, obuf,
-                 dl_sems, dsnd_sems, drcv_sems, w_sems, s1_sems, r1_sems, s2_sems, r2_sems, fs_sems, fr_sems, x_sems, o_sems):
+                 dl_sems, dsnd_sems, drcv_sems, w_sems, s1_sems, r1_sems, s2_sems, r2_sems, fs_sems, fr_sems, x_sems, o_sems, *sems):
+    del da1_in
     me = lax.axis_index('tp')
     core, chip = me % 2, me // 2
     partner = peer_of(me, 1)
@@ -527,12 +669,14 @@
         return pl.ds(pl.multiple_of(c * HALF, HALF), HALF)
 
     chips = (diag_chip, first_chip, second_chip, chip)
-    w_out = pltpu.make_async_remote_copy(
-        src_ref=w.at[half_rows(1 - core), :], dst_ref=w_all.at[1], send_sem=w_sems.at[0], recv_sem=w_sems.at[1],
-        device_id=(partner,), device_id_type=MESH)
-    w_own = pltpu.make_async_copy(w.at[half_rows(core), :], w_all.at[0], w_sems.at[2])
-    w_out.start()
-    w_own.start()
+    w_copies = []
+    for n, w in enumerate((wq, wk, wv)):
+        part = pl.ds(n * LOC, LOC)
+        w_copies.append(pltpu.make_async_remote_copy(
+            src_ref=w.at[half_rows(1 - core), :], dst_ref=w_all.at[1, :, part], send_sem=w_sems.at[n],
+            recv_sem=w_sems.at[3 + n], device_id=(partner,), device_id_type=MESH))
+        w_copies.append(pltpu.make_async_copy(w.at[half_rows(core), :], w_all.at[0, :, part], w_sems.at[6 + n]))
+    start(w_copies)
     swaps, loads = [], []
     for kind in range(4):
         for b in range(2):
@@ -547,8 +691,9 @@
     for load, swap in zip(loads, swaps):
         swap.start()
         load.start()
-    w_own.wait()
-    w_out.wait()
+    last_stage = stage3(me, da1, sems)
+    start(last_stage)
+    wait(w_copies)
 
     def arrived(n, b, blk):
         rows = rows_of(blk)
@@ -640,6 +785,7 @@
     def wo_body(i):
         acc[:LOC, :] += dot(obuf[i % 2].T, xbuf[i % 2])
 
+    wait(last_stage)
     for o_src, da_src in ((o0, da0), (o1, da1)):
         stream([(da_src, xbuf, x_sems), (o_src, obuf, o_sems)], wo_body)
     gwo_ref[...] = acc[:LOC, :].astype(BF)
@@ -669,61 +815,59 @@
     lax.fori_loop(0, 2, finish, 0)
 
 
-def grads(d0, d1, w, x0, x1, o0, o1, da0, da1, dy, cid):
+def grads(d0, d1, wq, wk, wv, x0, x1, o0, o1, da0, da1, dy, cid):
     vm = pl.BlockSpec(memory_space=pltpu.VMEM)
     far = pl.BlockSpec(memory_space=pl.ANY)
     dma = pltpu.SemaphoreType.DMA
     return pl.pallas_call(
         grads_kernel,
-        in_specs=[far] * 9 + [vm],
-        out_specs=[vm] * 5,
-        out_shape=[sds((2, TOK, DIM), BF)] + [sds((DIM, LOC), BF)] * 3 + [sds((LOC, DIM), BF)],
+        in_specs=[far] * 11 + [vm],
+        out_specs=[vm] * 5 + [far],
+        out_shape=[sds((2, TOK, DIM), BF)] + [sds((DIM, LOC), BF)] * 3 + [sds((LOC, DIM), BF), sds((SEQ, DIM), BF)],
+        input_output_aliases={10: 5},
         scratch_shapes=[pltpu.VMEM((2, 2, SEQ, 3 * LOC), BF), pltpu.VMEM((2, HALF, 3 * LOC), BF),
                         pltpu.VMEM((4, BLK, HALF), F32), pltpu.VMEM((4, BLK, HALF), F32), pltpu.VMEM((2, BLK, HALF), F32),
                         pltpu.VMEM((2, TOK, HALF), F32), pltpu.VMEM((3 * LOC, DIM), F32),
                         pltpu.VMEM((2, CH, DIM), BF), pltpu.VMEM((2, CH, LOC), BF),
-                        dma((8,)), dma((8,)), dma((8,)), dma((3,)), dma((4,)), dma((4,)), dma((2,)), dma((2,)),
-                        dma((2,)), dma((2,)), dma((2,)), dma((2,))],
+                        dma((8,)), dma((8,)), dma((8,)), dma((9,)), dma((4,)), dma((4,)), dma((2,)), dma((2,)),
+                        dma((2,)), dma((2,)), dma((2,)), dma((2,))] + BG_SEMS,
         compiler_params=pltpu.CompilerParams(vmem_limit_bytes=67043328, collective_id=cid, has_side_effects=True),
         cost_estimate=cost(100e9, 40e6),
         name="grads",
-    )(d0, d1, w, x0, x1, o0, o1, da0, da1, dy)
+    )(d0, d1, wq, wk, wv, x0, x1, o0, o1, da0, da1, dy)
 
 
 def local_block(x_loc, wq, wk, wv, wo, gq, gk, ga, dy_loc):
-    gather = functools.partial(lax.all_gather, axis_name='tp')
-    w_loc = jnp.concatenate([wq, wk, wv], axis=1)
     gq, gk, ga = gq[None, :], gk[None, :], ga[None, :]
-    cos, sin = rope_tables()
-    xs, dys = [x_loc[0], x_loc[1]], [dy_loc[0], dy_loc[1]]
-    x_full = [gather(xs[b], axis=0, tiled=True) for b in range(2)]
-
-    fwd, o_recv = [], []
+    x_full, cos, sin = first_gather(x_loc, 0)
+    gathered, fwd, o_recv = [x_full], [], []
     for b in range(2):
-        q_raw, k_raw, v, s, *through = project(x_full[b], w_loc, (wo,) if b == 0 else ())
-        if b == 0:
-            wo_full = gather(through[0], axis=0, tiled=True)
-        q_rot, k_rot, iq, ik = norm_rope(q_raw, k_raw, s, gq, gk, cos, sin, 1 + b)
-        o, lse, recv = attention(q_rot, k_rot, v, 3 + b)
+        shard, pick = (x_loc, 1) if b == 0 else (wo, None)
+        q_raw, k_raw, v, s, full = project(gathered[b], wq, wk, wv, shard, pick, 1 + b)
+        q_rot, k_rot, iq, ik, full = norm_rope(q_raw, k_raw, s, gq, gk, cos, sin, shard, full, pick, 3 + b)
+        o, lse, recv, full = attention(q_rot, k_rot, v, full, 5 + b)
+        gathered.append(full)
         o_recv.append(recv)
         fwd.append((q_raw, k_raw, v, q_rot, k_rot, iq, ik, o, lse))
     ys, das, dhs, ggas = [], [], [], []
     for b in range(2):
-        y, da, gga, dh = out_block(o_recv[b], wo_full, xs[b], dys[b], ga, 5 + b)
+        y, da, gga, dh = out_block(o_recv[b], gathered[2], x_loc, dy_loc, ga, b, 7 + b)
         ys.append(y)
         das.append(da)
         dhs.append(dh)
         ggas.append(gga)
-    da_full = [gather(das[b], axis=0, tiled=True) for b in range(2)]
-    ds, gga_sum, ggs = [], [], []
+    ds, gga_sum, ggs, da_full = [], [], [], []
     for b in range(2):
         q_raw, k_raw, v, q_rot, k_rot, iq, ik, o, lse = fwd[b]
-        dqu, dku, dv, dots, gg = attention_bwd(q_rot, k_rot, v, dhs[b], lse, q_raw, k_raw, iq, ik, gq, gk, cos, sin)
-        d, gsum = norm_bwd(dqu, dku, dv, q_raw, k_raw, iq, ik, dots, ggas[b], 7 + b)
+        dqu, dku, dv, dots, gg, full, *old = attention_bwd(
+            q_rot, k_rot, v, dhs[b], lse, q_raw, k_raw, iq, ik, gq, gk, cos, sin, das[b], da_full, 9 + b)
+        d, gsum, full = norm_bwd(dqu, dku, dv, q_raw, k_raw, iq, ik, dots, ggas[b], full, 11 + b)
+        da_full = list(old) + [full]
         ds.append(d)
         gga_sum.append(gsum)
         ggs.append(gg)
-    dx, gwq, gwk, gwv, gwo = grads(ds[0], ds[1], w_loc, x_full[0], x_full[1], fwd[0][7], fwd[1][7], da_full[0], da_full[1], dy_loc, 9)
+    dx, gwq, gwk, gwv, gwo, _ = grads(ds[0], ds[1], wq, wk, wv, gathered[0], gathered[1], fwd[0][7], fwd[1][7],
+                                      da_full[0], da_full[1], dy_loc, 13)
     gg = ggs[0] + ggs[1]
     grad_ga = (gga_sum[0] + gga_sum[1]).reshape(DIM).astype(BF)
     return (jnp.stack(ys), dx, gwq, gwk, gwv, gwo, gg[0].astype(BF), gg[1].astype(BF), grad_ga)

time: 538 us -> 550 us (1.022)
  Pallas kernels: 406 us -> 531 us
  waiting for transfers between devices: 87.1 us -> 0 us
  between operations: 14 us -> 0.81 us
  local copies, waits for them, and re-layouts: 20.6 us -> 12.6 us
    pallas_call x11 -> x12, Pallas kernels: 376 us -> 489 us  [the longest x1 152 us: grads(): pl.pallas_call(grads_kernel, in_specs=[far] * 11 + [vm], out_specs=[vm] *...]
    all_gather x5 -> x0, waiting for transfers between devices: 86.3 us -> none  [the longest x2 77.4 us: local_block(): x_full = [gather(xs[b], axis=0, tiled=True) for b in range(2)]]
    pallas_call x2, Pallas kernels: 30.1 us -> 41.9 us  [norm_bwd(): pl.pallas_call(norm_bwd_kernel, grid=(NB,), in_specs=[row, row, row, row,...]
    unnamed x43 -> x20, local copies, waits for them, and re-layouts: 13.5 us -> 8.38 us
  transfers between devices with their start and end apart: 5 -> 0, of which waited for: 3 -> 0; matrix products, arithmetic and copies ran while one was open for 3% -> 0% of each run, Pallas kernels for 45% -> 0%
where the time goes in v3:
time: 550 us; the launch traced here: 549 us
  Pallas kernels  531 us (97%)
  local copies, waits for them, and re-layouts  12.6 us (2%)
    pallas_call x1, Pallas kernels, grads(): pl.pallas_call(grads_kernel, in_specs=[far] * 11 + [vm], out_specs=[vm] *...  152 us
    pallas_call x2, Pallas kernels, attention_bwd(): pl.pallas_call(functools.partial(attn_bwd_kernel, bool(old)), grid=(2, NB...  89.3 us
    pallas_call x2, Pallas kernels, attention(): pl.pallas_call(attn_kernel, grid=(2, NB), in_specs=[full, full, full, ANY...  55.6 us
    pallas_call x1, Pallas kernels, first_gather(): pl.pallas_call(gather_kernel, in_specs=[ANYWHERE, vm], out_specs=[ANYWHER...  53.8 us
    pallas_call x2, Pallas kernels, out_block(): pl.pallas_call(out_kernel, grid=(1,), in_specs=[whole(TOK, DIM), whole(DI...  51.9 us
    pallas_call x2, Pallas kernels, project(): pl.pallas_call(functools.partial(proj_kernel, pick), grid=(NB,), in_specs...  43.9 us
    pallas_call x2, Pallas kernels, norm_rope(): pl.pallas_call(functools.partial(norm_kernel, pick), grid=(NB,), in_specs...  42.4 us
    pallas_call x2, Pallas kernels, norm_bwd(): pl.pallas_call(norm_bwd_kernel, grid=(NB,), in_specs=[row, row, row, row,...  41.9 us

profile of v3, /device:TPU:0, one launch (start us, length us, event | category | flops | bytes accessed | tf_op | source)
XLA Modules:
  0.0 548.9 jit_solution(4078359996161594772)
XLA Ops:
  0.7 0.6 maximum_bitcast_fusion.freq_ref
  1.2 1.2 broadcast_in_dim.13.gq_ref
  2.5 1.2 broadcast_in_dim.14.gk_ref
  3.7 1.3 broadcast_in_dim.15.ga_ref
  5.0 53.8 %gather.1 = (bf16[2048,2048]{1,0:T(8,128)(2,1)}, f32[2048,128]{1,0:T(8,128)}, f32[2048,128]{1,0:T(8,128)}) custom-call(bf16[2,256,2048]{2,1,0:T(8,128)(2,1)} %x_ref.5, f32[1,128]{1,0:T(1,128)} %maximum_bitcast_fusion.freq_ref), custom_call_target="tpu_custom_call" | custom-call | flops 20000000000 | bytes 20000000 | tf_op jit(solution)/shard_map/gather/pallas_call | solution.py:151
  58.8 21.7 %proj.2 = (f32[2048,256]{1,0:T(8,128)}, f32[2048,256]{1,0:T(8,128)}, bf16[2048,256]{1,0:T(8,128)(2,1)}, f32[8,512]{1,0:T(8,128)}, bf16[2048,2048]{1,0:T(8,128)(2,1)}) custom-call(bf16[2048,2048]{1,0:T(8,128)(2,1)} %get-tuple-element.72.x_ref.x0, bf16[2048,256]{1,0:T(8,128)(2,1)} %wq.1, bf16[2048,256]{1,0:T(8,128)(2,1)} %wk.1, bf16[2048,256]{1,0:T(8,128)(2,1)} %wv.1, ...), custom_call_target="tpu_custom_call" | custom-call | flops 6442450944 | bytes 16000000 | tf_op jit(solution)/shard_map/proj/pallas_call | solution.py:201
  80.5 21.1 %norm_rope.2 = (bf16[2048,256]{1,0:T(8,128)(2,1)}, bf16[2048,256]{1,0:T(8,128)(2,1)}, f32[2048,128]{1,0:T(8,128)}, f32[2048,128]{1,0:T(8,128)}, bf16[2048,2048]{1,0:T(8,128)(2,1)}) custom-call(f32[2048,256]{1,0:T(8,128)} %get-tuple-element.73.q_ref.qr_ref, f32[2048,256]{1,0:T(8,128)} %get-tuple-element.74.k_ref.kr_ref, ...), custom_call_target="tpu_custom_call", output_to_operand_aliasing={{4}: (8, {})} | custom-call | flops 2000000000 | bytes 10000000 | tf_op jit(solution)/shard_map/norm_rope/pallas_call | solution.py:271
  101.6 27.8 %attn_fwd.2 = (bf16[2048,256]{1,0:T(8,128)(2,1)}, f32[8,512]{1,0:T(8,128)}, bf16[256,2048]{1,0:T(8,128)(2,1)}, bf16[2048,2048]{1,0:T(8,128)(2,1)}) custom-call(bf16[2048,256]{1,0:T(8,128)(2,1)} %get-tuple-element.79.q_ref, bf16[2048,256]{1,0:T(8,128)(2,1)} %get-tuple-element.80.k_ref, ...), custom_call_target="tpu_custom_call", output_to_operand_aliasing={{3}: (3, {})} | custom-call | flops 8999999488 | bytes 6000000 | tf_op jit(solution)/shard_map/attn_fwd/pallas_call | solution.py:391
  129.5 22.2 %proj.3 = (f32[2048,256]{1,0:T(8,128)}, f32[2048,256]{1,0:T(8,128)}, bf16[2048,256]{1,0:T(8,128)(2,1)}, f32[8,512]{1,0:T(8,128)}, bf16[2048,2048]{1,0:T(8,128)(2,1)}) custom-call(bf16[2048,2048]{1,0:T(8,128)(2,1)} %get-tuple-element.84.x_ref.x1, bf16[2048,256]{1,0:T(8,128)(2,1)} %wq.1, bf16[2048,256]{1,0:T(8,128)(2,1)} %wk.1, bf16[2048,256]{1,0:T(8,128)(2,1)} %wv.1, ...), custom_call_target="tpu_custom_call" | custom-call | flops 6442450944 | bytes 16000000 | tf_op jit(solution)/shard_map/proj/pallas_call | solution.py:201
  151.7 21.3 %norm_rope.3 = (bf16[2048,256]{1,0:T(8,128)(2,1)}, bf16[2048,256]{1,0:T(8,128)(2,1)}, f32[2048,128]{1,0:T(8,128)}, f32[2048,128]{1,0:T(8,128)}, bf16[2048,2048]{1,0:T(8,128)(2,1)}) custom-call(f32[2048,256]{1,0:T(8,128)} %get-tuple-element.85.q_ref.qr_ref, f32[2048,256]{1,0:T(8,128)} %get-tuple-element.86.k_ref.kr_ref, ...), custom_call_target="tpu_custom_call", output_to_operand_aliasing={{4}: (8, {})} | custom-call | flops 2000000000 | bytes 10000000 | tf_op jit(solution)/shard_map/norm_rope/pallas_call | solution.py:271
  173.0 27.8 %attn_fwd.3 = (bf16[2048,256]{1,0:T(8,128)(2,1)}, f32[8,512]{1,0:T(8,128)}, bf16[256,2048]{1,0:T(8,128)(2,1)}, bf16[2048,2048]{1,0:T(8,128)(2,1)}) custom-call(bf16[2048,256]{1,0:T(8,128)(2,1)} %get-tuple-element.89.q_ref, bf16[2048,256]{1,0:T(8,128)(2,1)} %get-tuple-element.90.k_ref, ...), custom_call_target="tpu_custom_call", output_to_operand_aliasing={{3}: (3, {})} | custom-call | flops 8999999488 | bytes 6000000 | tf_op jit(solution)/shard_map/attn_fwd/pallas_call | solution.py:391
  200.8 25.7 %out_block.3 = (bf16[256,2048]{1,0:T(8,128)(2,1)}, bf16[256,2048]{1,0:T(8,128)(2,1)}, f32[8,256]{1,0:T(8,128)}, bf16[2048,256]{1,0:T(8,128)(2,1)}) custom-call(bf16[256,2048]{1,0:T(8,128)(2,1)} %get-tuple-element.95.o_ref, bf16[2048,2048]{1,0:T(8,128)(2,1)} %get-tuple-element.93.wo_ref, bf16[2,256,2048]{2,1,0:T(8,128)(2,1)} %x_ref.5, ...), custom_call_target="tpu_custom_call" | custom-call | flops 9294966784 | bytes 14000000 | tf_op jit(solution)/shard_map/out_block/pallas_call | solution.py:471
  226.4 0.0 copy-start.4
  226.4 26.3 %out_block.2 = (bf16[256,2048]{1,0:T(8,128)(2,1)}, bf16[256,2048]{1,0:T(8,128)(2,1)}, f32[8,256]{1,0:T(8,128)}, bf16[2048,256]{1,0:T(8,128)(2,1)}) custom-call(bf16[256,2048]{1,0:T(8,128)(2,1)} %get-tuple-element.83.o_ref, bf16[2048,2048]{1,0:T(8,128)(2,1)} %get-tuple-element.93.wo_ref, bf16[2,256,2048]{2,1,0:T(8,128)(2,1)} %x_ref.5, ...), custom_call_target="tpu_custom_call" | custom-call | flops 9294966784 | bytes 14000000 | tf_op jit(solution)/shard_map/out_block/pallas_call | solution.py:471
  252.7 2.7 pad_maximum_fusion
  255.5 44.6 %attn_bwd.2 = (f32[2048,256]{1,0:T(8,128)}, f32[2048,256]{1,0:T(8,128)}, bf16[2048,256]{1,0:T(8,128)(2,1)}, f32[8,512]{1,0:T(8,128)}, f32[8,256]{1,0:T(8,128)}, /*index=5*/bf16[2048,2048]{1,0:T(8,128)(2,1)}) custom-call(bf16[2048,256]{1,0:T(8,128)(2,1)} %get-tuple-element.79.q_ref, bf16[2048,256]{1,0:T(8,128)(2,1)} %get-tuple-element.80.k_ref, ...), custom_call_target="tpu_custom_call" | custom-call | flops 16000000000 | bytes 16000000 | tf_op jit(solution)/shard_map/attn_bwd/pallas_call | solution.py:576
  300.1 21.5 %norm_bwd.2 = (bf16[2048,768]{1,0:T(8,128)(2,1)}, f32[8,256]{1,0:T(8,128)}, bf16[2048,2048]{1,0:T(8,128)(2,1)}) custom-call(f32[2048,256]{1,0:T(8,128)} %get-tuple-element.102.dqu_ref, f32[2048,256]{1,0:T(8,128)} %get-tuple-element.103.dku_ref, bf16[2048,256]{1,0:T(8,128)(2,1)} %get-tuple-element.104.dv_ref, ...), custom_call_target="tpu_custom_call", output_to_operand_aliasing={{2}: (9, {})} | custom-call | flops 2000000000 | bytes 14000000 | tf_op jit(solution)/shard_map/norm_bwd/pallas_call | solution.py:628
  321.7 44.6 %attn_bwd.3 = (f32[2048,256]{1,0:T(8,128)}, f32[2048,256]{1,0:T(8,128)}, bf16[2048,256]{1,0:T(8,128)(2,1)}, f32[8,512]{1,0:T(8,128)}, f32[8,256]{1,0:T(8,128)}, ...) custom-call(bf16[2048,256]{1,0:T(8,128)(2,1)} %get-tuple-element.89.q_ref, ...), custom_call_target="tpu_custom_call", output_to_operand_aliasing={{6}: (14, {})} | custom-call | flops 16000000000 | bytes 16000000 | tf_op jit(solution)/shard_map/attn_bwd/pallas_call | solution.py:576
  366.3 0.7 add_convert_fusion.1
  367.0 0.5 slice_reduce_fusion
  367.6 20.3 %norm_bwd.3 = (bf16[2048,768]{1,0:T(8,128)(2,1)}, f32[8,256]{1,0:T(8,128)}, bf16[2048,2048]{1,0:T(8,128)(2,1)}) custom-call(f32[2048,256]{1,0:T(8,128)} %get-tuple-element.115.dqu_ref, f32[2048,256]{1,0:T(8,128)} %get-tuple-element.116.dku_ref, bf16[2048,256]{1,0:T(8,128)(2,1)} %get-tuple-element.117.dv_ref, ...), custom_call_target="tpu_custom_call", output_to_operand_aliasing={{2}: (9, {})} | custom-call | flops 2000000000 | bytes 14000000 | tf_op jit(solution)/shard_map/norm_bwd/pallas_call | solution.py:628
  387.9 0.7 fusion
  388.6 0.6 copy.26
  389.2 151.9 %grads.1 = (bf16[2,256,2048]{2,1,0:T(8,128)(2,1)}, bf16[2048,256]{1,0:T(8,128)(2,1)}, bf16[2048,256]{1,0:T(8,128)(2,1)}, bf16[2048,256]{1,0:T(8,128)(2,1)}, bf16...) custom-call(bf16[2048,768]{1,0:T(8,128)(2,1)} %get-tuple-element.108.d0, ...), custom_call_target="tpu_custom_call", output_to_operand_aliasing={{5}: (10, {})} | custom-call | flops 99999997952 | bytes 40000000 | tf_op jit(solution)/shard_map/grads/pallas_call | solution.py:822
  541.1 3.2 copy.40
  544.4 1.0 copy.41
  545.4 0.6 copy-done.2
  546.0 1.0 copy.42
  547.0 0.0 copy-done.1
  547.0 1.0 copy.43
  547.9 0.0 copy-done
  547.9 1.0 copy.44
  (11 shorter events, 0.0 us)
Async XLA Ops:
  226.4 26.3 %copy-start.4 = (bf16[256,2048]{1,0:T(8,128)(2,1)S(1)}, bf16[256,2048]{1,0:T(8,128)(2,1)}, u32[]{:S(2)}) copy-start(bf16[256,2048]{1,0:T(8,128)(2,1)} %get-tuple-element.96) | copy-start | bytes 3145732
  321.7 44.7 %copy-start.6 = (f32[8,256]{1,0:T(8,128)S(1)}, f32[8,256]{1,0:T(8,128)}, u32[]{:S(2)}) copy-start(f32[8,256]{1,0:T(8,128)} %get-tuple-element.131) | copy-start | bytes 24580
  367.6 20.3 %copy-start.5 = (f32[8,256]{1,0:T(8,128)S(1)}, f32[8,256]{1,0:T(8,128)}, u32[]{:S(2)}) copy-start(f32[8,256]{1,0:T(8,128)} %get-tuple-element.133) | copy-start | bytes 24580
  541.1 3.3 copy-start.3
  544.4 1.6 copy-start.2
  544.4 2.6 copy-start.1
  546.0 1.9 copy-start

commit v4 on v3

--- a/solution.py
+++ b/solution.py
@@ -72,39 +72,59 @@
 
 DMA = pltpu.SemaphoreType.DMA
 ANYWHERE = pl.BlockSpec(memory_space=pl.ANY)
-BG_SEMS = [DMA((8,)), DMA((8,)), DMA((2,))]
+BG_SEMS = [DMA((8,)), DMA((8,)), DMA((4,))]
+BG = BG_SEMS + [pltpu.VMEM((2, TOK, DIM), BF)]
 
 
 def shard_rows(dev, lo=0, count=TOK):
     return pl.ds(pl.multiple_of(dev * TOK + lo, HD), count)
 
 
-def stage1(me, src, full, sems, lo=0, count=TOK, at=0):
-    send, recv, own = sems
+class Stage:
+    def __init__(self, loads, copies):
+        self.loads, self.copies = loads, copies
+
+    def load(self):
+        start(self.loads)
+
+    def send(self):
+        wait(self.loads)
+        start(self.copies)
+
+    def wait(self):
+        wait(self.copies)
+
+
+def stage1(me, src, full, bg, lo=0, count=TOK):
+    send, recv, own, buf = bg
     there = full.at[shard_rows(me, lo, count), :]
-    part = src.at[pl.ds(lo, count), :]
+    part = buf.at[0, pl.ds(0, count), :]
     copies = [pltpu.make_async_remote_copy(
-        src_ref=part, dst_ref=there, send_sem=send.at[at + k], recv_sem=recv.at[at + k],
+        src_ref=part, dst_ref=there, send_sem=send.at[k], recv_sem=recv.at[k],
         device_id=(peer_of(me, mask),), device_id_type=MESH) for k, mask in enumerate((2, 4, 1))]
-    return copies + [pltpu.make_async_copy(part, there, own.at[0])]
-
-
-def stage2(me, full, sems, at=0):
-    send, recv, _ = sems
+    return Stage([pltpu.make_async_copy(src.at[pl.ds(lo, count), :], part, own.at[0])],
+                 copies + [pltpu.make_async_copy(part, there, own.at[2])])
+
+
+def stage2(me, full, bg):
+    send, recv, own, buf = bg
     xn, yn = peer_of(me, 2), peer_of(me, 4)
     half = TOK // 2
-    plan = ((shard_rows(yn, half, half), 2), (shard_rows(xn, 0, half), 4), (shard_rows(xn), 1), (shard_rows(yn), 1))
-    return [pltpu.make_async_remote_copy(
-        src_ref=full.at[rows, :], dst_ref=full.at[rows, :], send_sem=send.at[at + k], recv_sem=recv.at[at + k],
-        device_id=(peer_of(me, mask),), device_id_type=MESH) for k, (rows, mask) in enumerate(plan)]
-
-
-def stage3(me, full, sems, at=0):
-    send, recv, _ = sems
-    rows = shard_rows(peer_of(me, 6))
-    return [pltpu.make_async_remote_copy(
-        src_ref=full.at[rows, :], dst_ref=full.at[rows, :], send_sem=send.at[at], recv_sem=recv.at[at],
-        device_id=(peer_of(me, 1),), device_id_type=MESH)]
+    plan = ((1, half, half, yn, 2), (0, 0, half, xn, 4), (0, 0, TOK, xn, 1), (1, 0, TOK, yn, 1))
+    return Stage(
+        [pltpu.make_async_copy(full.at[shard_rows(dev), :], buf.at[n], own.at[n]) for n, dev in enumerate((xn, yn))],
+        [pltpu.make_async_remote_copy(
+            src_ref=buf.at[slot, pl.ds(lo, count), :], dst_ref=full.at[shard_rows(dev, lo, count), :],
+            send_sem=send.at[3 + k], recv_sem=recv.at[3 + k], device_id=(peer_of(me, mask),), device_id_type=MESH)
+         for k, (slot, lo, count, dev, mask) in enumerate(plan)])
+
+
+def stage3(me, full, bg):
+    send, recv, own, buf = bg
+    rows = full.at[shard_rows(peer_of(me, 6)), :]
+    return Stage([pltpu.make_async_copy(rows, buf.at[1], own.at[1])], [pltpu.make_async_remote_copy(
+        src_ref=buf.at[1], dst_ref=rows, send_sem=send.at[7], recv_sem=recv.at[7],
+        device_id=(peer_of(me, 1),), device_id_type=MESH)])
 
 
 def start(copies):
@@ -117,11 +137,12 @@
         c.wait()
 
 
-def gather_kernel(x_ref, freq_ref, full_ref, cos_ref, sin_ref, *sems):
+def gather_kernel(x_ref, freq_ref, full_ref, cos_ref, sin_ref, *bg):
     me = lax.axis_index('tp')
+    first = stage1(me, x_ref.at[0], full_ref, bg)
+    first.load()
     nbr_barrier(me)
-    first = stage1(me, x_ref.at[0], full_ref, sems)
-    start(first)
+    first.send()
     freq = freq_ref[...]
     sign = jnp.where(lax.broadcasted_iota(jnp.int32, (TOK, HD), 1) < HD // 2, -1.0, 1.0)
 
@@ -134,13 +155,11 @@
         return carry
 
     lax.fori_loop(0, SEQ // TOK, table, 0)
-    wait(first)
-    second = stage2(me, full_ref, sems, 3)
-    start(second)
-    wait(second)
-    third = stage3(me, full_ref, sems, 7)
-    start(third)
-    wait(third)
+    first.wait()
+    for stage in (stage2(me, full_ref, bg), stage3(me, full_ref, bg)):
+        stage.load()
+        stage.send()
+        stage.wait()
 
 
 def first_gather(x, cid):
@@ -153,7 +172,7 @@
         in_specs=[ANYWHERE, vm],
         out_specs=[ANYWHERE, vm, vm],
         out_shape=[sds((SEQ, DIM), BF), sds((SEQ, HD), F32), sds((SEQ, HD), F32)],
-        scratch_shapes=BG_SEMS,
+        scratch_shapes=BG,
         compiler_params=params(collective_id=cid, has_side_effects=True),
         cost_estimate=cost(20e9, 20e6),
         name="gather",
@@ -171,15 +190,17 @@
     return jnp.broadcast_to(row, (HD, row.shape[1])).T
 
 
-def proj_kernel(pick, x_ref, wq_ref, wk_ref, wv_ref, shard_ref, q_ref, k_ref, v_ref, s_ref, full_ref, *sems):
+def proj_kernel(pick, x_ref, wq_ref, wk_ref, wv_ref, shard_ref, q_ref, k_ref, v_ref, s_ref, full_ref, *bg):
     i = pl.program_id(0)
     me = lax.axis_index('tp')
     src = shard_ref if pick is None else shard_ref.at[pick]
 
     @pl.when(i == 0)
     def _():
+        stage = stage1(me, src, full_ref, bg, 0, TOK // 2)
+        stage.load()
         nbr_barrier(me)
-        start(stage1(me, src, full_ref, sems, 0, TOK // 2))
+        stage.send()
 
     x = x_ref[...]
     q = dot(x, wq_ref[...])
@@ -192,7 +213,7 @@
 
     @pl.when(i == NB - 1)
     def _():
-        wait(stage1(me, src, full_ref, sems, 0, TOK // 2))
+        stage1(me, src, full_ref, bg, 0, TOK // 2).wait()
 
 
 def project(x, wq, wk, wv, shard, pick, cid):
@@ -205,7 +226,7 @@
         out_specs=[row, row, row, pl.BlockSpec((2 * NB, BLK), lambda i: (0, 0)), ANYWHERE],
         out_shape=[sds((SEQ, LOC), F32), sds((SEQ, LOC), F32), sds((SEQ, LOC), BF), sds((2 * NB, BLK), F32),
                    sds((SEQ, DIM), BF)],
-        scratch_shapes=BG_SEMS,
+        scratch_shapes=BG,
         compiler_params=params(dimension_semantics=("arbitrary",), collective_id=cid, has_side_effects=True),
         cost_estimate=cost(2 * SEQ * DIM * 3 * LOC, 16e6),
         name="proj",
@@ -233,8 +254,8 @@
     return total
 
 
-def norm_kernel(pick, q_ref, k_ref, s_ref, gq_ref, gk_ref, cos_ref, sin_ref, shard_ref, full_in, qo_ref, ko_ref, iq_ref,
-                ik_ref, full_ref, slot, total, send_sems, recv_sems, *sems):
+def norm_kernel(pick, q_ref, k_ref, s_ref, gains_ref, cos_ref, sin_ref, shard_ref, full_in, qo_ref, ko_ref, iq_ref,
+                ik_ref, full_ref, slot, total, send_sems, recv_sems, *bg):
     del full_in
     i = pl.program_id(0)
     me = lax.axis_index('tp')
@@ -242,18 +263,21 @@
 
     @pl.when(i == 0)
     def _():
+        stage = stage1(me, src, full_ref, bg, TOK // 2, TOK // 2)
+        stage.load()
         entry_barrier(me)
         sums = exchange(me, [s_ref], [slot], send_sems, recv_sems)
         start(sums)
-        start(stage1(me, src, full_ref, sems, TOK // 2, TOK // 2))
+        stage.send()
         wait(sums)
         total[...] = lax.rsqrt(ordered_total(me, s_ref, slot) / DIM + EPS)
 
     cos, sin = cos_ref[...], sin_ref[...]
-    for raw, dst, inv_ref, g_ref, row in ((q_ref, qo_ref, iq_ref, gq_ref, i), (k_ref, ko_ref, ik_ref, gk_ref, i + NB)):
+    for n, (raw, dst, inv_ref) in enumerate(((q_ref, qo_ref, iq_ref), (k_ref, ko_ref, ik_ref))):
+        row = i + n * NB
         inv = as_column(total[pl.ds(row, 1), :])
         inv_ref[...] = inv
-        g = g_ref[...].astype(F32)
+        g = gains_ref[n:n + 1, :]
         for h in range(LOC // HD):
             sl = slice(h * HD, (h + 1) * HD)
             hat = raw[:, sl] * inv * g[:, sl]
@@ -261,26 +285,26 @@
 
     @pl.when(i == NB - 1)
     def _():
-        wait(stage1(me, src, full_ref, sems, TOK // 2, TOK // 2))
-
-
-def norm_rope(q, k, s, gq, gk, cos, sin, shard, full, pick, cid):
+        stage1(me, src, full_ref, bg, TOK // 2, TOK // 2).wait()
+
+
+def norm_rope(q, k, s, gains, cos, sin, shard, full, pick, cid):
     row = pl.BlockSpec((BLK, LOC), lambda i: (i, 0))
     half = pl.BlockSpec((BLK, HD), lambda i: (i, 0))
-    gain = pl.BlockSpec((1, LOC), lambda i: (0, 0))
+    gain = pl.BlockSpec((2 + DIM // LOC, LOC), lambda i: (0, 0))
     return pl.pallas_call(
         functools.partial(norm_kernel, pick),
         grid=(NB,),
-        in_specs=[row, row, pl.BlockSpec((2 * NB, BLK), lambda i: (0, 0)), gain, gain, half, half, ANYWHERE, ANYWHERE],
+        in_specs=[row, row, pl.BlockSpec((2 * NB, BLK), lambda i: (0, 0)), gain, half, half, ANYWHERE, ANYWHERE],
         out_specs=[row, row, half, half, ANYWHERE],
         out_shape=[sds((SEQ, LOC), BF), sds((SEQ, LOC), BF), sds((SEQ, HD), F32), sds((SEQ, HD), F32), sds((SEQ, DIM), BF)],
-        input_output_aliases={8: 4},
+        input_output_aliases={7: 4},
         scratch_shapes=[pltpu.VMEM((NDEV - 1, 2 * NB, BLK), F32), pltpu.VMEM((2 * NB, BLK), F32),
-                        DMA((1, NDEV - 1)), DMA((1, NDEV - 1))] + BG_SEMS,
+                        DMA((1, NDEV - 1)), DMA((1, NDEV - 1))] + BG,
         compiler_params=params(dimension_semantics=("arbitrary",), collective_id=cid, has_side_effects=True),
         cost_estimate=cost(2e9, 10e6),
         name="norm_rope",
-    )(q, k, s, gq, gk, cos, sin, shard, full)
+    )(q, k, s, gains, cos, sin, shard, full)
 
 
 def causal_mask():
@@ -289,9 +313,12 @@
     return keys <= queries
 
 
-def attn_kernel(q_ref, k_ref, v_ref, full_in, o_ref, lse_ref, recv_ref, full_ref, p_scr, vt_scr, acc_scr, o_scr, send_sems,
-                recv_sems, own_sems, *sems):
+def attn_kernel(b, q_ref, k_ref, v_ref, full_in, *rest):
     del full_in
+    if b:
+        _, *rest = rest
+    o_ref, lse_ref, both_ref, full_ref, p_scr, vt_scr, acc_scr, o_scr, send_sems, recv_sems, own_sems, *bg = rest
+    recv_ref = both_ref.at[b]
     h, step = pl.program_id(0), pl.program_id(1)
     me = lax.axis_index('tp')
     qi = (me // 2 + 1 + step) % NB
@@ -299,13 +326,17 @@
 
     @pl.when(jnp.logical_and(h == 0, step == 0))
     def _():
+        stage = stage2(me, full_ref, bg)
+        stage.load()
         entry_barrier(me)
-        start(stage2(me, full_ref, sems))
+        stage.send()
 
     @pl.when(jnp.logical_and(h == 1, step == NB - 2))
     def _():
-        wait(stage2(me, full_ref, sems))
-        start(stage3(me, full_ref, sems, 4))
+        stage2(me, full_ref, bg).wait()
+        stage = stage3(me, full_ref, bg)
+        stage.load()
+        stage.send()
 
     @pl.when(step == 0)
     def _():
@@ -366,7 +397,7 @@
 
     @pl.when(jnp.logical_and(h == 1, step == NB - 1))
     def _():
-        wait(stage3(me, full_ref, sems, 4))
+        stage3(me, full_ref, bg).wait()
         for hh in range(2):
             for st in range(NB):
                 for half in range(2):
@@ -386,29 +417,36 @@
                     device_id=(peer,), device_id_type=MESH).wait_recv()
 
 
-def attention(q, k, v, gathered, cid):
+def attention(b, q, k, v, gathered, both, cid):
     full = pl.BlockSpec((SEQ, HD), lambda h, i: (0, h))
     return pl.pallas_call(
-        attn_kernel,
+        functools.partial(attn_kernel, b),
         grid=(2, NB),
-        in_specs=[full, full, full, ANYWHERE],
+        in_specs=[full, full, full, ANYWHERE] + [ANYWHERE] * len(both),
         out_specs=[full, pl.BlockSpec((2 * NB, BLK), lambda h, i: (0, 0)), ANYWHERE, ANYWHERE],
-        out_shape=[sds((SEQ, LOC), BF), sds((2 * NB, BLK), F32), sds((TOK, DIM), BF), sds((SEQ, DIM), BF)],
-        input_output_aliases={3: 3},
+        out_shape=[sds((SEQ, LOC), BF), sds((2 * NB, BLK), F32), sds((2, TOK, DIM), BF), sds((SEQ, DIM), BF)],
+        input_output_aliases={3: 3, 4: 2} if both else {3: 3},
         scratch_shapes=[pltpu.VMEM((NB, BLK, BLK), F32), pltpu.VMEM((HD, SEQ), BF), pltpu.VMEM((HD, BLK), F32),
                         pltpu.VMEM((2, NB, BLK, HD), BF), pltpu.SemaphoreType.DMA((2, NB, 2)),
-                        DMA((2, NDEV)), DMA((2,))] + BG_SEMS,
+                        DMA((2, NDEV)), DMA((2,))] + BG,
         compiler_params=params(dimension_semantics=("arbitrary", "arbitrary"), collective_id=cid, has_side_effects=True),
         cost_estimate=cost(9e9, 6e6),
         name="attn_fwd",
-    )(q, k, v, gathered)
-
-
-def out_kernel(o_ref, wo_ref, x_ref, dy_ref, ga_ref, y_ref, da_ref, gga_ref, recv_ref, a_scr, dh_scr, send_sems, recv_sems, own_sem):
+    )(q, k, v, gathered, *both)
+
+
+def out_kernel(o_ref, wo_ref, x_ref, dy_ref, gains_ref, y_ref, da_ref, gga_ref, both_ref, a_scr, dh_scr, send_sems, recv_sems,
+               own_sems):
+    b = pl.program_id(0)
     me = lax.axis_index('tp')
-    entry_barrier(me)
+
+    @pl.when(b == 0)
+    def _():
+        entry_barrier(me)
+        gga_ref[...] = jnp.zeros_like(gga_ref)
+
     step = DIM // NB
-    o = o_ref[...]
+    o = o_ref[0]
 
     def fwd(j, carry):
         cols = pl.ds(pl.multiple_of(j * step, step), step)
@@ -419,90 +457,100 @@
     a = a_scr[...]
     r = lax.rsqrt(jnp.mean(a * a, axis=-1, keepdims=True) + EPS)
     n = a * r
-    ga = ga_ref[...].astype(F32)
+    ga = jnp.concatenate([gains_ref[2 + i:3 + i, :] for i in range(8)], axis=1)
     dy = dy_ref[0].astype(F32)
-    y_ref[...] = (x_ref[0].astype(F32) + n * ga).astype(BF)
+    y_ref[0] = (x_ref[0].astype(F32) + n * ga).astype(BF)
     col = jnp.sum(dy * n, axis=0, keepdims=True)
     for i in range(8):
-        gga_ref[i:i + 1, :] = col[:, i * (DIM // 8):(i + 1) * (DIM // 8)]
+        gga_ref[i:i + 1, :] += col[:, i * LOC:(i + 1) * LOC]
     gn = dy * ga
-    da_ref[...] = (r * (gn - n * jnp.mean(gn * n, axis=-1, keepdims=True))).astype(BF)
-    da = da_ref[...]
-    mine = recv_ref.at[pl.ds(pl.multiple_of(me * TOK, TOK), TOK), :]
-
-    def block_copy(st, half):
+    da_ref[0] = (r * (gn - n * jnp.mean(gn * n, axis=-1, keepdims=True))).astype(BF)
+    da = da_ref[0]
+
+    def block_copy(bb, st, half):
         dest = 2 * ((me // 2 + 1 + st) % NB) + half
-        src = dh_scr.at[st, :, pl.ds(half * LOC, LOC)]
+        src = dh_scr.at[bb, st, :, pl.ds(half * LOC, LOC)]
+        mine = both_ref.at[bb, shard_rows(me), :]
         away = pltpu.make_async_remote_copy(
-            src_ref=src, dst_ref=mine, send_sem=send_sems.at[st, half], recv_sem=recv_sems.at[me],
+            src_ref=src, dst_ref=mine, send_sem=send_sems.at[bb, st, half], recv_sem=recv_sems.at[bb, me],
             device_id=(dest,), device_id_type=MESH)
-        return dest, away, pltpu.make_async_copy(src, mine, own_sem)
+        return dest, away, pltpu.make_async_copy(src, mine, own_sems.at[bb])
 
     def bwd(st, carry):
         blk = (me // 2 + 1 + st) % NB
-        dh_scr[st] = dot(da, wo_ref[pl.ds(pl.multiple_of(blk * step, step), step), :], NT).astype(BF)
+        dh_scr[b, st] = dot(da, wo_ref[pl.ds(pl.multiple_of(blk * step, step), step), :], NT).astype(BF)
         for half in range(2):
-            dest, away, here = block_copy(st, half)
+            dest, away, here = block_copy(b, st, half)
             pl.when(dest != me)(away.start)
             pl.when(dest == me)(here.start)
         return carry
 
     lax.fori_loop(0, NB, bwd, 0)
-    for st in range(NB):
-        for half in range(2):
-            dest, away, here = block_copy(st, half)
-            if st < NB - 1:
-                away.wait_send()
-            else:
-                pl.when(dest != me)(away.wait_send)
-                pl.when(dest == me)(here.wait)
-    for mask in ORDER:
-        peer = peer_of(me, mask)
-        pltpu.make_async_remote_copy(
-            src_ref=dh_scr.at[0, :, pl.ds(0, LOC)], dst_ref=recv_ref.at[pl.ds(pl.multiple_of(peer * TOK, TOK), TOK), :],
-            send_sem=send_sems.at[0, 0], recv_sem=recv_sems.at[peer], device_id=(peer,), device_id_type=MESH).wait_recv()
-
-
-def out_block(o, wo, x, dy, ga, b, cid):
+
+    @pl.when(b == 1)
+    def _():
+        for bb in range(2):
+            for st in range(NB):
+                for half in range(2):
+                    dest, away, here = block_copy(bb, st, half)
+                    if st < NB - 1:
+                        away.wait_send()
+                    else:
+                        pl.when(dest != me)(away.wait_send)
+                        pl.when(dest == me)(here.wait)
+            for mask in ORDER:
+                peer = peer_of(me, mask)
+                pltpu.make_async_remote_copy(
+                    src_ref=dh_scr.at[0, 0, :, pl.ds(0, LOC)], dst_ref=both_ref.at[bb, shard_rows(peer), :],
+                    send_sem=send_sems.at[0, 0, 0], recv_sem=recv_sems.at[bb, peer], device_id=(peer,),
+                    device_id_type=MESH).wait_recv()
+
+
+def out_block(o, wo, x, dy, gains, cid):
     def whole(*shape):
         return pl.BlockSpec(shape, lambda i: (0,) * len(shape))
 
-    batch = pl.BlockSpec((1, TOK, DIM), lambda i: (b, 0, 0))
+    batch = pl.BlockSpec((1, TOK, DIM), lambda i: (i, 0, 0))
     return pl.pallas_call(
         out_kernel,
-        grid=(1,),
-        in_specs=[whole(TOK, DIM), whole(DIM, DIM), batch, batch, whole(1, DIM)],
-        out_specs=[whole(TOK, DIM), whole(TOK, DIM), whole(8, DIM // 8), ANYWHERE],
-        out_shape=[sds((TOK, DIM), BF), sds((TOK, DIM), BF), sds((8, DIM // 8), F32), sds((SEQ, LOC), BF)],
-        scratch_shapes=[pltpu.VMEM((TOK, DIM), F32), pltpu.VMEM((NB, TOK, DIM // NB), BF), pltpu.SemaphoreType.DMA((NB, 2)),
-                        pltpu.SemaphoreType.DMA((NDEV,)), pltpu.SemaphoreType.DMA],
+        grid=(2,),
+        in_specs=[batch, whole(DIM, DIM), batch, batch, whole(2 + DIM // LOC, LOC)],
+        out_specs=[batch, batch, whole(8, DIM // 8), ANYWHERE],
+        out_shape=[sds((2, TOK, DIM), BF), sds((2, TOK, DIM), BF), sds((8, DIM // 8), F32), sds((2, SEQ, LOC), BF)],
+        scratch_shapes=[pltpu.VMEM((TOK, DIM), F32), pltpu.VMEM((2, NB, TOK, DIM // NB), BF), DMA((2, NB, 2)),
+                        DMA((2, NDEV)), DMA((2,))],
         compiler_params=params(dimension_semantics=("arbitrary",), collective_id=cid, has_side_effects=True),
-        cost_estimate=cost(4 * TOK * DIM * DIM + 5e9, 14e6),
+        cost_estimate=cost(8 * TOK * DIM * DIM + 5e9, 18e6),
         name="out_block",
-    )(o, wo, x, dy, ga)
-
-
-def attn_bwd_kernel(older, q_ref, k_ref, v_ref, do_ref, lse_ref, qr_ref, kr_ref, iq_ref, ik_ref, gq_ref, gk_ref, cos_ref, sin_ref,
+    )(o, wo, x, dy, gains)
+
+
+def attn_bwd_kernel(b, older, q_ref, k_ref, v_ref, do_ref, lse_ref, qr_ref, kr_ref, iq_ref, ik_ref, gains_ref, cos_ref, sin_ref,
                     shard_ref, *rest):
     if older:
         _, dqu_ref, dku_ref, dv_ref, dots_ref, gg_ref, full_ref, old_ref, *rest = rest
     else:
         dqu_ref, dku_ref, dv_ref, dots_ref, gg_ref, full_ref, *rest = rest
-    p_scr, dp_scr, kt_scr, dqt_scr, dq_scr, dk_scr, dv_scr, *sems = rest
+    p_scr, dp_scr, kt_scr, dqt_scr, dq_scr, dk_scr, dv_scr, *bg = rest
     h, qi = pl.program_id(0), pl.program_id(1)
     me = lax.axis_index('tp')
 
     def moving():
-        return (stage3(me, old_ref, sems, 4) if older else []) + stage1(me, shard_ref, full_ref, sems)
+        return ([stage3(me, old_ref, bg)] if older else []) + [stage1(me, shard_ref.at[b], full_ref, bg)]
 
     @pl.when(jnp.logical_and(h == 0, qi == 0))
     def _():
+        stages = moving()
+        for stage in stages:
+            stage.load()
         nbr_barrier(me)
-        start(moving())
+        for stage in stages:
+            stage.send()
 
     @pl.when(jnp.logical_and(h == 1, qi == NB - 1))
     def _():
-        wait(moving())
+        for stage in moving():
+            stage.wait()
 
     @pl.when(qi == 0)
     def _():
@@ -553,13 +601,13 @@
         def tail(i, carry):
             rows = pl.ds(pl.multiple_of(i * BLK, BLK), BLK)
             cos, sin = cos_ref[rows, :], sin_ref[rows, :]
-            for n, (d_scr, raw_ref, inv_ref, g_ref, out_ref) in enumerate((
-                    (dq_scr, qr_ref, iq_ref, gq_ref, dqu_ref), (dk_scr, kr_ref, ik_ref, gk_ref, dku_ref))):
+            for n, (d_scr, raw_ref, inv_ref, out_ref) in enumerate((
+                    (dq_scr, qr_ref, iq_ref, dqu_ref), (dk_scr, kr_ref, ik_ref, dku_ref))):
                 d = d_scr[rows, :]
                 hat = d * cos - pltpu.roll(d, HD // 2, 1) * sin
                 unit = raw_ref[rows, :] * inv_ref[rows, :]
                 gg_ref[n:n + 1, :] += jnp.sum(hat * unit, axis=0, keepdims=True)
-                du = hat * g_ref[...].astype(F32)
+                du = hat * gains_ref[n:n + 1, :]
                 out_ref[rows, :] = du
                 dots_ref[pl.ds(i + n * NB, 1), :] += row_sums(du * unit)
             return carry
@@ -567,41 +615,44 @@
         lax.fori_loop(0, NB, tail, 0)
 
 
-def attention_bwd(q, k, v, do, lse, qr, kr, iq, ik, gq, gk, cos, sin, shard, old, cid):
+def attention_bwd(b, q, k, v, do, lse, qr, kr, iq, ik, gains, cos, sin, shard, old, cid):
     blk = pl.BlockSpec((BLK, HD), lambda h, i: (i, h))
     full = pl.BlockSpec((SEQ, HD), lambda h, i: (0, h))
     shared = pl.BlockSpec((SEQ, HD), lambda h, i: (0, 0))
-    gain = pl.BlockSpec((1, HD), lambda h, i: (0, h))
+    gain = pl.BlockSpec((2 + DIM // LOC, HD), lambda h, i: (0, h))
+    do_blk = pl.BlockSpec((None, BLK, HD), lambda h, i: (b, i, h))
     rows = pl.BlockSpec((2 * NB, BLK), lambda h, i: (0, 0))
     return pl.pallas_call(
-        functools.partial(attn_bwd_kernel, bool(old)),
+        functools.partial(attn_bwd_kernel, b, bool(old)),
         grid=(2, NB),
-        in_specs=[blk, full, full, blk, rows, full, full, shared, shared, gain, gain, shared, shared, ANYWHERE] + [ANYWHERE] * len(old),
+        in_specs=[blk, full, full, do_blk, rows, full, full, shared, shared, gain, shared, shared, ANYWHERE] + [ANYWHERE] * len(old),
         out_specs=[full, full, full, rows, pl.BlockSpec((8, HD), lambda h, i: (0, h)), ANYWHERE] + [ANYWHERE] * len(old),
         out_shape=[sds((SEQ, LOC), F32), sds((SEQ, LOC), F32), sds((SEQ, LOC), BF), sds((2 * NB, BLK), F32),
                    sds((8, LOC), F32), sds((SEQ, DIM), BF)] + [sds((SEQ, DIM), BF)] * len(old),
-        input_output_aliases={14: 6} if old else {},
+        input_output_aliases={13: 6} if old else {},
         scratch_shapes=[pltpu.VMEM((NB, BLK, BLK), F32), pltpu.VMEM((NB, BLK, BLK), F32), pltpu.VMEM((HD, SEQ), BF),
                         pltpu.VMEM((HD, BLK), F32), pltpu.VMEM((SEQ, HD), F32), pltpu.VMEM((SEQ, HD), F32),
-                        pltpu.VMEM((SEQ, HD), F32)] + BG_SEMS,
+                        pltpu.VMEM((SEQ, HD), F32)] + BG,
         compiler_params=params(dimension_semantics=("arbitrary", "arbitrary"), collective_id=cid, has_side_effects=True),
         cost_estimate=cost(16e9, 16e6),
         name="attn_bwd",
-    )(q, k, v, do, lse, qr, kr, iq, ik, gq, gk, cos, sin, shard, *old)
+    )(q, k, v, do, lse, qr, kr, iq, ik, gains, cos, sin, shard, *old)
 
 
 def norm_bwd_kernel(dqu_ref, dku_ref, dv_ref, qr_ref, kr_ref, iq_ref, ik_ref, dots_ref, ga_ref, full_in, out_ref, gga_ref,
-                    full_ref, slot, ga_slot, total, send_sems, recv_sems, *sems):
+                    full_ref, slot, ga_slot, total, send_sems, recv_sems, *bg):
     del full_in
     i = pl.program_id(0)
     me = lax.axis_index('tp')
 
     @pl.when(i == 0)
     def _():
+        stage = stage2(me, full_ref, bg)
+        stage.load()
         entry_barrier(me)
         sums = exchange(me, [dots_ref, ga_ref], [slot, ga_slot], send_sems, recv_sems)
         start(sums)
-        start(stage2(me, full_ref, sems))
+        stage.send()
         wait(sums)
         total[...] = ordered_total(me, dots_ref, slot) / DIM
         gga_ref[...] = ordered_total(me, ga_ref, ga_slot)
@@ -617,7 +668,7 @@
 
     @pl.when(i == NB - 1)
     def _():
-        wait(stage2(me, full_ref, sems))
+        stage2(me, full_ref, bg).wait()
 
 
 def norm_bwd(dqu, dku, dv, qr, kr, iq, ik, dots, gga, full, cid):
@@ -634,7 +685,7 @@
         input_output_aliases={9: 2},
         scratch_shapes=[pltpu.VMEM((NDEV - 1, 2 * NB, BLK), F32), pltpu.VMEM((NDEV - 1, 8, DIM // 8), F32),
                         pltpu.VMEM((2 * NB, BLK), F32),
-                        DMA((2, NDEV - 1)), DMA((2, NDEV - 1))] + BG_SEMS,
+                        DMA((2, NDEV - 1)), DMA((2, NDEV - 1))] + BG,
         compiler_params=params(dimension_semantics=("arbitrary",), collective_id=cid, has_side_effects=True),
         cost_estimate=cost(2e9, 14e6),
         name="norm_bwd",
@@ -691,8 +742,9 @@
     for load, swap in zip(loads, swaps):
         swap.start()
         load.start()
-    last_stage = stage3(me, da1, sems)
-    start(last_stage)
+    last_stage = stage3(me, da1, (*sems, xbuf))
+    last_stage.load()
+    last_stage.send()
     wait(w_copies)
 
     def arrived(n, b, blk):
@@ -774,6 +826,7 @@
         return carry
 
     acc[...] = jnp.zeros_like(acc)
+    last_stage.wait()
     wgrad(0, x0)
     forward_second(0, 0)
     wgrad(1, x1)
@@ -785,7 +838,6 @@
     def wo_body(i):
         acc[:LOC, :] += dot(obuf[i % 2].T, xbuf[i % 2])
 
-    wait(last_stage)
     for o_src, da_src in ((o0, da0), (o1, da1)):
         stream([(da_src, xbuf, x_sems), (o_src, obuf, o_sems)], wo_body)
     gwo_ref[...] = acc[:LOC, :].astype(BF)
@@ -838,30 +890,24 @@
 
 
 def local_block(x_loc, wq, wk, wv, wo, gq, gk, ga, dy_loc):
-    gq, gk, ga = gq[None, :], gk[None, :], ga[None, :]
+    gains = jnp.concatenate([gq, gk, ga]).astype(F32).reshape(2 + DIM // LOC, LOC)
     x_full, cos, sin = first_gather(x_loc, 0)
     gathered, fwd, o_recv = [x_full], [], []
     for b in range(2):
         shard, pick = (x_loc, 1) if b == 0 else (wo, None)
         q_raw, k_raw, v, s, full = project(gathered[b], wq, wk, wv, shard, pick, 1 + b)
-        q_rot, k_rot, iq, ik, full = norm_rope(q_raw, k_raw, s, gq, gk, cos, sin, shard, full, pick, 3 + b)
-        o, lse, recv, full = attention(q_rot, k_rot, v, full, 5 + b)
+        q_rot, k_rot, iq, ik, full = norm_rope(q_raw, k_raw, s, gains, cos, sin, shard, full, pick, 3 + b)
+        o, lse, recv, full = attention(b, q_rot, k_rot, v, full, o_recv, 5 + b)
         gathered.append(full)
-        o_recv.append(recv)
+        o_recv = [recv]
         fwd.append((q_raw, k_raw, v, q_rot, k_rot, iq, ik, o, lse))
-    ys, das, dhs, ggas = [], [], [], []
-    for b in range(2):
-        y, da, gga, dh = out_block(o_recv[b], gathered[2], x_loc, dy_loc, ga, b, 7 + b)
-        ys.append(y)
-        das.append(da)
-        dhs.append(dh)
-        ggas.append(gga)
+    y, da, gga, dh = out_block(o_recv[0], gathered[2], x_loc, dy_loc, gains, 7)
     ds, gga_sum, ggs, da_full = [], [], [], []
     for b in range(2):
         q_raw, k_raw, v, q_rot, k_rot, iq, ik, o, lse = fwd[b]
         dqu, dku, dv, dots, gg, full, *old = attention_bwd(
-            q_rot, k_rot, v, dhs[b], lse, q_raw, k_raw, iq, ik, gq, gk, cos, sin, das[b], da_full, 9 + b)
-        d, gsum, full = norm_bwd(dqu, dku, dv, q_raw, k_raw, iq, ik, dots, ggas[b], full, 11 + b)
+            b, q_rot, k_rot, v, dh, lse, q_raw, k_raw, iq, ik, gains, cos, sin, da, da_full, 9 + b)
+        d, gsum, full = norm_bwd(dqu, dku, dv, q_raw, k_raw, iq, ik, dots, gga, full, 11 + b)
         da_full = list(old) + [full]
         ds.append(d)
         gga_sum.append(gsum)
@@ -869,8 +915,8 @@
     dx, gwq, gwk, gwv, gwo, _ = grads(ds[0], ds[1], wq, wk, wv, gathered[0], gathered[1], fwd[0][7], fwd[1][7],
                                       da_full[0], da_full[1], dy_loc, 13)
     gg = ggs[0] + ggs[1]
-    grad_ga = (gga_sum[0] + gga_sum[1]).reshape(DIM).astype(BF)
-    return (jnp.stack(ys), dx, gwq, gwk, gwv, gwo, gg[0].astype(BF), gg[1].astype(BF), grad_ga)
+    grad_ga = gga_sum[0].reshape(DIM).astype(BF)
+    return (y, dx, gwq, gwk, gwv, gwo, gg[0].astype(BF), gg[1].astype(BF), grad_ga)
 
 
 def solution(mesh):

time: 550 us -> 500 us (0.909)
  Pallas kernels: 531 us -> 483 us
    pallas_call x6 -> x5, Pallas kernels: 197 us -> 165 us  [the longest x2 72.6 us: attention_bwd(): pl.pallas_call(functools.partial(attn_bwd_kernel, b, bool(old)), grid=(2,...]
    pallas_call x2, Pallas kernels: 43.9 us -> 37.3 us  [project(): pl.pallas_call(functools.partial(proj_kernel, pick), grid=(NB,), in_specs...]
    pallas_call x1, Pallas kernels: 53.8 us -> 47.9 us  [first_gather(): pl.pallas_call(gather_kernel, in_specs=[ANYWHERE, vm], out_specs=[ANYWHER...]
where the time goes in v4:
time: 500 us; the launch traced here: 498 us
  Pallas kernels  483 us (97%)
  local copies, waits for them, and re-layouts  11.5 us (2%)
    pallas_call x1, Pallas kernels, grads(): pl.pallas_call(grads_kernel, in_specs=[far] * 11 + [vm], out_specs=[vm] *...  152 us
    pallas_call x2, Pallas kernels, attention_bwd(): pl.pallas_call(functools.partial(attn_bwd_kernel, b, bool(old)), grid=(2,...  72.6 us
    pallas_call x2, Pallas kernels, attention(): pl.pallas_call(functools.partial(attn_kernel, b), grid=(2, NB), in_specs=...  55.1 us
    pallas_call x1, Pallas kernels, first_gather(): pl.pallas_call(gather_kernel, in_specs=[ANYWHERE, vm], out_specs=[ANYWHER...  47.9 us
    pallas_call x2, Pallas kernels, norm_bwd(): pl.pallas_call(norm_bwd_kernel, grid=(NB,), in_specs=[row, row, row, row,...  41.6 us
    pallas_call x2, Pallas kernels, norm_rope(): pl.pallas_call(functools.partial(norm_kernel, pick), grid=(NB,), in_specs...  38.5 us
    pallas_call x1, Pallas kernels, out_block(): pl.pallas_call(out_kernel, grid=(2,), in_specs=[batch, whole(DIM, DIM), b...  37.7 us
    pallas_call x2, Pallas kernels, project(): pl.pallas_call(functools.partial(proj_kernel, pick), grid=(NB,), in_specs...  37.3 us

profile of v4, /device:TPU:0, one launch (start us, length us, event | category | flops | bytes accessed | tf_op | source)
XLA Modules:
  0.0 497.7 jit_solution(2411697792511291553)
XLA Ops:
  0.7 0.6 maximum_bitcast_fusion.freq_ref
  1.2 0.7 maximum_convert_fusion
  2.0 0.6 reshape.26.gains_ref
  2.6 47.9 %gather.1 = (bf16[2048,2048]{1,0:T(8,128)(2,1)}, f32[2048,128]{1,0:T(8,128)}, f32[2048,128]{1,0:T(8,128)}) custom-call(bf16[2,256,2048]{2,1,0:T(8,128)(2,1)} %x_ref.3, f32[1,128]{1,0:T(1,128)} %maximum_bitcast_fusion.freq_ref), custom_call_target="tpu_custom_call" | custom-call | flops 20000000000 | bytes 20000000 | tf_op jit(solution)/shard_map/gather/pallas_call | solution.py:170
  50.5 17.9 %proj.2 = (f32[2048,256]{1,0:T(8,128)}, f32[2048,256]{1,0:T(8,128)}, bf16[2048,256]{1,0:T(8,128)(2,1)}, f32[8,512]{1,0:T(8,128)}, bf16[2048,2048]{1,0:T(8,128)(2,1)}) custom-call(bf16[2048,2048]{1,0:T(8,128)(2,1)} %get-tuple-element.67.x_ref.x0, bf16[2048,256]{1,0:T(8,128)(2,1)} %wq.1, bf16[2048,256]{1,0:T(8,128)(2,1)} %wk.1, bf16[2048,256]{1,0:T(8,128)(2,1)} %wv.1, ...), custom_call_target="tpu_custom_call" | custom-call | flops 6442450944 | bytes 16000000 | tf_op jit(solution)/shard_map/proj/pallas_call | solution.py:222
  68.5 19.4 %norm_rope.2 = (bf16[2048,256]{1,0:T(8,128)(2,1)}, bf16[2048,256]{1,0:T(8,128)(2,1)}, f32[2048,128]{1,0:T(8,128)}, f32[2048,128]{1,0:T(8,128)}, bf16[2048,2048]{1,0:T(8,128)(2,1)}) custom-call(f32[2048,256]{1,0:T(8,128)} %get-tuple-element.68.q_ref.qr_ref, f32[2048,256]{1,0:T(8,128)} %get-tuple-element.69.k_ref.kr_ref, ...), custom_call_target="tpu_custom_call", output_to_operand_aliasing={{4}: (7, {})} | custom-call | flops 2000000000 | bytes 10000000 | tf_op jit(solution)/shard_map/norm_rope/pallas_call | solution.py:295
  87.9 27.5 %attn_fwd.2 = (bf16[2048,256]{1,0:T(8,128)(2,1)}, f32[8,512]{1,0:T(8,128)}, bf16[2,256,2048]{2,1,0:T(8,128)(2,1)}, bf16[2048,2048]{1,0:T(8,128)(2,1)}) custom-call(bf16[2048,256]{1,0:T(8,128)(2,1)} %get-tuple-element.74.q_ref, bf16[2048,256]{1,0:T(8,128)(2,1)} %get-tuple-element.75.k_ref, ...), custom_call_target="tpu_custom_call", output_to_operand_aliasing={{3}: (3, {})} | custom-call | flops 8999999488 | bytes 6000000 | tf_op jit(solution)/shard_map/attn_fwd/pallas_call | solution.py:422
  115.3 19.4 %proj.3 = (f32[2048,256]{1,0:T(8,128)}, f32[2048,256]{1,0:T(8,128)}, bf16[2048,256]{1,0:T(8,128)(2,1)}, f32[8,512]{1,0:T(8,128)}, bf16[2048,2048]{1,0:T(8,128)(2,1)}) custom-call(bf16[2048,2048]{1,0:T(8,128)(2,1)} %get-tuple-element.78.x_ref.x1, bf16[2048,256]{1,0:T(8,128)(2,1)} %wq.1, bf16[2048,256]{1,0:T(8,128)(2,1)} %wk.1, bf16[2048,256]{1,0:T(8,128)(2,1)} %wv.1, ...), custom_call_target="tpu_custom_call" | custom-call | flops 6442450944 | bytes 16000000 | tf_op jit(solution)/shard_map/proj/pallas_call | solution.py:222
  134.7 19.1 %norm_rope.3 = (bf16[2048,256]{1,0:T(8,128)(2,1)}, bf16[2048,256]{1,0:T(8,128)(2,1)}, f32[2048,128]{1,0:T(8,128)}, f32[2048,128]{1,0:T(8,128)}, bf16[2048,2048]{1,0:T(8,128)(2,1)}) custom-call(f32[2048,256]{1,0:T(8,128)} %get-tuple-element.79.q_ref.qr_ref, f32[2048,256]{1,0:T(8,128)} %get-tuple-element.80.k_ref.kr_ref, ...), custom_call_target="tpu_custom_call", output_to_operand_aliasing={{4}: (7, {})} | custom-call | flops 2000000000 | bytes 10000000 | tf_op jit(solution)/shard_map/norm_rope/pallas_call | solution.py:295
  153.8 27.6 %attn_fwd.3 = (bf16[2048,256]{1,0:T(8,128)(2,1)}, f32[8,512]{1,0:T(8,128)}, bf16[2,256,2048]{2,1,0:T(8,128)(2,1)}, bf16[2048,2048]{1,0:T(8,128)(2,1)}) custom-call(bf16[2048,256]{1,0:T(8,128)(2,1)} %get-tuple-element.83.q_ref, bf16[2048,256]{1,0:T(8,128)(2,1)} %get-tuple-element.84.k_ref, ...), custom_call_target="tpu_custom_call", output_to_operand_aliasing={{3}: (3, {}), {2}: (4, {})} | custom-call | flops 8999999488 | bytes 6000000 | tf_op jit(solution)/shard_map/attn_fwd/pallas_call | solution.py:422
  181.5 37.7 %out_block.1 = (bf16[2,256,2048]{2,1,0:T(8,128)(2,1)}, bf16[2,256,2048]{2,1,0:T(8,128)(2,1)}, f32[8,256]{1,0:T(8,128)}, bf16[2,2048,256]{2,1,0:T(8,128)(2,1)}) custom-call(bf16[2,256,2048]{2,1,0:T(8,128)(2,1)} %get-tuple-element.88.o_ref, bf16[2048,2048]{1,0:T(8,128)(2,1)} %get-tuple-element.89.wo_ref, bf16[2,256,2048]{2,1,0:T(8,128)(2,1)} %x_ref.3, ...), custom_call_target="tpu_custom_call" | custom-call | flops 13589934080 | bytes 18000000 | tf_op jit(solution)/shard_map/out_block/pallas_call | solution.py:514
  219.1 36.8 %attn_bwd.2 = (f32[2048,256]{1,0:T(8,128)}, f32[2048,256]{1,0:T(8,128)}, bf16[2048,256]{1,0:T(8,128)(2,1)}, f32[8,512]{1,0:T(8,128)}, f32[8,256]{1,0:T(8,128)}, /*index=5*/bf16[2048,2048]{1,0:T(8,128)(2,1)}) custom-call(bf16[2048,256]{1,0:T(8,128)(2,1)} %get-tuple-element.74.q_ref, bf16[2048,256]{1,0:T(8,128)(2,1)} %get-tuple-element.75.k_ref, ...), custom_call_target="tpu_custom_call" | custom-call | flops 16000000000 | bytes 16000000 | tf_op jit(solution)/shard_map/attn_bwd/pallas_call | solution.py:625
  255.9 20.8 %norm_bwd.2 = (bf16[2048,768]{1,0:T(8,128)(2,1)}, f32[8,256]{1,0:T(8,128)}, bf16[2048,2048]{1,0:T(8,128)(2,1)}) custom-call(f32[2048,256]{1,0:T(8,128)} %get-tuple-element.96.dqu_ref, f32[2048,256]{1,0:T(8,128)} %get-tuple-element.97.dku_ref, bf16[2048,256]{1,0:T(8,128)(2,1)} %get-tuple-element.98.dv_ref, ...), custom_call_target="tpu_custom_call", output_to_operand_aliasing={{2}: (9, {})} | custom-call | flops 2000000000 | bytes 14000000 | tf_op jit(solution)/shard_map/norm_bwd/pallas_call | solution.py:679
  276.7 0.7 convert_bitcast_fusion
  277.4 0.6 copy.27
  278.0 35.9 %attn_bwd.3 = (f32[2048,256]{1,0:T(8,128)}, f32[2048,256]{1,0:T(8,128)}, bf16[2048,256]{1,0:T(8,128)(2,1)}, f32[8,512]{1,0:T(8,128)}, f32[8,256]{1,0:T(8,128)}, ...) custom-call(bf16[2048,256]{1,0:T(8,128)(2,1)} %get-tuple-element.83.q_ref, ...), custom_call_target="tpu_custom_call", output_to_operand_aliasing={{6}: (13, {})} | custom-call | flops 16000000000 | bytes 16000000 | tf_op jit(solution)/shard_map/attn_bwd/pallas_call | solution.py:625
  313.9 0.0 copy-done.5
  313.9 0.7 add_convert_fusion
  314.6 0.5 slice_reduce_fusion
  315.2 20.8 %norm_bwd.3 = (bf16[2048,768]{1,0:T(8,128)(2,1)}, f32[8,256]{1,0:T(8,128)}, bf16[2048,2048]{1,0:T(8,128)(2,1)}) custom-call(f32[2048,256]{1,0:T(8,128)} %get-tuple-element.107.dqu_ref, f32[2048,256]{1,0:T(8,128)} %get-tuple-element.108.dku_ref, bf16[2048,256]{1,0:T(8,128)(2,1)} %get-tuple-element.109.dv_ref, ...), custom_call_target="tpu_custom_call", output_to_operand_aliasing={{2}: (9, {})} | custom-call | flops 2000000000 | bytes 14000000 | tf_op jit(solution)/shard_map/norm_bwd/pallas_call | solution.py:679
  336.0 151.9 %grads.1 = (bf16[2,256,2048]{2,1,0:T(8,128)(2,1)}, bf16[2048,256]{1,0:T(8,128)(2,1)}, bf16[2048,256]{1,0:T(8,128)(2,1)}, bf16[2048,256]{1,0:T(8,128)(2,1)}, bf16...) custom-call(bf16[2048,768]{1,0:T(8,128)(2,1)} %get-tuple-element.102.d0, ...), custom_call_target="tpu_custom_call", output_to_operand_aliasing={{5}: (10, {})} | custom-call | flops 99999997952 | bytes 40000000 | tf_op jit(solution)/shard_map/grads/pallas_call | solution.py:874
  487.9 0.0 copy-start
  488.0 3.3 copy.43
  491.3 0.0 copy-done
  491.3 1.3 copy.44
  492.6 0.6 copy-done.4
  493.2 1.0 copy.45
  494.2 0.6 copy-done.3
  494.8 1.0 copy.46
  495.8 0.0 copy-done.2
  495.8 1.0 copy.47
  496.8 1.0 copy.48
  (7 shorter events, 0.0 us)
Async XLA Ops:
  278.0 35.9 %copy-start.5 = (f32[8,256]{1,0:T(8,128)S(1)}, f32[8,256]{1,0:T(8,128)}, u32[]{:S(2)}) copy-start(f32[8,256]{1,0:T(8,128)} %get-tuple-element.122) | copy-start | bytes 24580
  487.9 3.3 copy-start
  491.3 2.0 copy-start.4
  493.2 1.6 copy-start.3
  493.2 2.6 copy-start.2
  494.8 1.9 copy-start.1

commit v5 on v4

v5 whole, which is shorter than its diff:
```python
import functools
import math

import jax
import jax.numpy as jnp
from jax import lax
from jax.experimental import pallas as pl
from jax.experimental.pallas import tpu as pltpu
from jax.sharding import PartitionSpec as P

HD = 128
ROPE_THETA = 500000.0
EPS = 1e-6
DIM = 2048
SEQ = 2048
LOC = 256
TOK = 256
BLK = 512
NB = SEQ // BLK
NDEV = 8
SCALE = HD ** -0.5
C2 = SCALE * math.log2(math.e)
MESH = pl.DeviceIdType.MESH
BF = jnp.bfloat16
F32 = jnp.float32
VMEM_MAX = 60 * 1024 * 1024

NT = (((1,), (1,)), ((), ()))
NN = (((1,), (0,)), ((), ()))


def dot(a, b, dims=NN):
    return lax.dot_general(a, b, dims, preferred_element_type=F32)


def sds(shape, dtype):
    return jax.ShapeDtypeStruct(shape, dtype)


def cost(flops, nbytes, trans=0):
    return pl.CostEstimate(flops=int(flops), bytes_accessed=int(nbytes), transcendentals=int(trans))


def params(**kw):
    return pltpu.CompilerParams(vmem_limit_bytes=VMEM_MAX, **kw)


def peer_of(me, mask):
    core, ax, ay = me % 2, (me // 2) % 2, me // 4
    core = 1 - core if mask & 1 else core
    ax = 1 - ax if mask & 2 else ax
    ay = 1 - ay if mask & 4 else ay
    return ay * 4 + ax * 2 + core


ORDER = (6, 7, 2, 4, 3, 5, 1)


def entry_barrier(me):
    barrier = pltpu.get_barrier_semaphore()
    for mask in ORDER:
        pl.semaphore_signal(barrier, inc=1, device_id=(peer_of(me, mask),), device_id_type=MESH)
    pl.semaphore_wait(barrier, NDEV - 1)


def nbr_barrier(me):
    barrier = pltpu.get_barrier_semaphore()
    for mask in (1, 2, 4):
        pl.semaphore_signal(barrier, inc=1, device_id=(peer_of(me, mask),), device_id_type=MESH)
    pl.semaphore_wait(barrier, 3)


DMA = pltpu.SemaphoreType.DMA
ANYWHERE = pl.BlockSpec(memory_space=pl.ANY)
BG_SEMS = [DMA((8,)), DMA((8,)), DMA((4,))]
BG = BG_SEMS + [pltpu.VMEM((2, TOK, DIM), BF)]


def shard_rows(dev, lo=0, count=TOK):
    return pl.ds(pl.multiple_of(dev * TOK + lo, HD), count)


class Stage:
    def __init__(self, loads, copies):
        self.loads, self.copies = loads, copies

    def load(self):
        start(self.loads)

    def send(self):
        wait(self.loads)
        start(self.copies)

    def wait(self):
        wait(self.copies)


def stage1(me, src, full, bg, lo=0, count=TOK):
    send, recv, own, buf = bg
    there = full.at[shard_rows(me, lo, count), :]
    part = buf.at[0, pl.ds(0, count), :]
    copies = [pltpu.make_async_remote_copy(
        src_ref=part, dst_ref=there, send_sem=send.at[k], recv_sem=recv.at[k],
        device_id=(peer_of(me, mask),), device_id_type=MESH) for k, mask in enumerate((2, 4, 1))]
    return Stage([pltpu.make_async_copy(src.at[pl.ds(lo, count), :], part, own.at[0])],
                 copies + [pltpu.make_async_copy(part, there, own.at[2])])


def stage2(me, full, bg):
    send, recv, own, buf = bg
    xn, yn = peer_of(me, 2), peer_of(me, 4)
    half = TOK // 2
    plan = ((1, half, half, yn, 2), (0, 0, half, xn, 4), (0, 0, TOK, xn, 1), (1, 0, TOK, yn, 1))
    return Stage(
        [pltpu.make_async_copy(full.at[shard_rows(dev), :], buf.at[n], own.at[n]) for n, dev in enumerate((xn, yn))],
        [pltpu.make_async_remote_copy(
            src_ref=buf.at[slot, pl.ds(lo, count), :], dst_ref=full.at[shard_rows(dev, lo, count), :],
            send_sem=send.at[3 + k], recv_sem=recv.at[3 + k], device_id=(peer_of(me, mask),), device_id_type=MESH)
         for k, (slot, lo, count, dev, mask) in enumerate(plan)])


def stage3(me, full, bg):
    send, recv, own, buf = bg
    rows = full.at[shard_rows(peer_of(me, 6)), :]
    return Stage([pltpu.make_async_copy(rows, buf.at[1], own.at[1])], [pltpu.make_async_remote_copy(
        src_ref=buf.at[1], dst_ref=rows, send_sem=send.at[7], recv_sem=recv.at[7],
        device_id=(peer_of(me, 1),), device_id_type=MESH)])


def start(copies):
    for c in copies:
        c.start()


def wait(copies):
    for c in copies:
        c.wait()


def gather_kernel(x_ref, freq_ref, full_ref, cos_ref, sin_ref, *bg):
    me = lax.axis_index('tp')
    first = stage1(me, x_ref.at[0], full_ref, bg)
    first.load()
    nbr_barrier(me)
    first.send()
    freq = freq_ref[...]
    sign = jnp.where(lax.broadcasted_iota(jnp.int32, (TOK, HD), 1) < HD // 2, -1.0, 1.0)

    def table(i, carry):
        rows = pl.ds(pl.multiple_of(i * TOK, TOK), TOK)
        pos = (lax.broadcasted_iota(jnp.int32, (TOK, HD), 0) + i * TOK).astype(F32)
        angle = pos * freq
        cos_ref[rows, :] = jnp.cos(angle)
        sin_ref[rows, :] = jnp.sin(angle) * sign
        return carry

    lax.fori_loop(0, SEQ // TOK, table, 0)
    first.wait()
    for stage in (stage2(me, full_ref, bg), stage3(me, full_ref, bg)):
        stage.load()
        stage.send()
        stage.wait()


def first_gather(x, cid):
    half = HD // 2
    inv_freq = 1.0 / (ROPE_THETA ** (jnp.arange(half, dtype=F32) / half))
    freq = jnp.concatenate([inv_freq, inv_freq])[None, :]
    vm = pl.BlockSpec(memory_space=pltpu.VMEM)
    return pl.pallas_call(
        gather_kernel,
        in_specs=[ANYWHERE, vm],
        out_specs=[ANYWHERE, vm, vm],
        out_shape=[sds((SEQ, DIM), BF), sds((SEQ, HD), F32), sds((SEQ, HD), F32)],
        scratch_shapes=BG,
        compiler_params=params(collective_id=cid, has_side_effects=True),
        cost_estimate=cost(20e9, 20e6),
        name="gather",
    )(x, freq)


def row_sums(vals):
    folded = vals[:, :HD]
    for start in range(HD, vals.shape[1], HD):
        folded = folded + vals[:, start:start + HD]
    return jnp.sum(folded.T, axis=0, keepdims=True)


def as_column(row):
    return jnp.broadcast_to(row, (HD, row.shape[1])).T


def exchange(me, srcs, slots, send_sems, recv_sems):
    copies = []
    for n, (src, slot) in enumerate(zip(srcs, slots)):
        for p, mask in enumerate(ORDER):
            copies.append(pltpu.make_async_remote_copy(
                src_ref=src, dst_ref=slot.at[p], send_sem=send_sems.at[n, p], recv_sem=recv_sems.at[n, p],
                device_id=(peer_of(me, mask),), device_id_type=MESH))
    return copies


def ordered_total(me, src, slot):
    own = src[...]
    total = jnp.zeros_like(own)
    for dev in range(NDEV):
        term = jnp.where(me == dev, own, 0.0)
        for p, mask in enumerate(ORDER):
            term = term + jnp.where(peer_of(me, mask) == dev, slot[p], 0.0)
        total = total + term
    return total


def causal_mask():
    keys = lax.broadcasted_iota(jnp.int32, (BLK, BLK), 0)
    queries = lax.broadcasted_iota(jnp.int32, (BLK, BLK), 1)
    return keys <= queries


def block_rows(i):
    return pl.ds(pl.multiple_of(i * BLK, BLK), BLK)


def head_cols(h):
    return pl.ds(pl.multiple_of(h * HD, HD), HD)


def forward_kernel(b, pick, x_ref, wq_ref, wk_ref, wv_ref, gains_ref, cos_ref, sin_ref, shard_ref, *rest):
    if b:
        _, *rest = rest
    (raw_ref, qkv_ref, inv_ref, o_ref, lse_ref, both_ref, full_ref,
     raw, qkv, sums_scr, slot, p_scr, vt_scr, acc_scr, o_scr,
     ex_send, ex_recv, out_sems, send_sems, recv_sems, own_sems, *bg) = rest
    recv_ref = both_ref.at[b]
    t = pl.program_id(0)
    me = lax.axis_index('tp')
    src = shard_ref if pick is None else shard_ref.at[pick]

    def keep(n):
        return (pltpu.make_async_copy(raw, raw_ref, out_sems.at[0]), pltpu.make_async_copy(qkv, qkv_ref, out_sems.at[1]))[n]

    def sums():
        return exchange(me, [sums_scr], [slot], ex_send, ex_recv)

    def block_copy(hh, st, half):
        dest = 2 * ((me // 2 + 1 + st) % NB) + half
        part = o_scr.at[hh, st, pl.ds(half * TOK, TOK), :]
        dst = recv_ref.at[:, pl.ds(pl.multiple_of(me * LOC + hh * HD, HD), HD)]
        away = pltpu.make_async_remote_copy(
            src_ref=part, dst_ref=dst, send_sem=send_sems.at[hh, st, half], recv_sem=recv_sems.at[hh, me],
            device_id=(dest,), device_id_type=MESH)
        return dest, away, pltpu.make_async_copy(part, dst, own_sems.at[hh])

    @pl.when(t == 0)
    def _():
        stage = stage1(me, src, full_ref, bg)
        stage.load()
        entry_barrier(me)
        stage.send()

    @pl.when(t < NB)
    def _():
        rows = block_rows(t)
        x = x_ref[...]
        for n, w_ref in enumerate((wq_ref, wk_ref)):
            val = dot(x, w_ref[...])
            raw[n, rows, :] = val
            sums_scr[pl.ds(t + n * NB, 1), :] = row_sums(val * val)
        qkv[2, rows, :] = dot(x, wv_ref[...]).astype(BF)

    @pl.when(t == NB)
    def _():
        start(sums())
        keep(0).start()
        wait(sums())
        inv_ref[...] = lax.rsqrt(ordered_total(me, sums_scr, slot) / DIM + EPS)

    @pl.when(jnp.logical_and(t >= NB, t < 2 * NB))
    def _():
        i = t - NB
        rows = block_rows(i)
        cos, sin = cos_ref[rows, :], sin_ref[rows, :]
        for n in range(2):
            inv = as_column(inv_ref[pl.ds(i + n * NB, 1), :])
            g = gains_ref[n:n + 1, :]
            for h in range(LOC // HD):
                sl = slice(h * HD, (h + 1) * HD)
                hat = raw[n, rows, sl] * inv * g[:, sl]
                qkv[n, rows, sl] = (hat * cos + pltpu.roll(hat, HD // 2, 1) * sin).astype(BF)

    @pl.when(t == 2 * NB)
    def _():
        keep(1).start()
        stage1(me, src, full_ref, bg).wait()
        stage = stage2(me, full_ref, bg)
        stage.load()
        stage.send()

    @pl.when(t == 4 * NB - 2)
    def _():
        stage2(me, full_ref, bg).wait()
        stage = stage3(me, full_ref, bg)
        stage.load()
        stage.send()

    @pl.when(t >= 2 * NB)
    def _():
        h, step = t // NB - 2, t % NB
        qi = (me // 2 + 1 + step) % NB
        cols = head_cols(h)

        @pl.when(step == 0)
        def _():
            vt_scr[...] = qkv[2, :, cols].T

        qb = qkv[0, block_rows(qi), cols]

        def scores(j):
            return dot(qkv[1, block_rows(j), cols], qb, NT)

        def first(j, m):
            s = scores(j)
            p_scr[j] = s
            return jnp.maximum(m, jnp.max(s.reshape(BLK // 8, 8, BLK), axis=0))

        s = jnp.where(causal_mask(), scores(qi), -1e30)
        p_scr[qi] = s
        m = lax.fori_loop(0, qi, first, jnp.max(s.reshape(BLK // 8, 8, BLK), axis=0))
        m = jnp.max(m, axis=0, keepdims=True)

        def second(j, l):
            p = jnp.exp2((p_scr[j] - m) * C2)
            p_scr[j] = p
            return l + jnp.sum(p.reshape(BLK // 8, 8, BLK), axis=0)

        l = lax.fori_loop(0, qi + 1, second, jnp.zeros((8, BLK), F32))
        l = jnp.sum(l, axis=0, keepdims=True)
        rl = 1.0 / l
        lse_ref[pl.ds(h * NB + qi, 1), :] = m * C2 + jnp.log2(l)

        acc_scr[...] = jnp.zeros_like(acc_scr)

        def third(j, carry):
            p = (p_scr[j] * rl).astype(BF)
            acc_scr[...] += dot(vt_scr[:, block_rows(j)], p)
            return carry

        lax.fori_loop(0, qi + 1, third, 0)
        out = acc_scr[...].T.astype(BF)
        o_scr[h, step] = out
        o_ref[block_rows(qi), cols] = out

        for half in range(2):
            dest, away, here = block_copy(h, step, half)
            pl.when(dest != me)(away.start)
            pl.when(dest == me)(here.start)

    @pl.when(t == 4 * NB - 1)
    def _():
        keep(0).wait()
        keep(1).wait()
        stage3(me, full_ref, bg).wait()
        for hh in range(2):
            for st in range(NB):
                for half in range(2):
                    dest, away, here = block_copy(hh, st, half)
                    if st < NB - 1:
                        away.wait_send()
                    else:
                        pl.when(dest != me)(away.wait_send)
                        pl.when(dest == me)(here.wait)
            for mask in ORDER:
                peer = peer_of(me, mask)
                pltpu.make_async_remote_copy(
                    src_ref=o_scr.at[0, 0, pl.ds(0, TOK), :],
                    dst_ref=recv_ref.at[:, pl.ds(pl.multiple_of(peer * LOC + hh * HD, HD), HD)],
                    send_sem=send_sems.at[0, 0, 0], recv_sem=recv_sems.at[hh, peer],
                    device_id=(peer,), device_id_type=MESH).wait_recv()


def forward(b, x, wq, wk, wv, gains, cos, sin, shard, pick, both, cid):
    def whole(*shape):
        return pl.BlockSpec(shape, lambda t: (0,) * len(shape))

    wspec = whole(DIM, LOC)
    return pl.pallas_call(
        functools.partial(forward_kernel, b, pick),
        grid=(4 * NB,),
        in_specs=[pl.BlockSpec((BLK, DIM), lambda t: (jnp.minimum(t, NB - 1), 0)), wspec, wspec, wspec,
                  whole(2 + DIM // LOC, LOC), whole(SEQ, HD), whole(SEQ, HD), ANYWHERE] + [ANYWHERE] * len(both),
        out_specs=[ANYWHERE, ANYWHERE, whole(2 * NB, BLK), whole(SEQ, LOC), whole(2 * NB, BLK), ANYWHERE, ANYWHERE],
        out_shape=[sds((2, SEQ, LOC), F32), sds((3, SEQ, LOC), BF), sds((2 * NB, BLK), F32), sds((SEQ, LOC), BF),
                   sds((2 * NB, BLK), F32), sds((2, TOK, DIM), BF), sds((SEQ, DIM), BF)],
        input_output_aliases={8: 5} if both else {},
        scratch_shapes=[pltpu.VMEM((2, SEQ, LOC), F32), pltpu.VMEM((3, SEQ, LOC), BF), pltpu.VMEM((2 * NB, BLK), F32),
                        pltpu.VMEM((NDEV - 1, 2 * NB, BLK), F32),
                        pltpu.VMEM((NB, BLK, BLK), F32), pltpu.VMEM((HD, SEQ), BF), pltpu.VMEM((HD, BLK), F32),
                        pltpu.VMEM((2, NB, BLK, HD), BF), DMA((1, NDEV - 1)), DMA((1, NDEV - 1)), DMA((2,)),
                        DMA((2, NB, 2)), DMA((2, NDEV)), DMA((2,))] + BG,
        compiler_params=params(dimension_semantics=("arbitrary",), collective_id=cid, has_side_effects=True),
        cost_estimate=cost(30e9, 30e6),
        name="forward",
    )(x, wq, wk, wv, gains, cos, sin, shard, *both)


def out_kernel(o_ref, wo_ref, x_ref, dy_ref, gains_ref, y_ref, da_ref, gga_ref, both_ref, a_scr, dh_scr, send_sems, recv_sems,
               own_sems):
    b = pl.program_id(0)
    me = lax.axis_index('tp')

    @pl.when(b == 0)
    def _():
        entry_barrier(me)
        gga_ref[...] = jnp.zeros_like(gga_ref)

    step = DIM // NB
    o = o_ref[0]

    def fwd(j, carry):
        cols = pl.ds(pl.multiple_of(j * step, step), step)
        a_scr[:, cols] = dot(o, wo_ref[:, cols])
        return carry

    lax.fori_loop(0, NB, fwd, 0)
    a = a_scr[...]
    r = lax.rsqrt(jnp.mean(a * a, axis=-1, keepdims=True) + EPS)
    n = a * r
    ga = jnp.concatenate([gains_ref[2 + i:3 + i, :] for i in range(8)], axis=1)
    dy = dy_ref[0].astype(F32)
    y_ref[0] = (x_ref[0].astype(F32) + n * ga).astype(BF)
    col = jnp.sum(dy * n, axis=0, keepdims=True)
    for i in range(8):
        gga_ref[i:i + 1, :] += col[:, i * LOC:(i + 1) * LOC]
    gn = dy * ga
    da_ref[0] = (r * (gn - n * jnp.mean(gn * n, axis=-1, keepdims=True))).astype(BF)
    da = da_ref[0]

    def block_copy(bb, st, half):
        dest = 2 * ((me // 2 + 1 + st) % NB) + half
        src = dh_scr.at[bb, st, :, pl.ds(half * LOC, LOC)]
        mine = both_ref.at[bb, shard_rows(me), :]
        away = pltpu.make_async_remote_copy(
            src_ref=src, dst_ref=mine, send_sem=send_sems.at[bb, st, half], recv_sem=recv_sems.at[bb, me],
            device_id=(dest,), device_id_type=MESH)
        return dest, away, pltpu.make_async_copy(src, mine, own_sems.at[bb])

    def bwd(st, carry):
        blk = (me // 2 + 1 + st) % NB
        dh_scr[b, st] = dot(da, wo_ref[pl.ds(pl.multiple_of(blk * step, step), step), :], NT).astype(BF)
        for half in range(2):
            dest, away, here = block_copy(b, st, half)
            pl.when(dest != me)(away.start)
            pl.when(dest == me)(here.start)
        return carry

    lax.fori_loop(0, NB, bwd, 0)

    @pl.when(b == 1)
    def _():
        for bb in range(2):
            for st in range(NB):
                for half in range(2):
                    dest, away, here = block_copy(bb, st, half)
                    if st < NB - 1:
                        away.wait_send()
                    else:
                        pl.when(dest != me)(away.wait_send)
                        pl.when(dest == me)(here.wait)
            for mask in ORDER:
                peer = peer_of(me, mask)
                pltpu.make_async_remote_copy(
                    src_ref=dh_scr.at[0, 0, :, pl.ds(0, LOC)], dst_ref=both_ref.at[bb, shard_rows(peer), :],
                    send_sem=send_sems.at[0, 0, 0], recv_sem=recv_sems.at[bb, peer], device_id=(peer,),
                    device_id_type=MESH).wait_recv()


def out_block(o, wo, x, dy, gains, cid):
    def whole(*shape):
        return pl.BlockSpec(shape, lambda i: (0,) * len(shape))

    batch = pl.BlockSpec((1, TOK, DIM), lambda i: (i, 0, 0))
    return pl.pallas_call(
        out_kernel,
        grid=(2,),
        in_specs=[batch, whole(DIM, DIM), batch, batch, whole(2 + DIM // LOC, LOC)],
        out_specs=[batch, batch, whole(8, DIM // 8), ANYWHERE],
        out_shape=[sds((2, TOK, DIM), BF), sds((2, TOK, DIM), BF), sds((8, DIM // 8), F32), sds((2, SEQ, LOC), BF)],
        scratch_shapes=[pltpu.VMEM((TOK, DIM), F32), pltpu.VMEM((2, NB, TOK, DIM // NB), BF), DMA((2, NB, 2)),
                        DMA((2, NDEV)), DMA((2,))],
        compiler_params=params(dimension_semantics=("arbitrary",), collective_id=cid, has_side_effects=True),
        cost_estimate=cost(8 * TOK * DIM * DIM + 5e9, 18e6),
        name="out_block",
    )(o, wo, x, dy, gains)


def backward_kernel(b, qkv_ref, do_ref, lse_ref, raw_ref, inv_ref, gains_ref, cos_ref, sin_ref, gga_ref, shard_ref, *rest):
    if b:
        _, d_ref, pd_ref, gg_ref, gout_ref, full_ref, old_ref, *rest = rest
    else:
        d_ref, pd_ref, gg_ref, gout_ref, full_ref, *rest = rest
    (p_scr, dp_scr, kt_scr, dqt_scr, dq_scr, dk_scr, dv_scr, du_scr, d_scr, dots_scr, total, slot, ga_slot,
     ex_send, ex_recv, pd_send, pd_recv, d_sems, *bg) = rest
    h, qi = pl.program_id(0), pl.program_id(1)
    me = lax.axis_index('tp')
    gather = stage1(me, shard_ref.at[b], full_ref, bg)

    @pl.when(jnp.logical_and(h == 0, qi == 0))
    def _():
        stages = ([stage3(me, old_ref, bg)] if b else []) + [gather]
        for stage in stages:
            stage.load()
        entry_barrier(me)
        for stage in stages:
            stage.send()
        dots_scr[...] = jnp.zeros_like(dots_scr)

    @pl.when(qi == 0)
    def _():
        kt_scr[...] = qkv_ref[1].T
        dk_scr[...] = jnp.zeros_like(dk_scr)
        dv_scr[...] = jnp.zeros_like(dv_scr)

    qb = qkv_ref[0, block_rows(qi), :]
    dob = do_ref[...]
    lse = lse_ref[pl.ds(h * NB + qi, 1), :]

    def first(j, acc, diag=False):
        rows = block_rows(j)
        p = jnp.exp2(dot(qkv_ref[1, rows, :], qb, NT) * C2 - lse)
        if diag:
            p = jnp.where(causal_mask(), p, 0.0)
        dp = dot(qkv_ref[2, rows, :], dob, NT)
        p_scr[j] = p
        dp_scr[j] = dp
        dv_scr[rows, :] += dot(p.astype(BF), dob)
        return acc + jnp.sum((p * dp).reshape(BLK // 8, 8, BLK), axis=0)

    acc = first(qi, jnp.zeros((8, BLK), F32), True)
    acc = lax.fori_loop(0, qi, first, acc)
    delta = jnp.sum(acc, axis=0, keepdims=True)
    dqt_scr[...] = jnp.zeros_like(dqt_scr)

    def second(j, carry):
        rows = block_rows(j)
        ds = (p_scr[j] * (dp_scr[j] - delta) * SCALE).astype(BF)
        dk_scr[rows, :] += dot(ds, qb)
        dqt_scr[...] += dot(kt_scr[:, rows], ds)
        return carry

    lax.fori_loop(0, qi + 1, second, 0)
    dq_scr[block_rows(qi), :] = dqt_scr[...].T

    @pl.when(qi == NB - 1)
    def _():
        d_scr[:, pl.ds(pl.multiple_of(2 * LOC + h * HD, HD), HD)] = dv_scr[...].astype(BF)
        gg_ref[...] = jnp.zeros_like(gg_ref)
        cols = head_cols(h)

        def tail(i, carry):
            rows = block_rows(i)
            cos, sin = cos_ref[rows, :], sin_ref[rows, :]
            for n, from_scr in enumerate((dq_scr, dk_scr)):
                d = from_scr[rows, :]
                hat = d * cos - pltpu.roll(d, HD // 2, 1) * sin
                unit = raw_ref[n, rows, cols] * as_column(inv_ref[pl.ds(i + n * NB, 1), :])
                gg_ref[n:n + 1, :] += jnp.sum(hat * unit, axis=0, keepdims=True)
                du = hat * gains_ref[n:n + 1, :]
                du_scr[n, h, rows, :] = du
                dots_scr[pl.ds(i + n * NB, 1), :] += row_sums(du * unit)
            return carry

        lax.fori_loop(0, NB, tail, 0)

    @pl.when(jnp.logical_and(h == 1, qi == NB - 1))
    def _():
        gather.wait()
        if b:
            stage3(me, old_ref, bg).wait()
        sums = exchange(me, [dots_scr, gga_ref], [slot, ga_slot], ex_send, ex_recv)
        start(sums)
        more = stage2(me, full_ref, bg)
        more.load()
        more.send()
        wait(sums)
        total[...] = ordered_total(me, dots_scr, slot) / DIM
        gout_ref[...] = ordered_total(me, gga_ref, ga_slot)

        def copies(i):
            rows = block_rows(i)
            return [pltpu.make_async_copy(d_scr.at[rows, :], d_ref.at[rows, :], d_sems.at[i]),
                    pltpu.make_async_remote_copy(
                        src_ref=d_scr.at[rows, :], dst_ref=pd_ref.at[rows, :], send_sem=pd_send.at[i],
                        recv_sem=pd_recv.at[i], device_id=(peer_of(me, 1),), device_id_type=MESH)]

        def last(i, carry):
            rows = block_rows(i)
            for n in range(2):
                dots = as_column(total[pl.ds(i + n * NB, 1), :])
                inv = as_column(inv_ref[pl.ds(i + n * NB, 1), :])
                for hh in range(LOC // HD):
                    sl = slice(hh * HD, (hh + 1) * HD)
                    unit = raw_ref[n, rows, sl] * inv
                    val = inv * (du_scr[n, hh, rows, :] - unit * dots)
                    d_scr[rows, n * LOC + hh * HD:n * LOC + (hh + 1) * HD] = val.astype(BF)
            start(copies(i))
            return carry

        lax.fori_loop(0, NB, last, 0)
        for i in range(NB):
            wait(copies(i))
        more.wait()


def backward(b, qkv, do, lse, raw, inv, gains, cos, sin, gga, shard, old, cid):
    def whole(*shape):
        return pl.BlockSpec(shape, lambda h, i: (0,) * len(shape))

    gsp = whole(8, DIM // 8)
    return pl.pallas_call(
        functools.partial(backward_kernel, b),
        grid=(2, NB),
        in_specs=[pl.BlockSpec((3, SEQ, HD), lambda h, i: (0, 0, h)), pl.BlockSpec((None, BLK, HD), lambda h, i: (b, i, h)),
                  whole(2 * NB, BLK), whole(2, SEQ, LOC), whole(2 * NB, BLK),
                  pl.BlockSpec((2 + DIM // LOC, HD), lambda h, i: (0, h)), whole(SEQ, HD), whole(SEQ, HD), gsp, ANYWHERE]
        + [ANYWHERE] * len(old),
        out_specs=[ANYWHERE, ANYWHERE, pl.BlockSpec((8, HD), lambda h, i: (0, h)), gsp, ANYWHERE] + [ANYWHERE] * len(old),
        out_shape=[sds((SEQ, 3 * LOC), BF), sds((SEQ, 3 * LOC), BF), sds((8, LOC), F32), sds((8, DIM // 8), F32),
                   sds((SEQ, DIM), BF)] + [sds((SEQ, DIM), BF)] * len(old),
        input_output_aliases={10: 5} if old else {},
        scratch_shapes=[pltpu.VMEM((NB, BLK, BLK), F32), pltpu.VMEM((NB, BLK, BLK), F32), pltpu.VMEM((HD, SEQ), BF),
                        pltpu.VMEM((HD, BLK), F32), pltpu.VMEM((SEQ, HD), F32), pltpu.VMEM((SEQ, HD), F32),
                        pltpu.VMEM((SEQ, HD), F32), pltpu.VMEM((2, 2, SEQ, HD), F32), pltpu.VMEM((SEQ, 3 * LOC), BF),
                        pltpu.VMEM((2 * NB, BLK), F32), pltpu.VMEM((2 * NB, BLK), F32),
                        pltpu.VMEM((NDEV - 1, 2 * NB, BLK), F32), pltpu.VMEM((NDEV - 1, 8, DIM // 8), F32),
                        DMA((2, NDEV - 1)), DMA((2, NDEV - 1)), DMA((NB,)), DMA((NB,)), DMA((NB,))] + BG,
        compiler_params=params(dimension_semantics=("arbitrary", "arbitrary"), collective_id=cid, has_side_effects=True),
        cost_estimate=cost(20e9, 20e6),
        name="backward",
    )(qkv, do, lse, raw, inv, gains, cos, sin, gga, shard, *old)


HALF = DIM // 2
CH = 256


def grads_kernel(d0, d1, pd0, pd1, wq, wk, wv, x0, x1, o0, o1, da0, da1_in, dy_ref, dx_ref, gwq_ref, gwk_ref, gwv_ref, gwo_ref, da1,
                 d_all, w_all, sbuf, r1, r2, fin, acc, xbuf, obuf,
                 dl_sems, w_sems, s1_sems, r1_sems, s2_sems, r2_sems, fs_sems, fr_sems, x_sems, o_sems, *sems):
    del da1_in
    me = lax.axis_index('tp')
    core, chip = me % 2, me // 2
    partner = peer_of(me, 1)
    first = peer_of(me, 2) * (1 - core) + peer_of(me, 4) * core
    second = peer_of(me, 4) * (1 - core) + peer_of(me, 2) * core
    diag_chip, first_chip, second_chip = peer_of(me, 6) // 2, first // 2, second // 2

    barrier = pltpu.get_barrier_semaphore()
    for dev in (partner, first, second):
        pl.semaphore_signal(barrier, inc=1, device_id=(dev,), device_id_type=MESH)
    pl.semaphore_wait(barrier, 3)

    def rows_of(blk):
        return pl.ds(pl.multiple_of(blk * BLK, BLK), BLK)

    def half_rows(c):
        return pl.ds(pl.multiple_of(c * HALF, HALF), HALF)

    chips = (diag_chip, first_chip, second_chip, chip)
    w_copies = []
    for n, w in enumerate((wq, wk, wv)):
        part = pl.ds(n * LOC, LOC)
        w_copies.append(pltpu.make_async_remote_copy(
            src_ref=w.at[half_rows(1 - core), :], dst_ref=w_all.at[1, :, part], send_sem=w_sems.at[n],
            recv_sem=w_sems.at[3 + n], device_id=(partner,), device_id_type=MESH))
        w_copies.append(pltpu.make_async_copy(w.at[half_rows(core), :], w_all.at[0, :, part], w_sems.at[6 + n]))
    start(w_copies)
    loads = []
    for kind in range(4):
        for b in range(2):
            n = 2 * kind + b
            rows = rows_of(chips[kind])
            for side, d in enumerate(((d0, d1)[b], (pd0, pd1)[b])):
                loads.append(pltpu.make_async_copy(d.at[rows, :], d_all.at[side, b, rows, :], dl_sems.at[side, n]))
    start(loads)
    last_stage = stage3(me, da1, (*sems, xbuf))
    last_stage.load()
    last_stage.send()
    wait(w_copies)

    def arrived(n, b, blk):
        rows = rows_of(blk)
        for side in range(2):
            pltpu.make_async_copy(d0.at[rows, :], d_all.at[side, b, rows, :], dl_sems.at[side, n]).wait()

    def partial(b, blk):
        rows = rows_of(blk)
        return dot(d_all[0, b, rows, :], w_all[0], NT) + dot(d_all[1, b, rows, :], w_all[1], NT)

    def to_first(n):
        return pltpu.make_async_remote_copy(
            src_ref=sbuf.at[n], dst_ref=r1.at[n], send_sem=s1_sems.at[n], recv_sem=r1_sems.at[n],
            device_id=(first,), device_id_type=MESH)

    def to_second(b):
        return pltpu.make_async_remote_copy(
            src_ref=r1.at[b], dst_ref=r2.at[b], send_sem=s2_sems.at[b], recv_sem=r2_sems.at[b],
            device_id=(second,), device_id_type=MESH)

    def to_partner(b):
        return pltpu.make_async_remote_copy(
            src_ref=r1.at[2 + b, pl.ds(pl.multiple_of((1 - core) * TOK, TOK), TOK), :], dst_ref=fin.at[b],
            send_sem=fs_sems.at[b], recv_sem=fr_sems.at[b], device_id=(partner,), device_id_type=MESH)

    def phase1(n, carry):
        kind, b = n // 2, n % 2
        blk = diag_chip * (1 - kind) + first_chip * kind
        arrived(n, b, blk)
        sbuf[n] = partial(b, blk)
        to_first(n).start()
        return carry

    lax.fori_loop(0, 4, phase1, 0)
    for n in range(4, 8):
        arrived(n, n % 2, chips[n // 2])

    steps = SEQ // CH

    def chunk(i):
        return pl.ds(pl.multiple_of(i * CH, CH), CH)

    def stream(pairs, body):
        def fetch(i):
            return [pltpu.make_async_copy(src.at[chunk(i), :], buf.at[i % 2], sems.at[i % 2]) for src, buf, sems in pairs]

        for c in fetch(0):
            c.start()

        def it(i, carry):
            @pl.when(i + 1 < steps)
            def _():
                for c in fetch(i + 1):
                    c.start()

            for c in fetch(i):
                c.wait()
            body(i)
            return carry

        lax.fori_loop(0, steps, it, 0)

    def wgrad(b, src):
        def body(i):
            left = d_all[0, b, chunk(i), :].T
            for c in range(3):
                part = slice(c * LOC, (c + 1) * LOC)
                acc[part, :] += dot(left[part, :], xbuf[i % 2])

        stream([(src, xbuf, x_sems)], body)

    def forward_second(b, carry):
        to_first(b).wait_recv()
        r1[b] += partial(b, second_chip)
        to_second(b).start()
        return carry

    acc[...] = jnp.zeros_like(acc)
    last_stage.wait()
    wgrad(0, x0)
    forward_second(0, 0)
    wgrad(1, x1)
    for n, ref in enumerate((gwq_ref, gwk_ref, gwv_ref)):
        ref[...] = acc[n * LOC:(n + 1) * LOC, :].T.astype(BF)
    forward_second(1, 0)
    acc[:LOC, :] = jnp.zeros((LOC, DIM), F32)

    def wo_body(i):
        acc[:LOC, :] += dot(obuf[i % 2].T, xbuf[i % 2])

    for o_src, da_src in ((o0, da0), (o1, da1)):
        stream([(da_src, xbuf, x_sems), (o_src, obuf, o_sems)], wo_body)
    gwo_ref[...] = acc[:LOC, :].astype(BF)

    def own_part(b, carry):
        r1_own = partial(b, chip)
        to_first(2 + b).wait_recv()
        to_second(b).wait_recv()
        r1[2 + b] += r1_own + r2[b]
        to_partner(b).start()
        cols = half_rows(core)
        rows = pl.ds(pl.multiple_of(core * TOK, TOK), TOK)
        dx_ref[b, :, cols] = (r1[2 + b, rows, :] + dy_ref[b, :, cols].astype(F32)).astype(BF)
        return carry

    lax.fori_loop(0, 2, own_part, 0)

    def finish(b, carry):
        to_partner(b).wait()
        cols = half_rows(1 - core)
        dx_ref[b, :, cols] = (fin[b] + dy_ref[b, :, cols].astype(F32)).astype(BF)
        to_second(b).wait_send()
        to_first(b).wait_send()
        to_first(2 + b).wait_send()
        return carry

    lax.fori_loop(0, 2, finish, 0)


def grads(d0, d1, pd0, pd1, wq, wk, wv, x0, x1, o0, o1, da0, da1, dy, cid):
    vm = pl.BlockSpec(memory_space=pltpu.VMEM)
    far = pl.BlockSpec(memory_space=pl.ANY)
    dma = pltpu.SemaphoreType.DMA
    return pl.pallas_call(
        grads_kernel,
        in_specs=[far] * 13 + [vm],
        out_specs=[vm] * 5 + [far],
        out_shape=[sds((2, TOK, DIM), BF)] + [sds((DIM, LOC), BF)] * 3 + [sds((LOC, DIM), BF), sds((SEQ, DIM), BF)],
        input_output_aliases={12: 5},
        scratch_shapes=[pltpu.VMEM((2, 2, SEQ, 3 * LOC), BF), pltpu.VMEM((2, HALF, 3 * LOC), BF),
                        pltpu.VMEM((4, BLK, HALF), F32), pltpu.VMEM((4, BLK, HALF), F32), pltpu.VMEM((2, BLK, HALF), F32),
                        pltpu.VMEM((2, TOK, HALF), F32), pltpu.VMEM((3 * LOC, DIM), F32),
                        pltpu.VMEM((2, CH, DIM), BF), pltpu.VMEM((2, CH, LOC), BF),
                        dma((2, 8)), dma((9,)), dma((4,)), dma((4,)), dma((2,)), dma((2,)),
                        dma((2,)), dma((2,)), dma((2,)), dma((2,))] + BG_SEMS,
        compiler_params=pltpu.CompilerParams(vmem_limit_bytes=67043328, collective_id=cid, has_side_effects=True),
        cost_estimate=cost(100e9, 40e6),
        name="grads",
    )(d0, d1, pd0, pd1, wq, wk, wv, x0, x1, o0, o1, da0, da1, dy)


def local_block(x_loc, wq, wk, wv, wo, gq, gk, ga, dy_loc):
    gains = jnp.concatenate([gq, gk, ga]).astype(F32).reshape(2 + DIM // LOC, LOC)
    x_full, cos, sin = first_gather(x_loc, 0)
    gathered, fwd, o_recv = [x_full], [], []
    for b in range(2):
        shard, pick = (x_loc, 1) if b == 0 else (wo, None)
        raw, qkv, inv, o, lse, recv, full = forward(b, gathered[b], wq, wk, wv, gains, cos, sin, shard, pick, o_recv, 1 + b)
        gathered.append(full)
        o_recv = [recv]
        fwd.append((raw, qkv, inv, o, lse))
    y, da, gga, dh = out_block(o_recv[0], gathered[2], x_loc, dy_loc, gains, 3)
    ds, ggs, da_full = [], [], []
    for b in range(2):
        raw, qkv, inv, o, lse = fwd[b]
        d, pd, gg, gout, full, *old = backward(b, qkv, dh, lse, raw, inv, gains, cos, sin, gga, da, da_full, 4 + b)
        da_full = list(old) + [full]
        ds.append((d, pd))
        ggs.append(gg)
        if b == 0:
            grad_ga = gout.reshape(DIM).astype(BF)
    dx, gwq, gwk, gwv, gwo, _ = grads(ds[0][0], ds[1][0], ds[0][1], ds[1][1], wq, wk, wv, gathered[0], gathered[1],
                                      fwd[0][3], fwd[1][3], da_full[0], da_full[1], dy_loc, 6)
    gg = ggs[0] + ggs[1]
    return (y, dx, gwq, gwk, gwv, gwo, gg[0].astype(BF), gg[1].astype(BF), grad_ga)


def solution(mesh):
    act, col, row, vec = P(None, 'tp', None), P(None, 'tp'), P('tp', None), P('tp')
    in_specs = (act, col, col, col, row, vec, vec, P(), act)
    out_specs = (act, act, col, col, col, row, vec, vec, P())
    return jax.shard_map(local_block, mesh=mesh, in_specs=in_specs, out_specs=out_specs, check_vma=False)
```

time: 500 us -> 473 us (0.946)
  Pallas kernels: 483 us -> 458 us
    pallas_call x11 -> x5, Pallas kernels: 397 us -> 372 us  [the longest x1 153 us: grads(): pl.pallas_call(grads_kernel, in_specs=[far] * 13 + [vm], out_specs=[vm] *...]
where the time goes in v5:
time: 473 us; the launch traced here: 472 us
  Pallas kernels  458 us (97%)
  local copies, waits for them, and re-layouts  10.9 us (2%)
    pallas_call x1, Pallas kernels, grads(): pl.pallas_call(grads_kernel, in_specs=[far] * 13 + [vm], out_specs=[vm] *...  153 us
    pallas_call x2, Pallas kernels, forward(): pl.pallas_call(functools.partial(forward_kernel, b, pick), grid=(4 * NB,)...  123 us
    pallas_call x2, Pallas kernels, backward(): pl.pallas_call(functools.partial(backward_kernel, b), grid=(2, NB), in_sp...  96.3 us
    pallas_call x1, Pallas kernels, first_gather(): pl.pallas_call(gather_kernel, in_specs=[ANYWHERE, vm], out_specs=[ANYWHER...  47.9 us
    pallas_call x1, Pallas kernels, out_block(): pl.pallas_call(out_kernel, grid=(2,), in_specs=[batch, whole(DIM, DIM), b...  37.7 us
    unnamed x19, local copies, waits for them, and re-layouts  9.76 us

profile of v5, /device:TPU:0, one launch (start us, length us, event | category | flops | bytes accessed | tf_op | source)
XLA Modules:
  0.0 472.1 jit_solution(7117979067582446671)
XLA Ops:
  0.7 0.6 maximum_bitcast_fusion.freq_ref
  1.2 0.7 maximum_convert_fusion
  2.0 0.6 reshape.26.gains_ref
  2.6 47.9 %gather.1 = (bf16[2048,2048]{1,0:T(8,128)(2,1)}, f32[2048,128]{1,0:T(8,128)}, f32[2048,128]{1,0:T(8,128)}) custom-call(bf16[2,256,2048]{2,1,0:T(8,128)(2,1)} %x_ref.3, f32[1,128]{1,0:T(1,128)} %maximum_bitcast_fusion.freq_ref), custom_call_target="tpu_custom_call" | custom-call | flops 20000000000 | bytes 20000000 | tf_op jit(solution)/shard_map/gather/pallas_call | solution.py:170
  50.5 61.0 %forward.2 = (f32[2,2048,256]{2,1,0:T(8,128)}, bf16[3,2048,256]{2,1,0:T(8,128)(2,1)}, f32[8,512]{1,0:T(8,128)}, bf16[2048,256]{1,0:T(8,128)(2,1)}, f32[8,512]{1,...) custom-call(bf16[2048,2048]{1,0:T(8,128)(2,1)} %get-tuple-element.45.x_ref.x0, ...), custom_call_target="tpu_custom_call" | custom-call | flops 30000001024 | bytes 30000000 | tf_op jit(solution)/shard_map/forward/pallas_call | solution.py:386
  111.5 61.8 %forward.3 = (f32[2,2048,256]{2,1,0:T(8,128)}, bf16[3,2048,256]{2,1,0:T(8,128)(2,1)}, f32[8,512]{1,0:T(8,128)}, bf16[2048,256]{1,0:T(8,128)(2,1)}, f32[8,512]{1,...) custom-call(bf16[2048,2048]{1,0:T(8,128)(2,1)} %get-tuple-element.48.x_ref., ...), custom_call_target="tpu_custom_call", output_to_operand_aliasing={{5}: (8, {})} | custom-call | flops 30000001024 | bytes 30000000 | tf_op jit(solution)/shard_map/forward/pallas_call | solution.py:386
  173.4 37.7 %out_block.1 = (bf16[2,256,2048]{2,1,0:T(8,128)(2,1)}, bf16[2,256,2048]{2,1,0:T(8,128)(2,1)}, f32[8,256]{1,0:T(8,128)}, bf16[2,2048,256]{2,1,0:T(8,128)(2,1)}) custom-call(bf16[2,256,2048]{2,1,0:T(8,128)(2,1)} %get-tuple-element.50.o_ref, bf16[2048,2048]{1,0:T(8,128)(2,1)} %get-tuple-element.51.wo_ref, bf16[2,256,2048]{2,1,0:T(8,128)(2,1)} %x_ref.3, ...), custom_call_target="tpu_custom_call" | custom-call | flops 13589934080 | bytes 18000000 | tf_op jit(solution)/shard_map/out_block/pallas_call | solution.py:482
  211.0 48.7 %backward.2 = (bf16[2048,768]{1,0:T(8,128)(2,1)}, bf16[2048,768]{1,0:T(8,128)(2,1)}, f32[8,256]{1,0:T(8,128)}, f32[8,256]{1,0:T(8,128)}, bf16[2048,2048]{1,0:T(8,128)(2,1)}) custom-call(bf16[3,2048,256]{2,1,0:T(8,128)(2,1)} %get-tuple-element.53.qkv_ref, bf16[2,2048,256]{2,1,0:T(8,128)(2,1)} %get-tuple-element.54.do_ref, ...), custom_call_target="tpu_custom_call" | custom-call | flops 20000000000 | bytes 20000000 | tf_op jit(solution)/shard_map/backward/pallas_call | solution.py:619
  259.8 0.7 convert_bitcast_fusion
  260.5 0.6 copy.21
  261.1 0.0 copy-start.5
  261.1 47.6 %backward.3 = (bf16[2048,768]{1,0:T(8,128)(2,1)}, bf16[2048,768]{1,0:T(8,128)(2,1)}, f32[8,256]{1,0:T(8,128)}, f32[8,256]{1,0:T(8,128)}, bf16[2048,2048]{1,0:T(8,128)(2,1)}, /*index=5*/bf16[2048,2048]{1,0:T(8,128)(2,1)}) custom-call(bf16[3,2048,256]{2,1,0:T(8,128)(2,1)} %get-tuple-element.61.qkv_ref, ...), custom_call_target="tpu_custom_call", output_to_operand_aliasing={{5}: (10, {})} | custom-call | flops 20000000000 | bytes 20000000 | tf_op jit(solution)/shard_map/backward/pallas_call | solution.py:619
  308.7 0.0 copy-done.5
  308.7 0.7 add_convert_fusion
  309.4 0.5 slice_reduce_fusion
  309.9 153.0 %grads.1 = (bf16[2,256,2048]{2,1,0:T(8,128)(2,1)}, bf16[2048,256]{1,0:T(8,128)(2,1)}, bf16[2048,256]{1,0:T(8,128)(2,1)}, bf16[2048,256]{1,0:T(8,128)(2,1)}, bf16...) custom-call(bf16[2048,768]{1,0:T(8,128)(2,1)} %get-tuple-element.60.d0, ...), custom_call_target="tpu_custom_call", output_to_operand_aliasing={{5}: (12, {})} | custom-call | flops 99999997952 | bytes 40000000 | tf_op jit(solution)/shard_map/grads/pallas_call | solution.py:812
  462.9 0.0 copy-start
  463.0 3.3 copy.31
  466.3 0.0 copy-done
  466.3 0.0 copy-start.4
  466.3 0.0 copy-start.3
  466.3 1.3 copy.32
  467.6 0.6 copy-done.4
  468.2 0.0 copy-start.2
  468.2 0.0 copy-start.1
  468.2 1.0 copy.33
  469.2 0.0 copy-done.3
  469.2 1.0 copy.34
  470.2 0.0 copy-done.2
  470.2 1.0 copy.35
  471.1 0.0 copy-done.1
  471.1 1.0 copy.36
  (1 shorter events, 0.0 us)
Async XLA Ops:
  261.1 47.6 %copy-start.5 = (f32[8,256]{1,0:T(8,128)S(1)}, f32[8,256]{1,0:T(8,128)}, u32[]{:S(2)}) copy-start(f32[8,256]{1,0:T(8,128)} %get-tuple-element.78) | copy-start | bytes 24580
  462.9 3.3 copy-start
  466.3 2.0 copy-start.4
  466.3 2.9 copy-start.3
  468.2 1.9 copy-start.2
  468.2 2.9 copy-start.1

commit v6 on v5

--- a/solution.py
+++ b/solution.py
@@ -72,7 +72,7 @@
 
 DMA = pltpu.SemaphoreType.DMA
 ANYWHERE = pl.BlockSpec(memory_space=pl.ANY)
-BG_SEMS = [DMA((8,)), DMA((8,)), DMA((4,))]
+BG_SEMS = [DMA((11,)), DMA((11,)), DMA((5,))]
 BG = BG_SEMS + [pltpu.VMEM((2, TOK, DIM), BF)]
 
 
@@ -95,15 +95,16 @@
         wait(self.copies)
 
 
-def stage1(me, src, full, bg, lo=0, count=TOK):
+def stage1(me, src, full, bg, part=None):
     send, recv, own, buf = bg
+    lo, count, at = (0, TOK, 0) if part is None else (part * (TOK // 2), TOK // 2, 8 * part)
     there = full.at[shard_rows(me, lo, count), :]
-    part = buf.at[0, pl.ds(0, count), :]
+    mine = buf.at[0, pl.ds(lo, count), :]
     copies = [pltpu.make_async_remote_copy(
-        src_ref=part, dst_ref=there, send_sem=send.at[k], recv_sem=recv.at[k],
+        src_ref=mine, dst_ref=there, send_sem=send.at[at + k], recv_sem=recv.at[at + k],
         device_id=(peer_of(me, mask),), device_id_type=MESH) for k, mask in enumerate((2, 4, 1))]
-    return Stage([pltpu.make_async_copy(src.at[pl.ds(lo, count), :], part, own.at[0])],
-                 copies + [pltpu.make_async_copy(part, there, own.at[2])])
+    loads = [] if part == 1 else [pltpu.make_async_copy(src, buf.at[0], own.at[0])]
+    return Stage(loads, copies + [pltpu.make_async_copy(mine, there, own.at[3 if part == 1 else 2])])
 
 
 def stage2(me, full, bg):
@@ -137,48 +138,6 @@
         c.wait()
 
 
-def gather_kernel(x_ref, freq_ref, full_ref, cos_ref, sin_ref, *bg):
-    me = lax.axis_index('tp')
-    first = stage1(me, x_ref.at[0], full_ref, bg)
-    first.load()
-    nbr_barrier(me)
-    first.send()
-    freq = freq_ref[...]
-    sign = jnp.where(lax.broadcasted_iota(jnp.int32, (TOK, HD), 1) < HD // 2, -1.0, 1.0)
-
-    def table(i, carry):
-        rows = pl.ds(pl.multiple_of(i * TOK, TOK), TOK)
-        pos = (lax.broadcasted_iota(jnp.int32, (TOK, HD), 0) + i * TOK).astype(F32)
-        angle = pos * freq
-        cos_ref[rows, :] = jnp.cos(angle)
-        sin_ref[rows, :] = jnp.sin(angle) * sign
-        return carry
-
-    lax.fori_loop(0, SEQ // TOK, table, 0)
-    first.wait()
-    for stage in (stage2(me, full_ref, bg), stage3(me, full_ref, bg)):
-        stage.load()
-        stage.send()
-        stage.wait()
-
-
-def first_gather(x, cid):
-    half = HD // 2
-    inv_freq = 1.0 / (ROPE_THETA ** (jnp.arange(half, dtype=F32) / half))
-    freq = jnp.concatenate([inv_freq, inv_freq])[None, :]
-    vm = pl.BlockSpec(memory_space=pltpu.VMEM)
-    return pl.pallas_call(
-        gather_kernel,
-        in_specs=[ANYWHERE, vm],
-        out_specs=[ANYWHERE, vm, vm],
-        out_shape=[sds((SEQ, DIM), BF), sds((SEQ, HD), F32), sds((SEQ, HD), F32)],
-        scratch_shapes=BG,
-        compiler_params=params(collective_id=cid, has_side_effects=True),
-        cost_estimate=cost(20e9, 20e6),
-        name="gather",
-    )(x, freq)
-
-
 def row_sums(vals):
     folded = vals[:, :HD]
     for start in range(HD, vals.shape[1], HD):
@@ -225,55 +184,120 @@
     return pl.ds(pl.multiple_of(h * HD, HD), HD)
 
 
-def forward_kernel(b, pick, x_ref, wq_ref, wk_ref, wv_ref, gains_ref, cos_ref, sin_ref, shard_ref, *rest):
-    if b:
-        _, *rest = rest
-    (raw_ref, qkv_ref, inv_ref, o_ref, lse_ref, both_ref, full_ref,
-     raw, qkv, sums_scr, slot, p_scr, vt_scr, acc_scr, o_scr,
-     ex_send, ex_recv, out_sems, send_sems, recv_sems, own_sems, *bg) = rest
-    recv_ref = both_ref.at[b]
-    t = pl.program_id(0)
+def forward_kernel(freq_ref, wq_ref, wk_ref, wv_ref, gains_ref, x_ref, wo_ref,
+                   cos_ref, sin_ref, inv_ref, o_ref, lse_ref, raw_ref, qkv_ref, both_ref, full_ref, wof_ref,
+                   raw, qkv, xbuf, sums_scr, slot, p_scr, vt_scr, acc_scr, o_scr, buf0, buf1,
+                   ex_send, ex_recv, out_sems, send_sems, recv_sems, own_sems, x_sems, *bg_sems):
+    g = pl.program_id(0)
+    b, t = g // (4 * NB), g % (4 * NB)
     me = lax.axis_index('tp')
-    src = shard_ref if pick is None else shard_ref.at[pick]
-
-    def keep(n):
-        return (pltpu.make_async_copy(raw, raw_ref, out_sems.at[0]), pltpu.make_async_copy(qkv, qkv_ref, out_sems.at[1]))[n]
-
-    def sums():
-        return exchange(me, [sums_scr], [slot], ex_send, ex_recv)
-
-    def block_copy(hh, st, half):
+    bg0, bg1, bg2 = (*bg_sems[:3], buf0), (*bg_sems[3:6], buf1), (*bg_sems[6:], buf0)
+    x0f, x1f = full_ref.at[0], full_ref.at[1]
+
+    def x_gather(part=None):
+        return stage1(me, x_ref.at[1], x1f, bg1, part)
+
+    def wo_gather(part=None):
+        return stage1(me, wo_ref, wof_ref, bg2, part)
+
+    def keep(bb):
+        return [pltpu.make_async_copy(raw, raw_ref.at[bb], out_sems.at[0]),
+                pltpu.make_async_copy(qkv, qkv_ref.at[bb], out_sems.at[1])]
+
+    def sums(bb):
+        return exchange(me, [sums_scr.at[bb]], [slot.at[bb]], ex_send.at[bb], ex_recv.at[bb])
+
+    def fetch(bb, i):
+        return pltpu.make_async_copy(full_ref.at[bb, block_rows(i), :], xbuf.at[i % 2], x_sems.at[i % 2])
+
+    def block_copy(bb, hh, st, half):
         dest = 2 * ((me // 2 + 1 + st) % NB) + half
-        part = o_scr.at[hh, st, pl.ds(half * TOK, TOK), :]
-        dst = recv_ref.at[:, pl.ds(pl.multiple_of(me * LOC + hh * HD, HD), HD)]
+        part = o_scr.at[bb, hh, st, pl.ds(half * TOK, TOK), :]
+        dst = both_ref.at[bb, :, pl.ds(pl.multiple_of(me * LOC + hh * HD, HD), HD)]
         away = pltpu.make_async_remote_copy(
-            src_ref=part, dst_ref=dst, send_sem=send_sems.at[hh, st, half], recv_sem=recv_sems.at[hh, me],
+            src_ref=part, dst_ref=dst, send_sem=send_sems.at[bb, hh, st, half], recv_sem=recv_sems.at[bb, hh, me],
             device_id=(dest,), device_id_type=MESH)
-        return dest, away, pltpu.make_async_copy(part, dst, own_sems.at[hh])
-
-    @pl.when(t == 0)
-    def _():
-        stage = stage1(me, src, full_ref, bg)
+        return dest, away, pltpu.make_async_copy(part, dst, own_sems.at[bb, hh])
+
+    def run(stage):
         stage.load()
+        stage.send()
+
+    @pl.when(g == 0)
+    def _():
+        first = stage1(me, x_ref.at[0], x0f, bg0)
+        first.load()
         entry_barrier(me)
-        stage.send()
+        first.send()
+        x_gather(0).load()
+        freq = freq_ref[...]
+        sign = jnp.where(lax.broadcasted_iota(jnp.int32, (TOK, HD), 1) < HD // 2, -1.0, 1.0)
+
+        def table(i, carry):
+            rows = pl.ds(pl.multiple_of(i * TOK, TOK), TOK)
+            pos = (lax.broadcasted_iota(jnp.int32, (TOK, HD), 0) + i * TOK).astype(F32)
+            angle = pos * freq
+            cos_ref[rows, :] = jnp.cos(angle)
+            sin_ref[rows, :] = jnp.sin(angle) * sign
+            return carry
+
+        lax.fori_loop(0, SEQ // TOK, table, 0)
+        first.wait()
+        second, third = stage2(me, x0f, bg0), stage3(me, x0f, bg0)
+        run(second)
+        x_gather(0).send()
+        second.wait()
+        run(third)
+        third.wait()
+        fetch(0, 0).start()
+
+    @pl.when(g == 2 * NB + 2)
+    def _():
+        x_gather(0).wait()
+        x_gather(1).wait()
+        run(stage2(me, x1f, bg1))
+        run(wo_gather(0))
+
+    @pl.when(g == 4 * NB)
+    def _():
+        stage2(me, x1f, bg1).wait()
+        third = stage3(me, x1f, bg1)
+        run(third)
+        for c in keep(0):
+            c.wait()
+        third.wait()
+        fetch(1, 0).start()
+
+    @pl.when(g == 6 * NB + 2)
+    def _():
+        wo_gather(0).wait()
+        wo_gather(1).wait()
+        run(stage2(me, wof_ref, bg2))
 
     @pl.when(t < NB)
     def _():
         rows = block_rows(t)
-        x = x_ref[...]
+
+        @pl.when(t < NB - 1)
+        def _():
+            fetch(b, t + 1).start()
+
+        fetch(b, t).wait()
+        x = xbuf[t % 2]
         for n, w_ref in enumerate((wq_ref, wk_ref)):
             val = dot(x, w_ref[...])
             raw[n, rows, :] = val
-            sums_scr[pl.ds(t + n * NB, 1), :] = row_sums(val * val)
+            sums_scr[b, pl.ds(t + n * NB, 1), :] = row_sums(val * val)
         qkv[2, rows, :] = dot(x, wv_ref[...]).astype(BF)
 
     @pl.when(t == NB)
     def _():
-        start(sums())
-        keep(0).start()
-        wait(sums())
-        inv_ref[...] = lax.rsqrt(ordered_total(me, sums_scr, slot) / DIM + EPS)
+        start(sums(b))
+        keep(b)[0].start()
+        pl.when(b == 0)(x_gather(1).send)
+        pl.when(b == 1)(wo_gather(1).send)
+        wait(sums(b))
+        inv_ref[...] = lax.rsqrt(ordered_total(me, sums_scr.at[b], slot.at[b]) / DIM + EPS)
 
     @pl.when(jnp.logical_and(t >= NB, t < 2 * NB))
     def _():
@@ -282,26 +306,15 @@
         cos, sin = cos_ref[rows, :], sin_ref[rows, :]
         for n in range(2):
             inv = as_column(inv_ref[pl.ds(i + n * NB, 1), :])
-            g = gains_ref[n:n + 1, :]
+            gain = gains_ref[n:n + 1, :]
             for h in range(LOC // HD):
                 sl = slice(h * HD, (h + 1) * HD)
-                hat = raw[n, rows, sl] * inv * g[:, sl]
+                hat = raw[n, rows, sl] * inv * gain[:, sl]
                 qkv[n, rows, sl] = (hat * cos + pltpu.roll(hat, HD // 2, 1) * sin).astype(BF)
 
     @pl.when(t == 2 * NB)
     def _():
-        keep(1).start()
-        stage1(me, src, full_ref, bg).wait()
-        stage = stage2(me, full_ref, bg)
-        stage.load()
-        stage.send()
-
-    @pl.when(t == 4 * NB - 2)
-    def _():
-        stage2(me, full_ref, bg).wait()
-        stage = stage3(me, full_ref, bg)
-        stage.load()
-        stage.send()
+        keep(b)[1].start()
 
     @pl.when(t >= 2 * NB)
     def _():
@@ -347,23 +360,27 @@
 
         lax.fori_loop(0, qi + 1, third, 0)
         out = acc_scr[...].T.astype(BF)
-        o_scr[h, step] = out
+        o_scr[b, h, step] = out
         o_ref[block_rows(qi), cols] = out
 
         for half in range(2):
-            dest, away, here = block_copy(h, step, half)
+            dest, away, here = block_copy(b, h, step, half)
             pl.when(dest != me)(away.start)
             pl.when(dest == me)(here.start)
 
-    @pl.when(t == 4 * NB - 1)
-    def _():
-        keep(0).wait()
-        keep(1).wait()
-        stage3(me, full_ref, bg).wait()
-        for hh in range(2):
+    @pl.when(g == 8 * NB - 1)
+    def _():
+        stage2(me, wof_ref, bg2).wait()
+        third = stage3(me, wof_ref, bg2)
+        run(third)
+        for c in keep(1):
+            c.wait()
+
+        def drain(n, carry):
+            bb, hh = n // 2, n % 2
             for st in range(NB):
                 for half in range(2):
-                    dest, away, here = block_copy(hh, st, half)
+                    dest, away, here = block_copy(bb, hh, st, half)
                     if st < NB - 1:
                         away.wait_send()
                     else:
@@ -372,35 +389,46 @@
             for mask in ORDER:
                 peer = peer_of(me, mask)
                 pltpu.make_async_remote_copy(
-                    src_ref=o_scr.at[0, 0, pl.ds(0, TOK), :],
-                    dst_ref=recv_ref.at[:, pl.ds(pl.multiple_of(peer * LOC + hh * HD, HD), HD)],
-                    send_sem=send_sems.at[0, 0, 0], recv_sem=recv_sems.at[hh, peer],
+                    src_ref=o_scr.at[0, 0, 0, pl.ds(0, TOK), :],
+                    dst_ref=both_ref.at[bb, :, pl.ds(pl.multiple_of(peer * LOC + hh * HD, HD), HD)],
+                    send_sem=send_sems.at[0, 0, 0, 0], recv_sem=recv_sems.at[bb, hh, peer],
                     device_id=(peer,), device_id_type=MESH).wait_recv()
-
-
-def forward(b, x, wq, wk, wv, gains, cos, sin, shard, pick, both, cid):
+            return carry
+
+        lax.fori_loop(0, 4, drain, 0)
+        third.wait()
+
+
+def forward(x, wq, wk, wv, wo, gains, cid):
+    half = HD // 2
+    inv_freq = 1.0 / (ROPE_THETA ** (jnp.arange(half, dtype=F32) / half))
+    freq = jnp.concatenate([inv_freq, inv_freq])[None, :]
+
     def whole(*shape):
-        return pl.BlockSpec(shape, lambda t: (0,) * len(shape))
-
-    wspec = whole(DIM, LOC)
+        return pl.BlockSpec(shape, lambda g: (0,) * len(shape))
+
+    def per_batch(*shape):
+        return pl.BlockSpec((None,) + shape, lambda g: (g // (4 * NB),) + (0,) * len(shape))
+
+    wspec, rows = whole(DIM, LOC), per_batch(2 * NB, BLK)
     return pl.pallas_call(
-        functools.partial(forward_kernel, b, pick),
-        grid=(4 * NB,),
-        in_specs=[pl.BlockSpec((BLK, DIM), lambda t: (jnp.minimum(t, NB - 1), 0)), wspec, wspec, wspec,
-                  whole(2 + DIM // LOC, LOC), whole(SEQ, HD), whole(SEQ, HD), ANYWHERE] + [ANYWHERE] * len(both),
-        out_specs=[ANYWHERE, ANYWHERE, whole(2 * NB, BLK), whole(SEQ, LOC), whole(2 * NB, BLK), ANYWHERE, ANYWHERE],
-        out_shape=[sds((2, SEQ, LOC), F32), sds((3, SEQ, LOC), BF), sds((2 * NB, BLK), F32), sds((SEQ, LOC), BF),
-                   sds((2 * NB, BLK), F32), sds((2, TOK, DIM), BF), sds((SEQ, DIM), BF)],
-        input_output_aliases={8: 5} if both else {},
-        scratch_shapes=[pltpu.VMEM((2, SEQ, LOC), F32), pltpu.VMEM((3, SEQ, LOC), BF), pltpu.VMEM((2 * NB, BLK), F32),
-                        pltpu.VMEM((NDEV - 1, 2 * NB, BLK), F32),
+        forward_kernel,
+        grid=(8 * NB,),
+        in_specs=[whole(1, HD), wspec, wspec, wspec, whole(2 + DIM // LOC, LOC), ANYWHERE, ANYWHERE],
+        out_specs=[whole(SEQ, HD), whole(SEQ, HD), rows, per_batch(SEQ, LOC), rows] + [ANYWHERE] * 5,
+        out_shape=[sds((SEQ, HD), F32), sds((SEQ, HD), F32), sds((2, 2 * NB, BLK), F32), sds((2, SEQ, LOC), BF),
+                   sds((2, 2 * NB, BLK), F32), sds((2, 2, SEQ, LOC), F32), sds((2, 3, SEQ, LOC), BF),
+                   sds((2, TOK, DIM), BF), sds((2, SEQ, DIM), BF), sds((SEQ, DIM), BF)],
+        scratch_shapes=[pltpu.VMEM((2, SEQ, LOC), F32), pltpu.VMEM((3, SEQ, LOC), BF), pltpu.VMEM((2, BLK, DIM), BF),
+                        pltpu.VMEM((2, 2 * NB, BLK), F32), pltpu.VMEM((2, NDEV - 1, 2 * NB, BLK), F32),
                         pltpu.VMEM((NB, BLK, BLK), F32), pltpu.VMEM((HD, SEQ), BF), pltpu.VMEM((HD, BLK), F32),
-                        pltpu.VMEM((2, NB, BLK, HD), BF), DMA((1, NDEV - 1)), DMA((1, NDEV - 1)), DMA((2,)),
-                        DMA((2, NB, 2)), DMA((2, NDEV)), DMA((2,))] + BG,
+                        pltpu.VMEM((2, 2, NB, BLK, HD), BF), pltpu.VMEM((2, TOK, DIM), BF), pltpu.VMEM((2, TOK, DIM), BF),
+                        DMA((2, 1, NDEV - 1)), DMA((2, 1, NDEV - 1)), DMA((2,)),
+                        DMA((2, 2, NB, 2)), DMA((2, 2, NDEV)), DMA((2, 2)), DMA((2,))] + BG_SEMS * 3,
         compiler_params=params(dimension_semantics=("arbitrary",), collective_id=cid, has_side_effects=True),
-        cost_estimate=cost(30e9, 30e6),
+        cost_estimate=cost(60e9, 60e6),
         name="forward",
-    )(x, wq, wk, wv, gains, cos, sin, shard, *both)
+    )(freq, wq, wk, wv, gains, x, wo)
 
 
 def out_kernel(o_ref, wo_ref, x_ref, dy_ref, gains_ref, y_ref, da_ref, gga_ref, both_ref, a_scr, dh_scr, send_sems, recv_sems,
@@ -615,12 +643,15 @@
     def whole(*shape):
         return pl.BlockSpec(shape, lambda h, i: (0,) * len(shape))
 
+    def picked(*shape):
+        return pl.BlockSpec((None,) + shape, lambda h, i: (b,) + (0,) * len(shape))
+
     gsp = whole(8, DIM // 8)
     return pl.pallas_call(
         functools.partial(backward_kernel, b),
         grid=(2, NB),
-        in_specs=[pl.BlockSpec((3, SEQ, HD), lambda h, i: (0, 0, h)), pl.BlockSpec((None, BLK, HD), lambda h, i: (b, i, h)),
-                  whole(2 * NB, BLK), whole(2, SEQ, LOC), whole(2 * NB, BLK),
+        in_specs=[pl.BlockSpec((None, 3, SEQ, HD), lambda h, i: (b, 0, 0, h)), pl.BlockSpec((None, BLK, HD), lambda h, i: (b, i, h)),
+                  picked(2 * NB, BLK), picked(2, SEQ, LOC), picked(2 * NB, BLK),
                   pl.BlockSpec((2 + DIM // LOC, HD), lambda h, i: (0, h)), whole(SEQ, HD), whole(SEQ, HD), gsp, ANYWHERE]
         + [ANYWHERE] * len(old),
         out_specs=[ANYWHERE, ANYWHERE, pl.BlockSpec((8, HD), lambda h, i: (0, h)), gsp, ANYWHERE] + [ANYWHERE] * len(old),
@@ -643,7 +674,7 @@
 CH = 256
 
 
-def grads_kernel(d0, d1, pd0, pd1, wq, wk, wv, x0, x1, o0, o1, da0, da1_in, dy_ref, dx_ref, gwq_ref, gwk_ref, gwv_ref, gwo_ref, da1,
+def grads_kernel(d0, d1, pd0, pd1, wq, wk, wv, x_full, o_all, da0, da1_in, dy_ref, dx_ref, gwq_ref, gwk_ref, gwv_ref, gwo_ref, da1,
                  d_all, w_all, sbuf, r1, r2, fin, acc, xbuf, obuf,
                  dl_sems, w_sems, s1_sems, r1_sems, s2_sems, r2_sems, fs_sems, fr_sems, x_sems, o_sems, *sems):
     del da1_in
@@ -765,9 +796,9 @@
 
     acc[...] = jnp.zeros_like(acc)
     last_stage.wait()
-    wgrad(0, x0)
+    wgrad(0, x_full.at[0])
     forward_second(0, 0)
-    wgrad(1, x1)
+    wgrad(1, x_full.at[1])
     for n, ref in enumerate((gwq_ref, gwk_ref, gwv_ref)):
         ref[...] = acc[n * LOC:(n + 1) * LOC, :].T.astype(BF)
     forward_second(1, 0)
@@ -776,7 +807,7 @@
     def wo_body(i):
         acc[:LOC, :] += dot(obuf[i % 2].T, xbuf[i % 2])
 
-    for o_src, da_src in ((o0, da0), (o1, da1)):
+    for o_src, da_src in ((o_all.at[0], da0), (o_all.at[1], da1)):
         stream([(da_src, xbuf, x_sems), (o_src, obuf, o_sems)], wo_body)
     gwo_ref[...] = acc[:LOC, :].astype(BF)
 
@@ -805,16 +836,16 @@
     lax.fori_loop(0, 2, finish, 0)
 
 
-def grads(d0, d1, pd0, pd1, wq, wk, wv, x0, x1, o0, o1, da0, da1, dy, cid):
+def grads(d0, d1, pd0, pd1, wq, wk, wv, x_full, o_all, da0, da1, dy, cid):
     vm = pl.BlockSpec(memory_space=pltpu.VMEM)
     far = pl.BlockSpec(memory_space=pl.ANY)
     dma = pltpu.SemaphoreType.DMA
     return pl.pallas_call(
         grads_kernel,
-        in_specs=[far] * 13 + [vm],
+        in_specs=[far] * 11 + [vm],
         out_specs=[vm] * 5 + [far],
         out_shape=[sds((2, TOK, DIM), BF)] + [sds((DIM, LOC), BF)] * 3 + [sds((LOC, DIM), BF), sds((SEQ, DIM), BF)],
-        input_output_aliases={12: 5},
+        input_output_aliases={10: 5},
         scratch_shapes=[pltpu.VMEM((2, 2, SEQ, 3 * LOC), BF), pltpu.VMEM((2, HALF, 3 * LOC), BF),
                         pltpu.VMEM((4, BLK, HALF), F32), pltpu.VMEM((4, BLK, HALF), F32), pltpu.VMEM((2, BLK, HALF), F32),
                         pltpu.VMEM((2, TOK, HALF), F32), pltpu.VMEM((3 * LOC, DIM), F32),
@@ -824,31 +855,23 @@
         compiler_params=pltpu.CompilerParams(vmem_limit_bytes=67043328, collective_id=cid, has_side_effects=True),
         cost_estimate=cost(100e9, 40e6),
         name="grads",
-    )(d0, d1, pd0, pd1, wq, wk, wv, x0, x1, o0, o1, da0, da1, dy)
+    )(d0, d1, pd0, pd1, wq, wk, wv, x_full, o_all, da0, da1, dy)
 
 
 def local_block(x_loc, wq, wk, wv, wo, gq, gk, ga, dy_loc):
     gains = jnp.concatenate([gq, gk, ga]).astype(F32).reshape(2 + DIM // LOC, LOC)
-    x_full, cos, sin = first_gather(x_loc, 0)
-    gathered, fwd, o_recv = [x_full], [], []
-    for b in range(2):
-        shard, pick = (x_loc, 1) if b == 0 else (wo, None)
-        raw, qkv, inv, o, lse, recv, full = forward(b, gathered[b], wq, wk, wv, gains, cos, sin, shard, pick, o_recv, 1 + b)
-        gathered.append(full)
-        o_recv = [recv]
-        fwd.append((raw, qkv, inv, o, lse))
-    y, da, gga, dh = out_block(o_recv[0], gathered[2], x_loc, dy_loc, gains, 3)
+    cos, sin, inv, o, lse, raw, qkv, o_recv, x_full, wo_full = forward(x_loc, wq, wk, wv, wo, gains, 0)
+    y, da, gga, dh = out_block(o_recv, wo_full, x_loc, dy_loc, gains, 1)
     ds, ggs, da_full = [], [], []
     for b in range(2):
-        raw, qkv, inv, o, lse = fwd[b]
-        d, pd, gg, gout, full, *old = backward(b, qkv, dh, lse, raw, inv, gains, cos, sin, gga, da, da_full, 4 + b)
+        d, pd, gg, gout, full, *old = backward(b, qkv, dh, lse, raw, inv, gains, cos, sin, gga, da, da_full, 2 + b)
         da_full = list(old) + [full]
         ds.append((d, pd))
         ggs.append(gg)
         if b == 0:
             grad_ga = gout.reshape(DIM).astype(BF)
-    dx, gwq, gwk, gwv, gwo, _ = grads(ds[0][0], ds[1][0], ds[0][1], ds[1][1], wq, wk, wv, gathered[0], gathered[1],
-                                      fwd[0][3], fwd[1][3], da_full[0], da_full[1], dy_loc, 6)
+    dx, gwq, gwk, gwv, gwo, _ = grads(ds[0][0], ds[1][0], ds[0][1], ds[1][1], wq, wk, wv, x_full, o,
+                                      da_full[0], da_full[1], dy_loc, 4)
     gg = ggs[0] + ggs[1]
     return (y, dx, gwq, gwk, gwv, gwo, gg[0].astype(BF), gg[1].astype(BF), grad_ga)
 

time: 473 us -> 449 us (0.949)
  Pallas kernels: 458 us -> 434 us
    pallas_call x4 -> x2, Pallas kernels: 324 us -> 300 us  [the longest x1 153 us: grads(): pl.pallas_call(grads_kernel, in_specs=[far] * 11 + [vm], out_specs=[vm] *...]
where the time goes in v6:
time: 449 us; the launch traced here: 448 us
  Pallas kernels  434 us (97%)
  local copies, waits for them, and re-layouts  10.9 us (2%)
    pallas_call x1, Pallas kernels, grads(): pl.pallas_call(grads_kernel, in_specs=[far] * 11 + [vm], out_specs=[vm] *...  153 us
    pallas_call x1, Pallas kernels, forward(): pl.pallas_call(forward_kernel, grid=(8 * NB,), in_specs=[whole(1, HD), ws...  147 us
    pallas_call x2, Pallas kernels, backward(): pl.pallas_call(functools.partial(backward_kernel, b), grid=(2, NB), in_sp...  96.4 us
    pallas_call x1, Pallas kernels, out_block(): pl.pallas_call(out_kernel, grid=(2,), in_specs=[batch, whole(DIM, DIM), b...  37.2 us
    unnamed x19, local copies, waits for them, and re-layouts  9.76 us

profile of v6, /device:TPU:0, one launch (start us, length us, event | category | flops | bytes accessed | tf_op | source)
XLA Modules:
  0.0 448.0 jit_solution(13943466427792911822)
XLA Ops:
  0.7 0.6 maximum_bitcast_fusion.freq_ref
  1.2 0.7 maximum_convert_fusion
  2.0 0.6 reshape.26.gains_ref
  2.6 147.0 %forward.1 = (f32[2048,128]{1,0:T(8,128)}, f32[2048,128]{1,0:T(8,128)}, f32[2,8,512]{2,1,0:T(8,128)}, bf16[2,2048,256]{2,1,0:T(8,128)(2,1)}, f32[2,8,512]{2,1,0:...) custom-call(f32[1,128]{1,0:T(1,128)} %maximum_bitcast_fusion.freq_re, ...), custom_call_target="tpu_custom_call" | custom-call | flops 60000002048 | bytes 60000000 | tf_op jit(solution)/shard_map/forward/pallas_call | solution.py:414
  149.5 37.2 %out_block.1 = (bf16[2,256,2048]{2,1,0:T(8,128)(2,1)}, bf16[2,256,2048]{2,1,0:T(8,128)(2,1)}, f32[8,256]{1,0:T(8,128)}, bf16[2,2048,256]{2,1,0:T(8,128)(2,1)}) custom-call(bf16[2,256,2048]{2,1,0:T(8,128)(2,1)} %get-tuple-element.38.o_ref, bf16[2048,2048]{1,0:T(8,128)(2,1)} %get-tuple-element.39.wo_ref, bf16[2,256,2048]{2,1,0:T(8,128)(2,1)} %x_ref.3, ...), custom_call_target="tpu_custom_call" | custom-call | flops 13589934080 | bytes 18000000 | tf_op jit(solution)/shard_map/out_block/pallas_call | solution.py:510
  186.7 48.6 %backward.2 = (bf16[2048,768]{1,0:T(8,128)(2,1)}, bf16[2048,768]{1,0:T(8,128)(2,1)}, f32[8,256]{1,0:T(8,128)}, f32[8,256]{1,0:T(8,128)}, bf16[2048,2048]{1,0:T(8,128)(2,1)}) custom-call(bf16[2,3,2048,256]{3,2,1,0:T(8,128)(2,1)} %get-tuple-element.41.qkv_ref, bf16[2,2048,256]{2,1,0:T(8,128)(2,1)} %get-tuple-element.42.do_ref, ...), custom_call_target="tpu_custom_call" | custom-call | flops 20000000000 | bytes 20000000 | tf_op jit(solution)/shard_map/backward/pallas_call | solution.py:650
  235.3 0.7 convert_bitcast_fusion
  236.0 0.6 copy.20
  236.6 0.0 copy-start.5
  236.6 47.8 %backward.3 = (bf16[2048,768]{1,0:T(8,128)(2,1)}, bf16[2048,768]{1,0:T(8,128)(2,1)}, f32[8,256]{1,0:T(8,128)}, f32[8,256]{1,0:T(8,128)}, bf16[2048,2048]{1,0:T(8,128)(2,1)}, /*index=5*/bf16[2048,2048]{1,0:T(8,128)(2,1)}) custom-call(bf16[2,3,2048,256]{3,2,1,0:T(8,128)(2,1)} %get-tuple-element.41.qkv_ref, ...), custom_call_target="tpu_custom_call", output_to_operand_aliasing={{5}: (10, {})} | custom-call | flops 20000000000 | bytes 20000000 | tf_op jit(solution)/shard_map/backward/pallas_call | solution.py:650
  284.5 0.0 copy-done.5
  284.5 0.7 add_convert_fusion
  285.2 0.5 slice_reduce_fusion
  285.7 153.2 %grads.1 = (bf16[2,256,2048]{2,1,0:T(8,128)(2,1)}, bf16[2048,256]{1,0:T(8,128)(2,1)}, bf16[2048,256]{1,0:T(8,128)(2,1)}, bf16[2048,256]{1,0:T(8,128)(2,1)}, bf16...) custom-call(bf16[2048,768]{1,0:T(8,128)(2,1)} %get-tuple-element.50.d0, ...), custom_call_target="tpu_custom_call", output_to_operand_aliasing={{5}: (10, {})} | custom-call | flops 99999997952 | bytes 40000000 | tf_op jit(solution)/shard_map/grads/pallas_call | solution.py:843
  438.9 0.0 copy-start
  438.9 3.3 copy.29
  442.2 0.0 copy-done
  442.2 0.0 copy-start.4
  442.2 0.0 copy-start.3
  442.2 1.3 copy.30
  443.5 0.6 copy-done.4
  444.1 0.0 copy-start.2
  444.1 0.0 copy-start.1
  444.1 1.0 copy.31
  445.1 0.0 copy-done.3
  445.1 1.0 copy.32
  446.1 0.0 copy-done.2
  446.1 1.0 copy.33
  447.1 0.0 copy-done.1
  447.1 1.0 copy.34
  (1 shorter events, 0.0 us)
Async XLA Ops:
  236.6 47.9 %copy-start.5 = (f32[8,256]{1,0:T(8,128)S(1)}, f32[8,256]{1,0:T(8,128)}, u32[]{:S(2)}) copy-start(f32[8,256]{1,0:T(8,128)} %get-tuple-element.64) | copy-start | bytes 24580
  438.9 3.3 copy-start
  442.2 2.0 copy-start.4
  442.2 2.9 copy-start.3
  444.1 1.9 copy-start.2
  444.1 2.9 copy-start.1

commit v7 on v6

--- a/solution.py
+++ b/solution.py
@@ -95,7 +95,7 @@
         wait(self.copies)
 
 
-def stage1(me, src, full, bg, part=None):
+def stage1(me, src, full, bg, part=None, fresh=False):
     send, recv, own, buf = bg
     lo, count, at = (0, TOK, 0) if part is None else (part * (TOK // 2), TOK // 2, 8 * part)
     there = full.at[shard_rows(me, lo, count), :]
@@ -103,7 +103,7 @@
     copies = [pltpu.make_async_remote_copy(
         src_ref=mine, dst_ref=there, send_sem=send.at[at + k], recv_sem=recv.at[at + k],
         device_id=(peer_of(me, mask),), device_id_type=MESH) for k, mask in enumerate((2, 4, 1))]
-    loads = [] if part == 1 else [pltpu.make_async_copy(src, buf.at[0], own.at[0])]
+    loads = [] if part == 1 and not fresh else [pltpu.make_async_copy(src, buf.at[0], own.at[0])]
     return Stage(loads, copies + [pltpu.make_async_copy(mine, there, own.at[3 if part == 1 else 2])])
 
 
@@ -126,6 +126,17 @@
     return Stage([pltpu.make_async_copy(rows, buf.at[1], own.at[1])], [pltpu.make_async_remote_copy(
         src_ref=buf.at[1], dst_ref=rows, send_sem=send.at[7], recv_sem=recv.at[7],
         device_id=(peer_of(me, 1),), device_id_type=MESH)])
+
+
+def route(me):
+    core = me % 2
+    first = peer_of(me, 2) * (1 - core) + peer_of(me, 4) * core
+    second = peer_of(me, 4) * (1 - core) + peer_of(me, 2) * core
+    return core, peer_of(me, 1), first, second
+
+
+def half_rows(c):
+    return pl.ds(pl.multiple_of(c * (DIM // 2), DIM // 2), DIM // 2)
 
 
 def start(copies):
@@ -521,25 +532,54 @@
     )(o, wo, x, dy, gains)
 
 
-def backward_kernel(b, qkv_ref, do_ref, lse_ref, raw_ref, inv_ref, gains_ref, cos_ref, sin_ref, gga_ref, shard_ref, *rest):
+def backward_kernel(b, qkv_ref, do_ref, lse_ref, raw_ref, inv_ref, gains_ref, cos_ref, sin_ref, gga_ref, shard_ref,
+                    wq_ref, wk_ref, wv_ref, *rest):
     if b:
-        _, d_ref, pd_ref, gg_ref, gout_ref, full_ref, old_ref, *rest = rest
+        (d0_ref, pd0_ref, pw_ref, _, _, d_ref, pd_ref, gg_ref, gout_ref, full_ref, old_ref, first_ref,
+         w_all, d_two, sbuf, *rest) = rest
     else:
-        d_ref, pd_ref, gg_ref, gout_ref, full_ref, *rest = rest
+        d_ref, pd_ref, gg_ref, gout_ref, full_ref, next_ref, pw_ref, *rest = rest
     (p_scr, dp_scr, kt_scr, dqt_scr, dq_scr, dk_scr, dv_scr, du_scr, d_scr, dots_scr, total, slot, ga_slot,
-     ex_send, ex_recv, pd_send, pd_recv, d_sems, *bg) = rest
+     ex_send, ex_recv, pd_send, pd_recv, d_sems, rs_sems, ld_sems, buf0, buf1, *bg_sems) = rest
     h, qi = pl.program_id(0), pl.program_id(1)
     me = lax.axis_index('tp')
-    gather = stage1(me, shard_ref.at[b], full_ref, bg)
+    core, partner, first_dev, _ = route(me)
+    bg0, bg1 = (*bg_sems[:3], buf0), (*bg_sems[3:], buf1)
+    weights = (wq_ref, wk_ref, wv_ref)
+
+    if b:
+        gather = stage1(me, shard_ref.at[1], full_ref, bg0, 1, True)
+        beside = [stage3(me, old_ref, bg1)]
+        diag_rows = block_rows(peer_of(me, 6) // 2)
+        operands = [pltpu.make_async_copy(d.at[diag_rows, :], d_two.at[n], ld_sems.at[n])
+                    for n, d in enumerate((d0_ref, pd0_ref))]
+        operands += [pltpu.make_async_copy(w.at[half_rows(core), :], w_all.at[0, :, pl.ds(n * LOC, LOC)], ld_sems.at[2 + n])
+                     for n, w in enumerate(weights)]
+        operands.append(pltpu.make_async_copy(pw_ref, w_all.at[1], ld_sems.at[5]))
+        moved = [pltpu.make_async_remote_copy(
+            src_ref=sbuf, dst_ref=first_ref, send_sem=rs_sems.at[0], recv_sem=rs_sems.at[1], device_id=(first_dev,),
+            device_id_type=MESH)]
+    else:
+        gather = stage1(me, shard_ref.at[0], full_ref, bg0)
+        beside = [stage1(me, shard_ref.at[1], next_ref, bg1, 0)]
+        moved = [pltpu.make_async_remote_copy(
+            src_ref=w.at[half_rows(1 - core), :], dst_ref=pw_ref.at[:, pl.ds(n * LOC, LOC)], send_sem=rs_sems.at[n],
+            recv_sem=rs_sems.at[3 + n], device_id=(partner,), device_id_type=MESH) for n, w in enumerate(weights)]
 
     @pl.when(jnp.logical_and(h == 0, qi == 0))
     def _():
-        stages = ([stage3(me, old_ref, bg)] if b else []) + [gather]
+        stages = [gather] + beside
         for stage in stages:
             stage.load()
+        if b:
+            start(operands)
         entry_barrier(me)
         for stage in stages:
             stage.send()
+        if b:
+            wait(operands)
+            sbuf[...] = dot(d_two[0], w_all[0], NT) + dot(d_two[1], w_all[1], NT)
+        start(moved)
         dots_scr[...] = jnp.zeros_like(dots_scr)
 
     @pl.when(qi == 0)
@@ -602,11 +642,11 @@
     @pl.when(jnp.logical_and(h == 1, qi == NB - 1))
     def _():
         gather.wait()
-        if b:
-            stage3(me, old_ref, bg).wait()
+        for stage in beside:
+            stage.wait()
         sums = exchange(me, [dots_scr, gga_ref], [slot, ga_slot], ex_send, ex_recv)
         start(sums)
-        more = stage2(me, full_ref, bg)
+        more = stage2(me, full_ref, bg0)
         more.load()
         more.send()
         wait(sums)
@@ -636,10 +676,11 @@
         lax.fori_loop(0, NB, last, 0)
         for i in range(NB):
             wait(copies(i))
+        wait(moved)
         more.wait()
 
 
-def backward(b, qkv, do, lse, raw, inv, gains, cos, sin, gga, shard, old, cid):
+def backward(b, qkv, do, lse, raw, inv, gains, cos, sin, gga, shard, weights, older, cid):
     def whole(*shape):
         return pl.BlockSpec(shape, lambda h, i: (0,) * len(shape))
 
@@ -647,42 +688,45 @@
         return pl.BlockSpec((None,) + shape, lambda h, i: (b,) + (0,) * len(shape))
 
     gsp = whole(8, DIM // 8)
+    half = (DIM // 2, 3 * LOC)
+    extra = [sds((BLK, DIM // 2), F32)] if b else [sds(half, BF)]
+    early = [pltpu.VMEM((2,) + half, BF), pltpu.VMEM((2, BLK, 3 * LOC), BF), pltpu.VMEM((BLK, DIM // 2), F32)] if b else []
     return pl.pallas_call(
         functools.partial(backward_kernel, b),
         grid=(2, NB),
         in_specs=[pl.BlockSpec((None, 3, SEQ, HD), lambda h, i: (b, 0, 0, h)), pl.BlockSpec((None, BLK, HD), lambda h, i: (b, i, h)),
                   picked(2 * NB, BLK), picked(2, SEQ, LOC), picked(2 * NB, BLK),
-                  pl.BlockSpec((2 + DIM // LOC, HD), lambda h, i: (0, h)), whole(SEQ, HD), whole(SEQ, HD), gsp, ANYWHERE]
-        + [ANYWHERE] * len(old),
-        out_specs=[ANYWHERE, ANYWHERE, pl.BlockSpec((8, HD), lambda h, i: (0, h)), gsp, ANYWHERE] + [ANYWHERE] * len(old),
+                  pl.BlockSpec((2 + DIM // LOC, HD), lambda h, i: (0, h)), whole(SEQ, HD), whole(SEQ, HD), gsp]
+        + [ANYWHERE] * (4 + len(older)),
+        out_specs=[ANYWHERE, ANYWHERE, pl.BlockSpec((8, HD), lambda h, i: (0, h)), gsp] + [ANYWHERE] * 3,
         out_shape=[sds((SEQ, 3 * LOC), BF), sds((SEQ, 3 * LOC), BF), sds((8, LOC), F32), sds((8, DIM // 8), F32),
-                   sds((SEQ, DIM), BF)] + [sds((SEQ, DIM), BF)] * len(old),
-        input_output_aliases={10: 5} if old else {},
-        scratch_shapes=[pltpu.VMEM((NB, BLK, BLK), F32), pltpu.VMEM((NB, BLK, BLK), F32), pltpu.VMEM((HD, SEQ), BF),
-                        pltpu.VMEM((HD, BLK), F32), pltpu.VMEM((SEQ, HD), F32), pltpu.VMEM((SEQ, HD), F32),
-                        pltpu.VMEM((SEQ, HD), F32), pltpu.VMEM((2, 2, SEQ, HD), F32), pltpu.VMEM((SEQ, 3 * LOC), BF),
-                        pltpu.VMEM((2 * NB, BLK), F32), pltpu.VMEM((2 * NB, BLK), F32),
-                        pltpu.VMEM((NDEV - 1, 2 * NB, BLK), F32), pltpu.VMEM((NDEV - 1, 8, DIM // 8), F32),
-                        DMA((2, NDEV - 1)), DMA((2, NDEV - 1)), DMA((NB,)), DMA((NB,)), DMA((NB,))] + BG,
+                   sds((SEQ, DIM), BF), sds((SEQ, DIM), BF)] + extra,
+        input_output_aliases={16: 4, 17: 5} if b else {},
+        scratch_shapes=early + [
+            pltpu.VMEM((NB, BLK, BLK), F32), pltpu.VMEM((NB, BLK, BLK), F32), pltpu.VMEM((HD, SEQ), BF),
+            pltpu.VMEM((HD, BLK), F32), pltpu.VMEM((SEQ, HD), F32), pltpu.VMEM((SEQ, HD), F32),
+            pltpu.VMEM((SEQ, HD), F32), pltpu.VMEM((2, 2, SEQ, HD), F32), pltpu.VMEM((SEQ, 3 * LOC), BF),
+            pltpu.VMEM((2 * NB, BLK), F32), pltpu.VMEM((2 * NB, BLK), F32),
+            pltpu.VMEM((NDEV - 1, 2 * NB, BLK), F32), pltpu.VMEM((NDEV - 1, 8, DIM // 8), F32),
+            DMA((2, NDEV - 1)), DMA((2, NDEV - 1)), DMA((NB,)), DMA((NB,)), DMA((NB,)), DMA((6,)), DMA((6,)),
+            pltpu.VMEM((2, TOK, DIM), BF), pltpu.VMEM((2, TOK, DIM), BF)] + BG_SEMS * 2,
         compiler_params=params(dimension_semantics=("arbitrary", "arbitrary"), collective_id=cid, has_side_effects=True),
         cost_estimate=cost(20e9, 20e6),
         name="backward",
-    )(qkv, do, lse, raw, inv, gains, cos, sin, gga, shard, *old)
+    )(qkv, do, lse, raw, inv, gains, cos, sin, gga, shard, *weights, *older)
 
 
 HALF = DIM // 2
 CH = 256
 
 
-def grads_kernel(d0, d1, pd0, pd1, wq, wk, wv, x_full, o_all, da0, da1_in, dy_ref, dx_ref, gwq_ref, gwk_ref, gwv_ref, gwo_ref, da1,
+def grads_kernel(d0, d1, pd0, pd1, wq, wk, wv, pw, got, x_full, o_all, da0, da1_in, dy_ref, dx_ref, gwq_ref, gwk_ref, gwv_ref, gwo_ref, da1,
                  d_all, w_all, sbuf, r1, r2, fin, acc, xbuf, obuf,
                  dl_sems, w_sems, s1_sems, r1_sems, s2_sems, r2_sems, fs_sems, fr_sems, x_sems, o_sems, *sems):
     del da1_in
     me = lax.axis_index('tp')
-    core, chip = me % 2, me // 2
-    partner = peer_of(me, 1)
-    first = peer_of(me, 2) * (1 - core) + peer_of(me, 4) * core
-    second = peer_of(me, 4) * (1 - core) + peer_of(me, 2) * core
+    core, partner, first, second = route(me)
+    chip = me // 2
     diag_chip, first_chip, second_chip = peer_of(me, 6) // 2, first // 2, second // 2
 
     barrier = pltpu.get_barrier_semaphore()
@@ -693,35 +737,18 @@
     def rows_of(blk):
         return pl.ds(pl.multiple_of(blk * BLK, BLK), BLK)
 
-    def half_rows(c):
-        return pl.ds(pl.multiple_of(c * HALF, HALF), HALF)
-
     chips = (diag_chip, first_chip, second_chip, chip)
-    w_copies = []
-    for n, w in enumerate((wq, wk, wv)):
-        part = pl.ds(n * LOC, LOC)
-        w_copies.append(pltpu.make_async_remote_copy(
-            src_ref=w.at[half_rows(1 - core), :], dst_ref=w_all.at[1, :, part], send_sem=w_sems.at[n],
-            recv_sem=w_sems.at[3 + n], device_id=(partner,), device_id_type=MESH))
-        w_copies.append(pltpu.make_async_copy(w.at[half_rows(core), :], w_all.at[0, :, part], w_sems.at[6 + n]))
+    w_copies = [pltpu.make_async_copy(w.at[half_rows(core), :], w_all.at[0, :, pl.ds(n * LOC, LOC)], w_sems.at[n])
+                for n, w in enumerate((wq, wk, wv))]
+    w_copies.append(pltpu.make_async_copy(pw, w_all.at[1], w_sems.at[3]))
+    loads = []
+    for n in range(8):
+        rows, b = rows_of(chips[n // 2]), n % 2
+        loads.append([pltpu.make_async_copy(d.at[rows, :], d_all.at[side, b, rows, :], dl_sems.at[side, n])
+                      for side, d in enumerate(((d0, d1)[b], (pd0, pd1)[b]))])
     start(w_copies)
-    loads = []
-    for kind in range(4):
-        for b in range(2):
-            n = 2 * kind + b
-            rows = rows_of(chips[kind])
-            for side, d in enumerate(((d0, d1)[b], (pd0, pd1)[b])):
-                loads.append(pltpu.make_async_copy(d.at[rows, :], d_all.at[side, b, rows, :], dl_sems.at[side, n]))
-    start(loads)
-    last_stage = stage3(me, da1, (*sems, xbuf))
-    last_stage.load()
-    last_stage.send()
+    start(loads[1])
     wait(w_copies)
-
-    def arrived(n, b, blk):
-        rows = rows_of(blk)
-        for side in range(2):
-            pltpu.make_async_copy(d0.at[rows, :], d_all.at[side, b, rows, :], dl_sems.at[side, n]).wait()
 
     def partial(b, blk):
         rows = rows_of(blk)
@@ -729,7 +756,7 @@
 
     def to_first(n):
         return pltpu.make_async_remote_copy(
-            src_ref=sbuf.at[n], dst_ref=r1.at[n], send_sem=s1_sems.at[n], recv_sem=r1_sems.at[n],
+            src_ref=sbuf.at[n - 1], dst_ref=r1.at[n], send_sem=s1_sems.at[n], recv_sem=r1_sems.at[n],
             device_id=(first,), device_id_type=MESH)
 
     def to_second(b):
@@ -742,17 +769,21 @@
             src_ref=r1.at[2 + b, pl.ds(pl.multiple_of((1 - core) * TOK, TOK), TOK), :], dst_ref=fin.at[b],
             send_sem=fs_sems.at[b], recv_sem=fr_sems.at[b], device_id=(partner,), device_id_type=MESH)
 
-    def phase1(n, carry):
-        kind, b = n // 2, n % 2
-        blk = diag_chip * (1 - kind) + first_chip * kind
-        arrived(n, b, blk)
-        sbuf[n] = partial(b, blk)
+    taken = pltpu.make_async_copy(got, r1.at[0], w_sems.at[4])
+    last_stage = stage3(me, da1, (*sems, xbuf))
+    for n in range(1, 4):
+        wait(loads[n])
+        if n == 1:
+            start(loads[2] + loads[3])
+        sbuf[n - 1] = partial(n % 2, chips[n // 2])
         to_first(n).start()
-        return carry
-
-    lax.fori_loop(0, 4, phase1, 0)
-    for n in range(4, 8):
-        arrived(n, n % 2, chips[n // 2])
+        if n == 1:
+            start([taken] + loads[0] + loads[4] + loads[5] + loads[6] + loads[7])
+            last_stage.load()
+            last_stage.send()
+    for n in (0, 4, 5, 6, 7):
+        wait(loads[n])
+    taken.wait()
 
     steps = SEQ // CH
 
@@ -788,20 +819,20 @@
 
         stream([(src, xbuf, x_sems)], body)
 
-    def forward_second(b, carry):
-        to_first(b).wait_recv()
+    def forward_second(b):
+        if b:
+            to_first(b).wait_recv()
         r1[b] += partial(b, second_chip)
         to_second(b).start()
-        return carry
-
+
+    forward_second(0)
     acc[...] = jnp.zeros_like(acc)
     last_stage.wait()
     wgrad(0, x_full.at[0])
-    forward_second(0, 0)
     wgrad(1, x_full.at[1])
     for n, ref in enumerate((gwq_ref, gwk_ref, gwv_ref)):
         ref[...] = acc[n * LOC:(n + 1) * LOC, :].T.astype(BF)
-    forward_second(1, 0)
+    forward_second(1)
     acc[:LOC, :] = jnp.zeros((LOC, DIM), F32)
 
     def wo_body(i):
@@ -829,25 +860,25 @@
         cols = half_rows(1 - core)
         dx_ref[b, :, cols] = (fin[b] + dy_ref[b, :, cols].astype(F32)).astype(BF)
         to_second(b).wait_send()
-        to_first(b).wait_send()
         to_first(2 + b).wait_send()
         return carry
 
+    to_first(1).wait_send()
     lax.fori_loop(0, 2, finish, 0)
 
 
-def grads(d0, d1, pd0, pd1, wq, wk, wv, x_full, o_all, da0, da1, dy, cid):
+def grads(d0, d1, pd0, pd1, wq, wk, wv, pw, got, x_full, o_all, da0, da1, dy, cid):
     vm = pl.BlockSpec(memory_space=pltpu.VMEM)
     far = pl.BlockSpec(memory_space=pl.ANY)
     dma = pltpu.SemaphoreType.DMA
     return pl.pallas_call(
         grads_kernel,
-        in_specs=[far] * 11 + [vm],
+        in_specs=[far] * 13 + [vm],
         out_specs=[vm] * 5 + [far],
         out_shape=[sds((2, TOK, DIM), BF)] + [sds((DIM, LOC), BF)] * 3 + [sds((LOC, DIM), BF), sds((SEQ, DIM), BF)],
-        input_output_aliases={10: 5},
+        input_output_aliases={12: 5},
         scratch_shapes=[pltpu.VMEM((2, 2, SEQ, 3 * LOC), BF), pltpu.VMEM((2, HALF, 3 * LOC), BF),
-                        pltpu.VMEM((4, BLK, HALF), F32), pltpu.VMEM((4, BLK, HALF), F32), pltpu.VMEM((2, BLK, HALF), F32),
+                        pltpu.VMEM((3, BLK, HALF), F32), pltpu.VMEM((4, BLK, HALF), F32), pltpu.VMEM((2, BLK, HALF), F32),
                         pltpu.VMEM((2, TOK, HALF), F32), pltpu.VMEM((3 * LOC, DIM), F32),
                         pltpu.VMEM((2, CH, DIM), BF), pltpu.VMEM((2, CH, LOC), BF),
                         dma((2, 8)), dma((9,)), dma((4,)), dma((4,)), dma((2,)), dma((2,)),
@@ -855,24 +886,20 @@
         compiler_params=pltpu.CompilerParams(vmem_limit_bytes=67043328, collective_id=cid, has_side_effects=True),
         cost_estimate=cost(100e9, 40e6),
         name="grads",
-    )(d0, d1, pd0, pd1, wq, wk, wv, x_full, o_all, da0, da1, dy)
+    )(d0, d1, pd0, pd1, wq, wk, wv, pw, got, x_full, o_all, da0, da1, dy)
 
 
 def local_block(x_loc, wq, wk, wv, wo, gq, gk, ga, dy_loc):
     gains = jnp.concatenate([gq, gk, ga]).astype(F32).reshape(2 + DIM // LOC, LOC)
     cos, sin, inv, o, lse, raw, qkv, o_recv, x_full, wo_full = forward(x_loc, wq, wk, wv, wo, gains, 0)
     y, da, gga, dh = out_block(o_recv, wo_full, x_loc, dy_loc, gains, 1)
-    ds, ggs, da_full = [], [], []
-    for b in range(2):
-        d, pd, gg, gout, full, *old = backward(b, qkv, dh, lse, raw, inv, gains, cos, sin, gga, da, da_full, 2 + b)
-        da_full = list(old) + [full]
-        ds.append((d, pd))
-        ggs.append(gg)
-        if b == 0:
-            grad_ga = gout.reshape(DIM).astype(BF)
-    dx, gwq, gwk, gwv, gwo, _ = grads(ds[0][0], ds[1][0], ds[0][1], ds[1][1], wq, wk, wv, x_full, o,
-                                      da_full[0], da_full[1], dy_loc, 4)
-    gg = ggs[0] + ggs[1]
+    weights = (wq, wk, wv)
+    state = (qkv, dh, lse, raw, inv, gains, cos, sin, gga, da, weights)
+    d0, pd0, gg0, gout, da0, da1, pw = backward(0, *state, (), 2)
+    d1, pd1, gg1, _, da1, da0, got = backward(1, *state, (d0, pd0, pw, da1, da0), 3)
+    grad_ga = gout.reshape(DIM).astype(BF)
+    dx, gwq, gwk, gwv, gwo, _ = grads(d0, d1, pd0, pd1, *weights, pw, got, x_full, o, da0, da1, dy_loc, 4)
+    gg = gg0 + gg1
     return (y, dx, gwq, gwk, gwv, gwo, gg[0].astype(BF), gg[1].astype(BF), grad_ga)
 
 

time: 449 us -> 442 us (0.984)
  Pallas kernels: 434 us -> 427 us
    pallas_call x1, Pallas kernels: 153 us -> 128 us  [grads(): pl.pallas_call(grads_kernel, in_specs=[far] * 13 + [vm], out_specs=[vm] *...]
    pallas_call x2, Pallas kernels: 96.4 us -> 115 us  [backward(): pl.pallas_call(functools.partial(backward_kernel, b), grid=(2, NB), in_sp...]
where the time goes in v7:
time: 442 us; the launch traced here: 441 us
  Pallas kernels  427 us (97%)
  local copies, waits for them, and re-layouts  10.8 us (2%)
    pallas_call x1, Pallas kernels, forward(): pl.pallas_call(forward_kernel, grid=(8 * NB,), in_specs=[whole(1, HD), ws...  147 us
    pallas_call x1, Pallas kernels, grads(): pl.pallas_call(grads_kernel, in_specs=[far] * 13 + [vm], out_specs=[vm] *...  128 us
    pallas_call x2, Pallas kernels, backward(): pl.pallas_call(functools.partial(backward_kernel, b), grid=(2, NB), in_sp...  115 us
    pallas_call x1, Pallas kernels, out_block(): pl.pallas_call(out_kernel, grid=(2,), in_specs=[batch, whole(DIM, DIM), b...  37.2 us
    unnamed x19, local copies, waits for them, and re-layouts  9.61 us

profile of v7, /device:TPU:0, one launch (start us, length us, event | category | flops | bytes accessed | tf_op | source)
XLA Modules:
  0.0 441.0 jit_solution(6544948741925746879)
XLA Ops:
  0.7 0.6 maximum_bitcast_fusion.freq_ref
  1.2 0.7 maximum_convert_fusion
  2.0 0.6 reshape.26.gains_ref
  2.6 146.9 %forward.1 = (f32[2048,128]{1,0:T(8,128)}, f32[2048,128]{1,0:T(8,128)}, f32[2,8,512]{2,1,0:T(8,128)}, bf16[2,2048,256]{2,1,0:T(8,128)(2,1)}, f32[2,8,512]{2,1,0:...) custom-call(f32[1,128]{1,0:T(1,128)} %maximum_bitcast_fusion.freq_re, ...), custom_call_target="tpu_custom_call" | custom-call | flops 60000002048 | bytes 60000000 | tf_op jit(solution)/shard_map/forward/pallas_call | solution.py:425
  149.5 37.2 %out_block.1 = (bf16[2,256,2048]{2,1,0:T(8,128)(2,1)}, bf16[2,256,2048]{2,1,0:T(8,128)(2,1)}, f32[8,256]{1,0:T(8,128)}, bf16[2,2048,256]{2,1,0:T(8,128)(2,1)}) custom-call(bf16[2,256,2048]{2,1,0:T(8,128)(2,1)} %get-tuple-element.41.o_ref, bf16[2048,2048]{1,0:T(8,128)(2,1)} %get-tuple-element.42.wo_ref, bf16[2,256,2048]{2,1,0:T(8,128)(2,1)} %x_ref.3, ...), custom_call_target="tpu_custom_call" | custom-call | flops 13589934080 | bytes 18000000 | tf_op jit(solution)/shard_map/out_block/pallas_call | solution.py:521
  186.7 58.9 %backward.2 = (bf16[2048,768]{1,0:T(8,128)(2,1)}, bf16[2048,768]{1,0:T(8,128)(2,1)}, f32[8,256]{1,0:T(8,128)}, f32[8,256]{1,0:T(8,128)}, bf16[2048,2048]{1,0:T(8...) custom-call(bf16[2,3,2048,256]{3,2,1,0:T(8,128)(2,1)} %get-tuple-element.44.qkv_ref, ...), custom_call_target="tpu_custom_call" | custom-call | flops 20000000000 | bytes 20000000 | tf_op jit(solution)/shard_map/backward/pallas_call | solution.py:694
  245.6 0.0 copy-start.5
  245.6 56.1 %backward.3 = (bf16[2048,768]{1,0:T(8,128)(2,1)}, bf16[2048,768]{1,0:T(8,128)(2,1)}, f32[8,256]{1,0:T(8,128)}, f32[8,256]{1,0:T(8,128)}, bf16[2048,2048]{1,0:T(8...) custom-call(bf16[2,3,2048,256]{3,2,1,0:T(8,128)(2,1)} %get-tuple-elem, ...), custom_call_target="tpu_custom_call", output_to_operand_aliasing={{4}: (16, {}), {5}: (17, {})} | custom-call | flops 20000000000 | bytes 20000000 | tf_op jit(solution)/shard_map/backward/pallas_call | solution.py:694
  301.7 0.0 copy-done.5
  301.7 0.7 add_convert_fusion
  302.4 0.5 slice_reduce_fusion
  303.0 127.6 %grads.1 = (bf16[2,256,2048]{2,1,0:T(8,128)(2,1)}, bf16[2048,256]{1,0:T(8,128)(2,1)}, bf16[2048,256]{1,0:T(8,128)(2,1)}, bf16[2048,256]{1,0:T(8,128)(2,1)}, bf16...) custom-call(bf16[2048,768]{1,0:T(8,128)(2,1)} %get-tuple-element.53.rest_0_.d0, ...), custom_call_target="tpu_custom_call", output_to_operand_aliasing={{5}: (12, {})} | custom-call | flops 99999997952 | bytes 40000000 | tf_op jit(solution)/shard_map/grads/pallas_call | solution.py:874
  430.5 0.0 copy-start
  430.5 0.8 convert_bitcast_fusion
  431.4 0.6 copy.21
  432.0 3.2 copy.31
  435.2 0.0 copy-done
  435.2 0.0 copy-start.4
  435.2 0.0 copy-start.3
  435.2 1.3 copy.32
  436.5 0.6 copy-done.4
  437.1 0.0 copy-start.2
  437.1 0.0 copy-start.1
  437.1 1.0 copy.33
  438.1 0.0 copy-done.3
  438.1 1.0 copy.34
  439.1 0.0 copy-done.2
  439.1 1.0 copy.35
  440.0 0.0 copy-done.1
  440.0 1.0 copy.36
  (1 shorter events, 0.0 us)
Async XLA Ops:
  245.6 56.2 %copy-start.5 = (f32[8,256]{1,0:T(8,128)S(1)}, f32[8,256]{1,0:T(8,128)}, u32[]{:S(2)}) copy-start(f32[8,256]{1,0:T(8,128)} %get-tuple-element.70) | copy-start | bytes 24580
  430.5 4.6 %copy-start = (bf16[2,256,2048]{2,1,0:T(8,128)(2,1)S(1)}, bf16[2,256,2048]{2,1,0:T(8,128)(2,1)}, u32[]{:S(2)}) copy-start(bf16[2,256,2048]{2,1,0:T(8,128)(2,1)} %get-tuple-element.85) | copy-start | bytes 6291460
  435.2 2.0 copy-start.4
  435.2 2.9 copy-start.3
  437.1 1.9 copy-start.2
  437.1 2.9 copy-start.1

commit v8 on v7

--- a/solution.py
+++ b/solution.py
@@ -3,6 +3,7 @@
 
 import jax
 import jax.numpy as jnp
+import numpy as np
 from jax import lax
 from jax.experimental import pallas as pl
 from jax.experimental.pallas import tpu as pltpu
@@ -63,11 +64,13 @@
     pl.semaphore_wait(barrier, NDEV - 1)
 
 
-def nbr_barrier(me):
-    barrier = pltpu.get_barrier_semaphore()
+def nbr_signal(me):
     for mask in (1, 2, 4):
-        pl.semaphore_signal(barrier, inc=1, device_id=(peer_of(me, mask),), device_id_type=MESH)
-    pl.semaphore_wait(barrier, 3)
+        pl.semaphore_signal(pltpu.get_barrier_semaphore(), inc=1, device_id=(peer_of(me, mask),), device_id_type=MESH)
+
+
+def nbr_wait():
+    pl.semaphore_wait(pltpu.get_barrier_semaphore(), 3)
 
 
 DMA = pltpu.SemaphoreType.DMA
@@ -95,7 +98,7 @@
         wait(self.copies)
 
 
-def stage1(me, src, full, bg, part=None, fresh=False):
+def stage1(me, src, full, bg, part=None):
     send, recv, own, buf = bg
     lo, count, at = (0, TOK, 0) if part is None else (part * (TOK // 2), TOK // 2, 8 * part)
     there = full.at[shard_rows(me, lo, count), :]
@@ -103,7 +106,7 @@
     copies = [pltpu.make_async_remote_copy(
         src_ref=mine, dst_ref=there, send_sem=send.at[at + k], recv_sem=recv.at[at + k],
         device_id=(peer_of(me, mask),), device_id_type=MESH) for k, mask in enumerate((2, 4, 1))]
-    loads = [] if part == 1 and not fresh else [pltpu.make_async_copy(src, buf.at[0], own.at[0])]
+    loads = [] if part == 1 or src is None else [pltpu.make_async_copy(src, buf.at[0], own.at[0])]
     return Stage(loads, copies + [pltpu.make_async_copy(mine, there, own.at[3 if part == 1 else 2])])
 
 
@@ -411,9 +414,8 @@
 
 
 def forward(x, wq, wk, wv, wo, gains, cid):
-    half = HD // 2
-    inv_freq = 1.0 / (ROPE_THETA ** (jnp.arange(half, dtype=F32) / half))
-    freq = jnp.concatenate([inv_freq, inv_freq])[None, :]
+    inv_freq = np.float32(1.0) / np.float32(ROPE_THETA) ** (np.arange(HD // 2, dtype=np.float32) / np.float32(HD // 2))
+    freq = jnp.asarray(np.concatenate([inv_freq, inv_freq])[None, :], F32)
 
     def whole(*shape):
         return pl.BlockSpec(shape, lambda g: (0,) * len(shape))
@@ -442,22 +444,29 @@
     )(freq, wq, wk, wv, gains, x, wo)
 
 
-def out_kernel(o_ref, wo_ref, x_ref, dy_ref, gains_ref, y_ref, da_ref, gga_ref, both_ref, a_scr, dh_scr, send_sems, recv_sems,
-               own_sems):
+def out_kernel(o_ref, x_ref, dy_ref, gains_ref, wo_ref, y_ref, da_ref, gga_ref, full_ref, wo_scr, a_scr, wo_sems, buf, *bg_sems):
     b = pl.program_id(0)
     me = lax.axis_index('tp')
+    bg = (*bg_sems, buf)
+    step = DIM // NB
+
+    def piece(j):
+        cols = pl.ds(pl.multiple_of(j * step, step), step)
+        return cols, pltpu.make_async_copy(wo_ref.at[:, cols], wo_scr.at[:, cols], wo_sems.at[j])
 
     @pl.when(b == 0)
     def _():
-        entry_barrier(me)
+        nbr_signal(me)
+        for j in range(NB):
+            piece(j)[1].start()
         gga_ref[...] = jnp.zeros_like(gga_ref)
 
-    step = DIM // NB
     o = o_ref[0]
 
     def fwd(j, carry):
-        cols = pl.ds(pl.multiple_of(j * step, step), step)
-        a_scr[:, cols] = dot(o, wo_ref[:, cols])
+        cols, load = piece(j)
+        pl.when(b == 0)(load.wait)
+        a_scr[:, cols] = dot(o, wo_scr[:, cols])
         return carry
 
     lax.fori_loop(0, NB, fwd, 0)
@@ -466,51 +475,28 @@
     n = a * r
     ga = jnp.concatenate([gains_ref[2 + i:3 + i, :] for i in range(8)], axis=1)
     dy = dy_ref[0].astype(F32)
+    gn = dy * ga
+    da = (r * (gn - n * jnp.mean(gn * n, axis=-1, keepdims=True))).astype(BF)
+    da_ref[0] = da
+
+    @pl.when(b == 0)
+    def _():
+        buf[0] = da
+        nbr_wait()
+        stage1(me, None, full_ref, bg).send()
+
     y_ref[0] = (x_ref[0].astype(F32) + n * ga).astype(BF)
     col = jnp.sum(dy * n, axis=0, keepdims=True)
     for i in range(8):
         gga_ref[i:i + 1, :] += col[:, i * LOC:(i + 1) * LOC]
-    gn = dy * ga
-    da_ref[0] = (r * (gn - n * jnp.mean(gn * n, axis=-1, keepdims=True))).astype(BF)
-    da = da_ref[0]
-
-    def block_copy(bb, st, half):
-        dest = 2 * ((me // 2 + 1 + st) % NB) + half
-        src = dh_scr.at[bb, st, :, pl.ds(half * LOC, LOC)]
-        mine = both_ref.at[bb, shard_rows(me), :]
-        away = pltpu.make_async_remote_copy(
-            src_ref=src, dst_ref=mine, send_sem=send_sems.at[bb, st, half], recv_sem=recv_sems.at[bb, me],
-            device_id=(dest,), device_id_type=MESH)
-        return dest, away, pltpu.make_async_copy(src, mine, own_sems.at[bb])
-
-    def bwd(st, carry):
-        blk = (me // 2 + 1 + st) % NB
-        dh_scr[b, st] = dot(da, wo_ref[pl.ds(pl.multiple_of(blk * step, step), step), :], NT).astype(BF)
-        for half in range(2):
-            dest, away, here = block_copy(b, st, half)
-            pl.when(dest != me)(away.start)
-            pl.when(dest == me)(here.start)
-        return carry
-
-    lax.fori_loop(0, NB, bwd, 0)
 
     @pl.when(b == 1)
     def _():
-        for bb in range(2):
-            for st in range(NB):
-                for half in range(2):
-                    dest, away, here = block_copy(bb, st, half)
-                    if st < NB - 1:
-                        away.wait_send()
-                    else:
-                        pl.when(dest != me)(away.wait_send)
-                        pl.when(dest == me)(here.wait)
-            for mask in ORDER:
-                peer = peer_of(me, mask)
-                pltpu.make_async_remote_copy(
-                    src_ref=dh_scr.at[0, 0, :, pl.ds(0, LOC)], dst_ref=both_ref.at[bb, shard_rows(peer), :],
-                    send_sem=send_sems.at[0, 0, 0], recv_sem=recv_sems.at[bb, peer], device_id=(peer,),
-                    device_id_type=MESH).wait_recv()
+        stage1(me, None, full_ref, bg).wait()
+        for stage in (stage2(me, full_ref, bg), stage3(me, full_ref, bg)):
+            stage.load()
+            stage.send()
+            stage.wait()
 
 
 def out_block(o, wo, x, dy, gains, cid):
@@ -521,66 +507,76 @@
     return pl.pallas_call(
         out_kernel,
         grid=(2,),
-        in_specs=[batch, whole(DIM, DIM), batch, batch, whole(2 + DIM // LOC, LOC)],
+        in_specs=[batch, batch, batch, whole(2 + DIM // LOC, LOC), ANYWHERE],
         out_specs=[batch, batch, whole(8, DIM // 8), ANYWHERE],
-        out_shape=[sds((2, TOK, DIM), BF), sds((2, TOK, DIM), BF), sds((8, DIM // 8), F32), sds((2, SEQ, LOC), BF)],
-        scratch_shapes=[pltpu.VMEM((TOK, DIM), F32), pltpu.VMEM((2, NB, TOK, DIM // NB), BF), DMA((2, NB, 2)),
-                        DMA((2, NDEV)), DMA((2,))],
+        out_shape=[sds((2, TOK, DIM), BF), sds((2, TOK, DIM), BF), sds((8, DIM // 8), F32), sds((SEQ, DIM), BF)],
+        scratch_shapes=[pltpu.VMEM((DIM, DIM), BF), pltpu.VMEM((TOK, DIM), F32), DMA((NB,)),
+                        pltpu.VMEM((2, TOK, DIM), BF)] + BG_SEMS,
         compiler_params=params(dimension_semantics=("arbitrary",), collective_id=cid, has_side_effects=True),
         cost_estimate=cost(8 * TOK * DIM * DIM + 5e9, 18e6),
         name="out_block",
-    )(o, wo, x, dy, gains)
-
-
-def backward_kernel(b, qkv_ref, do_ref, lse_ref, raw_ref, inv_ref, gains_ref, cos_ref, sin_ref, gga_ref, shard_ref,
+    )(o, x, dy, gains, wo)
+
+
+def backward_kernel(b, qkv_ref, da_ref, wo_ref, lse_ref, raw_ref, inv_ref, gains_ref, cos_ref, sin_ref, gga_ref,
                     wq_ref, wk_ref, wv_ref, *rest):
     if b:
-        (d0_ref, pd0_ref, pw_ref, _, _, d_ref, pd_ref, gg_ref, gout_ref, full_ref, old_ref, first_ref,
-         w_all, d_two, sbuf, *rest) = rest
+        d0_ref, pd0_ref, pw_ref, d_ref, pd_ref, gg_ref, gout_ref, got_ref, w_all, d_two, sbuf, *rest = rest
     else:
-        d_ref, pd_ref, gg_ref, gout_ref, full_ref, next_ref, pw_ref, *rest = rest
-    (p_scr, dp_scr, kt_scr, dqt_scr, dq_scr, dk_scr, dv_scr, du_scr, d_scr, dots_scr, total, slot, ga_slot,
-     ex_send, ex_recv, pd_send, pd_recv, d_sems, rs_sems, ld_sems, buf0, buf1, *bg_sems) = rest
+        shard_ref, d_ref, pd_ref, gg_ref, gout_ref, full_ref, pw_ref, buf, *rest = rest
+    (p_scr, dp_scr, kt_scr, dqt_scr, dq_scr, dk_scr, dv_scr, du_scr, d_scr, dh_scr, dots_scr, total, slot, ga_slot,
+     ex_send, ex_recv, pd_send, pd_recv, d_sems, rs_sems, ld_sems, *bg_sems) = rest
     h, qi = pl.program_id(0), pl.program_id(1)
     me = lax.axis_index('tp')
     core, partner, first_dev, _ = route(me)
-    bg0, bg1 = (*bg_sems[:3], buf0), (*bg_sems[3:], buf1)
     weights = (wq_ref, wk_ref, wv_ref)
 
     if b:
-        gather = stage1(me, shard_ref.at[1], full_ref, bg0, 1, True)
-        beside = [stage3(me, old_ref, bg1)]
-        diag_rows = block_rows(peer_of(me, 6) // 2)
-        operands = [pltpu.make_async_copy(d.at[diag_rows, :], d_two.at[n], ld_sems.at[n])
-                    for n, d in enumerate((d0_ref, pd0_ref))]
-        operands += [pltpu.make_async_copy(w.at[half_rows(core), :], w_all.at[0, :, pl.ds(n * LOC, LOC)], ld_sems.at[2 + n])
+        operands = []
+        for blk, chip in enumerate((peer_of(me, 6) // 2, first_dev // 2)):
+            operands += [pltpu.make_async_copy(d.at[block_rows(chip), :], d_two.at[blk, n], ld_sems.at[2 * blk + n])
+                         for n, d in enumerate((d0_ref, pd0_ref))]
+        operands += [pltpu.make_async_copy(w.at[half_rows(core), :], w_all.at[0, :, pl.ds(n * LOC, LOC)], ld_sems.at[4 + n])
                      for n, w in enumerate(weights)]
-        operands.append(pltpu.make_async_copy(pw_ref, w_all.at[1], ld_sems.at[5]))
+        operands.append(pltpu.make_async_copy(pw_ref, w_all.at[1], ld_sems.at[7]))
         moved = [pltpu.make_async_remote_copy(
-            src_ref=sbuf, dst_ref=first_ref, send_sem=rs_sems.at[0], recv_sem=rs_sems.at[1], device_id=(first_dev,),
-            device_id_type=MESH)]
+            src_ref=sbuf.at[blk, pl.ds(lo, count), :], dst_ref=got_ref.at[blk, pl.ds(lo, count), :], send_sem=rs_sems.at[n],
+            recv_sem=rs_sems.at[3 + n], device_id=(first_dev,), device_id_type=MESH)
+            for n, (blk, lo, count) in enumerate(((0, 0, BLK), (1, 0, BLK // 2), (1, BLK // 2, BLK // 2)))]
     else:
-        gather = stage1(me, shard_ref.at[0], full_ref, bg0)
-        beside = [stage1(me, shard_ref.at[1], next_ref, bg1, 0)]
+        bg = (*bg_sems, buf)
+        gather = stage1(me, shard_ref.at[1], full_ref, bg)
         moved = [pltpu.make_async_remote_copy(
             src_ref=w.at[half_rows(1 - core), :], dst_ref=pw_ref.at[:, pl.ds(n * LOC, LOC)], send_sem=rs_sems.at[n],
             recv_sem=rs_sems.at[3 + n], device_id=(partner,), device_id_type=MESH) for n, w in enumerate(weights)]
 
     @pl.when(jnp.logical_and(h == 0, qi == 0))
     def _():
-        stages = [gather] + beside
-        for stage in stages:
-            stage.load()
         if b:
             start(operands)
-        entry_barrier(me)
-        for stage in stages:
-            stage.send()
-        if b:
+            entry_barrier(me)
             wait(operands)
-            sbuf[...] = dot(d_two[0], w_all[0], NT) + dot(d_two[1], w_all[1], NT)
-        start(moved)
+            for blk in range(2):
+                sbuf[blk] = dot(d_two[blk, 0], w_all[0], NT) + dot(d_two[blk, 1], w_all[1], NT)
+                moved[blk].start()
+        else:
+            gather.load()
+            entry_barrier(me)
+            gather.send()
+            start(moved)
         dots_scr[...] = jnp.zeros_like(dots_scr)
+
+    if not b:
+        @pl.when(jnp.logical_and(h == 1, qi == 1))
+        def _():
+            gather.wait()
+            more = stage2(me, full_ref, bg)
+            more.load()
+            more.send()
+
+    @pl.when(h == 0)
+    def _():
+        dh_scr[block_rows(qi), :] = dot(da_ref[...], wo_ref[...], NT).astype(BF)
 
     @pl.when(qi == 0)
     def _():
@@ -589,7 +585,7 @@
         dv_scr[...] = jnp.zeros_like(dv_scr)
 
     qb = qkv_ref[0, block_rows(qi), :]
-    dob = do_ref[...]
+    dob = dh_scr[block_rows(qi), head_cols(h)]
     lse = lse_ref[pl.ds(h * NB + qi, 1), :]
 
     def first(j, acc, diag=False):
@@ -641,15 +637,16 @@
 
     @pl.when(jnp.logical_and(h == 1, qi == NB - 1))
     def _():
-        gather.wait()
-        for stage in beside:
-            stage.wait()
         sums = exchange(me, [dots_scr, gga_ref], [slot, ga_slot], ex_send, ex_recv)
         start(sums)
-        more = stage2(me, full_ref, bg0)
-        more.load()
-        more.send()
+        if b:
+            moved[2].start()
         wait(sums)
+        if not b:
+            stage2(me, full_ref, bg).wait()
+            last_stage = stage3(me, full_ref, bg)
+            last_stage.load()
+            last_stage.send()
         total[...] = ordered_total(me, dots_scr, slot) / DIM
         gout_ref[...] = ordered_total(me, gga_ref, ga_slot)
 
@@ -677,10 +674,11 @@
         for i in range(NB):
             wait(copies(i))
         wait(moved)
-        more.wait()
-
-
-def backward(b, qkv, do, lse, raw, inv, gains, cos, sin, gga, shard, weights, older, cid):
+        if not b:
+            last_stage.wait()
+
+
+def backward(b, da, qkv, wo, lse, raw, inv, gains, cos, sin, gga, weights, others, cid):
     def whole(*shape):
         return pl.BlockSpec(shape, lambda h, i: (0,) * len(shape))
 
@@ -689,41 +687,43 @@
 
     gsp = whole(8, DIM // 8)
     half = (DIM // 2, 3 * LOC)
-    extra = [sds((BLK, DIM // 2), F32)] if b else [sds(half, BF)]
-    early = [pltpu.VMEM((2,) + half, BF), pltpu.VMEM((2, BLK, 3 * LOC), BF), pltpu.VMEM((BLK, DIM // 2), F32)] if b else []
+    if b:
+        extra = [sds((2, BLK, DIM // 2), F32)]
+        own = [pltpu.VMEM((2,) + half, BF), pltpu.VMEM((2, 2, BLK, 3 * LOC), BF), pltpu.VMEM((2, BLK, DIM // 2), F32)]
+    else:
+        extra = [sds((SEQ, DIM), BF), sds(half, BF)]
+        own = [pltpu.VMEM((2, TOK, DIM), BF)]
     return pl.pallas_call(
         functools.partial(backward_kernel, b),
         grid=(2, NB),
-        in_specs=[pl.BlockSpec((None, 3, SEQ, HD), lambda h, i: (b, 0, 0, h)), pl.BlockSpec((None, BLK, HD), lambda h, i: (b, i, h)),
+        in_specs=[pl.BlockSpec((None, 3, SEQ, HD), lambda h, i: (b, 0, 0, h)),
+                  pl.BlockSpec((BLK, DIM), lambda h, i: (jnp.where(h == 0, i, NB - 1), 0)), whole(LOC, DIM),
                   picked(2 * NB, BLK), picked(2, SEQ, LOC), picked(2 * NB, BLK),
                   pl.BlockSpec((2 + DIM // LOC, HD), lambda h, i: (0, h)), whole(SEQ, HD), whole(SEQ, HD), gsp]
-        + [ANYWHERE] * (4 + len(older)),
-        out_specs=[ANYWHERE, ANYWHERE, pl.BlockSpec((8, HD), lambda h, i: (0, h)), gsp] + [ANYWHERE] * 3,
-        out_shape=[sds((SEQ, 3 * LOC), BF), sds((SEQ, 3 * LOC), BF), sds((8, LOC), F32), sds((8, DIM // 8), F32),
-                   sds((SEQ, DIM), BF), sds((SEQ, DIM), BF)] + extra,
-        input_output_aliases={16: 4, 17: 5} if b else {},
-        scratch_shapes=early + [
+        + [ANYWHERE] * (3 + len(others)),
+        out_specs=[ANYWHERE, ANYWHERE, pl.BlockSpec((8, HD), lambda h, i: (0, h)), gsp] + [ANYWHERE] * len(extra),
+        out_shape=[sds((SEQ, 3 * LOC), BF), sds((SEQ, 3 * LOC), BF), sds((8, LOC), F32), sds((8, DIM // 8), F32)] + extra,
+        scratch_shapes=own + [
             pltpu.VMEM((NB, BLK, BLK), F32), pltpu.VMEM((NB, BLK, BLK), F32), pltpu.VMEM((HD, SEQ), BF),
             pltpu.VMEM((HD, BLK), F32), pltpu.VMEM((SEQ, HD), F32), pltpu.VMEM((SEQ, HD), F32),
             pltpu.VMEM((SEQ, HD), F32), pltpu.VMEM((2, 2, SEQ, HD), F32), pltpu.VMEM((SEQ, 3 * LOC), BF),
-            pltpu.VMEM((2 * NB, BLK), F32), pltpu.VMEM((2 * NB, BLK), F32),
+            pltpu.VMEM((SEQ, LOC), BF), pltpu.VMEM((2 * NB, BLK), F32), pltpu.VMEM((2 * NB, BLK), F32),
             pltpu.VMEM((NDEV - 1, 2 * NB, BLK), F32), pltpu.VMEM((NDEV - 1, 8, DIM // 8), F32),
-            DMA((2, NDEV - 1)), DMA((2, NDEV - 1)), DMA((NB,)), DMA((NB,)), DMA((NB,)), DMA((6,)), DMA((6,)),
-            pltpu.VMEM((2, TOK, DIM), BF), pltpu.VMEM((2, TOK, DIM), BF)] + BG_SEMS * 2,
+            DMA((2, NDEV - 1)), DMA((2, NDEV - 1)), DMA((NB,)), DMA((NB,)), DMA((NB,)), DMA((6,)), DMA((8,))]
+        + ([] if b else BG_SEMS),
         compiler_params=params(dimension_semantics=("arbitrary", "arbitrary"), collective_id=cid, has_side_effects=True),
-        cost_estimate=cost(20e9, 20e6),
+        cost_estimate=cost(25e9, 30e6),
         name="backward",
-    )(qkv, do, lse, raw, inv, gains, cos, sin, gga, shard, *weights, *older)
+    )(qkv, da, wo, lse, raw, inv, gains, cos, sin, gga, *weights, *others)
 
 
 HALF = DIM // 2
 CH = 256
 
 
-def grads_kernel(d0, d1, pd0, pd1, wq, wk, wv, pw, got, x_full, o_all, da0, da1_in, dy_ref, dx_ref, gwq_ref, gwk_ref, gwv_ref, gwo_ref, da1,
+def grads_kernel(d0, d1, pd0, pd1, wq, wk, wv, pw, got, x_full, o_all, da0, da1, dy_ref, dx_ref, gwq_ref, gwk_ref, gwv_ref, gwo_ref,
                  d_all, w_all, sbuf, r1, r2, fin, acc, xbuf, obuf,
-                 dl_sems, w_sems, s1_sems, r1_sems, s2_sems, r2_sems, fs_sems, fr_sems, x_sems, o_sems, *sems):
-    del da1_in
+                 dl_sems, w_sems, s1_sems, r1_sems, s2_sems, r2_sems, fs_sems, fr_sems, x_sems, o_sems):
     me = lax.axis_index('tp')
     core, partner, first, second = route(me)
     chip = me // 2
@@ -756,7 +756,7 @@
 
     def to_first(n):
         return pltpu.make_async_remote_copy(
-            src_ref=sbuf.at[n - 1], dst_ref=r1.at[n], send_sem=s1_sems.at[n], recv_sem=r1_sems.at[n],
+            src_ref=sbuf.at[n // 2], dst_ref=r1.at[n], send_sem=s1_sems.at[n], recv_sem=r1_sems.at[n],
             device_id=(first,), device_id_type=MESH)
 
     def to_second(b):
@@ -769,21 +769,20 @@
             src_ref=r1.at[2 + b, pl.ds(pl.multiple_of((1 - core) * TOK, TOK), TOK), :], dst_ref=fin.at[b],
             send_sem=fs_sems.at[b], recv_sem=fr_sems.at[b], device_id=(partner,), device_id_type=MESH)
 
-    taken = pltpu.make_async_copy(got, r1.at[0], w_sems.at[4])
-    last_stage = stage3(me, da1, (*sems, xbuf))
-    for n in range(1, 4):
+    taken = [pltpu.make_async_copy(got.at[n], r1.at[2 * n], w_sems.at[4 + n]) for n in range(2)]
+    for n in (1, 3):
         wait(loads[n])
         if n == 1:
-            start(loads[2] + loads[3])
-        sbuf[n - 1] = partial(n % 2, chips[n // 2])
+            start(loads[3])
+        sbuf[n // 2] = partial(1, chips[n // 2])
         to_first(n).start()
         if n == 1:
-            start([taken] + loads[0] + loads[4] + loads[5] + loads[6] + loads[7])
-            last_stage.load()
-            last_stage.send()
-    for n in (0, 4, 5, 6, 7):
+            start(taken)
+            for later in (4, 0, 2, 5, 6, 7):
+                start(loads[later])
+    for n in (0, 2, 4, 5, 6, 7):
         wait(loads[n])
-    taken.wait()
+    wait(taken)
 
     steps = SEQ // CH
 
@@ -827,7 +826,6 @@
 
     forward_second(0)
     acc[...] = jnp.zeros_like(acc)
-    last_stage.wait()
     wgrad(0, x_full.at[0])
     wgrad(1, x_full.at[1])
     for n, ref in enumerate((gwq_ref, gwk_ref, gwv_ref)):
@@ -844,7 +842,7 @@
 
     def own_part(b, carry):
         r1_own = partial(b, chip)
-        to_first(2 + b).wait_recv()
+        pl.when(b == 1)(to_first(3).wait_recv)
         to_second(b).wait_recv()
         r1[2 + b] += r1_own + r2[b]
         to_partner(b).start()
@@ -860,10 +858,10 @@
         cols = half_rows(1 - core)
         dx_ref[b, :, cols] = (fin[b] + dy_ref[b, :, cols].astype(F32)).astype(BF)
         to_second(b).wait_send()
-        to_first(2 + b).wait_send()
         return carry
 
     to_first(1).wait_send()
+    to_first(3).wait_send()
     lax.fori_loop(0, 2, finish, 0)
 
 
@@ -874,31 +872,56 @@
     return pl.pallas_call(
         grads_kernel,
         in_specs=[far] * 13 + [vm],
-        out_specs=[vm] * 5 + [far],
-        out_shape=[sds((2, TOK, DIM), BF)] + [sds((DIM, LOC), BF)] * 3 + [sds((LOC, DIM), BF), sds((SEQ, DIM), BF)],
-        input_output_aliases={12: 5},
+        out_specs=[vm] * 5,
+        out_shape=[sds((2, TOK, DIM), BF)] + [sds((DIM, LOC), BF)] * 3 + [sds((LOC, DIM), BF)],
         scratch_shapes=[pltpu.VMEM((2, 2, SEQ, 3 * LOC), BF), pltpu.VMEM((2, HALF, 3 * LOC), BF),
-                        pltpu.VMEM((3, BLK, HALF), F32), pltpu.VMEM((4, BLK, HALF), F32), pltpu.VMEM((2, BLK, HALF), F32),
+                        pltpu.VMEM((2, BLK, HALF), F32), pltpu.VMEM((4, BLK, HALF), F32), pltpu.VMEM((2, BLK, HALF), F32),
                         pltpu.VMEM((2, TOK, HALF), F32), pltpu.VMEM((3 * LOC, DIM), F32),
                         pltpu.VMEM((2, CH, DIM), BF), pltpu.VMEM((2, CH, LOC), BF),
                         dma((2, 8)), dma((9,)), dma((4,)), dma((4,)), dma((2,)), dma((2,)),
-                        dma((2,)), dma((2,)), dma((2,)), dma((2,))] + BG_SEMS,
+                        dma((2,)), dma((2,)), dma((2,)), dma((2,))],
         compiler_params=pltpu.CompilerParams(vmem_limit_bytes=67043328, collective_id=cid, has_side_effects=True),
         cost_estimate=cost(100e9, 40e6),
         name="grads",
     )(d0, d1, pd0, pd1, wq, wk, wv, pw, got, x_full, o_all, da0, da1, dy)
 
 
+def deliver_kernel(*refs):
+    count = (len(refs) - 2) // 3
+    srcs, dsts, bufs = refs[:count], refs[count:2 * count], refs[2 * count:3 * count]
+    loads = [pltpu.make_async_copy(src, buf, refs[-2].at[n]) for n, (src, buf) in enumerate(zip(srcs, bufs))]
+    stores = [pltpu.make_async_copy(buf, dst, refs[-1].at[n]) for n, (buf, dst) in enumerate(zip(bufs, dsts))]
+    start(loads)
+    for load, store in zip(loads, stores):
+        load.wait()
+        store.start()
+    wait(stores)
+
+
+def deliver(*arrays):
+    return pl.pallas_call(
+        deliver_kernel,
+        in_specs=[ANYWHERE] * len(arrays),
+        out_specs=[ANYWHERE] * len(arrays),
+        out_shape=[sds(t.shape, t.dtype) for t in arrays],
+        scratch_shapes=[pltpu.VMEM(t.shape, t.dtype) for t in arrays] + [DMA((len(arrays),)), DMA((len(arrays),))],
+        compiler_params=params(),
+        cost_estimate=cost(1e9, 16e6),
+        name="deliver",
+    )(*arrays)
+
+
 def local_block(x_loc, wq, wk, wv, wo, gq, gk, ga, dy_loc):
     gains = jnp.concatenate([gq, gk, ga]).astype(F32).reshape(2 + DIM // LOC, LOC)
+    weights = (wq, wk, wv)
     cos, sin, inv, o, lse, raw, qkv, o_recv, x_full, wo_full = forward(x_loc, wq, wk, wv, wo, gains, 0)
-    y, da, gga, dh = out_block(o_recv, wo_full, x_loc, dy_loc, gains, 1)
-    weights = (wq, wk, wv)
-    state = (qkv, dh, lse, raw, inv, gains, cos, sin, gga, da, weights)
-    d0, pd0, gg0, gout, da0, da1, pw = backward(0, *state, (), 2)
-    d1, pd1, gg1, _, da1, da0, got = backward(1, *state, (d0, pd0, pw, da1, da0), 3)
+    y, da, gga, da0 = out_block(o_recv, wo_full, x_loc, dy_loc, gains, 1)
+    state = (qkv, wo, lse, raw, inv, gains, cos, sin, gga, weights)
+    d0, pd0, gg0, gout, da1, pw = backward(0, da0, *state, (da,), 2)
+    d1, pd1, gg1, _, got = backward(1, da1, *state, (d0, pd0, pw), 3)
     grad_ga = gout.reshape(DIM).astype(BF)
-    dx, gwq, gwk, gwv, gwo, _ = grads(d0, d1, pd0, pd1, *weights, pw, got, x_full, o, da0, da1, dy_loc, 4)
+    big = grads(d0, d1, pd0, pd1, *weights, pw, got, x_full, o, da0, da1, dy_loc, 4)
+    y, dx, gwq, gwk, gwv, gwo = deliver(y, *big)
     gg = gg0 + gg1
     return (y, dx, gwq, gwk, gwv, gwo, gg[0].astype(BF), gg[1].astype(BF), grad_ga)
 

time: 442 us -> 433 us (0.980)
  local copies, waits for them, and re-layouts: 10.8 us -> 1.75 us
    pallas_call x1, Pallas kernels: 128 us -> 104 us  [grads(): pl.pallas_call(grads_kernel, in_specs=[far] * 13 + [vm], out_specs=[vm] *...]
    pallas_call x1 -> x2, Pallas kernels: 37.2 us -> 59.5 us  [the longest x1 52.9 us: out_block(): pl.pallas_call(out_kernel, grid=(2,), in_specs=[batch, batch, batch, whol...]
    unnamed x19 -> x3, local copies, waits for them, and re-layouts: 9.61 us -> 0.6 us
where the time goes in v8:
time: 433 us; the launch traced here: 432 us
  Pallas kernels  428 us (99%)
    pallas_call x1, Pallas kernels, forward(): pl.pallas_call(forward_kernel, grid=(8 * NB,), in_specs=[whole(1, HD), ws...  147 us
    pallas_call x2, Pallas kernels, backward(): pl.pallas_call(functools.partial(backward_kernel, b), grid=(2, NB), in_sp...  117 us
    pallas_call x1, Pallas kernels, grads(): pl.pallas_call(grads_kernel, in_specs=[far] * 13 + [vm], out_specs=[vm] *...  104 us
    pallas_call x1, Pallas kernels, out_block(): pl.pallas_call(out_kernel, grid=(2,), in_specs=[batch, batch, batch, whol...  52.9 us

profile of v8, /device:TPU:0, one launch (start us, length us, event | category | flops | bytes accessed | tf_op | source)
XLA Modules:
  0.0 432.1 jit_solution(3008673930176583427)
XLA Ops:
  0.6 0.7 maximum_convert_fusion
  1.4 0.6 reshape.26.gains_ref
  2.0 147.0 %forward.1 = (f32[2048,128]{1,0:T(8,128)}, f32[2048,128]{1,0:T(8,128)}, f32[2,8,512]{2,1,0:T(8,128)}, bf16[2,2048,256]{2,1,0:T(8,128)(2,1)}, f32[2,8,512]{2,1,0:...) custom-call(f32[1,128]{1,0:T(1,128)} %constant.2.clone.freq_ref, ...), custom_call_target="tpu_custom_call" | custom-call | flops 60000002048 | bytes 60000000 | tf_op jit(solution)/shard_map/forward/pallas_call | solution.py:427
  148.9 52.9 %out_block.1 = (bf16[2,256,2048]{2,1,0:T(8,128)(2,1)}, bf16[2,256,2048]{2,1,0:T(8,128)(2,1)}, f32[8,256]{1,0:T(8,128)}, bf16[2048,2048]{1,0:T(8,128)(2,1)}) custom-call(bf16[2,256,2048]{2,1,0:T(8,128)(2,1)} %get-tuple-element.44.o_ref, bf16[2,256,2048]{2,1,0:T(8,128)(2,1)} %x_ref.3, bf16[2,256,2048]{2,1,0:T(8,128)(2,1)} %dy_ref.3, ...), custom_call_target="tpu_custom_call" | custom-call | flops 13589934080 | bytes 18000000 | tf_op jit(solution)/shard_map/out_block/pallas_call | solution.py:507
  201.8 57.0 %backward.2 = (bf16[2048,768]{1,0:T(8,128)(2,1)}, bf16[2048,768]{1,0:T(8,128)(2,1)}, f32[8,256]{1,0:T(8,128)}, f32[8,256]{1,0:T(8,128)}, bf16[2048,2048]{1,0:T(8,128)(2,1)}, /*index=5*/bf16[1024,768]{1,0:T(8,128)(2,1)}) custom-call(bf16[2,3,2048,256]{3,2,1,0:T(8,128)(2,1)} %get-tuple-element.47.qkv_ref, bf16[2048,2048]{1,0:T(8,128)(2,1)} %get-tuple-element.48.da_ref.da0, ...), custom_call_target="tpu_custom_call" | custom-call | flops 24999999488 | bytes 30000000 | tf_op jit(solution)/shard_map/backward/pallas_call | solution.py:696
  258.8 60.4 %backward.3 = (bf16[2048,768]{1,0:T(8,128)(2,1)}, bf16[2048,768]{1,0:T(8,128)(2,1)}, f32[8,256]{1,0:T(8,128)}, f32[8,256]{1,0:T(8,128)}, f32[2,512,1024]{2,1,0:T(8,128)}) custom-call(bf16[2,3,2048,256]{3,2,1,0:T(8,128)(2,1)} %get-tuple-element.47.qkv_ref, bf16[2048,2048]{1,0:T(8,128)(2,1)} %get-tuple-element.57.da_ref.da1, bf16[256,2048]{1,0:T(8,128)(2,1)} %wo_ref.5, ...), custom_call_target="tpu_custom_call" | custom-call | flops 24999999488 | bytes 30000000 | tf_op jit(solution)/shard_map/backward/pallas_call | solution.py:696
  319.2 104.5 %grads.1 = (bf16[2,256,2048]{2,1,0:T(8,128)(2,1)}, bf16[2048,256]{1,0:T(8,128)(2,1)}, bf16[2048,256]{1,0:T(8,128)(2,1)}, bf16[2048,256]{1,0:T(8,128)(2,1)}, bf16[256,2048]{1,0:T(8,128)(2,1)}) custom-call(bf16[2048,768]{1,0:T(8,128)(2,1)} %get-tuple-element.56.rest_0_.d0, bf16[2048,768]{1,0:T(8,128)(2,1)} %get-tuple-element.60.d1, ...), custom_call_target="tpu_custom_call" | custom-call | flops 99999997952 | bytes 40000000 | tf_op jit(solution)/shard_map/grads/pallas_call | solution.py:872
  423.6 0.7 add_convert_fusion
  424.4 0.5 slice_reduce_fusion
  424.9 0.0 copy-start
  424.9 6.6 %deliver.1 = (bf16[2,256,2048]{2,1,0:T(8,128)(2,1)}, bf16[2,256,2048]{2,1,0:T(8,128)(2,1)}, bf16[2048,256]{1,0:T(8,128)(2,1)}, bf16[2048,256]{1,0:T(8,128)(2,1)}...) custom-call(bf16[2,256,2048]{2,1,0:T(8,128)(2,1)} %get-tuple-element.46.refs_0_, ...), custom_call_target="tpu_custom_call" | custom-call | flops 1000000000 | bytes 16000000 | tf_op jit(solution)/shard_map/deliver/pallas_call | solution.py:902
  431.5 0.0 copy-done
  431.5 0.6 copy.19
  (1 shorter events, 0.0 us)
Async XLA Ops:
  424.9 6.6 %copy-start = (f32[8,256]{1,0:T(8,128)S(1)}, f32[8,256]{1,0:T(8,128)}, u32[]{:S(2)}) copy-start(f32[8,256]{1,0:T(8,128)} %get-tuple-element.78) | copy-start | bytes 24580

commit v9 on v8

--- a/solution.py
+++ b/solution.py
@@ -94,8 +94,8 @@
         wait(self.loads)
         start(self.copies)
 
-    def wait(self):
-        wait(self.copies)
+    def wait(self, *which):
+        wait([self.copies[n] for n in which] or self.copies)
 
 
 def stage1(me, src, full, bg, part=None):
@@ -493,10 +493,6 @@
     @pl.when(b == 1)
     def _():
         stage1(me, None, full_ref, bg).wait()
-        for stage in (stage2(me, full_ref, bg), stage3(me, full_ref, bg)):
-            stage.load()
-            stage.send()
-            stage.wait()
 
 
 def out_block(o, wo, x, dy, gains, cid):
@@ -518,16 +514,25 @@
     )(o, x, dy, gains, wo)
 
 
-def backward_kernel(b, qkv_ref, da_ref, wo_ref, lse_ref, raw_ref, inv_ref, gains_ref, cos_ref, sin_ref, gga_ref,
-                    wq_ref, wk_ref, wv_ref, *rest):
+def backward_kernel(b, qkv_ref, wo_ref, lse_ref, raw_ref, inv_ref, gains_ref, cos_ref, sin_ref, gga_ref,
+                    wq_ref, wk_ref, wv_ref, da_ref, *rest):
     if b:
         d0_ref, pd0_ref, pw_ref, d_ref, pd_ref, gg_ref, gout_ref, got_ref, w_all, d_two, sbuf, *rest = rest
     else:
-        shard_ref, d_ref, pd_ref, gg_ref, gout_ref, full_ref, pw_ref, buf, *rest = rest
-    (p_scr, dp_scr, kt_scr, dqt_scr, dq_scr, dk_scr, dv_scr, du_scr, d_scr, dh_scr, dots_scr, total, slot, ga_slot,
-     ex_send, ex_recv, pd_send, pd_recv, d_sems, rs_sems, ld_sems, *bg_sems) = rest
-    h, qi = pl.program_id(0), pl.program_id(1)
+        shard_ref, d_ref, pd_ref, gg_ref, gout_ref, full_ref, pw_ref, da_ref, buf0, buf1, *rest = rest
+    (p_scr, dp_scr, kt_scr, dqt_scr, dq_scr, dk_scr, dv_scr, du_scr, d_scr, dh_scr, dbuf, dots_scr, total, slot, ga_slot,
+     ex_send, ex_recv, pd_send, pd_recv, d_sems, rs_sems, ld_sems, db_sems, *bg_sems) = rest
+    h, step = pl.program_id(0), pl.program_id(1)
     me = lax.axis_index('tp')
+
+    def chip_at(n):
+        ax, ay = (me // 2) % 2, me // 4
+        return (ay + (n // 2) * (1 - 2 * ay)) * 2 + ax + (n % 2) * (1 - 2 * ax)
+
+    def fetch(n):
+        return pltpu.make_async_copy(da_ref.at[block_rows(chip_at(n)), :], dbuf.at[n % 2], db_sems.at[n % 2])
+
+    qi = chip_at(step)
     core, partner, first_dev, _ = route(me)
     weights = (wq_ref, wk_ref, wv_ref)
 
@@ -544,14 +549,16 @@
             recv_sem=rs_sems.at[3 + n], device_id=(first_dev,), device_id_type=MESH)
             for n, (blk, lo, count) in enumerate(((0, 0, BLK), (1, 0, BLK // 2), (1, BLK // 2, BLK // 2)))]
     else:
-        bg = (*bg_sems, buf)
+        bg0, bg = (*bg_sems[:3], buf0), (*bg_sems[3:], buf1)
+        older2, older3 = stage2(me, da_ref, bg0), stage3(me, da_ref, bg0)
         gather = stage1(me, shard_ref.at[1], full_ref, bg)
         moved = [pltpu.make_async_remote_copy(
             src_ref=w.at[half_rows(1 - core), :], dst_ref=pw_ref.at[:, pl.ds(n * LOC, LOC)], send_sem=rs_sems.at[n],
             recv_sem=rs_sems.at[3 + n], device_id=(partner,), device_id_type=MESH) for n, w in enumerate(weights)]
 
-    @pl.when(jnp.logical_and(h == 0, qi == 0))
-    def _():
+    @pl.when(jnp.logical_and(h == 0, step == 0))
+    def _():
+        fetch(0).start()
         if b:
             start(operands)
             entry_barrier(me)
@@ -560,14 +567,21 @@
                 sbuf[blk] = dot(d_two[blk, 0], w_all[0], NT) + dot(d_two[blk, 1], w_all[1], NT)
                 moved[blk].start()
         else:
+            older2.load()
             gather.load()
             entry_barrier(me)
+            older2.send()
             gather.send()
             start(moved)
         dots_scr[...] = jnp.zeros_like(dots_scr)
 
     if not b:
-        @pl.when(jnp.logical_and(h == 1, qi == 1))
+        @pl.when(jnp.logical_and(h == 0, step == NB - 1))
+        def _():
+            older3.wait()
+            fetch(NB - 1).start()
+
+        @pl.when(jnp.logical_and(h == 1, step == 2))
         def _():
             gather.wait()
             more = stage2(me, full_ref, bg)
@@ -576,9 +590,28 @@
 
     @pl.when(h == 0)
     def _():
-        dh_scr[block_rows(qi), :] = dot(da_ref[...], wo_ref[...], NT).astype(BF)
-
-    @pl.when(qi == 0)
+        fetch(step).wait()
+        dh_scr[block_rows(qi), :] = dot(dbuf[step % 2], wo_ref[...], NT).astype(BF)
+        if b:
+            @pl.when(step < NB - 1)
+            def _():
+                fetch(step + 1).start()
+        else:
+            @pl.when(step == 0)
+            def _():
+                older2.wait(2, 3)
+
+            @pl.when(step < NB - 2)
+            def _():
+                fetch(step + 1).start()
+
+            @pl.when(step == NB - 2)
+            def _():
+                older2.wait(0, 1)
+                older3.load()
+                older3.send()
+
+    @pl.when(step == 0)
     def _():
         kt_scr[...] = qkv_ref[1].T
         dk_scr[...] = jnp.zeros_like(dk_scr)
@@ -614,7 +647,7 @@
     lax.fori_loop(0, qi + 1, second, 0)
     dq_scr[block_rows(qi), :] = dqt_scr[...].T
 
-    @pl.when(qi == NB - 1)
+    @pl.when(step == NB - 1)
     def _():
         d_scr[:, pl.ds(pl.multiple_of(2 * LOC + h * HD, HD), HD)] = dv_scr[...].astype(BF)
         gg_ref[...] = jnp.zeros_like(gg_ref)
@@ -635,7 +668,7 @@
 
         lax.fori_loop(0, NB, tail, 0)
 
-    @pl.when(jnp.logical_and(h == 1, qi == NB - 1))
+    @pl.when(jnp.logical_and(h == 1, step == NB - 1))
     def _():
         sums = exchange(me, [dots_scr, gga_ref], [slot, ga_slot], ex_send, ex_recv)
         start(sums)
@@ -691,30 +724,31 @@
         extra = [sds((2, BLK, DIM // 2), F32)]
         own = [pltpu.VMEM((2,) + half, BF), pltpu.VMEM((2, 2, BLK, 3 * LOC), BF), pltpu.VMEM((2, BLK, DIM // 2), F32)]
     else:
-        extra = [sds((SEQ, DIM), BF), sds(half, BF)]
-        own = [pltpu.VMEM((2, TOK, DIM), BF)]
+        extra = [sds((SEQ, DIM), BF), sds(half, BF), sds((SEQ, DIM), BF)]
+        own = [pltpu.VMEM((2, TOK, DIM), BF), pltpu.VMEM((2, TOK, DIM), BF)]
     return pl.pallas_call(
         functools.partial(backward_kernel, b),
         grid=(2, NB),
         in_specs=[pl.BlockSpec((None, 3, SEQ, HD), lambda h, i: (b, 0, 0, h)),
-                  pl.BlockSpec((BLK, DIM), lambda h, i: (jnp.where(h == 0, i, NB - 1), 0)), whole(LOC, DIM),
+                  whole(LOC, DIM),
                   picked(2 * NB, BLK), picked(2, SEQ, LOC), picked(2 * NB, BLK),
                   pl.BlockSpec((2 + DIM // LOC, HD), lambda h, i: (0, h)), whole(SEQ, HD), whole(SEQ, HD), gsp]
-        + [ANYWHERE] * (3 + len(others)),
+        + [ANYWHERE] * (4 + len(others)),
         out_specs=[ANYWHERE, ANYWHERE, pl.BlockSpec((8, HD), lambda h, i: (0, h)), gsp] + [ANYWHERE] * len(extra),
         out_shape=[sds((SEQ, 3 * LOC), BF), sds((SEQ, 3 * LOC), BF), sds((8, LOC), F32), sds((8, DIM // 8), F32)] + extra,
+        input_output_aliases={} if b else {12: 6},
         scratch_shapes=own + [
             pltpu.VMEM((NB, BLK, BLK), F32), pltpu.VMEM((NB, BLK, BLK), F32), pltpu.VMEM((HD, SEQ), BF),
             pltpu.VMEM((HD, BLK), F32), pltpu.VMEM((SEQ, HD), F32), pltpu.VMEM((SEQ, HD), F32),
             pltpu.VMEM((SEQ, HD), F32), pltpu.VMEM((2, 2, SEQ, HD), F32), pltpu.VMEM((SEQ, 3 * LOC), BF),
-            pltpu.VMEM((SEQ, LOC), BF), pltpu.VMEM((2 * NB, BLK), F32), pltpu.VMEM((2 * NB, BLK), F32),
+            pltpu.VMEM((SEQ, LOC), BF), pltpu.VMEM((2, BLK, DIM), BF), pltpu.VMEM((2 * NB, BLK), F32), pltpu.VMEM((2 * NB, BLK), F32),
             pltpu.VMEM((NDEV - 1, 2 * NB, BLK), F32), pltpu.VMEM((NDEV - 1, 8, DIM // 8), F32),
-            DMA((2, NDEV - 1)), DMA((2, NDEV - 1)), DMA((NB,)), DMA((NB,)), DMA((NB,)), DMA((6,)), DMA((8,))]
-        + ([] if b else BG_SEMS),
+            DMA((2, NDEV - 1)), DMA((2, NDEV - 1)), DMA((NB,)), DMA((NB,)), DMA((NB,)), DMA((6,)), DMA((8,)), DMA((2,))]
+        + ([] if b else BG_SEMS * 2),
         compiler_params=params(dimension_semantics=("arbitrary", "arbitrary"), collective_id=cid, has_side_effects=True),
         cost_estimate=cost(25e9, 30e6),
         name="backward",
-    )(qkv, da, wo, lse, raw, inv, gains, cos, sin, gga, *weights, *others)
+    )(qkv, wo, lse, raw, inv, gains, cos, sin, gga, *weights, da, *others)
 
 
 HALF = DIM // 2
@@ -917,7 +951,7 @@
     cos, sin, inv, o, lse, raw, qkv, o_recv, x_full, wo_full = forward(x_loc, wq, wk, wv, wo, gains, 0)
     y, da, gga, da0 = out_block(o_recv, wo_full, x_loc, dy_loc, gains, 1)
     state = (qkv, wo, lse, raw, inv, gains, cos, sin, gga, weights)
-    d0, pd0, gg0, gout, da1, pw = backward(0, da0, *state, (da,), 2)
+    d0, pd0, gg0, gout, da1, pw, da0 = backward(0, da0, *state, (da,), 2)
     d1, pd1, gg1, _, got = backward(1, da1, *state, (d0, pd0, pw), 3)
     grad_ga = gout.reshape(DIM).astype(BF)
     big = grads(d0, d1, pd0, pd1, *weights, pw, got, x_full, o, da0, da1, dy_loc, 4)

time: 433 us -> 425 us (0.982)
  Pallas kernels: 428 us -> 420 us
    pallas_call x1, Pallas kernels: 52.9 us -> 34.6 us  [out_block(): pl.pallas_call(out_kernel, grid=(2,), in_specs=[batch, batch, batch, whol...]
    pallas_call x2, Pallas kernels: 117 us -> 127 us  [backward(): pl.pallas_call(functools.partial(backward_kernel, b), grid=(2, NB), in_sp...]
where the time goes in v9:
time: 425 us; the launch traced here: 424 us
  Pallas kernels  420 us (99%)
    pallas_call x1, Pallas kernels, forward(): pl.pallas_call(forward_kernel, grid=(8 * NB,), in_specs=[whole(1, HD), ws...  147 us
    pallas_call x2, Pallas kernels, backward(): pl.pallas_call(functools.partial(backward_kernel, b), grid=(2, NB), in_sp...  127 us
    pallas_call x1, Pallas kernels, grads(): pl.pallas_call(grads_kernel, in_specs=[far] * 13 + [vm], out_specs=[vm] *...  105 us
    pallas_call x1, Pallas kernels, out_block(): pl.pallas_call(out_kernel, grid=(2,), in_specs=[batch, batch, batch, whol...  34.6 us

profile of v9, /device:TPU:0, one launch (start us, length us, event | category | flops | bytes accessed | tf_op | source)
XLA Modules:
  0.0 424.0 jit_solution(16503562471271230802)
XLA Ops:
  0.6 0.7 maximum_convert_fusion
  1.4 0.6 reshape.26.gains_ref
  2.0 147.0 %forward.1 = (f32[2048,128]{1,0:T(8,128)}, f32[2048,128]{1,0:T(8,128)}, f32[2,8,512]{2,1,0:T(8,128)}, bf16[2,2048,256]{2,1,0:T(8,128)(2,1)}, f32[2,8,512]{2,1,0:...) custom-call(f32[1,128]{1,0:T(1,128)} %constant.2.clone.freq_ref, ...), custom_call_target="tpu_custom_call" | custom-call | flops 60000002048 | bytes 60000000 | tf_op jit(solution)/shard_map/forward/pallas_call | solution.py:427
  148.9 34.6 %out_block.1 = (bf16[2,256,2048]{2,1,0:T(8,128)(2,1)}, bf16[2,256,2048]{2,1,0:T(8,128)(2,1)}, f32[8,256]{1,0:T(8,128)}, bf16[2048,2048]{1,0:T(8,128)(2,1)}) custom-call(bf16[2,256,2048]{2,1,0:T(8,128)(2,1)} %get-tuple-element.45.o_ref, bf16[2,256,2048]{2,1,0:T(8,128)(2,1)} %x_ref.3, bf16[2,256,2048]{2,1,0:T(8,128)(2,1)} %dy_ref.3, ...), custom_call_target="tpu_custom_call" | custom-call | flops 13589934080 | bytes 18000000 | tf_op jit(solution)/shard_map/out_block/pallas_call | solution.py:503
  183.6 67.4 %backward.2 = (bf16[2048,768]{1,0:T(8,128)(2,1)}, bf16[2048,768]{1,0:T(8,128)(2,1)}, f32[8,256]{1,0:T(8,128)}, f32[8,256]{1,0:T(8,128)}, bf16[2048,2048]{1,0:T(8...) custom-call(bf16[2,3,2048,256]{3,2,1,0:T(8,128)(2,1)} %get-tuple-element.48.qk, ...), custom_call_target="tpu_custom_call", output_to_operand_aliasing={{6}: (12, {})} | custom-call | flops 24999999488 | bytes 30000000 | tf_op jit(solution)/shard_map/backward/pallas_call | solution.py:729
  251.0 0.0 copy-start.1
  251.0 60.0 %backward.3 = (bf16[2048,768]{1,0:T(8,128)(2,1)}, bf16[2048,768]{1,0:T(8,128)(2,1)}, f32[8,256]{1,0:T(8,128)}, f32[8,256]{1,0:T(8,128)}, f32[2,512,1024]{2,1,0:T(8,128)}) custom-call(bf16[2,3,2048,256]{3,2,1,0:T(8,128)(2,1)} %get-tuple-element.48.qkv_ref, bf16[256,2048]{1,0:T(8,128)(2,1)} %wo_ref.5, f32[2,8,512]{2,1,0:T(8,128)} %get-tuple-element.49.lse_ref, ...), custom_call_target="tpu_custom_call" | custom-call | flops 24999999488 | bytes 30000000 | tf_op jit(solution)/shard_map/backward/pallas_call | solution.py:729
  310.9 0.0 copy-done.1
  311.0 0.7 add_convert_fusion
  311.7 0.5 slice_reduce_fusion
  312.2 104.5 %grads.1 = (bf16[2,256,2048]{2,1,0:T(8,128)(2,1)}, bf16[2048,256]{1,0:T(8,128)(2,1)}, bf16[2048,256]{1,0:T(8,128)(2,1)}, bf16[2048,256]{1,0:T(8,128)(2,1)}, bf16[256,2048]{1,0:T(8,128)(2,1)}) custom-call(bf16[2048,768]{1,0:T(8,128)(2,1)} %get-tuple-element.57.rest_0_.d0, bf16[2048,768]{1,0:T(8,128)(2,1)} %get-tuple-element.61.d1, ...), custom_call_target="tpu_custom_call" | custom-call | flops 99999997952 | bytes 40000000 | tf_op jit(solution)/shard_map/grads/pallas_call | solution.py:906
  416.7 0.0 copy-start
  416.7 6.6 %deliver.1 = (bf16[2,256,2048]{2,1,0:T(8,128)(2,1)}, bf16[2,256,2048]{2,1,0:T(8,128)(2,1)}, bf16[2048,256]{1,0:T(8,128)(2,1)}, bf16[2048,256]{1,0:T(8,128)(2,1)}...) custom-call(bf16[2,256,2048]{2,1,0:T(8,128)(2,1)} %get-tuple-element.47.refs_0_, ...), custom_call_target="tpu_custom_call" | custom-call | flops 1000000000 | bytes 16000000 | tf_op jit(solution)/shard_map/deliver/pallas_call | solution.py:936
  423.3 0.0 copy-done
  423.4 0.6 copy.20
  (1 shorter events, 0.0 us)
Async XLA Ops:
  251.0 60.0 %copy-start.1 = (f32[8,256]{1,0:T(8,128)S(1)}, f32[8,256]{1,0:T(8,128)}, u32[]{:S(2)}) copy-start(f32[8,256]{1,0:T(8,128)} %get-tuple-element.78) | copy-start | bytes 24580
  416.7 6.6 %copy-start = (f32[8,256]{1,0:T(8,128)S(1)}, f32[8,256]{1,0:T(8,128)}, u32[]{:S(2)}) copy-start(f32[8,256]{1,0:T(8,128)} %get-tuple-element.80) | copy-start | bytes 24580

commit v10 on v9

--- a/solution.py
+++ b/solution.py
@@ -514,14 +514,14 @@
     )(o, x, dy, gains, wo)
 
 
-def backward_kernel(b, qkv_ref, wo_ref, lse_ref, raw_ref, inv_ref, gains_ref, cos_ref, sin_ref, gga_ref,
+def backward_kernel(b, qkv_ref, wo_ref, lse_ref, raw_hbm, inv_ref, gains_ref, cos_hbm, sin_hbm, gga_ref,
                     wq_ref, wk_ref, wv_ref, da_ref, *rest):
     if b:
         d0_ref, pd0_ref, pw_ref, d_ref, pd_ref, gg_ref, gout_ref, got_ref, w_all, d_two, sbuf, *rest = rest
     else:
-        shard_ref, d_ref, pd_ref, gg_ref, gout_ref, full_ref, pw_ref, da_ref, buf0, buf1, *rest = rest
+        shard_ref, d_ref, pd_ref, gg_ref, gout_ref, full_ref, pw_ref, da_ref, buf0, buf1, w_half, *rest = rest
     (p_scr, dp_scr, kt_scr, dqt_scr, dq_scr, dk_scr, dv_scr, du_scr, d_scr, dh_scr, dbuf, dots_scr, total, slot, ga_slot,
-     ex_send, ex_recv, pd_send, pd_recv, d_sems, rs_sems, ld_sems, db_sems, *bg_sems) = rest
+     ex_send, ex_recv, pd_send, pd_recv, d_sems, rs_sems, ld_sems, db_sems, raw_ref, cos_ref, sin_ref, tb_sems, *bg_sems) = rest
     h, step = pl.program_id(0), pl.program_id(1)
     me = lax.axis_index('tp')
 
@@ -533,6 +533,8 @@
         return pltpu.make_async_copy(da_ref.at[block_rows(chip_at(n)), :], dbuf.at[n % 2], db_sems.at[n % 2])
 
     qi = chip_at(step)
+    tables = [pltpu.make_async_copy(src, dst, tb_sems.at[n]) for n, (src, dst) in enumerate(
+        ((raw_hbm.at[b], raw_ref), (cos_hbm, cos_ref), (sin_hbm, sin_ref)))]
     core, partner, first_dev, _ = route(me)
     weights = (wq_ref, wk_ref, wv_ref)
 
@@ -552,15 +554,18 @@
         bg0, bg = (*bg_sems[:3], buf0), (*bg_sems[3:], buf1)
         older2, older3 = stage2(me, da_ref, bg0), stage3(me, da_ref, bg0)
         gather = stage1(me, shard_ref.at[1], full_ref, bg)
+        operands = [pltpu.make_async_copy(w.at[half_rows(1 - core), :], w_half.at[:, pl.ds(n * LOC, LOC)], ld_sems.at[n])
+                    for n, w in enumerate(weights)]
         moved = [pltpu.make_async_remote_copy(
-            src_ref=w.at[half_rows(1 - core), :], dst_ref=pw_ref.at[:, pl.ds(n * LOC, LOC)], send_sem=rs_sems.at[n],
-            recv_sem=rs_sems.at[3 + n], device_id=(partner,), device_id_type=MESH) for n, w in enumerate(weights)]
+            src_ref=w_half, dst_ref=pw_ref, send_sem=rs_sems.at[0], recv_sem=rs_sems.at[3], device_id=(partner,),
+            device_id_type=MESH)]
 
     @pl.when(jnp.logical_and(h == 0, step == 0))
     def _():
-        fetch(0).start()
         if b:
             start(operands)
+            fetch(0).start()
+            start(tables)
             entry_barrier(me)
             wait(operands)
             for blk in range(2):
@@ -568,10 +573,14 @@
                 moved[blk].start()
         else:
             older2.load()
+            fetch(0).start()
             gather.load()
+            start(operands)
+            start(tables)
             entry_barrier(me)
             older2.send()
             gather.send()
+            wait(operands)
             start(moved)
         dots_scr[...] = jnp.zeros_like(dots_scr)
 
@@ -652,6 +661,11 @@
         d_scr[:, pl.ds(pl.multiple_of(2 * LOC + h * HD, HD), HD)] = dv_scr[...].astype(BF)
         gg_ref[...] = jnp.zeros_like(gg_ref)
         cols = head_cols(h)
+
+        @pl.when(h == 0)
+        def _():
+            wait(tables)
+
 
         def tail(i, carry):
             rows = block_rows(i)
@@ -725,14 +739,14 @@
         own = [pltpu.VMEM((2,) + half, BF), pltpu.VMEM((2, 2, BLK, 3 * LOC), BF), pltpu.VMEM((2, BLK, DIM // 2), F32)]
     else:
         extra = [sds((SEQ, DIM), BF), sds(half, BF), sds((SEQ, DIM), BF)]
-        own = [pltpu.VMEM((2, TOK, DIM), BF), pltpu.VMEM((2, TOK, DIM), BF)]
+        own = [pltpu.VMEM((2, TOK, DIM), BF), pltpu.VMEM((2, TOK, DIM), BF), pltpu.VMEM(half, BF)]
     return pl.pallas_call(
         functools.partial(backward_kernel, b),
         grid=(2, NB),
         in_specs=[pl.BlockSpec((None, 3, SEQ, HD), lambda h, i: (b, 0, 0, h)),
                   whole(LOC, DIM),
-                  picked(2 * NB, BLK), picked(2, SEQ, LOC), picked(2 * NB, BLK),
-                  pl.BlockSpec((2 + DIM // LOC, HD), lambda h, i: (0, h)), whole(SEQ, HD), whole(SEQ, HD), gsp]
+                  picked(2 * NB, BLK), ANYWHERE, picked(2 * NB, BLK),
+                  pl.BlockSpec((2 + DIM // LOC, HD), lambda h, i: (0, h)), ANYWHERE, ANYWHERE, gsp]
         + [ANYWHERE] * (4 + len(others)),
         out_specs=[ANYWHERE, ANYWHERE, pl.BlockSpec((8, HD), lambda h, i: (0, h)), gsp] + [ANYWHERE] * len(extra),
         out_shape=[sds((SEQ, 3 * LOC), BF), sds((SEQ, 3 * LOC), BF), sds((8, LOC), F32), sds((8, DIM // 8), F32)] + extra,
@@ -743,7 +757,8 @@
             pltpu.VMEM((SEQ, HD), F32), pltpu.VMEM((2, 2, SEQ, HD), F32), pltpu.VMEM((SEQ, 3 * LOC), BF),
             pltpu.VMEM((SEQ, LOC), BF), pltpu.VMEM((2, BLK, DIM), BF), pltpu.VMEM((2 * NB, BLK), F32), pltpu.VMEM((2 * NB, BLK), F32),
             pltpu.VMEM((NDEV - 1, 2 * NB, BLK), F32), pltpu.VMEM((NDEV - 1, 8, DIM // 8), F32),
-            DMA((2, NDEV - 1)), DMA((2, NDEV - 1)), DMA((NB,)), DMA((NB,)), DMA((NB,)), DMA((6,)), DMA((8,)), DMA((2,))]
+            DMA((2, NDEV - 1)), DMA((2, NDEV - 1)), DMA((NB,)), DMA((NB,)), DMA((NB,)), DMA((6,)), DMA((8,)), DMA((2,)),
+            pltpu.VMEM((2, SEQ, LOC), F32), pltpu.VMEM((SEQ, HD), F32), pltpu.VMEM((SEQ, HD), F32), DMA((3,))]
         + ([] if b else BG_SEMS * 2),
         compiler_params=params(dimension_semantics=("arbitrary", "arbitrary"), collective_id=cid, has_side_effects=True),
         cost_estimate=cost(25e9, 30e6),
@@ -755,9 +770,9 @@
 CH = 256
 
 
-def grads_kernel(d0, d1, pd0, pd1, wq, wk, wv, pw, got, x_full, o_all, da0, da1, dy_ref, dx_ref, gwq_ref, gwk_ref, gwv_ref, gwo_ref,
+def grads_kernel(d0, d1, pd0, pd1, wq, wk, wv, pw, got, x_full, o_all, da0, da1, dy_ref, dx_out, gwq_out, gwk_out, gwv_out, gwo_out,
                  d_all, w_all, sbuf, r1, r2, fin, acc, xbuf, obuf,
-                 dl_sems, w_sems, s1_sems, r1_sems, s2_sems, r2_sems, fs_sems, fr_sems, x_sems, o_sems):
+                 dl_sems, w_sems, s1_sems, r1_sems, s2_sems, r2_sems, fs_sems, fr_sems, x_sems, o_sems, dx_ref, gwq_ref, gwk_ref, gwv_ref, gwo_ref, out_sems):
     me = lax.axis_index('tp')
     core, partner, first, second = route(me)
     chip = me // 2
@@ -766,11 +781,12 @@
     barrier = pltpu.get_barrier_semaphore()
     for dev in (partner, first, second):
         pl.semaphore_signal(barrier, inc=1, device_id=(dev,), device_id_type=MESH)
-    pl.semaphore_wait(barrier, 3)
 
     def rows_of(blk):
         return pl.ds(pl.multiple_of(blk * BLK, BLK), BLK)
 
+    results = [pltpu.make_async_copy(src, dst, out_sems.at[n]) for n, (src, dst) in enumerate((
+        (gwq_ref, gwq_out), (gwk_ref, gwk_out), (gwv_ref, gwv_out), (gwo_ref, gwo_out)))]
     chips = (diag_chip, first_chip, second_chip, chip)
     w_copies = [pltpu.make_async_copy(w.at[half_rows(core), :], w_all.at[0, :, pl.ds(n * LOC, LOC)], w_sems.at[n])
                 for n, w in enumerate((wq, wk, wv))]
@@ -782,6 +798,7 @@
                       for side, d in enumerate(((d0, d1)[b], (pd0, pd1)[b]))])
     start(w_copies)
     start(loads[1])
+    pl.semaphore_wait(barrier, 3)
     wait(w_copies)
 
     def partial(b, blk):
@@ -864,6 +881,7 @@
     wgrad(1, x_full.at[1])
     for n, ref in enumerate((gwq_ref, gwk_ref, gwv_ref)):
         ref[...] = acc[n * LOC:(n + 1) * LOC, :].T.astype(BF)
+        results[n].start()
     forward_second(1)
     acc[:LOC, :] = jnp.zeros((LOC, DIM), F32)
 
@@ -873,6 +891,7 @@
     for o_src, da_src in ((o_all.at[0], da0), (o_all.at[1], da1)):
         stream([(da_src, xbuf, x_sems), (o_src, obuf, o_sems)], wo_body)
     gwo_ref[...] = acc[:LOC, :].astype(BF)
+    results[3].start()
 
     def own_part(b, carry):
         r1_own = partial(b, chip)
@@ -891,12 +910,16 @@
         to_partner(b).wait()
         cols = half_rows(1 - core)
         dx_ref[b, :, cols] = (fin[b] + dy_ref[b, :, cols].astype(F32)).astype(BF)
+        pltpu.make_async_copy(dx_ref.at[b], dx_out.at[b], out_sems.at[4 + b]).start()
         to_second(b).wait_send()
         return carry
 
     to_first(1).wait_send()
     to_first(3).wait_send()
     lax.fori_loop(0, 2, finish, 0)
+    wait(results)
+    for b in range(2):
+        pltpu.make_async_copy(dx_ref.at[b], dx_out.at[b], out_sems.at[4 + b]).wait()
 
 
 def grads(d0, d1, pd0, pd1, wq, wk, wv, pw, got, x_full, o_all, da0, da1, dy, cid):
@@ -906,14 +929,16 @@
     return pl.pallas_call(
         grads_kernel,
         in_specs=[far] * 13 + [vm],
-        out_specs=[vm] * 5,
+        out_specs=[far] * 5,
         out_shape=[sds((2, TOK, DIM), BF)] + [sds((DIM, LOC), BF)] * 3 + [sds((LOC, DIM), BF)],
         scratch_shapes=[pltpu.VMEM((2, 2, SEQ, 3 * LOC), BF), pltpu.VMEM((2, HALF, 3 * LOC), BF),
                         pltpu.VMEM((2, BLK, HALF), F32), pltpu.VMEM((4, BLK, HALF), F32), pltpu.VMEM((2, BLK, HALF), F32),
                         pltpu.VMEM((2, TOK, HALF), F32), pltpu.VMEM((3 * LOC, DIM), F32),
                         pltpu.VMEM((2, CH, DIM), BF), pltpu.VMEM((2, CH, LOC), BF),
                         dma((2, 8)), dma((9,)), dma((4,)), dma((4,)), dma((2,)), dma((2,)),
-                        dma((2,)), dma((2,)), dma((2,)), dma((2,))],
+                        dma((2,)), dma((2,)), dma((2,)), dma((2,)), pltpu.VMEM((2, TOK, DIM), BF),
+                        pltpu.VMEM((DIM, LOC), BF), pltpu.VMEM((DIM, LOC), BF), pltpu.VMEM((DIM, LOC), BF),
+                        pltpu.VMEM((LOC, DIM), BF), dma((6,))],
         compiler_params=pltpu.CompilerParams(vmem_limit_bytes=67043328, collective_id=cid, has_side_effects=True),
         cost_estimate=cost(100e9, 40e6),
         name="grads",
@@ -922,13 +947,19 @@
 
 def deliver_kernel(*refs):
     count = (len(refs) - 2) // 3
-    srcs, dsts, bufs = refs[:count], refs[count:2 * count], refs[2 * count:3 * count]
-    loads = [pltpu.make_async_copy(src, buf, refs[-2].at[n]) for n, (src, buf) in enumerate(zip(srcs, bufs))]
-    stores = [pltpu.make_async_copy(buf, dst, refs[-1].at[n]) for n, (buf, dst) in enumerate(zip(bufs, dsts))]
-    start(loads)
-    for load, store in zip(loads, stores):
+    loads, stores = [], []
+    for src, dst, buf in zip(refs[:count], refs[count:2 * count], refs[2 * count:3 * count]):
+        for part in range(2):
+            piece = (part,) if len(src.shape) == 3 else (pl.ds(part * (src.shape[0] // 2), src.shape[0] // 2),)
+            n = len(loads)
+            loads.append(pltpu.make_async_copy(src.at[piece], buf.at[piece], refs[-2].at[n]))
+            stores.append(pltpu.make_async_copy(buf.at[piece], dst.at[piece], refs[-1].at[n]))
+    ahead = 4
+    start(loads[:ahead])
+    for n, (load, store) in enumerate(zip(loads, stores)):
         load.wait()
         store.start()
+        start(loads[n + ahead:n + ahead + 1])
     wait(stores)
 
 
@@ -938,7 +969,7 @@
         in_specs=[ANYWHERE] * len(arrays),
         out_specs=[ANYWHERE] * len(arrays),
         out_shape=[sds(t.shape, t.dtype) for t in arrays],
-        scratch_shapes=[pltpu.VMEM(t.shape, t.dtype) for t in arrays] + [DMA((len(arrays),)), DMA((len(arrays),))],
+        scratch_shapes=[pltpu.VMEM(t.shape, t.dtype) for t in arrays] + [DMA((2 * len(arrays),)), DMA((2 * len(arrays),))],
         compiler_params=params(),
         cost_estimate=cost(1e9, 16e6),
         name="deliver",

time: 425 us -> 421 us (level)
  no operation moved by 1% of the time
where the time goes in v10:
time: 421 us; the launch traced here: 420 us
  Pallas kernels  416 us (99%)
    pallas_call x1, Pallas kernels, forward(): pl.pallas_call(forward_kernel, grid=(8 * NB,), in_specs=[whole(1, HD), ws...  147 us
    pallas_call x2, Pallas kernels, backward(): pl.pallas_call(functools.partial(backward_kernel, b), grid=(2, NB), in_sp...  126 us
    pallas_call x1, Pallas kernels, grads(): pl.pallas_call(grads_kernel, in_specs=[far] * 13 + [vm], out_specs=[far]...  102 us
    pallas_call x1, Pallas kernels, out_block(): pl.pallas_call(out_kernel, grid=(2,), in_specs=[batch, batch, batch, whol...  34.6 us

profile of v10, /device:TPU:0, one launch (start us, length us, event | category | flops | bytes accessed | tf_op | source)
XLA Modules:
  0.0 419.6 jit_solution(11920122396405936482)
XLA Ops:
  0.6 0.7 maximum_convert_fusion
  1.4 0.6 reshape.26.gains_ref
  2.0 147.0 %forward.1 = (f32[2048,128]{1,0:T(8,128)}, f32[2048,128]{1,0:T(8,128)}, f32[2,8,512]{2,1,0:T(8,128)}, bf16[2,2048,256]{2,1,0:T(8,128)(2,1)}, f32[2,8,512]{2,1,0:...) custom-call(f32[1,128]{1,0:T(1,128)} %constant.2.clone.freq_ref, ...), custom_call_target="tpu_custom_call" | custom-call | flops 60000002048 | bytes 60000000 | tf_op jit(solution)/shard_map/forward/pallas_call | solution.py:427
  148.9 34.6 %out_block.1 = (bf16[2,256,2048]{2,1,0:T(8,128)(2,1)}, bf16[2,256,2048]{2,1,0:T(8,128)(2,1)}, f32[8,256]{1,0:T(8,128)}, bf16[2048,2048]{1,0:T(8,128)(2,1)}) custom-call(bf16[2,256,2048]{2,1,0:T(8,128)(2,1)} %get-tuple-element.45.o_ref, bf16[2,256,2048]{2,1,0:T(8,128)(2,1)} %x_ref.3, bf16[2,256,2048]{2,1,0:T(8,128)(2,1)} %dy_ref.3, ...), custom_call_target="tpu_custom_call" | custom-call | flops 13589934080 | bytes 18000000 | tf_op jit(solution)/shard_map/out_block/pallas_call | solution.py:503
  183.6 66.5 %backward.2 = (bf16[2048,768]{1,0:T(8,128)(2,1)}, bf16[2048,768]{1,0:T(8,128)(2,1)}, f32[8,256]{1,0:T(8,128)}, f32[8,256]{1,0:T(8,128)}, bf16[2048,2048]{1,0:T(8...) custom-call(bf16[2,3,2048,256]{3,2,1,0:T(8,128)(2,1)} %get-tuple-element.48.qk, ...), custom_call_target="tpu_custom_call", output_to_operand_aliasing={{6}: (12, {})} | custom-call | flops 24999999488 | bytes 30000000 | tf_op jit(solution)/shard_map/backward/pallas_call | solution.py:743
  250.1 0.0 copy-start.1
  250.1 59.0 %backward.3 = (bf16[2048,768]{1,0:T(8,128)(2,1)}, bf16[2048,768]{1,0:T(8,128)(2,1)}, f32[8,256]{1,0:T(8,128)}, f32[8,256]{1,0:T(8,128)}, f32[2,512,1024]{2,1,0:T(8,128)}) custom-call(bf16[2,3,2048,256]{3,2,1,0:T(8,128)(2,1)} %get-tuple-element.48.qkv_ref, bf16[256,2048]{1,0:T(8,128)(2,1)} %wo_ref.5, f32[2,8,512]{2,1,0:T(8,128)} %get-tuple-element.49.lse_ref, ...), custom_call_target="tpu_custom_call" | custom-call | flops 24999999488 | bytes 30000000 | tf_op jit(solution)/shard_map/backward/pallas_call | solution.py:743
  309.1 0.0 copy-done.1
  309.1 0.7 add_convert_fusion
  309.8 0.5 slice_reduce_fusion
  310.4 101.8 %grads.1 = (bf16[2,256,2048]{2,1,0:T(8,128)(2,1)}, bf16[2048,256]{1,0:T(8,128)(2,1)}, bf16[2048,256]{1,0:T(8,128)(2,1)}, bf16[2048,256]{1,0:T(8,128)(2,1)}, bf16[256,2048]{1,0:T(8,128)(2,1)}) custom-call(bf16[2048,768]{1,0:T(8,128)(2,1)} %get-tuple-element.57.rest_0_.d0, bf16[2048,768]{1,0:T(8,128)(2,1)} %get-tuple-element.61.d1, ...), custom_call_target="tpu_custom_call" | custom-call | flops 99999997952 | bytes 40000000 | tf_op jit(solution)/shard_map/grads/pallas_call | solution.py:929
  412.2 0.0 copy-start
  412.2 6.8 %deliver.1 = (bf16[2,256,2048]{2,1,0:T(8,128)(2,1)}, bf16[2,256,2048]{2,1,0:T(8,128)(2,1)}, bf16[2048,256]{1,0:T(8,128)(2,1)}, bf16[2048,256]{1,0:T(8,128)(2,1)}...) custom-call(bf16[2,256,2048]{2,1,0:T(8,128)(2,1)} %get-tuple-element.47.refs_0_, ...), custom_call_target="tpu_custom_call" | custom-call | flops 1000000000 | bytes 16000000 | tf_op jit(solution)/shard_map/deliver/pallas_call | solution.py:967
  418.9 0.0 copy-done
  419.0 0.6 copy.20
  (1 shorter events, 0.0 us)
Async XLA Ops:
  250.1 59.1 %copy-start.1 = (f32[8,256]{1,0:T(8,128)S(1)}, f32[8,256]{1,0:T(8,128)}, u32[]{:S(2)}) copy-start(f32[8,256]{1,0:T(8,128)} %get-tuple-element.78) | copy-start | bytes 24580
  412.2 6.8 %copy-start = (f32[8,256]{1,0:T(8,128)S(1)}, f32[8,256]{1,0:T(8,128)}, u32[]{:S(2)}) copy-start(f32[8,256]{1,0:T(8,128)} %get-tuple-element.80) | copy-start | bytes 24580

commit v11 on v10

--- a/solution.py
+++ b/solution.py
@@ -157,6 +157,11 @@
     for start in range(HD, vals.shape[1], HD):
         folded = folded + vals[:, start:start + HD]
     return jnp.sum(folded.T, axis=0, keepdims=True)
+
+
+def columns_of(rows):
+    turned = rows.T
+    return [jnp.broadcast_to(turned[:, c:c + 1], (rows.shape[1], HD)) for c in range(rows.shape[0])]
 
 
 def as_column(row):
@@ -517,7 +522,7 @@
 def backward_kernel(b, qkv_ref, wo_ref, lse_ref, raw_hbm, inv_ref, gains_ref, cos_hbm, sin_hbm, gga_ref,
                     wq_ref, wk_ref, wv_ref, da_ref, *rest):
     if b:
-        d0_ref, pd0_ref, pw_ref, d_ref, pd_ref, gg_ref, gout_ref, got_ref, w_all, d_two, sbuf, *rest = rest
+        d0_ref, pd0_ref, pw_ref, d_ref, pd_ref, gg_ref, gout_ref, got_ref, da_ref, buf0, w_all, d_two, sbuf, *rest = rest
     else:
         shard_ref, d_ref, pd_ref, gg_ref, gout_ref, full_ref, pw_ref, da_ref, buf0, buf1, w_half, *rest = rest
     (p_scr, dp_scr, kt_scr, dqt_scr, dq_scr, dk_scr, dv_scr, du_scr, d_scr, dh_scr, dbuf, dots_scr, total, slot, ga_slot,
@@ -538,6 +543,8 @@
     core, partner, first_dev, _ = route(me)
     weights = (wq_ref, wk_ref, wv_ref)
 
+    bg0 = (*bg_sems[:3], buf0)
+    older3 = stage3(me, da_ref, bg0)
     if b:
         operands = []
         for blk, chip in enumerate((peer_of(me, 6) // 2, first_dev // 2)):
@@ -551,8 +558,8 @@
             recv_sem=rs_sems.at[3 + n], device_id=(first_dev,), device_id_type=MESH)
             for n, (blk, lo, count) in enumerate(((0, 0, BLK), (1, 0, BLK // 2), (1, BLK // 2, BLK // 2)))]
     else:
-        bg0, bg = (*bg_sems[:3], buf0), (*bg_sems[3:], buf1)
-        older2, older3 = stage2(me, da_ref, bg0), stage3(me, da_ref, bg0)
+        bg = (*bg_sems[3:], buf1)
+        older2 = stage2(me, da_ref, bg0)
         gather = stage1(me, shard_ref.at[1], full_ref, bg)
         operands = [pltpu.make_async_copy(w.at[half_rows(1 - core), :], w_half.at[:, pl.ds(n * LOC, LOC)], ld_sems.at[n])
                     for n, w in enumerate(weights)]
@@ -565,8 +572,10 @@
         if b:
             start(operands)
             fetch(0).start()
+            older3.load()
             start(tables)
             entry_barrier(me)
+            older3.send()
             wait(operands)
             for blk in range(2):
                 sbuf[blk] = dot(d_two[blk, 0], w_all[0], NT) + dot(d_two[blk, 1], w_all[1], NT)
@@ -584,25 +593,17 @@
             start(moved)
         dots_scr[...] = jnp.zeros_like(dots_scr)
 
-    if not b:
-        @pl.when(jnp.logical_and(h == 0, step == NB - 1))
-        def _():
-            older3.wait()
-            fetch(NB - 1).start()
-
-        @pl.when(jnp.logical_and(h == 1, step == 2))
-        def _():
-            gather.wait()
-            more = stage2(me, full_ref, bg)
-            more.load()
-            more.send()
+    @pl.when(jnp.logical_and(h == 0, step == NB - 1))
+    def _():
+        older3.wait()
+        fetch(NB - 1).start()
 
     @pl.when(h == 0)
     def _():
         fetch(step).wait()
         dh_scr[block_rows(qi), :] = dot(dbuf[step % 2], wo_ref[...], NT).astype(BF)
         if b:
-            @pl.when(step < NB - 1)
+            @pl.when(step < NB - 2)
             def _():
                 fetch(step + 1).start()
         else:
@@ -667,20 +668,18 @@
             wait(tables)
 
 
-        def tail(i, carry):
-            rows = block_rows(i)
+        inverse = columns_of(inv_ref[...])
+        for i in range(NB):
+            rows = pl.ds(i * BLK, BLK)
             cos, sin = cos_ref[rows, :], sin_ref[rows, :]
             for n, from_scr in enumerate((dq_scr, dk_scr)):
                 d = from_scr[rows, :]
                 hat = d * cos - pltpu.roll(d, HD // 2, 1) * sin
-                unit = raw_ref[n, rows, cols] * as_column(inv_ref[pl.ds(i + n * NB, 1), :])
+                unit = raw_ref[n, rows, cols] * inverse[i + n * NB]
                 gg_ref[n:n + 1, :] += jnp.sum(hat * unit, axis=0, keepdims=True)
                 du = hat * gains_ref[n:n + 1, :]
                 du_scr[n, h, rows, :] = du
-                dots_scr[pl.ds(i + n * NB, 1), :] += row_sums(du * unit)
-            return carry
-
-        lax.fori_loop(0, NB, tail, 0)
+                dots_scr[i + n * NB:i + n * NB + 1, :] += row_sums(du * unit)
 
     @pl.when(jnp.logical_and(h == 1, step == NB - 1))
     def _():
@@ -688,12 +687,12 @@
         start(sums)
         if b:
             moved[2].start()
+        else:
+            gather.wait()
+            more = stage2(me, full_ref, bg)
+            more.load()
+            more.send()
         wait(sums)
-        if not b:
-            stage2(me, full_ref, bg).wait()
-            last_stage = stage3(me, full_ref, bg)
-            last_stage.load()
-            last_stage.send()
         total[...] = ordered_total(me, dots_scr, slot) / DIM
         gout_ref[...] = ordered_total(me, gga_ref, ga_slot)
 
@@ -704,25 +703,22 @@
                         src_ref=d_scr.at[rows, :], dst_ref=pd_ref.at[rows, :], send_sem=pd_send.at[i],
                         recv_sem=pd_recv.at[i], device_id=(peer_of(me, 1),), device_id_type=MESH)]
 
-        def last(i, carry):
-            rows = block_rows(i)
+        inverse, dots = columns_of(inv_ref[...]), columns_of(total[...])
+        for i in range(NB):
+            rows = pl.ds(i * BLK, BLK)
             for n in range(2):
-                dots = as_column(total[pl.ds(i + n * NB, 1), :])
-                inv = as_column(inv_ref[pl.ds(i + n * NB, 1), :])
+                inv = inverse[i + n * NB]
                 for hh in range(LOC // HD):
                     sl = slice(hh * HD, (hh + 1) * HD)
                     unit = raw_ref[n, rows, sl] * inv
-                    val = inv * (du_scr[n, hh, rows, :] - unit * dots)
+                    val = inv * (du_scr[n, hh, rows, :] - unit * dots[i + n * NB])
                     d_scr[rows, n * LOC + hh * HD:n * LOC + (hh + 1) * HD] = val.astype(BF)
             start(copies(i))
-            return carry
-
-        lax.fori_loop(0, NB, last, 0)
         for i in range(NB):
             wait(copies(i))
         wait(moved)
         if not b:
-            last_stage.wait()
+            more.wait()
 
 
 def backward(b, da, qkv, wo, lse, raw, inv, gains, cos, sin, gga, weights, others, cid):
@@ -735,8 +731,8 @@
     gsp = whole(8, DIM // 8)
     half = (DIM // 2, 3 * LOC)
     if b:
-        extra = [sds((2, BLK, DIM // 2), F32)]
-        own = [pltpu.VMEM((2,) + half, BF), pltpu.VMEM((2, 2, BLK, 3 * LOC), BF), pltpu.VMEM((2, BLK, DIM // 2), F32)]
+        extra = [sds((2, BLK, DIM // 2), F32), sds((SEQ, DIM), BF)]
+        own = [pltpu.VMEM((2, TOK, DIM), BF), pltpu.VMEM((2,) + half, BF), pltpu.VMEM((2, 2, BLK, 3 * LOC), BF), pltpu.VMEM((2, BLK, DIM // 2), F32)]
     else:
         extra = [sds((SEQ, DIM), BF), sds(half, BF), sds((SEQ, DIM), BF)]
         own = [pltpu.VMEM((2, TOK, DIM), BF), pltpu.VMEM((2, TOK, DIM), BF), pltpu.VMEM(half, BF)]
@@ -750,7 +746,7 @@
         + [ANYWHERE] * (4 + len(others)),
         out_specs=[ANYWHERE, ANYWHERE, pl.BlockSpec((8, HD), lambda h, i: (0, h)), gsp] + [ANYWHERE] * len(extra),
         out_shape=[sds((SEQ, 3 * LOC), BF), sds((SEQ, 3 * LOC), BF), sds((8, LOC), F32), sds((8, DIM // 8), F32)] + extra,
-        input_output_aliases={} if b else {12: 6},
+        input_output_aliases={12: 5 if b else 6},
         scratch_shapes=own + [
             pltpu.VMEM((NB, BLK, BLK), F32), pltpu.VMEM((NB, BLK, BLK), F32), pltpu.VMEM((HD, SEQ), BF),
             pltpu.VMEM((HD, BLK), F32), pltpu.VMEM((SEQ, HD), F32), pltpu.VMEM((SEQ, HD), F32),
@@ -759,7 +755,7 @@
             pltpu.VMEM((NDEV - 1, 2 * NB, BLK), F32), pltpu.VMEM((NDEV - 1, 8, DIM // 8), F32),
             DMA((2, NDEV - 1)), DMA((2, NDEV - 1)), DMA((NB,)), DMA((NB,)), DMA((NB,)), DMA((6,)), DMA((8,)), DMA((2,)),
             pltpu.VMEM((2, SEQ, LOC), F32), pltpu.VMEM((SEQ, HD), F32), pltpu.VMEM((SEQ, HD), F32), DMA((3,))]
-        + ([] if b else BG_SEMS * 2),
+        + BG_SEMS * (1 if b else 2),
         compiler_params=params(dimension_semantics=("arbitrary", "arbitrary"), collective_id=cid, has_side_effects=True),
         cost_estimate=cost(25e9, 30e6),
         name="backward",
@@ -983,7 +979,7 @@
     y, da, gga, da0 = out_block(o_recv, wo_full, x_loc, dy_loc, gains, 1)
     state = (qkv, wo, lse, raw, inv, gains, cos, sin, gga, weights)
     d0, pd0, gg0, gout, da1, pw, da0 = backward(0, da0, *state, (da,), 2)
-    d1, pd1, gg1, _, got = backward(1, da1, *state, (d0, pd0, pw), 3)
+    d1, pd1, gg1, _, got, da1 = backward(1, da1, *state, (d0, pd0, pw), 3)
     grad_ga = gout.reshape(DIM).astype(BF)
     big = grads(d0, d1, pd0, pd1, *weights, pw, got, x_full, o, da0, da1, dy_loc, 4)
     y, dx, gwq, gwk, gwv, gwo = deliver(y, *big)

time: 421 us -> 417 us (level)
  no operation moved by 1% of the time
where the time goes in v11:
time: 417 us; the launch traced here: 416 us
  Pallas kernels  412 us (99%)
    pallas_call x1, Pallas kernels, forward(): pl.pallas_call(forward_kernel, grid=(8 * NB,), in_specs=[whole(1, HD), ws...  147 us
    pallas_call x2, Pallas kernels, backward(): pl.pallas_call(functools.partial(backward_kernel, b), grid=(2, NB), in_sp...  122 us
    pallas_call x1, Pallas kernels, grads(): pl.pallas_call(grads_kernel, in_specs=[far] * 13 + [vm], out_specs=[far]...  102 us
    pallas_call x1, Pallas kernels, out_block(): pl.pallas_call(out_kernel, grid=(2,), in_specs=[batch, batch, batch, whol...  34.6 us

profile of v11, /device:TPU:0, one launch (start us, length us, event | category | flops | bytes accessed | tf_op | source)
XLA Modules:
  0.0 415.7 jit_solution(7202743701650284310)
XLA Ops:
  0.6 0.7 maximum_convert_fusion
  1.4 0.6 reshape.26.gains_ref
  2.0 147.0 %forward.1 = (f32[2048,128]{1,0:T(8,128)}, f32[2048,128]{1,0:T(8,128)}, f32[2,8,512]{2,1,0:T(8,128)}, bf16[2,2048,256]{2,1,0:T(8,128)(2,1)}, f32[2,8,512]{2,1,0:...) custom-call(f32[1,128]{1,0:T(1,128)} %constant.2.clone.freq_ref, ...), custom_call_target="tpu_custom_call" | custom-call | flops 60000002048 | bytes 60000000 | tf_op jit(solution)/shard_map/forward/pallas_call | solution.py:432
  148.9 34.6 %out_block.1 = (bf16[2,256,2048]{2,1,0:T(8,128)(2,1)}, bf16[2,256,2048]{2,1,0:T(8,128)(2,1)}, f32[8,256]{1,0:T(8,128)}, bf16[2048,2048]{1,0:T(8,128)(2,1)}) custom-call(bf16[2,256,2048]{2,1,0:T(8,128)(2,1)} %get-tuple-element.46.o_ref, bf16[2,256,2048]{2,1,0:T(8,128)(2,1)} %x_ref.3, bf16[2,256,2048]{2,1,0:T(8,128)(2,1)} %dy_ref.3, ...), custom_call_target="tpu_custom_call" | custom-call | flops 13589934080 | bytes 18000000 | tf_op jit(solution)/shard_map/out_block/pallas_call | solution.py:508
  183.6 61.4 %backward.2 = (bf16[2048,768]{1,0:T(8,128)(2,1)}, bf16[2048,768]{1,0:T(8,128)(2,1)}, f32[8,256]{1,0:T(8,128)}, f32[8,256]{1,0:T(8,128)}, bf16[2048,2048]{1,0:T(8...) custom-call(bf16[2,3,2048,256]{3,2,1,0:T(8,128)(2,1)} %get-tuple-element.49.qk, ...), custom_call_target="tpu_custom_call", output_to_operand_aliasing={{6}: (12, {})} | custom-call | flops 24999999488 | bytes 30000000 | tf_op jit(solution)/shard_map/backward/pallas_call | solution.py:739
  245.0 0.0 copy-start.1
  245.0 60.4 %backward.3 = (bf16[2048,768]{1,0:T(8,128)(2,1)}, bf16[2048,768]{1,0:T(8,128)(2,1)}, f32[8,256]{1,0:T(8,128)}, f32[8,256]{1,0:T(8,128)}, f32[2,512,1024]{2,1,0:T(8,128)}, /*index=5*/bf16[2048,2048]{1,0:T(8,128)(2,1)}) custom-call(bf16[2,3,2048,256]{3,2,1,0:T(8,128)(2,1)} %get-tuple-element.49.qkv_ref, ...), custom_call_target="tpu_custom_call", output_to_operand_aliasing={{5}: (12, {})} | custom-call | flops 24999999488 | bytes 30000000 | tf_op jit(solution)/shard_map/backward/pallas_call | solution.py:739
  305.4 0.0 copy-done.1
  305.5 0.7 add_convert_fusion
  306.2 0.5 slice_reduce_fusion
  306.7 101.5 %grads.1 = (bf16[2,256,2048]{2,1,0:T(8,128)(2,1)}, bf16[2048,256]{1,0:T(8,128)(2,1)}, bf16[2048,256]{1,0:T(8,128)(2,1)}, bf16[2048,256]{1,0:T(8,128)(2,1)}, bf16[256,2048]{1,0:T(8,128)(2,1)}) custom-call(bf16[2048,768]{1,0:T(8,128)(2,1)} %get-tuple-element.58.rest_0_.d0, bf16[2048,768]{1,0:T(8,128)(2,1)} %get-tuple-element.62.d1, ...), custom_call_target="tpu_custom_call" | custom-call | flops 99999997952 | bytes 40000000 | tf_op jit(solution)/shard_map/grads/pallas_call | solution.py:925
  408.2 0.0 copy-start
  408.3 6.8 %deliver.1 = (bf16[2,256,2048]{2,1,0:T(8,128)(2,1)}, bf16[2,256,2048]{2,1,0:T(8,128)(2,1)}, bf16[2048,256]{1,0:T(8,128)(2,1)}, bf16[2048,256]{1,0:T(8,128)(2,1)}...) custom-call(bf16[2,256,2048]{2,1,0:T(8,128)(2,1)} %get-tuple-element.48.refs_0_, ...), custom_call_target="tpu_custom_call" | custom-call | flops 1000000000 | bytes 16000000 | tf_op jit(solution)/shard_map/deliver/pallas_call | solution.py:963
  415.0 0.0 copy-done
  415.1 0.6 copy.21
  (1 shorter events, 0.0 us)
Async XLA Ops:
  245.0 60.5 %copy-start.1 = (f32[8,256]{1,0:T(8,128)S(1)}, f32[8,256]{1,0:T(8,128)}, u32[]{:S(2)}) copy-start(f32[8,256]{1,0:T(8,128)} %get-tuple-element.80) | copy-start | bytes 24580
  408.2 6.8 %copy-start = (f32[8,256]{1,0:T(8,128)S(1)}, f32[8,256]{1,0:T(8,128)}, u32[]{:S(2)}) copy-start(f32[8,256]{1,0:T(8,128)} %get-tuple-element.82) | copy-start | bytes 24580

commit v12 on v11

--- a/solution.py
+++ b/solution.py
@@ -57,11 +57,13 @@
 ORDER = (6, 7, 2, 4, 3, 5, 1)
 
 
-def entry_barrier(me):
-    barrier = pltpu.get_barrier_semaphore()
+def entry_signal(me):
     for mask in ORDER:
-        pl.semaphore_signal(barrier, inc=1, device_id=(peer_of(me, mask),), device_id_type=MESH)
-    pl.semaphore_wait(barrier, NDEV - 1)
+        pl.semaphore_signal(pltpu.get_barrier_semaphore(), inc=1, device_id=(peer_of(me, mask),), device_id_type=MESH)
+
+
+def entry_wait():
+    pl.semaphore_wait(pltpu.get_barrier_semaphore(), NDEV - 1)
 
 
 def nbr_signal(me):
@@ -245,8 +247,9 @@
     @pl.when(g == 0)
     def _():
         first = stage1(me, x_ref.at[0], x0f, bg0)
+        entry_signal(me)
         first.load()
-        entry_barrier(me)
+        entry_wait()
         first.send()
         x_gather(0).load()
         freq = freq_ref[...]
@@ -556,7 +559,7 @@
         moved = [pltpu.make_async_remote_copy(
             src_ref=sbuf.at[blk, pl.ds(lo, count), :], dst_ref=got_ref.at[blk, pl.ds(lo, count), :], send_sem=rs_sems.at[n],
             recv_sem=rs_sems.at[3 + n], device_id=(first_dev,), device_id_type=MESH)
-            for n, (blk, lo, count) in enumerate(((0, 0, BLK), (1, 0, BLK // 2), (1, BLK // 2, BLK // 2)))]
+            for n, (blk, lo, count) in enumerate(((0, 0, BLK), (1, 0, BLK * 3 // 4), (1, BLK * 3 // 4, BLK // 4)))]
     else:
         bg = (*bg_sems[3:], buf1)
         older2 = stage2(me, da_ref, bg0)
@@ -569,24 +572,29 @@
 
     @pl.when(jnp.logical_and(h == 0, step == 0))
     def _():
+        entry_signal(me)
         if b:
-            start(operands)
+            needed, rest_of = operands[:2] + operands[4:], operands[2:4]
+            start(needed)
             fetch(0).start()
+            start(rest_of)
             older3.load()
             start(tables)
-            entry_barrier(me)
+            wait(needed)
+            sbuf[0] = dot(d_two[0, 0], w_all[0], NT) + dot(d_two[0, 1], w_all[1], NT)
+            entry_wait()
+            moved[0].start()
             older3.send()
-            wait(operands)
-            for blk in range(2):
-                sbuf[blk] = dot(d_two[blk, 0], w_all[0], NT) + dot(d_two[blk, 1], w_all[1], NT)
-                moved[blk].start()
+            wait(rest_of)
+            sbuf[1] = dot(d_two[1, 0], w_all[0], NT) + dot(d_two[1, 1], w_all[1], NT)
+            moved[1].start()
         else:
             older2.load()
             fetch(0).start()
             gather.load()
             start(operands)
             start(tables)
-            entry_barrier(me)
+            entry_wait()
             older2.send()
             gather.send()
             wait(operands)
@@ -683,7 +691,8 @@
 
     @pl.when(jnp.logical_and(h == 1, step == NB - 1))
     def _():
-        sums = exchange(me, [dots_scr, gga_ref], [slot, ga_slot], ex_send, ex_recv)
+        srcs, slots = ([dots_scr], [slot]) if b else ([dots_scr, gga_ref], [slot, ga_slot])
+        sums = exchange(me, srcs, slots, ex_send, ex_recv)
         start(sums)
         if b:
             moved[2].start()
@@ -694,7 +703,7 @@
             more.send()
         wait(sums)
         total[...] = ordered_total(me, dots_scr, slot) / DIM
-        gout_ref[...] = ordered_total(me, gga_ref, ga_slot)
+        gout_ref[...] = gga_ref[...] if b else ordered_total(me, gga_ref, ga_slot)
 
         def copies(i):
             rows = block_rows(i)

time: 417 us -> 415 us (level)
  no operation moved by 1% of the time
where the time goes in v12:
time: 415 us; the launch traced here: 414 us
  Pallas kernels  410 us (99%)
    pallas_call x1, Pallas kernels, forward(): pl.pallas_call(forward_kernel, grid=(8 * NB,), in_specs=[whole(1, HD), ws...  147 us
    pallas_call x2, Pallas kernels, backward(): pl.pallas_call(functools.partial(backward_kernel, b), grid=(2, NB), in_sp...  119 us
    pallas_call x1, Pallas kernels, grads(): pl.pallas_call(grads_kernel, in_specs=[far] * 13 + [vm], out_specs=[far]...  102 us
    pallas_call x1, Pallas kernels, out_block(): pl.pallas_call(out_kernel, grid=(2,), in_specs=[batch, batch, batch, whol...  34.6 us

profile of v12, /device:TPU:0, one launch (start us, length us, event | category | flops | bytes accessed | tf_op | source)
XLA Modules:
  0.0 413.6 jit_solution(6378627492397001273)
XLA Ops:
  0.6 0.7 maximum_convert_fusion
  1.4 0.6 reshape.26.gains_ref
  2.0 147.0 %forward.1 = (f32[2048,128]{1,0:T(8,128)}, f32[2048,128]{1,0:T(8,128)}, f32[2,8,512]{2,1,0:T(8,128)}, bf16[2,2048,256]{2,1,0:T(8,128)(2,1)}, f32[2,8,512]{2,1,0:...) custom-call(f32[1,128]{1,0:T(1,128)} %constant.2.clone.freq_ref, ...), custom_call_target="tpu_custom_call" | custom-call | flops 60000002048 | bytes 60000000 | tf_op jit(solution)/shard_map/forward/pallas_call | solution.py:435
  148.9 34.6 %out_block.1 = (bf16[2,256,2048]{2,1,0:T(8,128)(2,1)}, bf16[2,256,2048]{2,1,0:T(8,128)(2,1)}, f32[8,256]{1,0:T(8,128)}, bf16[2048,2048]{1,0:T(8,128)(2,1)}) custom-call(bf16[2,256,2048]{2,1,0:T(8,128)(2,1)} %get-tuple-element.46.o_ref, bf16[2,256,2048]{2,1,0:T(8,128)(2,1)} %x_ref.3, bf16[2,256,2048]{2,1,0:T(8,128)(2,1)} %dy_ref.3, ...), custom_call_target="tpu_custom_call" | custom-call | flops 13589934080 | bytes 18000000 | tf_op jit(solution)/shard_map/out_block/pallas_call | solution.py:511
  183.6 61.7 %backward.2 = (bf16[2048,768]{1,0:T(8,128)(2,1)}, bf16[2048,768]{1,0:T(8,128)(2,1)}, f32[8,256]{1,0:T(8,128)}, f32[8,256]{1,0:T(8,128)}, bf16[2048,2048]{1,0:T(8...) custom-call(bf16[2,3,2048,256]{3,2,1,0:T(8,128)(2,1)} %get-tuple-element.49.qk, ...), custom_call_target="tpu_custom_call", output_to_operand_aliasing={{6}: (12, {})} | custom-call | flops 24999999488 | bytes 30000000 | tf_op jit(solution)/shard_map/backward/pallas_call | solution.py:748
  245.3 0.0 copy-start.1
  245.3 57.5 %backward.3 = (bf16[2048,768]{1,0:T(8,128)(2,1)}, bf16[2048,768]{1,0:T(8,128)(2,1)}, f32[8,256]{1,0:T(8,128)}, f32[8,256]{1,0:T(8,128)}, f32[2,512,1024]{2,1,0:T(8,128)}, /*index=5*/bf16[2048,2048]{1,0:T(8,128)(2,1)}) custom-call(bf16[2,3,2048,256]{3,2,1,0:T(8,128)(2,1)} %get-tuple-element.49.qkv_ref, ...), custom_call_target="tpu_custom_call", output_to_operand_aliasing={{5}: (12, {})} | custom-call | flops 24999999488 | bytes 30000000 | tf_op jit(solution)/shard_map/backward/pallas_call | solution.py:748
  302.8 0.0 copy-done.1
  302.8 0.7 add_convert_fusion
  303.5 0.5 slice_reduce_fusion
  304.1 102.1 %grads.1 = (bf16[2,256,2048]{2,1,0:T(8,128)(2,1)}, bf16[2048,256]{1,0:T(8,128)(2,1)}, bf16[2048,256]{1,0:T(8,128)(2,1)}, bf16[2048,256]{1,0:T(8,128)(2,1)}, bf16[256,2048]{1,0:T(8,128)(2,1)}) custom-call(bf16[2048,768]{1,0:T(8,128)(2,1)} %get-tuple-element.58.rest_0_.d0, bf16[2048,768]{1,0:T(8,128)(2,1)} %get-tuple-element.62.d1, ...), custom_call_target="tpu_custom_call" | custom-call | flops 99999997952 | bytes 40000000 | tf_op jit(solution)/shard_map/grads/pallas_call | solution.py:934
  406.2 0.0 copy-start
  406.2 6.8 %deliver.1 = (bf16[2,256,2048]{2,1,0:T(8,128)(2,1)}, bf16[2,256,2048]{2,1,0:T(8,128)(2,1)}, bf16[2048,256]{1,0:T(8,128)(2,1)}, bf16[2048,256]{1,0:T(8,128)(2,1)}...) custom-call(bf16[2,256,2048]{2,1,0:T(8,128)(2,1)} %get-tuple-element.48.refs_0_, ...), custom_call_target="tpu_custom_call" | custom-call | flops 1000000000 | bytes 16000000 | tf_op jit(solution)/shard_map/deliver/pallas_call | solution.py:972
  413.0 0.0 copy-done
  413.0 0.6 copy.21
  (1 shorter events, 0.0 us)
Async XLA Ops:
  245.3 57.5 %copy-start.1 = (f32[8,256]{1,0:T(8,128)S(1)}, f32[8,256]{1,0:T(8,128)}, u32[]{:S(2)}) copy-start(f32[8,256]{1,0:T(8,128)} %get-tuple-element.80) | copy-start | bytes 24580
  406.2 6.8 %copy-start = (f32[8,256]{1,0:T(8,128)S(1)}, f32[8,256]{1,0:T(8,128)}, u32[]{:S(2)}) copy-start(f32[8,256]{1,0:T(8,128)} %get-tuple-element.82) | copy-start | bytes 24580

commit v13 on v12

--- a/solution.py
+++ b/solution.py
@@ -82,7 +82,7 @@
 
 
 def shard_rows(dev, lo=0, count=TOK):
-    return pl.ds(pl.multiple_of(dev * TOK + lo, HD), count)
+    return pl.ds(pl.multiple_of(dev * TOK + lo, TOK // 4), count)
 
 
 class Stage:
@@ -112,17 +112,20 @@
     return Stage(loads, copies + [pltpu.make_async_copy(mine, there, own.at[3 if part == 1 else 2])])
 
 
-def stage2(me, full, bg):
+def stage2(me, full, bg, part=None):
     send, recv, own, buf = bg
     xn, yn = peer_of(me, 2), peer_of(me, 4)
     half = TOK // 2
-    plan = ((1, half, half, yn, 2), (0, 0, half, xn, 4), (0, 0, TOK, xn, 1), (1, 0, TOK, yn, 1))
-    return Stage(
-        [pltpu.make_async_copy(full.at[shard_rows(dev), :], buf.at[n], own.at[n]) for n, dev in enumerate((xn, yn))],
-        [pltpu.make_async_remote_copy(
-            src_ref=buf.at[slot, pl.ds(lo, count), :], dst_ref=full.at[shard_rows(dev, lo, count), :],
-            send_sem=send.at[3 + k], recv_sem=recv.at[3 + k], device_id=(peer_of(me, mask),), device_id_type=MESH)
-         for k, (slot, lo, count, dev, mask) in enumerate(plan)])
+    lo, count = (0, half) if part is None else (part * (half // 2), half // 2)
+    at = 8 if part == 1 else 3
+    plan = [(1, half + lo, count, yn, 2, at), (0, lo, count, xn, 4, at + 1)]
+    if part != 0:
+        plan += [(0, 0, TOK, xn, 1, 5), (1, 0, TOK, yn, 1, 6)]
+    loads = [pltpu.make_async_copy(full.at[shard_rows(dev), :], buf.at[n], own.at[n]) for n, dev in enumerate((xn, yn))]
+    return Stage([] if part == 1 else loads, [pltpu.make_async_remote_copy(
+        src_ref=buf.at[slot, pl.ds(first, rows), :], dst_ref=full.at[shard_rows(dev, first, rows), :],
+        send_sem=send.at[sem], recv_sem=recv.at[sem], device_id=(peer_of(me, mask),), device_id_type=MESH)
+        for slot, first, rows, dev, mask, sem in plan])
 
 
 def stage3(me, full, bg):
@@ -601,6 +604,14 @@
             start(moved)
         dots_scr[...] = jnp.zeros_like(dots_scr)
 
+    if not b:
+        @pl.when(jnp.logical_and(h == 1, step == NB - 1))
+        def _():
+            gather.wait()
+            early = stage2(me, full_ref, bg, 0)
+            early.load()
+            early.send()
+
     @pl.when(jnp.logical_and(h == 0, step == NB - 1))
     def _():
         older3.wait()
@@ -697,10 +708,7 @@
         if b:
             moved[2].start()
         else:
-            gather.wait()
-            more = stage2(me, full_ref, bg)
-            more.load()
-            more.send()
+            stage2(me, full_ref, bg, 1).send()
         wait(sums)
         total[...] = ordered_total(me, dots_scr, slot) / DIM
         gout_ref[...] = gga_ref[...] if b else ordered_total(me, gga_ref, ga_slot)
@@ -727,7 +735,8 @@
             wait(copies(i))
         wait(moved)
         if not b:
-            more.wait()
+            stage2(me, full_ref, bg, 0).wait()
+            stage2(me, full_ref, bg, 1).wait()
 
 
 def backward(b, da, qkv, wo, lse, raw, inv, gains, cos, sin, gga, weights, others, cid):

time: 415 us -> 414 us (level)
  no operation moved by 1% of the time
where the time goes in v13:
time: 414 us; the launch traced here: 413 us
  Pallas kernels  409 us (99%)
    pallas_call x1, Pallas kernels, forward(): pl.pallas_call(forward_kernel, grid=(8 * NB,), in_specs=[whole(1, HD), ws...  147 us
    pallas_call x2, Pallas kernels, backward(): pl.pallas_call(functools.partial(backward_kernel, b), grid=(2, NB), in_sp...  119 us
    pallas_call x1, Pallas kernels, grads(): pl.pallas_call(grads_kernel, in_specs=[far] * 13 + [vm], out_specs=[far]...  102 us
    pallas_call x1, Pallas kernels, out_block(): pl.pallas_call(out_kernel, grid=(2,), in_specs=[batch, batch, batch, whol...  34.6 us

profile of v13, /device:TPU:0, one launch (start us, length us, event | category | flops | bytes accessed | tf_op | source)
XLA Modules:
  0.0 412.9 jit_solution(5843071599498392720)
XLA Ops:
  0.6 0.7 maximum_convert_fusion
  1.4 0.6 reshape.26.gains_ref
  2.0 147.0 %forward.1 = (f32[2048,128]{1,0:T(8,128)}, f32[2048,128]{1,0:T(8,128)}, f32[2,8,512]{2,1,0:T(8,128)}, bf16[2,2048,256]{2,1,0:T(8,128)(2,1)}, f32[2,8,512]{2,1,0:...) custom-call(f32[1,128]{1,0:T(1,128)} %constant.2.clone.freq_ref, ...), custom_call_target="tpu_custom_call" | custom-call | flops 60000002048 | bytes 60000000 | tf_op jit(solution)/shard_map/forward/pallas_call | solution.py:438
  148.9 34.6 %out_block.1 = (bf16[2,256,2048]{2,1,0:T(8,128)(2,1)}, bf16[2,256,2048]{2,1,0:T(8,128)(2,1)}, f32[8,256]{1,0:T(8,128)}, bf16[2048,2048]{1,0:T(8,128)(2,1)}) custom-call(bf16[2,256,2048]{2,1,0:T(8,128)(2,1)} %get-tuple-element.46.o_ref, bf16[2,256,2048]{2,1,0:T(8,128)(2,1)} %x_ref.3, bf16[2,256,2048]{2,1,0:T(8,128)(2,1)} %dy_ref.3, ...), custom_call_target="tpu_custom_call" | custom-call | flops 13589934080 | bytes 18000000 | tf_op jit(solution)/shard_map/out_block/pallas_call | solution.py:514
  183.6 60.9 %backward.2 = (bf16[2048,768]{1,0:T(8,128)(2,1)}, bf16[2048,768]{1,0:T(8,128)(2,1)}, f32[8,256]{1,0:T(8,128)}, f32[8,256]{1,0:T(8,128)}, bf16[2048,2048]{1,0:T(8...) custom-call(bf16[2,3,2048,256]{3,2,1,0:T(8,128)(2,1)} %get-tuple-element.49.qk, ...), custom_call_target="tpu_custom_call", output_to_operand_aliasing={{6}: (12, {})} | custom-call | flops 24999999488 | bytes 30000000 | tf_op jit(solution)/shard_map/backward/pallas_call | solution.py:757
  244.5 0.0 copy-start.1
  244.5 57.7 %backward.3 = (bf16[2048,768]{1,0:T(8,128)(2,1)}, bf16[2048,768]{1,0:T(8,128)(2,1)}, f32[8,256]{1,0:T(8,128)}, f32[8,256]{1,0:T(8,128)}, f32[2,512,1024]{2,1,0:T(8,128)}, /*index=5*/bf16[2048,2048]{1,0:T(8,128)(2,1)}) custom-call(bf16[2,3,2048,256]{3,2,1,0:T(8,128)(2,1)} %get-tuple-element.49.qkv_ref, ...), custom_call_target="tpu_custom_call", output_to_operand_aliasing={{5}: (12, {})} | custom-call | flops 24999999488 | bytes 30000000 | tf_op jit(solution)/shard_map/backward/pallas_call | solution.py:757
  302.3 0.0 copy-done.1
  302.3 0.7 add_convert_fusion
  303.0 0.5 slice_reduce_fusion
  303.5 102.0 %grads.1 = (bf16[2,256,2048]{2,1,0:T(8,128)(2,1)}, bf16[2048,256]{1,0:T(8,128)(2,1)}, bf16[2048,256]{1,0:T(8,128)(2,1)}, bf16[2048,256]{1,0:T(8,128)(2,1)}, bf16[256,2048]{1,0:T(8,128)(2,1)}) custom-call(bf16[2048,768]{1,0:T(8,128)(2,1)} %get-tuple-element.58.rest_0_.d0, bf16[2048,768]{1,0:T(8,128)(2,1)} %get-tuple-element.62.d1, ...), custom_call_target="tpu_custom_call" | custom-call | flops 99999997952 | bytes 40000000 | tf_op jit(solution)/shard_map/grads/pallas_call | solution.py:943
  405.5 0.0 copy-start
  405.5 6.8 %deliver.1 = (bf16[2,256,2048]{2,1,0:T(8,128)(2,1)}, bf16[2,256,2048]{2,1,0:T(8,128)(2,1)}, bf16[2048,256]{1,0:T(8,128)(2,1)}, bf16[2048,256]{1,0:T(8,128)(2,1)}...) custom-call(bf16[2,256,2048]{2,1,0:T(8,128)(2,1)} %get-tuple-element.48.refs_0_, ...), custom_call_target="tpu_custom_call" | custom-call | flops 1000000000 | bytes 16000000 | tf_op jit(solution)/shard_map/deliver/pallas_call | solution.py:981
  412.3 0.0 copy-done
  412.3 0.6 copy.21
  (1 shorter events, 0.0 us)
Async XLA Ops:
  244.5 57.8 %copy-start.1 = (f32[8,256]{1,0:T(8,128)S(1)}, f32[8,256]{1,0:T(8,128)}, u32[]{:S(2)}) copy-start(f32[8,256]{1,0:T(8,128)} %get-tuple-element.80) | copy-start | bytes 24580
  405.5 6.8 %copy-start = (f32[8,256]{1,0:T(8,128)S(1)}, f32[8,256]{1,0:T(8,128)}, u32[]{:S(2)}) copy-start(f32[8,256]{1,0:T(8,128)} %get-tuple-element.82) | copy-start | bytes 24580

commit v14 on v13

--- a/solution.py
+++ b/solution.py
@@ -968,7 +968,7 @@
             n = len(loads)
             loads.append(pltpu.make_async_copy(src.at[piece], buf.at[piece], refs[-2].at[n]))
             stores.append(pltpu.make_async_copy(buf.at[piece], dst.at[piece], refs[-1].at[n]))
-    ahead = 4
+    ahead = len(loads)
     start(loads[:ahead])
     for n, (load, store) in enumerate(zip(loads, stores)):
         load.wait()

time: 414 us -> 414 us (level)
  no operation moved by 1% of the time
where the time goes in v14:
time: 414 us; the launch traced here: 413 us
  Pallas kernels  409 us (99%)
    pallas_call x1, Pallas kernels, forward(): pl.pallas_call(forward_kernel, grid=(8 * NB,), in_specs=[whole(1, HD), ws...  147 us
    pallas_call x2, Pallas kernels, backward(): pl.pallas_call(functools.partial(backward_kernel, b), grid=(2, NB), in_sp...  119 us
    pallas_call x1, Pallas kernels, grads(): pl.pallas_call(grads_kernel, in_specs=[far] * 13 + [vm], out_specs=[far]...  102 us
    pallas_call x1, Pallas kernels, out_block(): pl.pallas_call(out_kernel, grid=(2,), in_specs=[batch, batch, batch, whol...  34.6 us

profile of v14, /device:TPU:0, one launch (start us, length us, event | category | flops | bytes accessed | tf_op | source)
XLA Modules:
  0.0 412.8 jit_solution(12263824965599925554)
XLA Ops:
  0.6 0.7 maximum_convert_fusion
  1.4 0.6 reshape.26.gains_ref
  2.0 147.0 %forward.1 = (f32[2048,128]{1,0:T(8,128)}, f32[2048,128]{1,0:T(8,128)}, f32[2,8,512]{2,1,0:T(8,128)}, bf16[2,2048,256]{2,1,0:T(8,128)(2,1)}, f32[2,8,512]{2,1,0:...) custom-call(f32[1,128]{1,0:T(1,128)} %constant.2.clone.freq_ref, ...), custom_call_target="tpu_custom_call" | custom-call | flops 60000002048 | bytes 60000000 | tf_op jit(solution)/shard_map/forward/pallas_call | solution.py:438
  148.9 34.6 %out_block.1 = (bf16[2,256,2048]{2,1,0:T(8,128)(2,1)}, bf16[2,256,2048]{2,1,0:T(8,128)(2,1)}, f32[8,256]{1,0:T(8,128)}, bf16[2048,2048]{1,0:T(8,128)(2,1)}) custom-call(bf16[2,256,2048]{2,1,0:T(8,128)(2,1)} %get-tuple-element.46.o_ref, bf16[2,256,2048]{2,1,0:T(8,128)(2,1)} %x_ref.3, bf16[2,256,2048]{2,1,0:T(8,128)(2,1)} %dy_ref.3, ...), custom_call_target="tpu_custom_call" | custom-call | flops 13589934080 | bytes 18000000 | tf_op jit(solution)/shard_map/out_block/pallas_call | solution.py:514
  183.6 60.9 %backward.2 = (bf16[2048,768]{1,0:T(8,128)(2,1)}, bf16[2048,768]{1,0:T(8,128)(2,1)}, f32[8,256]{1,0:T(8,128)}, f32[8,256]{1,0:T(8,128)}, bf16[2048,2048]{1,0:T(8...) custom-call(bf16[2,3,2048,256]{3,2,1,0:T(8,128)(2,1)} %get-tuple-element.49.qk, ...), custom_call_target="tpu_custom_call", output_to_operand_aliasing={{6}: (12, {})} | custom-call | flops 24999999488 | bytes 30000000 | tf_op jit(solution)/shard_map/backward/pallas_call | solution.py:757
  244.5 0.0 copy-start.1
  244.5 57.7 %backward.3 = (bf16[2048,768]{1,0:T(8,128)(2,1)}, bf16[2048,768]{1,0:T(8,128)(2,1)}, f32[8,256]{1,0:T(8,128)}, f32[8,256]{1,0:T(8,128)}, f32[2,512,1024]{2,1,0:T(8,128)}, /*index=5*/bf16[2048,2048]{1,0:T(8,128)(2,1)}) custom-call(bf16[2,3,2048,256]{3,2,1,0:T(8,128)(2,1)} %get-tuple-element.49.qkv_ref, ...), custom_call_target="tpu_custom_call", output_to_operand_aliasing={{5}: (12, {})} | custom-call | flops 24999999488 | bytes 30000000 | tf_op jit(solution)/shard_map/backward/pallas_call | solution.py:757
  302.3 0.0 copy-done.1
  302.3 0.7 add_convert_fusion
  303.0 0.5 slice_reduce_fusion
  303.5 102.0 %grads.1 = (bf16[2,256,2048]{2,1,0:T(8,128)(2,1)}, bf16[2048,256]{1,0:T(8,128)(2,1)}, bf16[2048,256]{1,0:T(8,128)(2,1)}, bf16[2048,256]{1,0:T(8,128)(2,1)}, bf16[256,2048]{1,0:T(8,128)(2,1)}) custom-call(bf16[2048,768]{1,0:T(8,128)(2,1)} %get-tuple-element.58.rest_0_.d0, bf16[2048,768]{1,0:T(8,128)(2,1)} %get-tuple-element.62.d1, ...), custom_call_target="tpu_custom_call" | custom-call | flops 99999997952 | bytes 40000000 | tf_op jit(solution)/shard_map/grads/pallas_call | solution.py:943
  405.5 0.0 copy-start
  405.5 6.6 %deliver.1 = (bf16[2,256,2048]{2,1,0:T(8,128)(2,1)}, bf16[2,256,2048]{2,1,0:T(8,128)(2,1)}, bf16[2048,256]{1,0:T(8,128)(2,1)}, bf16[2048,256]{1,0:T(8,128)(2,1)}...) custom-call(bf16[2,256,2048]{2,1,0:T(8,128)(2,1)} %get-tuple-element.48.refs_0_, ...), custom_call_target="tpu_custom_call" | custom-call | flops 1000000000 | bytes 16000000 | tf_op jit(solution)/shard_map/deliver/pallas_call | solution.py:981
  412.1 0.0 copy-done
  412.2 0.6 copy.21
  (1 shorter events, 0.0 us)
Async XLA Ops:
  244.5 57.8 %copy-start.1 = (f32[8,256]{1,0:T(8,128)S(1)}, f32[8,256]{1,0:T(8,128)}, u32[]{:S(2)}) copy-start(f32[8,256]{1,0:T(8,128)} %get-tuple-element.80) | copy-start | bytes 24580
  405.5 6.6 %copy-start = (f32[8,256]{1,0:T(8,128)S(1)}, f32[8,256]{1,0:T(8,128)}, u32[]{:S(2)}) copy-start(f32[8,256]{1,0:T(8,128)} %get-tuple-element.82) | copy-start | bytes 24580
